TPU v7x, 128 devices: a whole 4x4x4 slice. The times are simulated.
128 devices in a mesh: dp: 16 (over z, y), tp: 8 (over x, core).
Axes of the slice: x: 4, y: 4, z: 4, core: 2. Of those that a mesh axis runs over, the one named last changes fastest.
Arguments:
- hidden: bfloat16 [1024, 640], P('dp')
- w_final: float32 [640], replicated
- emb_table: bfloat16 [262144, 640], P('tp')
- teacher: bfloat16 [1024, 262144], P('dp', 'tp')
- tok_mask: float32 [1024], P('dp')
Outputs:
- output 1: float32 [], replicated
- output 2: bfloat16 [1024, 640], P('dp')
- output 3: float32 [640], replicated
- output 4: float32 [262144, 640], P('tp')
All inputs are finite; a program needn't handle non-finite values.
Results may differ from a plain program's by a relative error of at most 0.001.
Values sent between devices are 32-bit elements.
A program may use at most 1 GiB of HBM per device.

v0:
```python
import jax
import jax.numpy as jnp
from jax import lax
from jax.experimental import pallas as pl
from jax.experimental.pallas import tpu as pltpu
from jax.sharding import PartitionSpec as P


SOFT_CAP = 30.0
INV_CAP = 1.0 / SOFT_CAP
NORM_EPS = 1e-6
SIDE, N_DP, N_TP, LANES = 4, 16, 8, 128
UP, DOWN, AWAY = 1, 3, 2
MIB = 2 ** 20
MESH = pl.DeviceIdType.MESH
VM = pl.BlockSpec(memory_space=pltpu.VMEM)
HB = pl.BlockSpec(memory_space=pltpu.HBM)
F32, BF16 = jnp.float32, jnp.bfloat16
ROWS_BY_ROWS = (((1,), (1,)), ((), ()))
COLS_BY_COLS = (((0,), (0,)), ((), ()))

OFFSETS = tuple((dz, dy) for dz in range(SIDE) for dy in range(SIDE))
ORDER = tuple(sorted(OFFSETS, key=lambda o: -sum(min(d, SIDE - d) for d in o)))


def shift(dp, dz, dy):
    return (dp // SIDE + dz + SIDE) % SIDE * SIDE + (dp % SIDE + dy + SIDE) % SIDE


def aligned(start, size, unit=LANES):
    return pl.ds(pl.multiple_of(start, unit), size)


def hops(kind, dz, dy):
    along_z = [(dz, 0)] if dz % 2 else [(UP if dy < AWAY else DOWN, 0)] * dz
    along_y = [(0, dy)] if dy % 2 else [(0, UP if dz < AWAY else DOWN)] * dy
    return along_y + along_z if kind else along_z + along_y


JOBS = tuple((kind, o) for o in ORDER[:-1] for kind in range(2))
PATHS = tuple(hops(kind, *o) for kind, o in JOBS)
STEPS = tuple((j, level) for level in range(SIDE) for j, path in enumerate(PATHS) if len(path) > level)
MIDDLE = tuple((j, level) for j, level in STEPS if len(PATHS[j]) > level + 1)


def front(hidden, gain_row, mask_row, teacher, table):
    tokens, vocab = teacher.shape
    dim = hidden.shape[1]
    part = vocab // N_DP
    half = tokens // 2
    few = tokens // N_TP
    pack = 16
    sub = 512
    tile = part // 2
    tiles = vocab // tile
    depth = 3

    def kern(hid_hbm, gain_ref, mask_in, tea_ref, tab_ref, got_ref, x_out, tab_out, coef_ref, all_ref, gh_ref, gg_ref,
             hid_ref, w_ref, raw, sends, stage, tabs, n_buf, x_buf, inv_buf, square, pay, pay_got, mask_own, mask_got, x_got, tp_got, own_col,
             own_row, rel, dx, rs_got, ag_own, ag_got, gn_own, gn_got, raw_sem, tab_sem, in_sem, hop_sem, dp_sem, tp_sem):
        me, col = lax.axis_index('dp'), lax.axis_index('tp')
        my_few = aligned(col * few, few, few)

        def fetch(k):
            d = shift(me, *ORDER[k])
            return pltpu.make_async_copy(tea_ref.at[:, aligned(d * part, part)], raw.at[d], raw_sem.at[k])

        def tab_copy(i):
            slot = lax.rem(i, depth)
            return pltpu.make_async_copy(tab_ref.at[aligned(lax.rem(i, tiles) * tile, tile)], tabs.at[slot], tab_sem.at[slot])

        own_hid = pltpu.make_async_copy(hid_hbm, hid_ref, in_sem.at[0])
        own_tab = pltpu.make_async_copy(tab_ref.at[aligned(me * part, part)], tab_out, in_sem.at[1])
        own_hid.start()
        for k in range(N_DP):
            fetch(k).start()
        for i in range(depth - 1):
            tab_copy(i).start()
        own_tab.start()
        barrier = pltpu.get_barrier_semaphore()
        for dz, dy in ORDER[:-1]:
            pl.semaphore_signal(barrier, inc=1, device_id=(shift(me, dz, dy), col), device_id_type=MESH)
        for j in range(1, N_TP):
            pl.semaphore_signal(barrier, inc=1, device_id=(me, (col + j) % N_TP), device_id_type=MESH)

        w_ref[...] = 1.0 + gain_ref[...]
        own_hid.wait()
        hid = hid_ref[...].astype(F32)
        inv = lax.rsqrt(jnp.mean(hid * hid, axis=1, keepdims=True) + NORM_EPS)
        n_buf[...] = hid * inv
        x_buf[...] = (n_buf[...] * w_ref[...]).astype(BF16)
        inv_buf[...] = jnp.broadcast_to(inv, (tokens, LANES))
        pay[...] = n_buf[my_few]
        square[...] = jnp.zeros((LANES, LANES), F32)
        square[0:1, 0:tokens] = mask_in[...]
        mask_own[...] = square[0:few]
        mask_col = jnp.transpose(square[...])[0:tokens, 0:1]
        pl.semaphore_wait(barrier, N_DP + N_TP - 2)

        def remote(src, dst, out, into, dp, tp):
            return pltpu.make_async_remote_copy(src_ref=src, dst_ref=dst, send_sem=out, recv_sem=into, device_id=(dp, tp), device_id_type=MESH)

        def to_dp(src, dst, x):
            def send(o):
                d = shift(me, *o)
                return remote(src, dst.at[me], dp_sem.at[x, 0, d], dp_sem.at[x, 1, me], d, col)

            def came(o):
                d = shift(me, *o)
                return remote(src, dst.at[d], dp_sem.at[x, 0, d], dp_sem.at[x, 1, d], d, col)

            return [send(o) for o in ORDER[:-1]], [came(o) for o in ORDER[:-1]]

        def to_tp(srcs, dst, x):
            def send(j):
                c = (col + j) % N_TP
                return remote(srcs(c), dst.at[col], tp_sem.at[x, 0, c], tp_sem.at[x, 1, col], me, c)

            def came(j):
                c = (col + j) % N_TP
                return remote(srcs(c), dst.at[c], tp_sem.at[x, 0, c], tp_sem.at[x, 1, c], me, c)

            return [send(j) for j in range(1, N_TP)], [came(j) for j in range(1, N_TP)]

        def start(copies):
            for cp in copies:
                cp.start()

        def arrive(copies):
            for cp in copies:
                cp.wait_recv()

        def added(ref, here=slice(None)):
            total = ref[0, here]
            for d in range(1, ref.shape[0]):
                total = total + ref[d, here]
            return total

        def hop(j, level):
            kind, (dz, dy) = JOBS[j]
            tok = pl.ds(kind * half, half)
            src = stage.at[MIDDLE.index((j, level - 1))] if level else sends.at[shift(me, dz, dy), tok]
            dst = stage.at[MIDDLE.index((j, level))] if (j, level) in MIDDLE else got_ref.at[dz * SIDE + dy, tok]
            k = STEPS.index((j, level))
            return remote(src, dst, hop_sem.at[0, k], hop_sem.at[1, k], shift(me, *PATHS[j][level]), col)

        def relay(level):
            for j, at in MIDDLE:
                if at == level:
                    hop(j, level).wait_recv()
                    hop(j, level + 1).start()

        pay_sends, pay_came = to_dp(pay, pay_got, 0)
        start(pay_sends)
        pay_got[me] = pay[...]
        mask_sends, mask_came = to_dp(mask_own, mask_got, 1)
        start(mask_sends)
        mask_got[me] = mask_own[...]

        for k, o in enumerate(ORDER):
            fetch(k).wait()
            d = shift(me, *o)

            def weigh(r, _):
                here = aligned(r * pack, pack, pack)
                cap = jnp.tanh(raw[d, here].astype(F32) * INV_CAP)
                sends[d, here] = jnp.exp(SOFT_CAP * cap - SOFT_CAP)
                return 0

            lax.fori_loop(0, tokens // pack, weigh, 0)
            for j, (_, to) in enumerate(JOBS):
                if to == o:
                    hop(j, 0).start()

        def keep(r, _):
            here = aligned(r * pack, pack, pack)
            got_ref[0, here] = sends[me, here]
            return 0

        lax.fori_loop(0, tokens // pack, keep, 0)

        def fold(v):
            total = v[:, :LANES]
            for c in range(LANES, v.shape[1], LANES):
                total = total + v[:, c:c + LANES]
            return total

        def student(slot, here):
            z = lax.dot_general(x_buf[...], tabs[slot, here], ROWS_BY_ROWS, preferred_element_type=F32)
            ratio = jnp.tanh(z * INV_CAP)
            return ratio, jnp.exp(SOFT_CAP * ratio - SOFT_CAP)

        def forward(i, sums):
            slot = lax.rem(i, depth)
            tab_copy(i).wait()
            tab_copy(i + depth - 1).start()
            s_sum, t_sum, k_sum = sums
            for c in range(0, tile, sub):
                ratio, stu = student(slot, pl.ds(c, sub))
                here = aligned(i % 2 * tile + c, sub)
                cap = jnp.tanh(raw[i // 2, :, here].astype(F32) * INV_CAP)
                tea = sends[i // 2, :, here]
                s_sum = s_sum + fold(stu)
                t_sum = t_sum + fold(tea)
                k_sum = k_sum + fold(tea * (cap - ratio))
            return s_sum, t_sum, k_sum

        zero = jnp.zeros((tokens, LANES), F32)
        s_sum, t_sum, k_sum = lax.fori_loop(0, tiles, forward, (zero, zero, zero))
        lane = lax.broadcasted_iota(jnp.int32, (tokens, LANES), 1)
        sums = jnp.where(lane == 0, jnp.sum(s_sum, axis=1, keepdims=True), 0.0)
        sums = jnp.where(lane == 1, jnp.sum(t_sum, axis=1, keepdims=True), sums)
        sums = jnp.where(lane == AWAY, SOFT_CAP * jnp.sum(k_sum, axis=1, keepdims=True), sums)
        own_col[...] = sums
        tp_got[col] = sums
        tp_sends, tp_came = to_tp(lambda c: own_col, tp_got, 0)
        start(tp_sends)
        arrive(tp_came)
        total = added(tp_got)
        square[0:tokens] = jnp.where(lane == DOWN, mask_col, total)
        line = jnp.transpose(square[...])[0:few]
        own_row[...] = line
        all_ref[me] = line
        dp_sends, dp_came = to_dp(own_row, all_ref, 2)
        start(dp_sends)
        relay(0)

        arrive((*pay_came, *mask_came))
        x_got[col] = pay_got[...]
        xt_sends, xt_came = to_tp(lambda c: pay_got, x_got, 1)
        start(xt_sends)
        count = jnp.sum(added(mask_got, slice(1)), axis=1, keepdims=True)
        inv_s, inv_t, weight = 1.0 / total[:, 0:1], 1.0 / total[:, 1:2], mask_col / count
        dx[...] = jnp.zeros((tokens, dim), F32)

        def backward(i, _):
            slot = lax.rem(i, depth)
            tab_copy(i).wait()

            @pl.when(i + depth - 1 < 2 * tiles)
            def _():
                tab_copy(i + depth - 1).start()

            for c in range(0, tile, sub):
                here = pl.ds(c, sub)
                ratio, stu = student(slot, here)
                tea = sends[(i - tiles) // 2, :, aligned(i % 2 * tile + c, sub)]
                diff = (stu * inv_s - tea * inv_t) * weight
                g = (diff * (1.0 - ratio * ratio)).astype(BF16)
                dx[...] += jnp.dot(g, tabs[slot, here], preferred_element_type=F32)
            return 0

        lax.fori_loop(tiles, 2 * tiles, backward, 0)
        relay(1)

        rs_got[col] = dx[my_few]
        rs_sends, rs_came = to_tp(lambda c: dx.at[aligned(c * few, few, few)], rs_got, 2)
        start(rs_sends)
        arrive(rs_came)
        my_x = added(rs_got)
        my_n = n_buf[my_few]
        grad_n = my_x * w_ref[...]
        my_h = inv_buf[my_few, 0:1] * (grad_n - my_n * jnp.mean(grad_n * my_n, axis=1, keepdims=True))
        ag_own[...] = jnp.zeros((2 * few, dim), F32)
        ag_own[0:few] = my_h
        ag_own[few:few + 1] = jnp.sum(my_x * my_n, axis=0, keepdims=True)
        ag_got[col] = ag_own[...]
        ag_sends, ag_came = to_tp(lambda c: ag_own, ag_got, DOWN)
        start(ag_sends)
        arrive(ag_came)
        gh_ref[...] = jnp.concatenate([ag_got[j, 0:few] for j in range(N_TP)], axis=0)
        line = added(ag_got, slice(few, 2 * few))
        gn_own[...] = line
        gn_got[me] = line
        gn_sends, gn_came = to_dp(gn_own, gn_got, DOWN)
        start(gn_sends)

        arrive(xt_came)

        def widen(d, _):
            rows = jnp.concatenate([x_got[j, d] for j in range(N_TP)], axis=0)
            x_out[aligned(d * tokens, tokens, tokens)] = (rows * w_ref[...]).astype(BF16)
            return 0

        lax.fori_loop(0, N_DP, widen, 0)
        arrive(dp_came)
        row = lax.broadcasted_iota(jnp.int32, (few, LANES), 0)
        lanes = lax.broadcasted_iota(jnp.int32, (few, LANES), 1)
        for d in range(N_DP):
            block = all_ref[d]
            safe = jnp.where((row < AWAY) & (lanes < tokens), block, 1.0)
            rel[d * few:(d + 1) * few] = jnp.where(row < AWAY, 1.0 / safe, block / count)
        for k, (dz, dy) in enumerate(OFFSETS):
            square[k * few:(k + 1) * few] = rel[aligned(shift(me, -dz, -dy) * few, few, few)]
        coef_ref[...] = jnp.transpose(square[...])

        relay(2)
        arrive(gn_came)
        gg_ref[...] = added(gn_got)
        own_tab.wait()
        for j, path in enumerate(PATHS):
            hop(j, len(path) - 1).wait_recv()
        for j, level in STEPS:
            hop(j, level).wait_send()
        for cp in (*pay_sends, *mask_sends, *tp_sends, *dp_sends, *xt_sends, *rs_sends, *ag_sends, *gn_sends):
            cp.wait_send()

    dma = pltpu.SemaphoreType.DMA
    wide, flat = (tokens, dim), (few, LANES)
    return pl.pallas_call(
        kern,
        out_shape=tuple(jax.ShapeDtypeStruct(shape, kind) for shape, kind in (
            ((N_DP, tokens, part), F32), ((N_DP * tokens, dim), BF16), ((part, dim), BF16), ((LANES, LANES), F32), ((N_DP, *flat), F32), (wide, F32),
            ((few, dim), F32))),
        in_specs=[HB, VM, VM, HB, HB], out_specs=(VM,) * 7,
        scratch_shapes=[pltpu.VMEM(shape, kind) for shape, kind in (
            (wide, BF16), ((1, dim), F32), ((N_DP, tokens, part), BF16), ((N_DP, tokens, part), F32), ((len(MIDDLE), half, part), F32),
            ((depth, tile, dim), BF16), (wide, F32), (wide, BF16), ((tokens, LANES), F32), ((LANES, LANES), F32), ((few, dim), F32),
            ((N_DP, few, dim), F32), (flat, F32), ((N_DP, *flat), F32), ((N_TP, N_DP, few, dim), F32), ((N_TP, tokens, LANES), F32),
            ((tokens, LANES), F32), (flat, F32), ((LANES, LANES), F32), (wide, F32), ((N_TP, few, dim), F32), ((2 * few, dim), F32),
            ((N_TP, 2 * few, dim), F32), ((few, dim), F32), ((N_DP, few, dim), F32))] + [
            dma((N_DP,)), dma((depth,)), dma((2,)), dma((2, len(STEPS))), dma((SIDE, 2, N_DP)), dma((SIDE, 2, N_TP))],
        compiler_params=pltpu.CompilerParams(collective_id=0, has_side_effects=True, vmem_limit_bytes=40 * MIB),
        cost_estimate=pl.CostEstimate(flops=3 * 10 ** 9, bytes_accessed=100 * MIB, transcendentals=0), name='front')(
            pltpu.with_memory_space_constraint(hidden, pltpu.HBM), gain_row, mask_row,
            pltpu.with_memory_space_constraint(teacher, pltpu.HBM), pltpu.with_memory_space_constraint(table, pltpu.HBM))


def finish(teas, x_all, tab_part, coef, block):
    tokens, part = teas.shape[1:]
    total, dim = x_all.shape
    span = part // SIDE
    few = LANES // N_DP

    def kern(tea_ref, x_ref, tab_ref, coef_ref, out_ref, z_buf, g_buf):
        me = lax.axis_index('dp')
        mine = pl.ds(block * span, span)
        z_buf[...] = lax.dot_general(x_ref[...], tab_ref[mine], ROWS_BY_ROWS, preferred_element_type=F32)
        for k, (dz, dy) in enumerate(OFFSETS):
            here = aligned(shift(me, -dz, -dy) * tokens, tokens, tokens)
            ratio = jnp.tanh(z_buf[here] * INV_CAP)
            stu = jnp.exp(SOFT_CAP * ratio - SOFT_CAP)
            inv_s, inv_t, _, weight = (coef_ref[0:tokens, k * few + i:k * few + i + 1] for i in range(SIDE))
            diff = (stu * inv_s - tea_ref[k, :, mine] * inv_t) * weight
            g_buf[here] = (diff * (1.0 - ratio * ratio)).astype(BF16)
        out_ref[...] = lax.dot_general(g_buf[...], x_ref[...], COLS_BY_COLS, preferred_element_type=F32)

    return pl.pallas_call(kern, out_shape=jax.ShapeDtypeStruct((span, dim), F32), in_specs=[VM] * 4, out_specs=VM,
        scratch_shapes=[pltpu.VMEM((total, span), F32), pltpu.VMEM((total, span), BF16)], name='finish',
        compiler_params=pltpu.CompilerParams(vmem_limit_bytes=22 * MIB),
        cost_estimate=pl.CostEstimate(flops=10 ** 9, bytes_accessed=8 * MIB, transcendentals=0))(teas, x_all, tab_part, coef)


def place(table, pieces, vocab):
    arrays = [p[0] for p in pieces]
    n = len(arrays)
    dim = arrays[0].shape[1]
    rows = vocab // N_DP
    cut = 256
    chunks = [(i, r) for i in range(n) for r in range(0, arrays[i].shape[0], cut)]
    size = sum(a.size for a in arrays)

    def kern(*refs):
        dst, sem = refs[-2], refs[-1]
        me = lax.axis_index('dp')
        copies = []
        for k, (i, r) in enumerate(chunks):
            _, dz, dy, first = pieces[i]
            there = aligned(shift(me, dz, dy) * rows + first + r, cut, cut)
            copies.append(pltpu.make_async_copy(refs[i].at[pl.ds(r, cut)], dst.at[there], sem.at[k]))
        for cp in copies:
            cp.start()
        for cp in copies:
            cp.wait()

    args = arrays if table is None else [*arrays, table]
    return pl.pallas_call(kern, out_shape=jax.ShapeDtypeStruct((vocab, dim), F32), in_specs=[VM] * n + [HB] * (len(args) - n), out_specs=HB,
        scratch_shapes=[pltpu.SemaphoreType.DMA((len(chunks),))], input_output_aliases={} if table is None else {n: 0}, name='place',
        compiler_params=pltpu.CompilerParams(vmem_limit_bytes=4 * size + MIB),
        cost_estimate=pl.CostEstimate(flops=10 * MIB, bytes_accessed=8 * size, transcendentals=0))(*args)


def gather(blocks, vocab):
    quarter = blocks[0].shape[0]
    sets, ways = range(2), (UP, DOWN)
    table, event = None, 0

    def send(pair, axis, step):
        out = []
        for k in sets:
            dz, dy = (step, 0) if axis == k else (0, step)
            out.append(lax.ppermute(pair[k], 'dp', [(d, shift(d, dz, dy)) for d in range(N_DP)]))
        return out

    def put(pair, a, b, c=0):
        return [(pair[k], *((b, a) if k else (a, b)), (2 * k + c) * quarter) for k in sets]

    def settle(*pieces):
        nonlocal table
        table = place(table, [p for ps in pieces for p in ps], vocab)

    def wait(*pairs):
        nonlocal table, event
        event += 1
        table, *flat = lax.optimization_barrier((table, *(x for pair in pairs for x in pair)))
        return [flat[2 * i:2 * i + 2] for i in range(len(pairs))]

    def join(one, other):
        return [jnp.concatenate(pair) for pair in zip(one, other)]

    own = [[blocks[c], blocks[2 + c]] for c in range(2)]
    low, high = ([send(own[c], 0, way) for c in range(2)] for way in ways)
    whole = join(*own)
    side = {way: send(whole, 1, way) for way in ways}
    settle(put(own[0], 0, 0, 0), put(own[1], 0, 0, 1))

    low[0], high[0] = wait(low[0], high[0])
    far_low = send(low[0], 0, UP)
    settle(put(low[0], DOWN, 0, 0), put(high[0], UP, 0, 0))

    low[1], high[1] = wait(low[1], high[1])
    far_high = send(high[1], 0, DOWN)
    low_whole, high_whole = join(*low), join(*high)
    low_side = {way: send(low_whole, 1, way) for way in ways}
    settle(put(low[1], DOWN, 0, 1), put(high[1], UP, 0, 1))

    side[UP], side[DOWN], high_whole = wait(side[UP], side[DOWN], high_whole)
    high_side = {way: send(high_whole, 1, way) for way in ways}
    side_far = send(side[UP], 1, UP)
    settle(put(side[UP], 0, DOWN))
    settle(put(side[DOWN], 0, UP))

    far_low, far_high = wait(far_low, far_high)
    far_side = {(c, way): send(pair, 1, way) for way in ways for c, pair in enumerate((far_low, far_high))}
    settle(put(far_low, AWAY, 0, 0), put(far_high, AWAY, 0, 1))

    low_side[UP], low_side[DOWN] = wait(low_side[UP], low_side[DOWN])
    low_far = send(low_side[DOWN], 1, DOWN)
    settle(put(low_side[UP], DOWN, DOWN))
    settle(put(low_side[DOWN], DOWN, UP))

    high_side[UP], high_side[DOWN] = wait(high_side[UP], high_side[DOWN])
    high_far = [send([x[:quarter] for x in high_side[UP]], 1, UP), send([x[quarter:] for x in high_side[DOWN]], 1, DOWN)]
    settle(put(high_side[UP], UP, DOWN))
    settle(put(high_side[DOWN], UP, UP))

    far_side[0, DOWN], far_side[1, DOWN], side_far = wait(far_side[0, DOWN], far_side[1, DOWN], side_far)
    last_down = send(far_side[1, DOWN], 1, DOWN)
    settle(put(far_side[0, DOWN], AWAY, UP, 0), put(far_side[1, DOWN], AWAY, UP, 1))
    settle(put(side_far, 0, AWAY))

    far_side[0, UP], = wait(far_side[0, UP])
    last_up = send(far_side[0, UP], 1, UP)
    settle(put(far_side[0, UP], AWAY, DOWN, 0))

    far_side[1, UP], low_far = wait(far_side[1, UP], low_far)
    settle(put(far_side[1, UP], AWAY, DOWN, 1))
    settle(put(low_far, DOWN, AWAY))

    high_far = wait(*high_far)
    settle(put(high_far[0], UP, AWAY, 0), put(high_far[1], UP, AWAY, 1))
    last_up, last_down = wait(last_up, last_down)
    settle(put(last_up, AWAY, AWAY, 0), put(last_down, AWAY, AWAY, 1))
    return table


def solution(mesh):
    def local_step(hid_rows, w_final, tab_rows, tea_rows, mask_rows):
        tokens = hid_rows.shape[0]
        teas, x_all, tab_part, coef, stats, grad_h, gain_lines = front(hid_rows, w_final[None], mask_rows[None], tea_rows, tab_rows)
        blocks = [None] * SIDE
        for i in (0, 2, 1, 3):
            blocks[i] = finish(teas, x_all, tab_part, coef, i)
            coef, blocks[i] = lax.optimization_barrier((coef, blocks[i]))
        table = gather(blocks, tab_rows.shape[0])
        s_sum, t_sum, k_sum, masks = (stats[:, i, :tokens] for i in range(SIDE))
        all_kl = k_sum / t_sum + jnp.log(s_sum) - jnp.log(t_sum)
        loss_val = jnp.sum(masks * all_kl) / jnp.sum(masks)
        return loss_val, grad_h.astype(BF16), gain_lines[0], table

    return jax.shard_map(local_step, mesh=mesh, in_specs=(P('dp', None), P(None), P('tp', None), P('dp', 'tp'), P('dp')), out_specs=(P(), P('dp', None), P(None), P('tp', None)), check_vma=False)
```

profile of v0, /device:TPU:0, one launch (start us, length us, event | category | flops | bytes accessed | tf_op | source)
XLA Modules:
  0.0 647.2 jit_solution(8851908512624947880)
XLA Ops:
  2.0 111.8 %front.1 = (f32[16,64,2048]{2,1,0:T(8,128)S(1)}, bf16[1024,640]{1,0:T(8,128)(2,1)S(1)}, bf16[2048,640]{1,0:T(8,128)(2,1)S(1)}, f32[128,128]{1,0:T(8,128)S(1)}, f...) custom-call(bf16[64,640]{1,0:T(8,128)(2,1)} %hid_hbm.1, ...), custom_call_target="tpu_custom_call" | custom-call | flops 3000000000 | bytes 104857600 | tf_op jit(solution)/shard_map/front/pallas_call | solution.py:310
  113.8 3.6 finish.4.refs_0_
  117.7 3.6 finish.5.refs_1_
  121.4 3.1 collective-permute-start.2
  124.4 3.2 collective-permute-start.3
  127.6 3.6 finish.6.refs_2_
  131.3 3.6 finish.7.refs_3_
  135.1 15.2 %collective-permute-done.refs_0_ = f32[512,640]{1,0:T(8,128)S(1)} collective-permute-done((f32[512,640]{1,0:T(8,128)S(1)}, f32[512,640]{1,0:T(8,128)S(1)}, u32[]{:S(2)}, u32[]{:S(2)}) %collective-permute-start) | collective-permute-done | bytes 1310752 | tf_op jit(solution)/shard_map/ppermute | solution.py:392
  150.5 3.7 collective-permute-done.1.refs_1_
  157.5 20.9 %collective-permute-done.4.refs_0_ = f32[512,640]{1,0:T(8,128)S(1)} collective-permute-done((f32[512,640]{1,0:T(8,128)S(1)}, f32[512,640]{1,0:T(8,128)S(1)}, u32[]{:S(2)}, u32[]{:S(2)}) %collective-permute-start.4) | collective-permute-done | bytes 1310752 | tf_op jit(solution)/shard_map/ppermute | solution.py:392
  179.4 3.7 collective-permute-done.5.refs_1_
  183.6 2.0 collective-permute-start.11
  185.6 2.4 place.17.refs_4_
  188.0 2.4 place.18.refs_4_
  190.5 71.6 %collective-permute-done.7.refs_3_ = f32[512,640]{1,0:T(8,128)S(1)} collective-permute-done((f32[512,640]{1,0:T(8,128)S(1)}, f32[512,640]{1,0:T(8,128)S(1)}, u32[]{:S(2)}, u32[]{:S(2)}) %collective-permute-start.7) | collective-permute-done | bytes 1310752 | tf_op jit(solution)/shard_map/ppermute | solution.py:392
  264.1 3.2 collective-permute-start.14
  272.6 22.3 %collective-permute-done.12.refs_0_ = f32[512,640]{1,0:T(8,128)S(1)} collective-permute-done((f32[512,640]{1,0:T(8,128)S(1)}, f32[512,640]{1,0:T(8,128)S(1)}, u32[]{:S(2)}, u32[]{:S(2)}) %collective-permute-start.12) | collective-permute-done | bytes 1310752 | tf_op jit(solution)/shard_map/ppermute | solution.py:392
  294.9 3.7 collective-permute-start.18
  298.7 3.2 collective-permute-start.19
  301.8 2.4 place.19.refs_2_
  304.2 2.7 pad_maximum_fusion
  307.0 2.4 place.20.refs_2_
  309.4 2.7 place.21.refs_4_
  312.1 68.1 %collective-permute-done.15.refs_3_ = f32[512,640]{1,0:T(8,128)S(1)} collective-permute-done((f32[512,640]{1,0:T(8,128)S(1)}, f32[512,640]{1,0:T(8,128)S(1)}, u32[]{:S(2)}, u32[]{:S(2)}) %collective-permute-start.15) | collective-permute-done | bytes 1310752 | tf_op jit(solution)/shard_map/ppermute | solution.py:392
  380.3 3.7 collective-permute-start.24
  386.1 27.0 %collective-permute-done.24.refs_0_ = f32[512,640]{1,0:T(8,128)S(1)} collective-permute-done((f32[512,640]{1,0:T(8,128)S(1)}, f32[512,640]{1,0:T(8,128)S(1)}, u32[]{:S(2)}, u32[]{:S(2)}) %collective-permute-start.24) | collective-permute-done | bytes 1310752 | tf_op jit(solution)/shard_map/ppermute | solution.py:392
  416.7 20.4 %collective-permute-done.26.refs_2_ = f32[512,640]{1,0:T(8,128)} collective-permute-done((f32[512,640]{1,0:T(8,128)S(1)}, f32[512,640]{1,0:T(8,128)}, u32[]{:S(2)}, u32[]{:S(2)}) %collective-permute-start.26) | collective-permute-done | bytes 1310752 | tf_op jit(solution)/shard_map/ppermute | solution.py:392
  437.1 3.9 collective-permute-start.22
  441.0 3.2 collective-permute-start.23
  444.2 56.5 %collective-permute-done.32.refs_0_ = f32[512,640]{1,0:T(8,128)S(1)} collective-permute-done((f32[512,640]{1,0:T(8,128)S(1)}, f32[512,640]{1,0:T(8,128)S(1)}, u32[]{:S(2)}, u32[]{:S(2)}) %collective-permute-start.32) | collective-permute-done | bytes 1310752 | tf_op jit(solution)/shard_map/ppermute | solution.py:392
  501.8 2.4 place.22.refs_2_
  504.3 3.3 collective-permute-start.34
  507.5 3.2 collective-permute-start.35
  510.8 2.4 place.23.refs_2_
  513.2 4.9 place.24.refs_2_
  520.5 66.1 %collective-permute-done.33.refs_1_ = f32[512,640]{1,0:T(8,128)S(1)} collective-permute-done((f32[512,640]{1,0:T(8,128)S(1)}, f32[512,640]{1,0:T(8,128)S(1)}, u32[]{:S(2)}, u32[]{:S(2)}) %collective-permute-start.33) | collective-permute-done | bytes 1310752 | tf_op jit(solution)/shard_map/ppermute | solution.py:392
  588.1 3.2 collective-permute-start.38
  592.5 2.4 place.25.refs_2_
  594.9 2.7 place.26.refs_4_
  598.4 4.1 place.27.refs_2_
  602.6 3.1 collective-permute-start.39
  605.7 2.4 place.28.refs_2_
  611.6 8.1 %collective-permute-done.37.refs_1_ = f32[512,640]{1,0:T(8,128)} collective-permute-done((f32[512,640]{1,0:T(8,128)}, f32[512,640]{1,0:T(8,128)}, u32[]{:S(2)}, u32[]{:S(2)}) %collective-permute-start.37) | collective-permute-done | bytes 1310752 | tf_op jit(solution)/shard_map/ppermute | solution.py:392
  619.7 3.2 collective-permute-start.43
  626.2 3.4 place.29.refs_2_
  631.2 4.9 place.31.refs_4_
  636.1 4.9 place.32.refs_4_
  641.1 4.9 place.33
  (101 shorter events, 33.7 us)
Async XLA Ops:
  117.4 32.9 %collective-permute-start = (f32[512,640]{1,0:T(8,128)S(1)}, f32[512,640]{1,0:T(8,128)S(1)}, u32[]{:S(2)}, u32[]{:S(2)}) collective-permute-start(f32[512,640]{1,0:T(8,128)S(1)} %finish.4.refs_0_), channel_id=1, source_target_pairs={{0,32},{8,40},{16,48},{24,56},{32,64},{40,72},{48,80},{56,88},{64,... | collective-permute-start | bytes 3932168 | tf_op jit(solution)/shard_map/ppermute | solution.py:392
  121.3 32.9 %collective-permute-start.1 = (f32[512,640]{1,0:T(8,128)S(1)}, f32[512,640]{1,0:T(8,128)S(1)}, u32[]{:S(2)}, u32[]{:S(2)}) collective-permute-start(f32[512,640]{1,0:T(8,128)S(1)} %finish.5.refs_1_), channel_id=1, source_target_pairs={{0,8},{8,16},{16,24},{24,0},{32,40},{40,48},{48,56},{56,32},{64,72... | collective-permute-start | bytes 3932168 | tf_op jit(solution)/shard_map/ppermute | solution.py:392
  121.4 32.9 %collective-permute-start.2 = (f32[512,640]{1,0:T(8,128)S(1)}, f32[512,640]{1,0:T(8,128)S(1)}, u32[]{:S(2)}, u32[]{:S(2)}) collective-permute-start(f32[512,640]{1,0:T(8,128)S(1)} %finish.4.refs_0_), channel_id=1, source_target_pairs={{0,96},{8,104},{16,112},{24,120},{32,0},{40,8},{48,16},{56,24},{64... | collective-permute-start | bytes 3932168 | tf_op jit(solution)/shard_map/ppermute | solution.py:392
  124.4 31.4 %collective-permute-start.3 = (f32[512,640]{1,0:T(8,128)S(1)}, f32[512,640]{1,0:T(8,128)S(1)}, u32[]{:S(2)}, u32[]{:S(2)}) collective-permute-start(f32[512,640]{1,0:T(8,128)S(1)} %finish.5.refs_1_), channel_id=1, source_target_pairs={{0,24},{8,0},{16,8},{24,16},{32,56},{40,32},{48,40},{56,48},{64,88... | collective-permute-start | bytes 3932168 | tf_op jit(solution)/shard_map/ppermute | solution.py:392
  131.2 47.2 %collective-permute-start.4 = (f32[512,640]{1,0:T(8,128)S(1)}, f32[512,640]{1,0:T(8,128)S(1)}, u32[]{:S(2)}, u32[]{:S(2)}) collective-permute-start(f32[512,640]{1,0:T(8,128)S(1)} %finish.6.refs_2_), channel_id=1, source_target_pairs={{0,32},{8,40},{16,48},{24,56},{32,64},{40,72},{48,80},{56,88},{64,... | collective-permute-start | bytes 3932168 | tf_op jit(solution)/shard_map/ppermute | solution.py:392
  150.3 32.9 %collective-permute-start.5 = (f32[512,640]{1,0:T(8,128)S(1)}, f32[512,640]{1,0:T(8,128)S(1)}, u32[]{:S(2)}, u32[]{:S(2)}) collective-permute-start(f32[512,640]{1,0:T(8,128)S(1)} %finish.7.refs_3_), channel_id=1, source_target_pairs={{0,8},{8,16},{16,24},{24,0},{32,40},{40,48},{48,56},{56,32},{64,72... | collective-permute-start | bytes 3932168 | tf_op jit(solution)/shard_map/ppermute | solution.py:392
  154.2 109.0 %collective-permute-start.8 = (f32[1024,640]{1,0:T(8,128)S(1)}, f32[1024,640]{1,0:T(8,128)S(1)}, u32[]{:S(2)}, u32[]{:S(2)}) collective-permute-start(f32[1024,640]{1,0:T(8,128)S(1)} %constant_dynamic-update-slice_fusion), channel_id=1, source_target_pairs={{0,8},{8,16},{16,24},{24,0},{32,40},{40,48},{48,56},{56,32},{64,72... | collective-permute-start | bytes 7864328 | tf_op jit(solution)/shard_map/ppermute | solution.py:392
  154.2 109.9 %collective-permute-start.9 = (f32[1024,640]{1,0:T(8,128)S(1)}, f32[1024,640]{1,0:T(8,128)S(1)}, u32[]{:S(2)}, u32[]{:S(2)}) collective-permute-start(f32[1024,640]{1,0:T(8,128)S(1)} %constant_dynamic-update-slice_fusion.2), channel_id=1, source_target_pairs={{0,32},{8,40},{16,48},{24,56},{32,64},{40,72},{48,80},{56,88},{64,... | collective-permute-start | bytes 7864328 | tf_op jit(solution)/shard_map/ppermute | solution.py:392
  155.8 27.7 %collective-permute-start.6 = (f32[512,640]{1,0:T(8,128)S(1)}, f32[512,640]{1,0:T(8,128)S(1)}, u32[]{:S(2)}, u32[]{:S(2)}) collective-permute-start(f32[512,640]{1,0:T(8,128)S(1)} %finish.6.refs_2_), channel_id=1, source_target_pairs={{0,96},{8,104},{16,112},{24,120},{32,0},{40,8},{48,16},{56,24},{64... | collective-permute-start | bytes 3932168 | tf_op jit(solution)/shard_map/ppermute | solution.py:392
  178.4 90.1 %collective-permute-start.10 = (f32[1024,640]{1,0:T(8,128)S(1)}, f32[1024,640]{1,0:T(8,128)S(1)}, u32[]{:S(2)}, u32[]{:S(2)}) collective-permute-start(f32[1024,640]{1,0:T(8,128)S(1)} %constant_dynamic-update-slice_fusion), channel_id=1, source_target_pairs={{0,24},{8,0},{16,8},{24,16},{32,56},{40,32},{48,40},{56,48},{64,88... | collective-permute-start | bytes 7864328 | tf_op jit(solution)/shard_map/ppermute | solution.py:392
  183.2 78.9 %collective-permute-start.7 = (f32[512,640]{1,0:T(8,128)S(1)}, f32[512,640]{1,0:T(8,128)S(1)}, u32[]{:S(2)}, u32[]{:S(2)}) collective-permute-start(f32[512,640]{1,0:T(8,128)S(1)} %finish.7.refs_3_), channel_id=1, source_target_pairs={{0,24},{8,0},{16,8},{24,16},{32,56},{40,32},{48,40},{56,48},{64,88... | collective-permute-start | bytes 3932168 | tf_op jit(solution)/shard_map/ppermute | solution.py:392
  183.6 89.0 %collective-permute-start.11 = (f32[1024,640]{1,0:T(8,128)S(1)}, f32[1024,640]{1,0:T(8,128)S(1)}, u32[]{:S(2)}, u32[]{:S(2)}) collective-permute-start(f32[1024,640]{1,0:T(8,128)S(1)} %constant_dynamic-update-slice_fusion.2), channel_id=1, source_target_pairs={{0,96},{8,104},{16,112},{24,120},{32,0},{40,8},{48,16},{56,24},{64... | collective-permute-start | bytes 7864328 | tf_op jit(solution)/shard_map/ppermute | solution.py:392
  262.1 32.9 %collective-permute-start.12 = (f32[512,640]{1,0:T(8,128)S(1)}, f32[512,640]{1,0:T(8,128)S(1)}, u32[]{:S(2)}, u32[]{:S(2)}) collective-permute-start(f32[512,640]{1,0:T(8,128)S(1)} %collective-permute-done.refs_0_), channel_id=1, source_target_pairs={{0,32},{8,40},{16,48},{24,56},{32,64},{40,72},{48,80},{56,88},{64,... | collective-permute-start | bytes 3932168 | tf_op jit(solution)/shard_map/ppermute | solution.py:392
  263.2 35.4 %collective-permute-start.13 = (f32[512,640]{1,0:T(8,128)S(1)}, f32[512,640]{1,0:T(8,128)S(1)}, u32[]{:S(2)}, u32[]{:S(2)}) collective-permute-start(f32[512,640]{1,0:T(8,128)S(1)} %collective-permute-done.1.refs_1_), channel_id=1, source_target_pairs={{0,8},{8,16},{16,24},{24,0},{32,40},{40,48},{48,56},{56,32},{64,72... | collective-permute-start | bytes 3932168 | tf_op jit(solution)/shard_map/ppermute | solution.py:392
  264.1 34.6 %collective-permute-start.14 = (f32[512,640]{1,0:T(8,128)S(1)}, f32[512,640]{1,0:T(8,128)S(1)}, u32[]{:S(2)}, u32[]{:S(2)}) collective-permute-start(f32[512,640]{1,0:T(8,128)S(1)} %collective-permute-done.6.refs_2_), channel_id=1, source_target_pairs={{0,96},{8,104},{16,112},{24,120},{32,0},{40,8},{48,16},{56,24},{64... | collective-permute-start | bytes 3932168 | tf_op jit(solution)/shard_map/ppermute | solution.py:392
  268.5 115.4 %collective-permute-start.16 = (f32[1024,640]{1,0:T(8,128)}, f32[1024,640]{1,0:T(8,128)S(1)}, u32[]{:S(2)}, u32[]{:S(2)}) collective-permute-start(f32[1024,640]{1,0:T(8,128)} %constant_dynamic-update-slice_fusion.4), channel_id=1, source_target_pairs={{0,8},{8,16},{16,24},{24,0},{32,40},{40,48},{48,56},{56,32},{64,72... | collective-permute-start | bytes 7864328 | tf_op jit(solution)/shard_map/ppermute | solution.py:392
  272.6 111.4 %collective-permute-start.17 = (f32[1024,640]{1,0:T(8,128)}, f32[1024,640]{1,0:T(8,128)S(1)}, u32[]{:S(2)}, u32[]{:S(2)}) collective-permute-start(f32[1024,640]{1,0:T(8,128)} %constant_dynamic-update-slice_fusion.6), channel_id=1, source_target_pairs={{0,32},{8,40},{16,48},{24,56},{32,64},{40,72},{48,80},{56,88},{64,... | collective-permute-start | bytes 7864328 | tf_op jit(solution)/shard_map/ppermute | solution.py:392
  294.9 89.1 %collective-permute-start.18 = (f32[1024,640]{1,0:T(8,128)}, f32[1024,640]{1,0:T(8,128)}, u32[]{:S(2)}, u32[]{:S(2)}) collective-permute-start(f32[1024,640]{1,0:T(8,128)} %constant_dynamic-update-slice_fusion.4), channel_id=1, source_target_pairs={{0,24},{8,0},{16,8},{24,16},{32,56},{40,32},{48,40},{56,48},{64,88... | collective-permute-start | bytes 7864328 | tf_op jit(solution)/shard_map/ppermute | solution.py:392
  298.6 81.6 %collective-permute-start.15 = (f32[512,640]{1,0:T(8,128)S(1)}, f32[512,640]{1,0:T(8,128)S(1)}, u32[]{:S(2)}, u32[]{:S(2)}) collective-permute-start(f32[512,640]{1,0:T(8,128)S(1)} %collective-permute-done.7.refs_3_), channel_id=1, source_target_pairs={{0,24},{8,0},{16,8},{24,16},{32,56},{40,32},{48,40},{56,48},{64,88... | collective-permute-start | bytes 3932168 | tf_op jit(solution)/shard_map/ppermute | solution.py:392
  298.7 85.5 %collective-permute-start.19 = (f32[1024,640]{1,0:T(8,128)}, f32[1024,640]{1,0:T(8,128)}, u32[]{:S(2)}, u32[]{:S(2)}) collective-permute-start(f32[1024,640]{1,0:T(8,128)} %constant_dynamic-update-slice_fusion.6), channel_id=1, source_target_pairs={{0,96},{8,104},{16,112},{24,120},{32,0},{40,8},{48,16},{56,24},{64... | collective-permute-start | bytes 7864328 | tf_op jit(solution)/shard_map/ppermute | solution.py:392
  309.4 107.3 %copy-start.10 = (f32[1024,640]{1,0:T(8,128)S(1)}, f32[1024,640]{1,0:T(8,128)}, u32[]{:S(2)}) copy-start(f32[1024,640]{1,0:T(8,128)} %get-tuple-element.114) | copy-start | bytes 7864324
  309.4 127.7 %copy-start.9 = (f32[1024,640]{1,0:T(8,128)S(1)}, f32[1024,640]{1,0:T(8,128)}, u32[]{:S(2)}) copy-start(f32[1024,640]{1,0:T(8,128)} %get-tuple-element.115) | copy-start | bytes 7864324
  380.3 32.9 %collective-permute-start.24 = (f32[512,640]{1,0:T(8,128)S(1)}, f32[512,640]{1,0:T(8,128)S(1)}, u32[]{:S(2)}, u32[]{:S(2)}) collective-permute-start(f32[512,640]{1,0:T(8,128)S(1)} %collective-permute-done.12.refs_0_), channel_id=1, source_target_pairs={{0,24},{8,0},{16,8},{24,16},{32,56},{40,32},{48,40},{56,48},{64,88... | collective-permute-start | bytes 3932168 | tf_op jit(solution)/shard_map/ppermute | solution.py:392
  384.0 31.6 %collective-permute-start.25 = (f32[512,640]{1,0:T(8,128)S(1)}, f32[512,640]{1,0:T(8,128)S(1)}, u32[]{:S(2)}, u32[]{:S(2)}) collective-permute-start(f32[512,640]{1,0:T(8,128)S(1)} %collective-permute-done.13.refs_1_), channel_id=1, source_target_pairs={{0,96},{8,104},{16,112},{24,120},{32,0},{40,8},{48,16},{56,24},{64... | collective-permute-start | bytes 3932168 | tf_op jit(solution)/shard_map/ppermute | solution.py:392
  384.0 53.1 %collective-permute-start.26 = (f32[512,640]{1,0:T(8,128)S(1)}, f32[512,640]{1,0:T(8,128)}, u32[]{:S(2)}, u32[]{:S(2)}) collective-permute-start(f32[512,640]{1,0:T(8,128)S(1)} %collective-permute-done.14.refs_2_), channel_id=1, source_target_pairs={{0,24},{8,0},{16,8},{24,16},{32,56},{40,32},{48,40},{56,48},{64,88... | collective-permute-start | bytes 3932168 | tf_op jit(solution)/shard_map/ppermute | solution.py:392
  384.1 53.1 %collective-permute-start.27 = (f32[512,640]{1,0:T(8,128)S(1)}, f32[512,640]{1,0:T(8,128)}, u32[]{:S(2)}, u32[]{:S(2)}) collective-permute-start(f32[512,640]{1,0:T(8,128)S(1)} %collective-permute-done.15.refs_3_), channel_id=1, source_target_pairs={{0,96},{8,104},{16,112},{24,120},{32,0},{40,8},{48,16},{56,24},{64... | collective-permute-start | bytes 3932168 | tf_op jit(solution)/shard_map/ppermute | solution.py:392
  384.2 56.8 %collective-permute-start.30 = (f32[512,640]{1,0:T(8,128)S(1)}, f32[512,640]{1,0:T(8,128)}, u32[]{:S(2)}, u32[]{:S(2)}) collective-permute-start(f32[512,640]{1,0:T(8,128)S(1)} %collective-permute-done.12.refs_0_), channel_id=1, source_target_pairs={{0,8},{8,16},{16,24},{24,0},{32,40},{40,48},{48,56},{56,32},{64,72... | collective-permute-start | bytes 3932168 | tf_op jit(solution)/shard_map/ppermute | solution.py:392
  414.3 29.9 %collective-permute-start.31 = (f32[512,640]{1,0:T(8,128)S(1)}, f32[512,640]{1,0:T(8,128)}, u32[]{:S(2)}, u32[]{:S(2)}) collective-permute-start(f32[512,640]{1,0:T(8,128)S(1)} %collective-permute-done.13.refs_1_), channel_id=1, source_target_pairs={{0,32},{8,40},{16,48},{24,56},{32,64},{40,72},{48,80},{56,88},{64,... | collective-permute-start | bytes 3932168 | tf_op jit(solution)/shard_map/ppermute | solution.py:392
  416.7 85.1 %collective-permute-start.20 = (f32[1024,640]{1,0:T(8,128)S(1)}, f32[1024,640]{1,0:T(8,128)S(1)}, u32[]{:S(2)}, u32[]{:S(2)}) collective-permute-start(f32[1024,640]{1,0:T(8,128)S(1)} %copy-done.10), channel_id=1, source_target_pairs={{0,8},{8,16},{16,24},{24,0},{32,40},{40,48},{48,56},{56,32},{64,72... | collective-permute-start | bytes 7864328 | tf_op jit(solution)/shard_map/ppermute | solution.py:392
  437.1 67.1 %collective-permute-start.21 = (f32[1024,640]{1,0:T(8,128)S(1)}, f32[1024,640]{1,0:T(8,128)S(1)}, u32[]{:S(2)}, u32[]{:S(2)}) collective-permute-start(f32[1024,640]{1,0:T(8,128)S(1)} %copy-done.9), channel_id=1, source_target_pairs={{0,32},{8,40},{16,48},{24,56},{32,64},{40,72},{48,80},{56,88},{64,... | collective-permute-start | bytes 7864328 | tf_op jit(solution)/shard_map/ppermute | solution.py:392
  437.1 70.4 %collective-permute-start.22 = (f32[1024,640]{1,0:T(8,128)S(1)}, f32[1024,640]{1,0:T(8,128)S(1)}, u32[]{:S(2)}, u32[]{:S(2)}) collective-permute-start(f32[1024,640]{1,0:T(8,128)S(1)} %copy-done.10), channel_id=1, source_target_pairs={{0,24},{8,0},{16,8},{24,16},{32,56},{40,32},{48,40},{56,48},{64,88... | collective-permute-start | bytes 7864328 | tf_op jit(solution)/shard_map/ppermute | solution.py:392
  441.0 69.8 %collective-permute-start.23 = (f32[1024,640]{1,0:T(8,128)S(1)}, f32[1024,640]{1,0:T(8,128)S(1)}, u32[]{:S(2)}, u32[]{:S(2)}) collective-permute-start(f32[1024,640]{1,0:T(8,128)S(1)} %copy-done.9), channel_id=1, source_target_pairs={{0,96},{8,104},{16,112},{24,120},{32,0},{40,8},{48,16},{56,24},{64... | collective-permute-start | bytes 7864328 | tf_op jit(solution)/shard_map/ppermute | solution.py:392
  444.2 56.5 %collective-permute-start.32 = (f32[512,640]{1,0:T(8,128)S(1)}, f32[512,640]{1,0:T(8,128)S(1)}, u32[]{:S(2)}, u32[]{:S(2)}) collective-permute-start(f32[512,640]{1,0:T(8,128)S(1)} %collective-permute-done.14.refs_2_), channel_id=1, source_target_pairs={{0,8},{8,16},{16,24},{24,0},{32,40},{40,48},{48,56},{56,32},{64,72... | collective-permute-start | bytes 3932168 | tf_op jit(solution)/shard_map/ppermute | solution.py:392
  501.8 84.8 %collective-permute-start.28 = (f32[1024,640]{1,0:T(8,128)S(1)}, f32[1024,640]{1,0:T(8,128)S(1)}, u32[]{:S(2)}, u32[]{:S(2)}) collective-permute-start(f32[1024,640]{1,0:T(8,128)S(1)} %collective-permute-done.8.refs_0_), channel_id=1, source_target_pairs={{0,8},{8,16},{16,24},{24,0},{32,40},{40,48},{48,56},{56,32},{64,72... | collective-permute-start | bytes 7864328 | tf_op jit(solution)/shard_map/ppermute | solution.py:392
  501.8 86.3 %collective-permute-start.29 = (f32[1024,640]{1,0:T(8,128)S(1)}, f32[1024,640]{1,0:T(8,128)S(1)}, u32[]{:S(2)}, u32[]{:S(2)}) collective-permute-start(f32[1024,640]{1,0:T(8,128)S(1)} %collective-permute-done.9.refs_1_), channel_id=1, source_target_pairs={{0,32},{8,40},{16,48},{24,56},{32,64},{40,72},{48,80},{56,88},{64,... | collective-permute-start | bytes 7864328 | tf_op jit(solution)/shard_map/ppermute | solution.py:392
  504.3 98.3 %collective-permute-start.34 = (f32[1024,640]{1,0:T(8,128)}, f32[1024,640]{1,0:T(8,128)}, u32[]{:S(2)}, u32[]{:S(2)}) collective-permute-start(f32[1024,640]{1,0:T(8,128)} %collective-permute-done.18.refs_0_), channel_id=1, source_target_pairs={{0,24},{8,0},{16,8},{24,16},{32,56},{40,32},{48,40},{56,48},{64,88... | collective-permute-start | bytes 7864328 | tf_op jit(solution)/shard_map/ppermute | solution.py:392
  507.5 100.6 %collective-permute-start.35 = (f32[1024,640]{1,0:T(8,128)}, f32[1024,640]{1,0:T(8,128)}, u32[]{:S(2)}, u32[]{:S(2)}) collective-permute-start(f32[1024,640]{1,0:T(8,128)} %collective-permute-done.19.refs_1_), channel_id=1, source_target_pairs={{0,96},{8,104},{16,112},{24,120},{32,0},{40,8},{48,16},{56,24},{64... | collective-permute-start | bytes 7864328 | tf_op jit(solution)/shard_map/ppermute | solution.py:392
  510.8 75.9 %collective-permute-start.33 = (f32[512,640]{1,0:T(8,128)S(1)}, f32[512,640]{1,0:T(8,128)S(1)}, u32[]{:S(2)}, u32[]{:S(2)}) collective-permute-start(f32[512,640]{1,0:T(8,128)S(1)} %collective-permute-done.15.refs_3_), channel_id=1, source_target_pairs={{0,32},{8,40},{16,48},{24,56},{32,64},{40,72},{48,80},{56,88},{64,... | collective-permute-start | bytes 3932168 | tf_op jit(solution)/shard_map/ppermute | solution.py:392
  586.6 8.3 %copy-start.6 = (f32[512,640]{1,0:T(8,128)}, f32[512,640]{1,0:T(8,128)S(1)}, u32[]{:S(2)}) copy-start(f32[512,640]{1,0:T(8,128)S(1)} %collective-permute-done.33.refs_1_) | copy-start | bytes 3932164
  586.6 25.0 %collective-permute-start.36 = (f32[512,640]{1,0:T(8,128)}, f32[512,640]{1,0:T(8,128)}, u32[]{:S(2)}, u32[]{:S(2)}) collective-permute-start(f32[512,640]{1,0:T(8,128)} %slice.32), channel_id=1, source_target_pairs={{0,8},{8,16},{16,24},{24,0},{32,40},{40,48},{48,56},{56,32},{64,72... | collective-permute-start | bytes 3932168 | tf_op jit(solution)/shard_map/ppermute | solution.py:392
  586.6 33.1 %collective-permute-start.37 = (f32[512,640]{1,0:T(8,128)}, f32[512,640]{1,0:T(8,128)}, u32[]{:S(2)}, u32[]{:S(2)}) collective-permute-start(f32[512,640]{1,0:T(8,128)} %slice.33), channel_id=1, source_target_pairs={{0,32},{8,40},{16,48},{24,56},{32,64},{40,72},{48,80},{56,88},{64,... | collective-permute-start | bytes 3932168 | tf_op jit(solution)/shard_map/ppermute | solution.py:392
  588.1 31.7 %collective-permute-start.38 = (f32[512,640]{1,0:T(8,128)}, f32[512,640]{1,0:T(8,128)}, u32[]{:S(2)}, u32[]{:S(2)}) collective-permute-start(f32[512,640]{1,0:T(8,128)} %slice.34), channel_id=1, source_target_pairs={{0,24},{8,0},{16,8},{24,16},{32,56},{40,32},{48,40},{56,48},{64,88... | collective-permute-start | bytes 3932168 | tf_op jit(solution)/shard_map/ppermute | solution.py:392
  594.9 3.5 copy-start.3
  602.6 33.6 %collective-permute-start.39 = (f32[512,640]{1,0:T(8,128)}, f32[512,640]{1,0:T(8,128)}, u32[]{:S(2)}, u32[]{:S(2)}) collective-permute-start(f32[512,640]{1,0:T(8,128)} %slice.35), channel_id=1, source_target_pairs={{0,96},{8,104},{16,112},{24,120},{32,0},{40,8},{48,16},{56,24},{64... | collective-permute-start | bytes 3932168 | tf_op jit(solution)/shard_map/ppermute | solution.py:392
  608.1 33.0 %collective-permute-start.42 = (f32[512,640]{1,0:T(8,128)}, f32[512,640]{1,0:T(8,128)}, u32[]{:S(2)}, u32[]{:S(2)}) collective-permute-start(f32[512,640]{1,0:T(8,128)} %collective-permute-done.26.refs_2_), channel_id=1, source_target_pairs={{0,24},{8,0},{16,8},{24,16},{32,56},{40,32},{48,40},{56,48},{64,88... | collective-permute-start | bytes 3932168 | tf_op jit(solution)/shard_map/ppermute | solution.py:392
  611.6 29.4 %collective-permute-start.40 = (f32[512,640]{1,0:T(8,128)}, f32[512,640]{1,0:T(8,128)}, u32[]{:S(2)}, u32[]{:S(2)}) collective-permute-start(f32[512,640]{1,0:T(8,128)} %collective-permute-done.30.refs_0_), channel_id=1, source_target_pairs={{0,8},{8,16},{16,24},{24,0},{32,40},{40,48},{48,56},{56,32},{64,72... | collective-permute-start | bytes 3932168 | tf_op jit(solution)/shard_map/ppermute | solution.py:392
  619.7 21.4 %collective-permute-start.41 = (f32[512,640]{1,0:T(8,128)}, f32[512,640]{1,0:T(8,128)}, u32[]{:S(2)}, u32[]{:S(2)}) collective-permute-start(f32[512,640]{1,0:T(8,128)} %collective-permute-done.31.refs_1_), channel_id=1, source_target_pairs={{0,32},{8,40},{16,48},{24,56},{32,64},{40,72},{48,80},{56,88},{64,... | collective-permute-start | bytes 3932168 | tf_op jit(solution)/shard_map/ppermute | solution.py:392
  619.7 21.4 %collective-permute-start.43 = (f32[512,640]{1,0:T(8,128)}, f32[512,640]{1,0:T(8,128)}, u32[]{:S(2)}, u32[]{:S(2)}) collective-permute-start(f32[512,640]{1,0:T(8,128)} %collective-permute-done.27.refs_3_), channel_id=1, source_target_pairs={{0,96},{8,104},{16,112},{24,120},{32,0},{40,8},{48,16},{56,24},{64... | collective-permute-start | bytes 3932168 | tf_op jit(solution)/shard_map/ppermute | solution.py:392
  (7 other events, 13.5 us)
where the time goes:
time: 648 us; the launch traced here: 647 us
  waiting for transfers between devices  387 us (60%)
  Pallas kernels  180 us (28%)
  starting transfers between devices  56.8 us (9%)
  local copies, waits for them, and re-layouts  16 us (2%)
    ppermute x44, waiting for transfers between devices, send(): lax.ppermute(pair[k], 'dp', [(d, shift(d, dz, dy)) for d in range(N_DP)])  387 us
    pallas_call x1, Pallas kernels, front(): pl.pallas_call(kern, out_shape=tuple((jax.ShapeDtypeStruct(shape, kind) f...  112 us
    ppermute x44, starting transfers between devices, send(): lax.ppermute(pair[k], 'dp', [(d, shift(d, dz, dy)) for d in range(N_DP)])  56.8 us
    pallas_call x17, Pallas kernels, place(): pl.pallas_call(kern, out_shape=jax.ShapeDtypeStruct((vocab, dim), F32), i...  53.6 us
    pallas_call x4, Pallas kernels, finish(): pl.pallas_call(kern, out_shape=jax.ShapeDtypeStruct((span, dim), F32), in...  14.4 us
  transfers between devices with their start and end apart: 44, of which 15 were waited for; matrix products, arithmetic and copies ran while one was open for 2% of the time, Pallas kernels for 9%

commit v1 on v0

v1 whole, which is shorter than its diff:
```python
import jax
import jax.numpy as jnp
from jax import lax
from jax.experimental import pallas as pl
from jax.experimental.pallas import tpu as pltpu
from jax.sharding import PartitionSpec as P


SOFT_CAP = 30.0
INV_CAP = 1.0 / SOFT_CAP
NORM_EPS = 1e-6
SIDE, N_DP, N_TP, LANES = 4, 16, 8, 128
UP, DOWN, AWAY = 1, 3, 2
MIB = 2 ** 20
L_FRONT = 41
MESH = pl.DeviceIdType.MESH
VM = pl.BlockSpec(memory_space=pltpu.VMEM)
HB = pl.BlockSpec(memory_space=pltpu.HBM)
F32, BF16 = jnp.float32, jnp.bfloat16
ROWS_BY_ROWS = (((1,), (1,)), ((), ()))
COLS_BY_COLS = (((0,), (0,)), ((), ()))

OFFSETS = tuple((dz, dy) for dz in range(SIDE) for dy in range(SIDE))
ORDER = tuple(sorted(OFFSETS, key=lambda o: -sum(min(d, SIDE - d) for d in o)))


def shift(dp, dz, dy):
    return (dp // SIDE + dz + SIDE) % SIDE * SIDE + (dp % SIDE + dy + SIDE) % SIDE


def peers():
    me = lax.axis_index('dp')
    z, y = lax.div(me, SIDE), lax.rem(me, SIDE)
    zs = [lax.rem(z + d, SIDE) * SIDE for d in range(SIDE)]
    ys = [lax.rem(y + d, SIDE) for d in range(SIDE)]
    return me, {(dz, dy): zs[dz] + ys[dy] for dz in range(-DOWN, SIDE) for dy in range(-DOWN, SIDE)}


def aligned(start, size, unit=LANES):
    return pl.ds(pl.multiple_of(start, unit), size)


def hops(kind, dz, dy):
    along_z = [(dz, 0)] if dz % 2 else [(UP if dy < AWAY else DOWN, 0)] * dz
    along_y = [(0, dy)] if dy % 2 else [(0, UP if dz < AWAY else DOWN)] * dy
    return along_y + along_z if kind else along_z + along_y


JOBS = tuple((kind, o) for o in ORDER[:-1] for kind in range(2))
PATHS = tuple(hops(kind, *o) for kind, o in JOBS)
MIDDLE = tuple((j, level) for level in range(SIDE) for j, path in enumerate(PATHS) if len(path) > level + 1)


def waves(j, level):
    return (None,) if (j, level) in MIDDLE and level < 2 else (0, 1)


COPIES = tuple((j, level, w) for j, path in enumerate(PATHS) for level in range(len(path)) for w in waves(j, level))


def grad_block(at, tea_ref, x_ref, tab_rows, coef_ref, z_buf, g_buf, out_ref, block):
    tokens = tea_ref.shape[1]
    span = tab_rows.shape[0]
    few = LANES // N_DP
    cols = aligned(block * span, span)
    z_buf[:, :span] = lax.dot_general(x_ref[...], tab_rows, ROWS_BY_ROWS, preferred_element_type=F32)
    for k, (dz, dy) in enumerate(OFFSETS):
        here = aligned(at[-dz, -dy] * tokens, tokens, tokens)
        ratio = jnp.tanh(z_buf[here, :span] * INV_CAP)
        stu = jnp.exp(SOFT_CAP * ratio - SOFT_CAP)
        inv_s, inv_t, _, weight = (coef_ref[0:tokens, k * few + i:k * few + i + 1] for i in range(SIDE))
        diff = (stu * inv_s - tea_ref[k, :, cols] * inv_t) * weight
        g_buf[here, :span] = (diff * (1.0 - ratio * ratio)).astype(BF16)
    out_ref[block] = lax.dot_general(g_buf[:, :span], x_ref[...], COLS_BY_COLS, preferred_element_type=F32)


def front(hidden, gain_row, mask_row, teacher, table):
    tokens, vocab = teacher.shape
    dim = hidden.shape[1]
    part = vocab // N_DP
    half = tokens // 2
    few = tokens // N_TP
    pack = 16
    sub = 512
    tile = part // 2
    tiles = vocab // tile
    depth = 3

    def kern(hid_hbm, gain_hbm, mask_hbm, tea_ref, tab_ref, got_late, blocks_ref, x_out, tab_out, coef_ref, all_ref, gh_ref, gg_ref,
             hid_ref, gain_ref, mask_in, w_ref, raw, sends, stage, got_soon, tabs, n_buf, x_buf, inv_buf, square, pay, pay_got, mask_own, mask_got, x_got, tp_got, own_col,
             own_row, rel, dx, rs_got, ag_own, ag_got, gn_own, gn_got, raw_sem, tab_sem, in_sem, hop_sem, dp_sem, tp_sem):
        me, at = peers()
        col = lax.axis_index('tp')
        mates = [lax.rem(col + j, N_TP) for j in range(N_TP)]
        my_few = aligned(col * few, few, few)

        def fetch(k):
            d = at[ORDER[k]]
            return pltpu.make_async_copy(tea_ref.at[:, aligned(d * part, part)], raw.at[aligned(d * tokens, tokens, tokens)], raw_sem.at[k])

        def tab_copy(i):
            slot = lax.rem(i, depth)
            return pltpu.make_async_copy(tab_ref.at[aligned(lax.rem(i, tiles) * tile, tile)], tabs.at[slot], tab_sem.at[slot])

        inputs = [pltpu.make_async_copy(src, dst, in_sem.at[2 + i])
                  for i, (src, dst) in enumerate(((hid_hbm, hid_ref), (gain_hbm, gain_ref), (mask_hbm, mask_in)))]
        own_tab = pltpu.make_async_copy(tab_ref.at[aligned(me * part, part)], tab_out, in_sem.at[1])
        for cp in inputs:
            cp.start()
        for k in range(N_DP):
            fetch(k).start()
        for i in range(depth - 1):
            tab_copy(i).start()
        own_tab.start()
        barrier = pltpu.get_barrier_semaphore()
        for dz, dy in ORDER[:-1]:
            pl.semaphore_signal(barrier, inc=1, device_id=(at[dz, dy], col), device_id_type=MESH)
        for j in range(1, N_TP):
            pl.semaphore_signal(barrier, inc=1, device_id=(me, mates[j]), device_id_type=MESH)

        for cp in inputs:
            cp.wait()
        w_ref[...] = 1.0 + jnp.concatenate([gain_ref[i:i + 1] for i in range(dim // LANES)], axis=1)
        hid = hid_ref[...].astype(F32)
        inv = lax.rsqrt(jnp.mean(hid * hid, axis=1, keepdims=True) + NORM_EPS)
        n_buf[...] = hid * inv
        x_buf[...] = (n_buf[...] * w_ref[...]).astype(BF16)
        inv_buf[...] = jnp.broadcast_to(inv, (tokens, LANES))
        pay[...] = n_buf[my_few]
        square[...] = jnp.zeros((LANES, LANES), F32)
        square[0:1, 0:tokens] = mask_in[...]
        mask_own[...] = square[0:few]
        mask_col = jnp.transpose(square[...])[0:tokens, 0:1]
        pl.semaphore_wait(barrier, N_DP + N_TP - 2)

        def remote(src, dst, out, into, dp, tp):
            return pltpu.make_async_remote_copy(src_ref=src, dst_ref=dst, send_sem=out, recv_sem=into, device_id=(dp, tp), device_id_type=MESH)

        def to_dp(src, dst, x, rows=slice(None)):
            def send(o):
                d = at[o]
                return remote(src.at[rows], dst.at[me, rows], dp_sem.at[x, 0, d], dp_sem.at[x, 1, me], d, col)

            def into(o):
                d = at[o]
                return remote(src.at[rows], dst.at[d, rows], dp_sem.at[x, 0, d], dp_sem.at[x, 1, d], d, col)

            return [send(o) for o in ORDER[:-1]], [into(o) for o in ORDER[:-1]]

        def to_tp(srcs, dst, x):
            def send(j):
                c = mates[j]
                return remote(srcs(c), dst.at[col], tp_sem.at[x, 0, c], tp_sem.at[x, 1, col], me, c)

            def into(j):
                c = mates[j]
                return remote(srcs(c), dst.at[c], tp_sem.at[x, 0, c], tp_sem.at[x, 1, c], me, c)

            return [send(j) for j in range(1, N_TP)], [into(j) for j in range(1, N_TP)]

        def start(copies):
            for cp in copies:
                cp.start()

        def arrive(copies):
            for cp in copies:
                cp.wait_recv()

        def added(ref, here=slice(None)):
            total = ref[0, here]
            for d in range(1, ref.shape[0]):
                total = total + ref[d, here]
            return total

        gots = (got_soon, got_late)
        late = part // 2

        def hop(j, level, w):
            kind, (dz, dy) = JOBS[j]
            tok = pl.ds(kind * half, half)
            rows = slice(None) if w is None else pl.ds(w * late, late)
            src = stage.at[MIDDLE.index((j, level - 1)), :, rows] if level else sends.at[aligned(at[dz, dy] * tokens + kind * half, half, half), rows]
            dst = stage.at[MIDDLE.index((j, level)), :, rows] if (j, level) in MIDDLE else gots[w].at[dz * SIDE + dy, tok]
            k = COPIES.index((j, level, w))
            return remote(src, dst, hop_sem.at[0, k], hop_sem.at[1, k], at[PATHS[j][level]], col)

        def came(level, w=None):
            for j, at in MIDDLE:
                if at == level:
                    hop(j, level, w).wait_recv()

        def onward(level, far, *ws):
            for w in ws:
                for j, at in MIDDLE:
                    if at == level - 1 and far == (len(PATHS[j]) > 2):
                        hop(j, level, w).start()

        pay_sends, pay_came = to_dp(pay, pay_got, 0)
        start(pay_sends)
        pay_got[me] = pay[...]
        mask_sends, mask_came = to_dp(mask_own, mask_got, 1, pl.ds(0, 1))
        start(mask_sends)
        mask_got[me] = mask_own[...]

        for k, o in enumerate(ORDER):
            fetch(k).wait()
            d = at[o]

            def weigh(r, _):
                here = aligned(d * tokens + r * pack, pack, pack)
                cap = jnp.tanh(raw[here].astype(F32) * INV_CAP)
                sends[here] = jnp.exp(SOFT_CAP * cap - SOFT_CAP)
                return 0

            lax.fori_loop(0, tokens // pack, weigh, 0)
            for j, (_, to) in enumerate(JOBS):
                if to == o:
                    for w in waves(j, 0):
                        hop(j, 0, w).start()

        def keep(r, _):
            here, there = aligned(me * tokens + r * pack, pack, pack), aligned(r * pack, pack, pack)
            got_soon[0, there] = sends[here, :late]
            got_late[0, there] = sends[here, late:]
            return 0

        lax.fori_loop(0, tokens // pack, keep, 0)

        def fold(v):
            total = v[:, :LANES]
            for c in range(LANES, v.shape[1], LANES):
                total = total + v[:, c:c + LANES]
            return total

        def student(slot, here):
            z = lax.dot_general(x_buf[...], tabs[slot, here], ROWS_BY_ROWS, preferred_element_type=F32)
            ratio = jnp.tanh(z * INV_CAP)
            return ratio, jnp.exp(SOFT_CAP * ratio - SOFT_CAP)

        def forward(i, sums):
            slot = lax.rem(i, depth)
            tab_copy(i).wait()
            tab_copy(i + depth - 1).start()
            s_sum, t_sum, k_sum = sums
            for c in range(0, tile, sub):
                ratio, stu = student(slot, pl.ds(c, sub))
                toks, here = aligned(lax.div(i, 2) * tokens, tokens, tokens), aligned(lax.rem(i, 2) * tile + c, sub)
                cap = jnp.tanh(raw[toks, here].astype(F32) * INV_CAP)
                tea = sends[toks, here]
                s_sum = s_sum + fold(stu)
                t_sum = t_sum + fold(tea)
                k_sum = k_sum + fold(tea * (cap - ratio))
            return s_sum, t_sum, k_sum

        zero = jnp.zeros((tokens, LANES), F32)
        s_sum, t_sum, k_sum = lax.fori_loop(0, tiles, forward, (zero, zero, zero))
        lane = lax.broadcasted_iota(jnp.int32, (tokens, LANES), 1)
        sums = jnp.where(lane == 0, jnp.sum(s_sum, axis=1, keepdims=True), 0.0)
        sums = jnp.where(lane == 1, jnp.sum(t_sum, axis=1, keepdims=True), sums)
        sums = jnp.where(lane == AWAY, SOFT_CAP * jnp.sum(k_sum, axis=1, keepdims=True), sums)
        own_col[...] = sums
        tp_got[col] = sums
        tp_sends, tp_came = to_tp(lambda c: own_col, tp_got, 0)
        start(tp_sends)
        arrive(tp_came)
        total = added(tp_got)
        square[0:tokens] = jnp.where(lane == DOWN, mask_col, total)
        line = jnp.transpose(square[...])[0:few]
        own_row[...] = line
        all_ref[me] = line
        dp_sends, dp_came = to_dp(own_row, all_ref, 2)
        start(dp_sends)
        came(0)
        onward(1, True, None)
        onward(1, False, 0, 1)

        arrive((*pay_came, *mask_came))
        x_got[col] = pay_got[...]
        xt_sends, xt_came = to_tp(lambda c: pay_got, x_got, 1)
        start(xt_sends)
        count = jnp.sum(added(mask_got, slice(1)), axis=1, keepdims=True)
        inv_s, inv_t, weight = 1.0 / total[:, 0:1], 1.0 / total[:, 1:2], mask_col / count
        dx[...] = jnp.zeros((tokens, dim), F32)

        def backward(i, _):
            slot = lax.rem(i, depth)
            tab_copy(i).wait()

            @pl.when(i + depth - 1 < 2 * tiles)
            def _():
                tab_copy(i + depth - 1).start()

            for c in range(0, tile, sub):
                here = pl.ds(c, sub)
                ratio, stu = student(slot, here)
                tea = sends[aligned(lax.div(i - tiles, 2) * tokens, tokens, tokens), aligned(lax.rem(i, 2) * tile + c, sub)]
                diff = (stu * inv_s - tea * inv_t) * weight
                g = (diff * (1.0 - ratio * ratio)).astype(BF16)
                dx[...] += jnp.dot(g, tabs[slot, here], preferred_element_type=F32)
            return 0

        lax.fori_loop(tiles, 2 * tiles, backward, 0)
        came(1)
        onward(2, True, 0)

        rs_got[col] = dx[my_few]
        rs_sends, rs_came = to_tp(lambda c: dx.at[aligned(c * few, few, few)], rs_got, 2)
        start(rs_sends)
        arrive(rs_came)
        my_x = added(rs_got)
        my_n = n_buf[my_few]
        grad_n = my_x * w_ref[...]
        my_h = inv_buf[my_few, 0:1] * (grad_n - my_n * jnp.mean(grad_n * my_n, axis=1, keepdims=True))
        ag_own[...] = jnp.zeros((2 * few, dim), F32)
        ag_own[0:few] = my_h
        ag_own[few:few + 1] = jnp.sum(my_x * my_n, axis=0, keepdims=True)
        ag_got[col] = ag_own[...]
        ag_sends, ag_came = to_tp(lambda c: ag_own, ag_got, DOWN)
        start(ag_sends)
        arrive(ag_came)
        gh_ref[...] = jnp.concatenate([ag_got[j, 0:few] for j in range(N_TP)], axis=0)
        line = added(ag_got, slice(few, few + 1))
        gn_own[0:1] = line
        gn_got[me, 0:1] = line
        gn_sends, gn_came = to_dp(gn_own, gn_got, DOWN, pl.ds(0, 1))
        start(gn_sends)

        arrive(xt_came)

        def widen(d, _):
            rows = jnp.concatenate([x_got[j, d] for j in range(N_TP)], axis=0)
            x_out[aligned(d * tokens, tokens, tokens)] = (rows * w_ref[...]).astype(BF16)
            return 0

        lax.fori_loop(0, N_DP, widen, 0)
        arrive(dp_came)
        row = lax.broadcasted_iota(jnp.int32, (few, LANES), 0)
        lanes = lax.broadcasted_iota(jnp.int32, (few, LANES), 1)
        for d in range(N_DP):
            block = all_ref[d]
            safe = jnp.where((row < AWAY) & (lanes < tokens), block, 1.0)
            rel[d * few:(d + 1) * few] = jnp.where(row < AWAY, 1.0 / safe, block / count)
        for k, (dz, dy) in enumerate(OFFSETS):
            square[k * few:(k + 1) * few] = rel[aligned(at[-dz, -dy] * few, few, few)]
        coef_ref[...] = jnp.transpose(square[...])

        arrive(gn_came)
        gg_ref[...] = added(gn_got, slice(1))
        own_tab.wait()
        came(2, 0)
        onward(DOWN, True, 0)
        onward(2, True, 1)
        for j, path in enumerate(PATHS):
            hop(j, len(path) - 1, 0).wait_recv()
        for j, level, w in COPIES:
            if level == 0:
                hop(j, level, w).wait_send()
        came(2, 1)
        onward(DOWN, True, 1)

        def block(b, _):
            grad_block(at, got_soon, x_out, tab_out[aligned(b * sub, sub)], coef_ref, sends, raw, blocks_ref, b)
            return 0

        lax.fori_loop(0, 2, block, 0)
        for j, path in enumerate(PATHS):
            hop(j, len(path) - 1, 1).wait_recv()
        for j, level, w in COPIES:
            if level:
                hop(j, level, w).wait_send()
        for cp in (*pay_sends, *mask_sends, *tp_sends, *dp_sends, *xt_sends, *rs_sends, *ag_sends, *gn_sends):
            cp.wait_send()

    dma = pltpu.SemaphoreType.DMA
    wide, flat = (tokens, dim), (few, LANES)
    return pl.pallas_call(
        kern,
        out_shape=tuple(jax.ShapeDtypeStruct(shape, kind) for shape, kind in (
            ((N_DP, tokens, part // 2), F32), ((2, sub, dim), F32), ((N_DP * tokens, dim), BF16), ((part, dim), BF16), ((LANES, LANES), F32), ((N_DP, *flat), F32), (wide, F32),
            ((1, dim), F32))),
        in_specs=[HB] * 5, out_specs=(VM,) * 8,
        scratch_shapes=[pltpu.VMEM(shape, kind) for shape, kind in (
            (wide, BF16), ((dim // LANES, LANES), F32), ((1, tokens), F32), ((1, dim), F32), ((N_DP * tokens, part), BF16), ((N_DP * tokens, part), F32),
            ((len(MIDDLE), half, part), F32), ((N_DP, tokens, part // 2), F32),
            ((depth, tile, dim), BF16), (wide, F32), (wide, BF16), ((tokens, LANES), F32), ((LANES, LANES), F32), ((few, dim), F32),
            ((N_DP, few, dim), F32), (flat, F32), ((N_DP, *flat), F32), ((N_TP, N_DP, few, dim), F32), ((N_TP, tokens, LANES), F32),
            ((tokens, LANES), F32), (flat, F32), ((LANES, LANES), F32), (wide, F32), ((N_TP, few, dim), F32), ((2 * few, dim), F32),
            ((N_TP, 2 * few, dim), F32), ((few, dim), F32), ((N_DP, few, dim), F32))] + [
            dma((N_DP,)), dma((depth,)), dma((5,)), dma((2, len(COPIES))), dma((SIDE, 2, N_DP)), dma((SIDE, 2, N_TP))],
        compiler_params=pltpu.CompilerParams(collective_id=0, has_side_effects=True, vmem_limit_bytes=L_FRONT * MIB),
        cost_estimate=pl.CostEstimate(flops=3 * 10 ** 9, bytes_accessed=100 * MIB, transcendentals=0), name='front')(
            *(pltpu.with_memory_space_constraint(a, pltpu.HBM) for a in (hidden, gain_row, mask_row, teacher, table)))


def finish(teas, x_all, tab_part, coef):
    n, tokens, late = teas.shape
    dim = x_all.shape[1]
    span = late // 2

    def kern(tea_ref, x_ref, tab_ref, coef_ref, out_ref, z_buf, g_buf):
        at = peers()[1]

        def block(b, _):
            grad_block(at, tea_ref, x_ref, tab_ref[aligned(late + b * span, span)], coef_ref, z_buf, g_buf, out_ref, b)
            return 0

        lax.fori_loop(0, 2, block, 0)

    return pl.pallas_call(kern, out_shape=jax.ShapeDtypeStruct((2, span, dim), F32), in_specs=[VM] * 4, out_specs=VM,
        scratch_shapes=[pltpu.VMEM((n * tokens, span), F32), pltpu.VMEM((n * tokens, span), BF16)], name='finish',
        compiler_params=pltpu.CompilerParams(vmem_limit_bytes=22 * MIB),
        cost_estimate=pl.CostEstimate(flops=10 ** 9, bytes_accessed=8 * MIB, transcendentals=0))(teas, x_all, tab_part, coef)


def place(table, pieces, vocab):
    arrays = [p[0] for p in pieces]
    n = len(arrays)
    dim = arrays[0].shape[1]
    rows = vocab // N_DP
    quarter = rows // SIDE
    cut = 256
    chunks = [(i, r) for i in range(n) for r in range(0, arrays[i].shape[0], cut)]

    def kern(*refs):
        dst, buf, sem = refs[-DOWN:]
        at = peers()[1]
        reads, writes = [], []
        for k, (i, r) in enumerate(chunks):
            _, dz, dy, kind, half = pieces[i]
            first = (2 * (half + r // quarter) + kind) * quarter + r % quarter
            there = aligned(at[dz, dy] * rows + first, cut, cut)
            reads.append(pltpu.make_async_copy(refs[i].at[pl.ds(r, cut)], buf.at[k], sem.at[0, k]))
            writes.append(pltpu.make_async_copy(buf.at[k], dst.at[there], sem.at[1, k]))
        for cp in reads:
            cp.start()
        for read, write in zip(reads, writes):
            read.wait()
            write.start()
        for cp in writes:
            cp.wait()

    args = arrays if table is None else [*arrays, table]
    size = len(chunks) * cut * dim
    return pl.pallas_call(kern, out_shape=jax.ShapeDtypeStruct((vocab, dim), F32), in_specs=[pl.BlockSpec(memory_space=pl.ANY)] * n + [HB] * (len(args) - n),
        out_specs=HB, scratch_shapes=[pltpu.VMEM((len(chunks), cut, dim), F32), pltpu.SemaphoreType.DMA((2, len(chunks)))],
        input_output_aliases={} if table is None else {n: 0}, name='place', compiler_params=pltpu.CompilerParams(vmem_limit_bytes=4 * size + MIB),
        cost_estimate=pl.CostEstimate(flops=10 * MIB, bytes_accessed=8 * size, transcendentals=0))(*args)


def gather(first, rest, vocab):
    quarter = first[0].shape[0]
    sets, ways = range(2), (UP, DOWN)
    table, event = None, 0

    def send(pair, axis, step):
        out = []
        for k in sets:
            dz, dy = (step, 0) if axis == k else (0, step)
            out.append(lax.ppermute(pair[k], 'dp', [(d, shift(d, dz, dy)) for d in range(N_DP)]))
        return out

    def put(pair, a, b, c=0):
        return [(pair[k], *((b, a) if k else (a, b)), k, c) for k in sets]

    def settle(*pieces):
        nonlocal table
        table = place(table, [p for ps in pieces for p in ps], vocab)

    def wait(*pairs):
        nonlocal table, event
        event += 1
        table, *flat = lax.optimization_barrier((table, *(x for pair in pairs for x in pair)))
        return [flat[2 * i:2 * i + 2] for i in range(len(pairs))]

    def join(one, other):
        return [jnp.concatenate(pair) for pair in zip(one, other)]

    own = [first]
    low, high = ([send(own[0], 0, way)] for way in ways)
    later = rest()
    event = 1
    own.append([later[k] for k in sets])
    low.append(send(own[1], 0, UP))
    high.append(send(own[1], 0, DOWN))
    whole = join(*own)
    side = {way: send(whole, 1, way) for way in ways}
    settle(put(own[0], 0, 0, 0), put(own[1], 0, 0, 1))

    low[0], high[0] = wait(low[0], high[0])
    far_low = send(low[0], 0, UP)
    settle(put(low[0], DOWN, 0, 0), put(high[0], UP, 0, 0))

    low[1], high[1] = wait(low[1], high[1])
    far_high = send(high[1], 0, DOWN)
    low_whole, high_whole = join(*low), join(*high)
    low_side = {way: send(low_whole, 1, way) for way in ways}
    settle(put(low[1], DOWN, 0, 1), put(high[1], UP, 0, 1))

    side[UP], side[DOWN], high_whole = wait(side[UP], side[DOWN], high_whole)
    high_side = {way: send(high_whole, 1, way) for way in ways}
    side_far = send(side[UP], 1, UP)
    settle(put(side[UP], 0, DOWN))
    settle(put(side[DOWN], 0, UP))

    far_low, far_high = wait(far_low, far_high)
    far_side = {(c, way): send(pair, 1, way) for way in ways for c, pair in enumerate((far_low, far_high))}
    settle(put(far_low, AWAY, 0, 0), put(far_high, AWAY, 0, 1))

    low_side[UP], low_side[DOWN] = wait(low_side[UP], low_side[DOWN])
    low_far = send(low_side[DOWN], 1, DOWN)
    settle(put(low_side[UP], DOWN, DOWN))
    settle(put(low_side[DOWN], DOWN, UP))

    high_side[UP], high_side[DOWN] = wait(high_side[UP], high_side[DOWN])
    high_far = [send([x[:quarter] for x in high_side[UP]], 1, UP), send([x[quarter:] for x in high_side[DOWN]], 1, DOWN)]
    settle(put(high_side[UP], UP, DOWN))
    settle(put(high_side[DOWN], UP, UP))

    far_side[0, DOWN], far_side[1, DOWN], side_far = wait(far_side[0, DOWN], far_side[1, DOWN], side_far)
    last_down = send(far_side[1, DOWN], 1, DOWN)
    settle(put(far_side[0, DOWN], AWAY, UP, 0), put(far_side[1, DOWN], AWAY, UP, 1))
    settle(put(side_far, 0, AWAY))

    far_side[0, UP], = wait(far_side[0, UP])
    last_up = send(far_side[0, UP], 1, UP)
    settle(put(far_side[0, UP], AWAY, DOWN, 0))

    far_side[1, UP], low_far = wait(far_side[1, UP], low_far)
    settle(put(far_side[1, UP], AWAY, DOWN, 1))
    settle(put(low_far, DOWN, AWAY))

    high_far = wait(*high_far)
    settle(put(high_far[0], UP, AWAY, 0), put(high_far[1], UP, AWAY, 1))
    for k in (1, 0):
        table, up, down = lax.optimization_barrier((table, last_up[k], last_down[k]))
        table = place(table, [put([up] * 2, AWAY, AWAY, 0)[k], put([down] * 2, AWAY, AWAY, 1)[k]], vocab)
    return table


def solution(mesh):
    def local_step(hid_rows, w_final, tab_rows, tea_rows, mask_rows):
        tokens = hid_rows.shape[0]
        late, soon, x_all, tab_part, coef, stats, grad_h, gain_line = front(hid_rows, w_final.reshape(-1, LANES), mask_rows[None], tea_rows, tab_rows)
        coef, *first = lax.optimization_barrier((coef, soon[0], soon[1]))
        table = gather(first, lambda: finish(late, x_all, tab_part, coef), tab_rows.shape[0])
        s_sum, t_sum, k_sum, masks = (stats[:, i, :tokens] for i in range(SIDE))
        all_kl = k_sum / t_sum + jnp.log(s_sum) - jnp.log(t_sum)
        loss_val = jnp.sum(masks * all_kl) / jnp.sum(masks)
        return loss_val, grad_h.astype(BF16), gain_line[0], table

    return jax.shard_map(local_step, mesh=mesh, in_specs=(P('dp', None), P(None), P('tp', None), P('dp', 'tp'), P('dp')), out_specs=(P(), P('dp', None), P(None), P('tp', None)), check_vma=False)
```

time: 648 us -> 643 us (level)
  Pallas kernels: 180 us -> 198 us
  waiting for transfers between devices: 387 us -> 371 us
    pallas_call x17 -> x18, Pallas kernels: 53.6 us -> 70.3 us  [place(): pl.pallas_call(kern, out_shape=jax.ShapeDtypeStruct((vocab, dim), F32), i...]
    ppermute x44, waiting for transfers between devices: 387 us -> 371 us  [send(): lax.ppermute(pair[k], 'dp', [(d, shift(d, dz, dy)) for d in range(N_DP)])]
    pallas_call x1, Pallas kernels: 112 us -> 120 us  [front(): pl.pallas_call(kern, out_shape=tuple((jax.ShapeDtypeStruct(shape, kind) f...]
    pallas_call x4 -> x1, Pallas kernels: 14.4 us -> 7.21 us  [finish(): pl.pallas_call(kern, out_shape=jax.ShapeDtypeStruct((2, span, dim), F32),...]
  transfers between devices with their start and end apart: 44 -> 44, of which waited for: 15 -> 12; matrix products, arithmetic and copies ran while one was open for 2% -> 2% of each run, Pallas kernels for 9% -> 12%
where the time goes in v1:
time: 643 us; the launch traced here: 642 us
  waiting for transfers between devices  371 us (58%)
  Pallas kernels  198 us (31%)
  starting transfers between devices  55.5 us (9%)
  local copies, waits for them, and re-layouts  10.5 us (2%)
    ppermute x44, waiting for transfers between devices, send(): lax.ppermute(pair[k], 'dp', [(d, shift(d, dz, dy)) for d in range(N_DP)])  371 us
    pallas_call x1, Pallas kernels, front(): pl.pallas_call(kern, out_shape=tuple((jax.ShapeDtypeStruct(shape, kind) f...  120 us
    pallas_call x18, Pallas kernels, place(): pl.pallas_call(kern, out_shape=jax.ShapeDtypeStruct((vocab, dim), F32), i...  70.3 us
    ppermute x44, starting transfers between devices, send(): lax.ppermute(pair[k], 'dp', [(d, shift(d, dz, dy)) for d in range(N_DP)])  55.5 us
  transfers between devices with their start and end apart: 44, of which 12 were waited for; matrix products, arithmetic and copies ran while one was open for 2% of the time, Pallas kernels for 12%

profile of v1, /device:TPU:0, one launch (start us, length us, event | category | flops | bytes accessed | tf_op | source)
XLA Modules:
  0.0 641.9 jit_solution(10015474380948853359)
XLA Ops:
  0.6 120.1 %front.1 = (f32[16,64,1024]{2,1,0:T(8,128)S(1)}, f32[2,512,640]{2,1,0:T(8,128)S(1)}, bf16[1024,640]{1,0:T(8,128)(2,1)S(1)}, bf16[2048,640]{1,0:T(8,128)(2,1)S(1)...) custom-call(bf16[64,640]{1,0:T(8,128)(2,1)} %hid_hbm.1, ...), custom_call_target="tpu_custom_call" | custom-call | flops 3000000000 | bytes 104857600 | tf_op jit(solution)/shard_map/front/pallas_call | solution.py:376
  121.6 2.6 collective-permute-start.2
  124.2 3.2 collective-permute-start.3
  127.5 7.2 %finish.1 = f32[2,512,640]{2,1,0:T(8,128)S(1)} custom-call(f32[16,64,1024]{2,1,0:T(8,128)S(1)} %get-tuple-element.80.tea_ref, bf16[1024,640]{1,0:T(8,128)(2,1)S(1)} %get-tuple-element.81.x_ref, bf16[2048,640]{1,0:T(8,128)(2,1)S(1)} %get-tuple-element.82.tab_ref, f32[128,128]{1,0:T(8,128)S(1)} %get-tuple-element.83.coef_ref), custom_call_target="tpu_custom_call" | custom-call | flops 1000000000 | bytes 8388608 | tf_op jit(solution)/shard_map/finish/pallas_call | solution.py:409
  135.1 18.7 %collective-permute-done.refs_0_ = f32[512,640]{1,0:T(8,128)S(1)} collective-permute-done((f32[512,640]{1,0:T(8,128)S(1)}, f32[512,640]{1,0:T(8,128)S(1)}, u32[]{:S(2)}, u32[]{:S(2)}) %collective-permute-start) | collective-permute-done | bytes 1310752 | tf_op jit(solution)/shard_map/ppermute | solution.py:459
  155.4 3.2 collective-permute-start.6
  158.6 23.3 %collective-permute-done.4.refs_0_ = f32[512,640]{1,0:T(8,128)S(1)} collective-permute-done((f32[512,640]{1,0:T(8,128)S(1)}, f32[512,640]{1,0:T(8,128)S(1)}, u32[]{:S(2)}, u32[]{:S(2)}) %collective-permute-start.4) | collective-permute-done | bytes 1310752 | tf_op jit(solution)/shard_map/ppermute | solution.py:459
  181.9 2.4 collective-permute-start.10
  184.3 2.4 collective-permute-done.5.refs_1_
  187.9 4.1 place.18.refs_4_
  192.0 4.2 place.19.refs_4_
  196.2 66.8 %collective-permute-done.7.refs_3_ = f32[512,640]{1,0:T(8,128)S(1)} collective-permute-done((f32[512,640]{1,0:T(8,128)S(1)}, f32[512,640]{1,0:T(8,128)S(1)}, u32[]{:S(2)}, u32[]{:S(2)}) %collective-permute-start.7) | collective-permute-done | bytes 1310752 | tf_op jit(solution)/shard_map/ppermute | solution.py:459
  264.5 3.2 collective-permute-start.14
  269.0 1.8 collective-permute-start.16
  273.2 22.7 %collective-permute-done.12.refs_0_ = f32[512,640]{1,0:T(8,128)S(1)} collective-permute-done((f32[512,640]{1,0:T(8,128)S(1)}, f32[512,640]{1,0:T(8,128)S(1)}, u32[]{:S(2)}, u32[]{:S(2)}) %collective-permute-start.12) | collective-permute-done | bytes 1310752 | tf_op jit(solution)/shard_map/ppermute | solution.py:459
  295.9 3.7 collective-permute-start.18
  300.8 2.0 collective-permute-start.15
  302.8 4.1 place.20.refs_2_
  308.7 4.1 place.21.refs_2_
  312.9 4.1 place.22.refs_4_
  317.0 64.1 %collective-permute-done.15.refs_3_ = f32[512,640]{1,0:T(8,128)S(1)} collective-permute-done((f32[512,640]{1,0:T(8,128)S(1)}, f32[512,640]{1,0:T(8,128)S(1)}, u32[]{:S(2)}, u32[]{:S(2)}) %collective-permute-start.15) | collective-permute-done | bytes 1310752 | tf_op jit(solution)/shard_map/ppermute | solution.py:459
  381.1 3.7 collective-permute-start.24
  385.0 2.0 collective-permute-start.30
  387.0 24.4 %collective-permute-done.24.refs_0_ = f32[512,640]{1,0:T(8,128)S(1)} collective-permute-done((f32[512,640]{1,0:T(8,128)S(1)}, f32[512,640]{1,0:T(8,128)S(1)}, u32[]{:S(2)}, u32[]{:S(2)}) %collective-permute-start.24) | collective-permute-done | bytes 1310752 | tf_op jit(solution)/shard_map/ppermute | solution.py:459
  411.5 26.7 %collective-permute-done.26.refs_2_ = f32[512,640]{1,0:T(8,128)} collective-permute-done((f32[512,640]{1,0:T(8,128)S(1)}, f32[512,640]{1,0:T(8,128)}, u32[]{:S(2)}, u32[]{:S(2)}) %collective-permute-start.26) | collective-permute-done | bytes 1310752 | tf_op jit(solution)/shard_map/ppermute | solution.py:459
  438.1 3.8 collective-permute-start.22
  441.9 3.2 collective-permute-start.23
  445.2 53.1 %collective-permute-done.32.refs_0_ = f32[512,640]{1,0:T(8,128)S(1)} collective-permute-done((f32[512,640]{1,0:T(8,128)S(1)}, f32[512,640]{1,0:T(8,128)S(1)}, u32[]{:S(2)}, u32[]{:S(2)}) %collective-permute-start.32) | collective-permute-done | bytes 1310752 | tf_op jit(solution)/shard_map/ppermute | solution.py:459
  498.6 4.1 place.23.refs_2_
  502.7 3.2 collective-permute-start.34
  505.9 3.0 collective-permute-start.35
  509.0 4.1 place.24.refs_2_
  513.1 4.6 place.25.refs_2_
  518.9 63.1 %collective-permute-done.33.refs_1_ = f32[512,640]{1,0:T(8,128)S(1)} collective-permute-done((f32[512,640]{1,0:T(8,128)S(1)}, f32[512,640]{1,0:T(8,128)S(1)}, u32[]{:S(2)}, u32[]{:S(2)}) %collective-permute-start.33) | collective-permute-done | bytes 1310752 | tf_op jit(solution)/shard_map/ppermute | solution.py:459
  584.7 3.0 collective-permute-start.38
  589.0 4.1 place.26.refs_2_
  593.1 4.1 place.27.refs_4_
  597.2 4.7 place.28.refs_2_
  601.9 3.3 collective-permute-start.39
  605.2 4.1 place.29.refs_2_
  609.5 4.5 collective-permute-done.36.refs_0_
  614.0 3.2 collective-permute-start.43
  620.5 2.8 place.30.refs_2_
  623.8 2.4 place.31.refs_2_
  626.2 4.6 place.32.refs_4_
  630.8 4.6 place.33.refs_2_
  635.5 2.6 place.34.refs_2_
  638.2 2.6 place.35
  (86 shorter events, 20.3 us)
Async XLA Ops:
  120.9 32.9 %collective-permute-start = (f32[512,640]{1,0:T(8,128)S(1)}, f32[512,640]{1,0:T(8,128)S(1)}, u32[]{:S(2)}, u32[]{:S(2)}) collective-permute-start(f32[512,640]{1,0:T(8,128)S(1)} %get-tuple-element.78.refs_0_), channel_id=1, source_target_pairs={{0,32},{8,40},{16,48},{24,56},{32,64},{40,72},{48,80},{56,88},{64,... | collective-permute-start | bytes 3932168 | tf_op jit(solution)/shard_map/ppermute | solution.py:459
  121.6 33.7 %collective-permute-start.2 = (f32[512,640]{1,0:T(8,128)S(1)}, f32[512,640]{1,0:T(8,128)S(1)}, u32[]{:S(2)}, u32[]{:S(2)}) collective-permute-start(f32[512,640]{1,0:T(8,128)S(1)} %get-tuple-element.78.refs_0_), channel_id=1, source_target_pairs={{0,96},{8,104},{16,112},{24,120},{32,0},{40,8},{48,16},{56,24},{64... | collective-permute-start | bytes 3932168 | tf_op jit(solution)/shard_map/ppermute | solution.py:459
  124.2 30.7 %collective-permute-start.1 = (f32[512,640]{1,0:T(8,128)S(1)}, f32[512,640]{1,0:T(8,128)S(1)}, u32[]{:S(2)}, u32[]{:S(2)}) collective-permute-start(f32[512,640]{1,0:T(8,128)S(1)} %get-tuple-element.79.refs_1_), channel_id=1, source_target_pairs={{0,8},{8,16},{16,24},{24,0},{32,40},{40,48},{48,56},{56,32},{64,72... | collective-permute-start | bytes 3932168 | tf_op jit(solution)/shard_map/ppermute | solution.py:459
  124.2 31.1 %collective-permute-start.3 = (f32[512,640]{1,0:T(8,128)S(1)}, f32[512,640]{1,0:T(8,128)S(1)}, u32[]{:S(2)}, u32[]{:S(2)}) collective-permute-start(f32[512,640]{1,0:T(8,128)S(1)} %get-tuple-element.79.refs_1_), channel_id=1, source_target_pairs={{0,24},{8,0},{16,8},{24,16},{32,56},{40,32},{48,40},{56,48},{64,88... | collective-permute-start | bytes 3932168 | tf_op jit(solution)/shard_map/ppermute | solution.py:459
  134.9 47.1 %collective-permute-start.4 = (f32[512,640]{1,0:T(8,128)S(1)}, f32[512,640]{1,0:T(8,128)S(1)}, u32[]{:S(2)}, u32[]{:S(2)}) collective-permute-start(f32[512,640]{1,0:T(8,128)S(1)} %get-tuple-element.145.refs_2_), channel_id=1, source_target_pairs={{0,32},{8,40},{16,48},{24,56},{32,64},{40,72},{48,80},{56,88},{64,... | collective-permute-start | bytes 3932168 | tf_op jit(solution)/shard_map/ppermute | solution.py:459
  153.8 32.9 %collective-permute-start.5 = (f32[512,640]{1,0:T(8,128)S(1)}, f32[512,640]{1,0:T(8,128)S(1)}, u32[]{:S(2)}, u32[]{:S(2)}) collective-permute-start(f32[512,640]{1,0:T(8,128)S(1)} %get-tuple-element.144.refs_3_), channel_id=1, source_target_pairs={{0,8},{8,16},{16,24},{24,0},{32,40},{40,48},{48,56},{56,32},{64,72... | collective-permute-start | bytes 3932168 | tf_op jit(solution)/shard_map/ppermute | solution.py:459
  154.9 109.3 %collective-permute-start.8 = (f32[1024,640]{1,0:T(8,128)S(1)}, f32[1024,640]{1,0:T(8,128)S(1)}, u32[]{:S(2)}, u32[]{:S(2)}) collective-permute-start(f32[1024,640]{1,0:T(8,128)S(1)} %pad_maximum_fusion), channel_id=1, source_target_pairs={{0,8},{8,16},{16,24},{24,0},{32,40},{40,48},{48,56},{56,32},{64,72... | collective-permute-start | bytes 7864328 | tf_op jit(solution)/shard_map/ppermute | solution.py:459
  155.3 109.2 %collective-permute-start.9 = (f32[1024,640]{1,0:T(8,128)S(1)}, f32[1024,640]{1,0:T(8,128)S(1)}, u32[]{:S(2)}, u32[]{:S(2)}) collective-permute-start(f32[1024,640]{1,0:T(8,128)S(1)} %pad_maximum_fusion.1), channel_id=1, source_target_pairs={{0,32},{8,40},{16,48},{24,56},{32,64},{40,72},{48,80},{56,88},{64,... | collective-permute-start | bytes 7864328 | tf_op jit(solution)/shard_map/ppermute | solution.py:459
  155.4 32.5 %collective-permute-start.6 = (f32[512,640]{1,0:T(8,128)S(1)}, f32[512,640]{1,0:T(8,128)S(1)}, u32[]{:S(2)}, u32[]{:S(2)}) collective-permute-start(f32[512,640]{1,0:T(8,128)S(1)} %get-tuple-element.145.refs_2_), channel_id=1, source_target_pairs={{0,96},{8,104},{16,112},{24,120},{32,0},{40,8},{48,16},{56,24},{64... | collective-permute-start | bytes 3932168 | tf_op jit(solution)/shard_map/ppermute | solution.py:459
  181.9 87.0 %collective-permute-start.10 = (f32[1024,640]{1,0:T(8,128)S(1)}, f32[1024,640]{1,0:T(8,128)S(1)}, u32[]{:S(2)}, u32[]{:S(2)}) collective-permute-start(f32[1024,640]{1,0:T(8,128)S(1)} %pad_maximum_fusion), channel_id=1, source_target_pairs={{0,24},{8,0},{16,8},{24,16},{32,56},{40,32},{48,40},{56,48},{64,88... | collective-permute-start | bytes 7864328 | tf_op jit(solution)/shard_map/ppermute | solution.py:459
  186.7 76.3 %collective-permute-start.7 = (f32[512,640]{1,0:T(8,128)S(1)}, f32[512,640]{1,0:T(8,128)S(1)}, u32[]{:S(2)}, u32[]{:S(2)}) collective-permute-start(f32[512,640]{1,0:T(8,128)S(1)} %get-tuple-element.144.refs_3_), channel_id=1, source_target_pairs={{0,24},{8,0},{16,8},{24,16},{32,56},{40,32},{48,40},{56,48},{64,88... | collective-permute-start | bytes 3932168 | tf_op jit(solution)/shard_map/ppermute | solution.py:459
  187.9 85.3 %collective-permute-start.11 = (f32[1024,640]{1,0:T(8,128)S(1)}, f32[1024,640]{1,0:T(8,128)S(1)}, u32[]{:S(2)}, u32[]{:S(2)}) collective-permute-start(f32[1024,640]{1,0:T(8,128)S(1)} %pad_maximum_fusion.1), channel_id=1, source_target_pairs={{0,96},{8,104},{16,112},{24,120},{32,0},{40,8},{48,16},{56,24},{64... | collective-permute-start | bytes 7864328 | tf_op jit(solution)/shard_map/ppermute | solution.py:459
  263.0 32.9 %collective-permute-start.12 = (f32[512,640]{1,0:T(8,128)S(1)}, f32[512,640]{1,0:T(8,128)S(1)}, u32[]{:S(2)}, u32[]{:S(2)}) collective-permute-start(f32[512,640]{1,0:T(8,128)S(1)} %collective-permute-done.refs_0_), channel_id=1, source_target_pairs={{0,32},{8,40},{16,48},{24,56},{32,64},{40,72},{48,80},{56,88},{64,... | collective-permute-start | bytes 3932168 | tf_op jit(solution)/shard_map/ppermute | solution.py:459
  264.2 35.4 %collective-permute-start.13 = (f32[512,640]{1,0:T(8,128)S(1)}, f32[512,640]{1,0:T(8,128)S(1)}, u32[]{:S(2)}, u32[]{:S(2)}) collective-permute-start(f32[512,640]{1,0:T(8,128)S(1)} %collective-permute-done.1.refs_1_), channel_id=1, source_target_pairs={{0,8},{8,16},{16,24},{24,0},{32,40},{40,48},{48,56},{56,32},{64,72... | collective-permute-start | bytes 3932168 | tf_op jit(solution)/shard_map/ppermute | solution.py:459
  264.5 36.2 %collective-permute-start.14 = (f32[512,640]{1,0:T(8,128)S(1)}, f32[512,640]{1,0:T(8,128)S(1)}, u32[]{:S(2)}, u32[]{:S(2)}) collective-permute-start(f32[512,640]{1,0:T(8,128)S(1)} %collective-permute-done.6.refs_2_), channel_id=1, source_target_pairs={{0,96},{8,104},{16,112},{24,120},{32,0},{40,8},{48,16},{56,24},{64... | collective-permute-start | bytes 3932168 | tf_op jit(solution)/shard_map/ppermute | solution.py:459
  269.0 115.8 %collective-permute-start.16 = (f32[1024,640]{1,0:T(8,128)}, f32[1024,640]{1,0:T(8,128)S(1)}, u32[]{:S(2)}, u32[]{:S(2)}) collective-permute-start(f32[1024,640]{1,0:T(8,128)} %constant_dynamic-update-slice_fusion), channel_id=1, source_target_pairs={{0,8},{8,16},{16,24},{24,0},{32,40},{40,48},{48,56},{56,32},{64,72... | collective-permute-start | bytes 7864328 | tf_op jit(solution)/shard_map/ppermute | solution.py:459
  273.2 111.6 %collective-permute-start.17 = (f32[1024,640]{1,0:T(8,128)}, f32[1024,640]{1,0:T(8,128)S(1)}, u32[]{:S(2)}, u32[]{:S(2)}) collective-permute-start(f32[1024,640]{1,0:T(8,128)} %constant_dynamic-update-slice_fusion.2), channel_id=1, source_target_pairs={{0,32},{8,40},{16,48},{24,56},{32,64},{40,72},{48,80},{56,88},{64,... | collective-permute-start | bytes 7864328 | tf_op jit(solution)/shard_map/ppermute | solution.py:459
  295.9 89.0 %collective-permute-start.18 = (f32[1024,640]{1,0:T(8,128)}, f32[1024,640]{1,0:T(8,128)}, u32[]{:S(2)}, u32[]{:S(2)}) collective-permute-start(f32[1024,640]{1,0:T(8,128)} %constant_dynamic-update-slice_fusion), channel_id=1, source_target_pairs={{0,24},{8,0},{16,8},{24,16},{32,56},{40,32},{48,40},{56,48},{64,88... | collective-permute-start | bytes 7864328 | tf_op jit(solution)/shard_map/ppermute | solution.py:459
  299.6 85.4 %collective-permute-start.19 = (f32[1024,640]{1,0:T(8,128)}, f32[1024,640]{1,0:T(8,128)}, u32[]{:S(2)}, u32[]{:S(2)}) collective-permute-start(f32[1024,640]{1,0:T(8,128)} %constant_dynamic-update-slice_fusion.2), channel_id=1, source_target_pairs={{0,96},{8,104},{16,112},{24,120},{32,0},{40,8},{48,16},{56,24},{64... | collective-permute-start | bytes 7864328 | tf_op jit(solution)/shard_map/ppermute | solution.py:459
  300.8 80.3 %collective-permute-start.15 = (f32[512,640]{1,0:T(8,128)S(1)}, f32[512,640]{1,0:T(8,128)S(1)}, u32[]{:S(2)}, u32[]{:S(2)}) collective-permute-start(f32[512,640]{1,0:T(8,128)S(1)} %collective-permute-done.7.refs_3_), channel_id=1, source_target_pairs={{0,24},{8,0},{16,8},{24,16},{32,56},{40,32},{48,40},{56,48},{64,88... | collective-permute-start | bytes 3932168 | tf_op jit(solution)/shard_map/ppermute | solution.py:459
  312.8 98.5 %copy-start.4 = (f32[1024,640]{1,0:T(8,128)S(1)}, f32[1024,640]{1,0:T(8,128)}, u32[]{:S(2)}) copy-start(f32[1024,640]{1,0:T(8,128)} %get-tuple-element.109) | copy-start | bytes 7864324
  381.1 30.3 %collective-permute-start.24 = (f32[512,640]{1,0:T(8,128)S(1)}, f32[512,640]{1,0:T(8,128)S(1)}, u32[]{:S(2)}, u32[]{:S(2)}) collective-permute-start(f32[512,640]{1,0:T(8,128)S(1)} %collective-permute-done.12.refs_0_), channel_id=1, source_target_pairs={{0,24},{8,0},{16,8},{24,16},{32,56},{40,32},{48,40},{56,48},{64,88... | collective-permute-start | bytes 3932168 | tf_op jit(solution)/shard_map/ppermute | solution.py:459
  384.8 26.6 %collective-permute-start.25 = (f32[512,640]{1,0:T(8,128)S(1)}, f32[512,640]{1,0:T(8,128)S(1)}, u32[]{:S(2)}, u32[]{:S(2)}) collective-permute-start(f32[512,640]{1,0:T(8,128)S(1)} %collective-permute-done.13.refs_1_), channel_id=1, source_target_pairs={{0,96},{8,104},{16,112},{24,120},{32,0},{40,8},{48,16},{56,24},{64... | collective-permute-start | bytes 3932168 | tf_op jit(solution)/shard_map/ppermute | solution.py:459
  384.8 53.3 %collective-permute-start.26 = (f32[512,640]{1,0:T(8,128)S(1)}, f32[512,640]{1,0:T(8,128)}, u32[]{:S(2)}, u32[]{:S(2)}) collective-permute-start(f32[512,640]{1,0:T(8,128)S(1)} %collective-permute-done.14.refs_2_), channel_id=1, source_target_pairs={{0,24},{8,0},{16,8},{24,16},{32,56},{40,32},{48,40},{56,48},{64,88... | collective-permute-start | bytes 3932168 | tf_op jit(solution)/shard_map/ppermute | solution.py:459
  384.9 53.2 %collective-permute-start.27 = (f32[512,640]{1,0:T(8,128)S(1)}, f32[512,640]{1,0:T(8,128)}, u32[]{:S(2)}, u32[]{:S(2)}) collective-permute-start(f32[512,640]{1,0:T(8,128)S(1)} %collective-permute-done.15.refs_3_), channel_id=1, source_target_pairs={{0,96},{8,104},{16,112},{24,120},{32,0},{40,8},{48,16},{56,24},{64... | collective-permute-start | bytes 3932168 | tf_op jit(solution)/shard_map/ppermute | solution.py:459
  385.0 56.9 %collective-permute-start.30 = (f32[512,640]{1,0:T(8,128)S(1)}, f32[512,640]{1,0:T(8,128)}, u32[]{:S(2)}, u32[]{:S(2)}) collective-permute-start(f32[512,640]{1,0:T(8,128)S(1)} %collective-permute-done.12.refs_0_), channel_id=1, source_target_pairs={{0,8},{8,16},{16,24},{24,0},{32,40},{40,48},{48,56},{56,32},{64,72... | collective-permute-start | bytes 3932168 | tf_op jit(solution)/shard_map/ppermute | solution.py:459
  411.4 33.8 %collective-permute-start.31 = (f32[512,640]{1,0:T(8,128)S(1)}, f32[512,640]{1,0:T(8,128)}, u32[]{:S(2)}, u32[]{:S(2)}) collective-permute-start(f32[512,640]{1,0:T(8,128)S(1)} %collective-permute-done.13.refs_1_), channel_id=1, source_target_pairs={{0,32},{8,40},{16,48},{24,56},{32,64},{40,72},{48,80},{56,88},{64,... | collective-permute-start | bytes 3932168 | tf_op jit(solution)/shard_map/ppermute | solution.py:459
  411.4 86.9 %collective-permute-start.20 = (f32[1024,640]{1,0:T(8,128)S(1)}, f32[1024,640]{1,0:T(8,128)S(1)}, u32[]{:S(2)}, u32[]{:S(2)}) collective-permute-start(f32[1024,640]{1,0:T(8,128)S(1)} %copy-done.4), channel_id=1, source_target_pairs={{0,8},{8,16},{16,24},{24,0},{32,40},{40,48},{48,56},{56,32},{64,72... | collective-permute-start | bytes 7864328 | tf_op jit(solution)/shard_map/ppermute | solution.py:459
  438.1 64.6 %collective-permute-start.21 = (f32[1024,640]{1,0:T(8,128)S(1)}, f32[1024,640]{1,0:T(8,128)S(1)}, u32[]{:S(2)}, u32[]{:S(2)}) collective-permute-start(f32[1024,640]{1,0:T(8,128)S(1)} %get-tuple-element.110), channel_id=1, source_target_pairs={{0,32},{8,40},{16,48},{24,56},{32,64},{40,72},{48,80},{56,88},{64,... | collective-permute-start | bytes 7864328 | tf_op jit(solution)/shard_map/ppermute | solution.py:459
  438.1 67.8 %collective-permute-start.22 = (f32[1024,640]{1,0:T(8,128)S(1)}, f32[1024,640]{1,0:T(8,128)S(1)}, u32[]{:S(2)}, u32[]{:S(2)}) collective-permute-start(f32[1024,640]{1,0:T(8,128)S(1)} %copy-done.4), channel_id=1, source_target_pairs={{0,24},{8,0},{16,8},{24,16},{32,56},{40,32},{48,40},{56,48},{64,88... | collective-permute-start | bytes 7864328 | tf_op jit(solution)/shard_map/ppermute | solution.py:459
  441.9 67.0 %collective-permute-start.23 = (f32[1024,640]{1,0:T(8,128)S(1)}, f32[1024,640]{1,0:T(8,128)S(1)}, u32[]{:S(2)}, u32[]{:S(2)}) collective-permute-start(f32[1024,640]{1,0:T(8,128)S(1)} %get-tuple-element.110), channel_id=1, source_target_pairs={{0,96},{8,104},{16,112},{24,120},{32,0},{40,8},{48,16},{56,24},{64... | collective-permute-start | bytes 7864328 | tf_op jit(solution)/shard_map/ppermute | solution.py:459
  445.2 53.1 %collective-permute-start.32 = (f32[512,640]{1,0:T(8,128)S(1)}, f32[512,640]{1,0:T(8,128)S(1)}, u32[]{:S(2)}, u32[]{:S(2)}) collective-permute-start(f32[512,640]{1,0:T(8,128)S(1)} %collective-permute-done.14.refs_2_), channel_id=1, source_target_pairs={{0,8},{8,16},{16,24},{24,0},{32,40},{40,48},{48,56},{56,32},{64,72... | collective-permute-start | bytes 3932168 | tf_op jit(solution)/shard_map/ppermute | solution.py:459
  498.3 4.4 copy-start
  498.3 85.3 %collective-permute-start.28 = (f32[1024,640]{1,0:T(8,128)S(1)}, f32[1024,640]{1,0:T(8,128)S(1)}, u32[]{:S(2)}, u32[]{:S(2)}) collective-permute-start(f32[1024,640]{1,0:T(8,128)S(1)} %collective-permute-done.8.refs_0_), channel_id=1, source_target_pairs={{0,8},{8,16},{16,24},{24,0},{32,40},{40,48},{48,56},{56,32},{64,72... | collective-permute-start | bytes 7864328 | tf_op jit(solution)/shard_map/ppermute | solution.py:459
  498.3 86.4 %collective-permute-start.29 = (f32[1024,640]{1,0:T(8,128)S(1)}, f32[1024,640]{1,0:T(8,128)S(1)}, u32[]{:S(2)}, u32[]{:S(2)}) collective-permute-start(f32[1024,640]{1,0:T(8,128)S(1)} %collective-permute-done.9.refs_1_), channel_id=1, source_target_pairs={{0,32},{8,40},{16,48},{24,56},{32,64},{40,72},{48,80},{56,88},{64,... | collective-permute-start | bytes 7864328 | tf_op jit(solution)/shard_map/ppermute | solution.py:459
  502.7 99.2 %collective-permute-start.34 = (f32[1024,640]{1,0:T(8,128)}, f32[1024,640]{1,0:T(8,128)}, u32[]{:S(2)}, u32[]{:S(2)}) collective-permute-start(f32[1024,640]{1,0:T(8,128)} %collective-permute-done.18.refs_0_), channel_id=1, source_target_pairs={{0,24},{8,0},{16,8},{24,16},{32,56},{40,32},{48,40},{56,48},{64,88... | collective-permute-start | bytes 7864328 | tf_op jit(solution)/shard_map/ppermute | solution.py:459
  505.9 103.4 %collective-permute-start.35 = (f32[1024,640]{1,0:T(8,128)}, f32[1024,640]{1,0:T(8,128)}, u32[]{:S(2)}, u32[]{:S(2)}) collective-permute-start(f32[1024,640]{1,0:T(8,128)} %collective-permute-done.19.refs_1_), channel_id=1, source_target_pairs={{0,96},{8,104},{16,112},{24,120},{32,0},{40,8},{48,16},{56,24},{64... | collective-permute-start | bytes 7864328 | tf_op jit(solution)/shard_map/ppermute | solution.py:459
  509.0 73.1 %collective-permute-start.33 = (f32[512,640]{1,0:T(8,128)S(1)}, f32[512,640]{1,0:T(8,128)S(1)}, u32[]{:S(2)}, u32[]{:S(2)}) collective-permute-start(f32[512,640]{1,0:T(8,128)S(1)} %collective-permute-done.15.refs_3_), channel_id=1, source_target_pairs={{0,32},{8,40},{16,48},{24,56},{32,64},{40,72},{48,80},{56,88},{64,... | collective-permute-start | bytes 3932168 | tf_op jit(solution)/shard_map/ppermute | solution.py:459
  582.0 6.9 %copy-start.2 = (f32[512,640]{1,0:T(8,128)}, f32[512,640]{1,0:T(8,128)S(1)}, u32[]{:S(2)}) copy-start(f32[512,640]{1,0:T(8,128)S(1)} %collective-permute-done.33.refs_1_) | copy-start | bytes 3932164
  582.0 32.0 %collective-permute-start.36 = (f32[512,640]{1,0:T(8,128)}, f32[512,640]{1,0:T(8,128)}, u32[]{:S(2)}, u32[]{:S(2)}) collective-permute-start(f32[512,640]{1,0:T(8,128)} %slice.44), channel_id=1, source_target_pairs={{0,8},{8,16},{16,24},{24,0},{32,40},{40,48},{48,56},{56,32},{64,72... | collective-permute-start | bytes 3932168 | tf_op jit(solution)/shard_map/ppermute | solution.py:459
  583.5 30.4 %collective-permute-start.37 = (f32[512,640]{1,0:T(8,128)}, f32[512,640]{1,0:T(8,128)}, u32[]{:S(2)}, u32[]{:S(2)}) collective-permute-start(f32[512,640]{1,0:T(8,128)} %slice.45), channel_id=1, source_target_pairs={{0,32},{8,40},{16,48},{24,56},{32,64},{40,72},{48,80},{56,88},{64,... | collective-permute-start | bytes 3932168 | tf_op jit(solution)/shard_map/ppermute | solution.py:459
  584.7 29.3 %collective-permute-start.38 = (f32[512,640]{1,0:T(8,128)}, f32[512,640]{1,0:T(8,128)}, u32[]{:S(2)}, u32[]{:S(2)}) collective-permute-start(f32[512,640]{1,0:T(8,128)} %slice.46), channel_id=1, source_target_pairs={{0,24},{8,0},{16,8},{24,16},{32,56},{40,32},{48,40},{56,48},{64,88... | collective-permute-start | bytes 3932168 | tf_op jit(solution)/shard_map/ppermute | solution.py:459
  601.9 28.9 %collective-permute-start.39 = (f32[512,640]{1,0:T(8,128)}, f32[512,640]{1,0:T(8,128)}, u32[]{:S(2)}, u32[]{:S(2)}) collective-permute-start(f32[512,640]{1,0:T(8,128)} %slice.47), channel_id=1, source_target_pairs={{0,96},{8,104},{16,112},{24,120},{32,0},{40,8},{48,16},{56,24},{64... | collective-permute-start | bytes 3932168 | tf_op jit(solution)/shard_map/ppermute | solution.py:459
  609.4 26.1 %collective-permute-start.40 = (f32[512,640]{1,0:T(8,128)}, f32[512,640]{1,0:T(8,128)}, u32[]{:S(2)}, u32[]{:S(2)}) collective-permute-start(f32[512,640]{1,0:T(8,128)} %collective-permute-done.31.refs_1_), channel_id=1, source_target_pairs={{0,32},{8,40},{16,48},{24,56},{32,64},{40,72},{48,80},{56,88},{64,... | collective-permute-start | bytes 3932168 | tf_op jit(solution)/shard_map/ppermute | solution.py:459
  614.0 21.5 %collective-permute-start.41 = (f32[512,640]{1,0:T(8,128)}, f32[512,640]{1,0:T(8,128)}, u32[]{:S(2)}, u32[]{:S(2)}) collective-permute-start(f32[512,640]{1,0:T(8,128)} %collective-permute-done.27.refs_3_), channel_id=1, source_target_pairs={{0,96},{8,104},{16,112},{24,120},{32,0},{40,8},{48,16},{56,24},{64... | collective-permute-start | bytes 3932168 | tf_op jit(solution)/shard_map/ppermute | solution.py:459
  614.0 24.1 %collective-permute-start.42 = (f32[512,640]{1,0:T(8,128)}, f32[512,640]{1,0:T(8,128)}, u32[]{:S(2)}, u32[]{:S(2)}) collective-permute-start(f32[512,640]{1,0:T(8,128)} %collective-permute-done.30.refs_0_), channel_id=1, source_target_pairs={{0,8},{8,16},{16,24},{24,0},{32,40},{40,48},{48,56},{56,32},{64,72... | collective-permute-start | bytes 3932168 | tf_op jit(solution)/shard_map/ppermute | solution.py:459
  614.0 24.1 %collective-permute-start.43 = (f32[512,640]{1,0:T(8,128)}, f32[512,640]{1,0:T(8,128)}, u32[]{:S(2)}, u32[]{:S(2)}) collective-permute-start(f32[512,640]{1,0:T(8,128)} %collective-permute-done.26.refs_2_), channel_id=1, source_target_pairs={{0,24},{8,0},{16,8},{24,16},{32,56},{40,32},{48,40},{56,48},{64,88... | collective-permute-start | bytes 3932168 | tf_op jit(solution)/shard_map/ppermute | solution.py:459
  620.5 3.3 copy-start.3
  (1 other events, 2.8 us)

commit v2 on v1

--- a/solution.py
+++ b/solution.py
@@ -82,9 +82,9 @@
     few = tokens // N_TP
     pack = 16
     sub = 512
-    tile = part // 2
-    tiles = vocab // tile
-    depth = 3
+    per = part // sub
+    tiles = vocab // sub
+    depth = 6
 
     def kern(hid_hbm, gain_hbm, mask_hbm, tea_ref, tab_ref, got_late, blocks_ref, x_out, tab_out, coef_ref, all_ref, gh_ref, gg_ref,
              hid_ref, gain_ref, mask_in, w_ref, raw, sends, stage, got_soon, tabs, n_buf, x_buf, inv_buf, square, pay, pay_got, mask_own, mask_got, x_got, tp_got, own_col,
@@ -100,7 +100,7 @@
 
         def tab_copy(i):
             slot = lax.rem(i, depth)
-            return pltpu.make_async_copy(tab_ref.at[aligned(lax.rem(i, tiles) * tile, tile)], tabs.at[slot], tab_sem.at[slot])
+            return pltpu.make_async_copy(tab_ref.at[aligned(lax.rem(i, tiles) * sub, sub)], tabs.at[slot], tab_sem.at[slot])
 
         inputs = [pltpu.make_async_copy(src, dst, in_sem.at[2 + i])
                   for i, (src, dst) in enumerate(((hid_hbm, hid_ref), (gain_hbm, gain_ref), (mask_hbm, mask_in)))]
@@ -131,6 +131,21 @@
         square[0:1, 0:tokens] = mask_in[...]
         mask_own[...] = square[0:few]
         mask_col = jnp.transpose(square[...])[0:tokens, 0:1]
+
+        def weigh(k):
+            fetch(k).wait()
+            d = at[ORDER[k]]
+
+            def rows(r, _):
+                here = aligned(d * tokens + r * pack, pack, pack)
+                cap = jnp.tanh(raw[here].astype(F32) * INV_CAP)
+                sends[here] = jnp.exp(SOFT_CAP * cap - SOFT_CAP)
+                return 0
+
+            lax.fori_loop(0, tokens // pack, rows, 0)
+
+        weigh(0)
+        weigh(1)
         pl.semaphore_wait(barrier, N_DP + N_TP - 2)
 
         def remote(src, dst, out, into, dp, tp):
@@ -203,16 +218,8 @@
         mask_got[me] = mask_own[...]
 
         for k, o in enumerate(ORDER):
-            fetch(k).wait()
-            d = at[o]
-
-            def weigh(r, _):
-                here = aligned(d * tokens + r * pack, pack, pack)
-                cap = jnp.tanh(raw[here].astype(F32) * INV_CAP)
-                sends[here] = jnp.exp(SOFT_CAP * cap - SOFT_CAP)
-                return 0
-
-            lax.fori_loop(0, tokens // pack, weigh, 0)
+            if k > 1:
+                weigh(k)
             for j, (_, to) in enumerate(JOBS):
                 if to == o:
                     for w in waves(j, 0):
@@ -232,8 +239,8 @@
                 total = total + v[:, c:c + LANES]
             return total
 
-        def student(slot, here):
-            z = lax.dot_general(x_buf[...], tabs[slot, here], ROWS_BY_ROWS, preferred_element_type=F32)
+        def student(slot):
+            z = lax.dot_general(x_buf[...], tabs[slot], ROWS_BY_ROWS, preferred_element_type=F32)
             ratio = jnp.tanh(z * INV_CAP)
             return ratio, jnp.exp(SOFT_CAP * ratio - SOFT_CAP)
 
@@ -242,15 +249,11 @@
             tab_copy(i).wait()
             tab_copy(i + depth - 1).start()
             s_sum, t_sum, k_sum = sums
-            for c in range(0, tile, sub):
-                ratio, stu = student(slot, pl.ds(c, sub))
-                toks, here = aligned(lax.div(i, 2) * tokens, tokens, tokens), aligned(lax.rem(i, 2) * tile + c, sub)
-                cap = jnp.tanh(raw[toks, here].astype(F32) * INV_CAP)
-                tea = sends[toks, here]
-                s_sum = s_sum + fold(stu)
-                t_sum = t_sum + fold(tea)
-                k_sum = k_sum + fold(tea * (cap - ratio))
-            return s_sum, t_sum, k_sum
+            ratio, stu = student(slot)
+            toks, here = aligned(lax.div(i, per) * tokens, tokens, tokens), aligned(lax.rem(i, per) * sub, sub)
+            cap = jnp.tanh(raw[toks, here].astype(F32) * INV_CAP)
+            tea = sends[toks, here]
+            return s_sum + fold(stu), t_sum + fold(tea), k_sum + fold(tea * (cap - ratio))
 
         zero = jnp.zeros((tokens, LANES), F32)
         s_sum, t_sum, k_sum = lax.fori_loop(0, tiles, forward, (zero, zero, zero))
@@ -272,7 +275,7 @@
         start(dp_sends)
         came(0)
         onward(1, True, None)
-        onward(1, False, 0, 1)
+        onward(1, False, 0)
 
         arrive((*pay_came, *mask_came))
         x_got[col] = pay_got[...]
@@ -290,13 +293,11 @@
             def _():
                 tab_copy(i + depth - 1).start()
 
-            for c in range(0, tile, sub):
-                here = pl.ds(c, sub)
-                ratio, stu = student(slot, here)
-                tea = sends[aligned(lax.div(i - tiles, 2) * tokens, tokens, tokens), aligned(lax.rem(i, 2) * tile + c, sub)]
-                diff = (stu * inv_s - tea * inv_t) * weight
-                g = (diff * (1.0 - ratio * ratio)).astype(BF16)
-                dx[...] += jnp.dot(g, tabs[slot, here], preferred_element_type=F32)
+            ratio, stu = student(slot)
+            tea = sends[aligned(lax.div(i - tiles, per) * tokens, tokens, tokens), aligned(lax.rem(i, per) * sub, sub)]
+            diff = (stu * inv_s - tea * inv_t) * weight
+            g = (diff * (1.0 - ratio * ratio)).astype(BF16)
+            dx[...] += jnp.dot(g, tabs[slot], preferred_element_type=F32)
             return 0
 
         lax.fori_loop(tiles, 2 * tiles, backward, 0)
@@ -325,6 +326,10 @@
         gn_sends, gn_came = to_dp(gn_own, gn_got, DOWN, pl.ds(0, 1))
         start(gn_sends)
 
+        came(2, 0)
+        onward(DOWN, True, 0)
+        onward(2, True, 1)
+        onward(1, False, 1)
         arrive(xt_came)
 
         def widen(d, _):
@@ -344,25 +349,25 @@
             square[k * few:(k + 1) * few] = rel[aligned(at[-dz, -dy] * few, few, few)]
         coef_ref[...] = jnp.transpose(square[...])
 
-        arrive(gn_came)
-        gg_ref[...] = added(gn_got, slice(1))
         own_tab.wait()
-        came(2, 0)
-        onward(DOWN, True, 0)
-        onward(2, True, 1)
         for j, path in enumerate(PATHS):
             hop(j, len(path) - 1, 0).wait_recv()
         for j, level, w in COPIES:
             if level == 0:
                 hop(j, level, w).wait_send()
-        came(2, 1)
-        onward(DOWN, True, 1)
 
         def block(b, _):
+            @pl.when(b == 1)
+            def _():
+                came(2, 1)
+                onward(DOWN, True, 1)
+
             grad_block(at, got_soon, x_out, tab_out[aligned(b * sub, sub)], coef_ref, sends, raw, blocks_ref, b)
             return 0
 
         lax.fori_loop(0, 2, block, 0)
+        arrive(gn_came)
+        gg_ref[...] = added(gn_got, slice(1))
         for j, path in enumerate(PATHS):
             hop(j, len(path) - 1, 1).wait_recv()
         for j, level, w in COPIES:
@@ -382,7 +387,7 @@
         scratch_shapes=[pltpu.VMEM(shape, kind) for shape, kind in (
             (wide, BF16), ((dim // LANES, LANES), F32), ((1, tokens), F32), ((1, dim), F32), ((N_DP * tokens, part), BF16), ((N_DP * tokens, part), F32),
             ((len(MIDDLE), half, part), F32), ((N_DP, tokens, part // 2), F32),
-            ((depth, tile, dim), BF16), (wide, F32), (wide, BF16), ((tokens, LANES), F32), ((LANES, LANES), F32), ((few, dim), F32),
+            ((depth, sub, dim), BF16), (wide, F32), (wide, BF16), ((tokens, LANES), F32), ((LANES, LANES), F32), ((few, dim), F32),
             ((N_DP, few, dim), F32), (flat, F32), ((N_DP, *flat), F32), ((N_TP, N_DP, few, dim), F32), ((N_TP, tokens, LANES), F32),
             ((tokens, LANES), F32), (flat, F32), ((LANES, LANES), F32), (wide, F32), ((N_TP, few, dim), F32), ((2 * few, dim), F32),
             ((N_TP, 2 * few, dim), F32), ((few, dim), F32), ((N_DP, few, dim), F32))] + [
@@ -418,7 +423,7 @@
     dim = arrays[0].shape[1]
     rows = vocab // N_DP
     quarter = rows // SIDE
-    cut = 256
+    cut = 128
     chunks = [(i, r) for i in range(n) for r in range(0, arrays[i].shape[0], cut)]
 
     def kern(*refs):
@@ -426,8 +431,8 @@
         at = peers()[1]
         reads, writes = [], []
         for k, (i, r) in enumerate(chunks):
-            _, dz, dy, kind, half = pieces[i]
-            first = (2 * (half + r // quarter) + kind) * quarter + r % quarter
+            _, dz, dy, kind, half, start = pieces[i]
+            first = (2 * (half + r // quarter) + kind) * quarter + start + r % quarter
             there = aligned(at[dz, dy] * rows + first, cut, cut)
             reads.append(pltpu.make_async_copy(refs[i].at[pl.ds(r, cut)], buf.at[k], sem.at[0, k]))
             writes.append(pltpu.make_async_copy(buf.at[k], dst.at[there], sem.at[1, k]))
@@ -450,6 +455,8 @@
 def gather(first, rest, vocab):
     quarter = first[0].shape[0]
     sets, ways = range(2), (UP, DOWN)
+    most = quarter - LANES
+    cuts = slice(0, most), slice(most, quarter)
     table, event = None, 0
 
     def send(pair, axis, step):
@@ -459,8 +466,8 @@
             out.append(lax.ppermute(pair[k], 'dp', [(d, shift(d, dz, dy)) for d in range(N_DP)]))
         return out
 
-    def put(pair, a, b, c=0):
-        return [(pair[k], *((b, a) if k else (a, b)), k, c) for k in sets]
+    def put(pair, a, b, c=0, start=0):
+        return [(pair[k], *((b, a) if k else (a, b)), k, c, start) for k in sets]
 
     def settle(*pieces):
         nonlocal table
@@ -517,12 +524,12 @@
     settle(put(high_side[DOWN], UP, UP))
 
     far_side[0, DOWN], far_side[1, DOWN], side_far = wait(far_side[0, DOWN], far_side[1, DOWN], side_far)
-    last_down = send(far_side[1, DOWN], 1, DOWN)
+    last_down = [send([x[cut] for x in far_side[1, DOWN]], 1, DOWN) for cut in cuts]
     settle(put(far_side[0, DOWN], AWAY, UP, 0), put(far_side[1, DOWN], AWAY, UP, 1))
     settle(put(side_far, 0, AWAY))
 
     far_side[0, UP], = wait(far_side[0, UP])
-    last_up = send(far_side[0, UP], 1, UP)
+    last_up = [send([x[cut] for x in far_side[0, UP]], 1, UP) for cut in cuts]
     settle(put(far_side[0, UP], AWAY, DOWN, 0))
 
     far_side[1, UP], low_far = wait(far_side[1, UP], low_far)
@@ -531,9 +538,9 @@
 
     high_far = wait(*high_far)
     settle(put(high_far[0], UP, AWAY, 0), put(high_far[1], UP, AWAY, 1))
-    for k in (1, 0):
-        table, up, down = lax.optimization_barrier((table, last_up[k], last_down[k]))
-        table = place(table, [put([up] * 2, AWAY, AWAY, 0)[k], put([down] * 2, AWAY, AWAY, 1)[k]], vocab)
+    for up, down, cut in zip(last_up, last_down, cuts):
+        up, down = wait(up, down)
+        settle(put(up, AWAY, AWAY, 0, cut.start), put(down, AWAY, AWAY, 1, cut.start))
     return table
 
 

time: 643 us -> 672 us (1.045)
  the two profiles are of different devices: /device:TPU:0 before, /device:TPU:6 now
where the time goes in v2:
time: 672 us; the launch traced here: 665 us
  waiting for transfers between devices  384 us (57%)
  Pallas kernels  200 us (30%)
  starting transfers between devices  56.3 us (8%)
  local copies, waits for them, and re-layouts  19 us (3%)
    ppermute x48, waiting for transfers between devices, send(): lax.ppermute(pair[k], 'dp', [(d, shift(d, dz, dy)) for d in range(N_DP)])  384 us
    pallas_call x1, Pallas kernels, front(): pl.pallas_call(kern, out_shape=tuple((jax.ShapeDtypeStruct(shape, kind) f...  119 us
    pallas_call x18, Pallas kernels, place(): pl.pallas_call(kern, out_shape=jax.ShapeDtypeStruct((vocab, dim), F32), i...  72.9 us
    ppermute x48, starting transfers between devices, send(): lax.ppermute(pair[k], 'dp', [(d, shift(d, dz, dy)) for d in range(N_DP)])  56.3 us
  transfers between devices with their start and end apart: 48, of which 17 were waited for; matrix products, arithmetic and copies ran while one was open for 2% of the time, Pallas kernels for 12%

profile of v2, /device:TPU:6, one launch (start us, length us, event | category | flops | bytes accessed | tf_op | source)
XLA Modules:
  0.0 665.0 jit_solution(15213055000700811994)
XLA Ops:
  0.6 119.5 %front.1 = (f32[16,64,1024]{2,1,0:T(8,128)S(1)}, f32[2,512,640]{2,1,0:T(8,128)S(1)}, bf16[1024,640]{1,0:T(8,128)(2,1)S(1)}, bf16[2048,640]{1,0:T(8,128)(2,1)S(1)...) custom-call(bf16[64,640]{1,0:T(8,128)(2,1)} %hid_hbm.1, ...), custom_call_target="tpu_custom_call" | custom-call | flops 3000000000 | bytes 104857600 | tf_op jit(solution)/shard_map/front/pallas_call | solution.py:381
  121.6 2.6 collective-permute-start.2
  124.2 3.1 collective-permute-start.3
  127.3 7.2 %finish.1 = f32[2,512,640]{2,1,0:T(8,128)S(1)} custom-call(f32[16,64,1024]{2,1,0:T(8,128)S(1)} %get-tuple-element.84.tea_ref, bf16[1024,640]{1,0:T(8,128)(2,1)S(1)} %get-tuple-element.85.x_ref, bf16[2048,640]{1,0:T(8,128)(2,1)S(1)} %get-tuple-element.86.tab_ref, f32[128,128]{1,0:T(8,128)S(1)} %get-tuple-element.87.coef_ref), custom_call_target="tpu_custom_call" | custom-call | flops 1000000000 | bytes 8388608 | tf_op jit(solution)/shard_map/finish/pallas_call | solution.py:414
  134.7 18.5 %collective-permute-done.refs_0_ = f32[512,640]{1,0:T(8,128)S(1)} collective-permute-done((f32[512,640]{1,0:T(8,128)S(1)}, f32[512,640]{1,0:T(8,128)S(1)}, u32[]{:S(2)}, u32[]{:S(2)}) %collective-permute-start) | collective-permute-done | bytes 1310752 | tf_op jit(solution)/shard_map/ppermute | solution.py:466
  157.6 23.7 %collective-permute-done.4.refs_0_ = f32[512,640]{1,0:T(8,128)S(1)} collective-permute-done((f32[512,640]{1,0:T(8,128)S(1)}, f32[512,640]{1,0:T(8,128)S(1)}, u32[]{:S(2)}, u32[]{:S(2)}) %collective-permute-start.4) | collective-permute-done | bytes 1310752 | tf_op jit(solution)/shard_map/ppermute | solution.py:466
  183.0 3.1 collective-permute-done.5.refs_1_
  187.4 4.2 place.18.refs_4_
  191.6 74.9 %collective-permute-done.7.refs_3_ = f32[512,640]{1,0:T(8,128)S(1)} collective-permute-done((f32[512,640]{1,0:T(8,128)S(1)}, f32[512,640]{1,0:T(8,128)S(1)}, u32[]{:S(2)}, u32[]{:S(2)}) %collective-permute-start.7) | collective-permute-done | bytes 1310752 | tf_op jit(solution)/shard_map/ppermute | solution.py:466
  266.5 4.2 place.19.refs_4_
  271.4 3.2 collective-permute-start.14
  280.6 18.8 %collective-permute-done.12.refs_0_ = f32[512,640]{1,0:T(8,128)S(1)} collective-permute-done((f32[512,640]{1,0:T(8,128)S(1)}, f32[512,640]{1,0:T(8,128)S(1)}, u32[]{:S(2)}, u32[]{:S(2)}) %collective-permute-start.12) | collective-permute-done | bytes 1310752 | tf_op jit(solution)/shard_map/ppermute | solution.py:466
  299.3 2.9 collective-permute-start.18
  305.4 3.4 collective-permute-start.19
  308.8 4.2 place.20.refs_2_
  313.4 4.3 place.21.refs_2_
  317.7 4.3 place.22.refs_4_
  322.0 62.6 %collective-permute-done.15.refs_3_ = f32[512,640]{1,0:T(8,128)} collective-permute-done((f32[512,640]{1,0:T(8,128)S(1)}, f32[512,640]{1,0:T(8,128)}, u32[]{:S(2)}, u32[]{:S(2)}) %collective-permute-start.15) | collective-permute-done | bytes 1310752 | tf_op jit(solution)/shard_map/ppermute | solution.py:466
  384.6 3.0 collective-permute-start.24
  387.7 3.2 collective-permute-start.26
  391.1 25.7 %collective-permute-done.24.refs_0_ = f32[512,640]{1,0:T(8,128)S(1)} collective-permute-done((f32[512,640]{1,0:T(8,128)S(1)}, f32[512,640]{1,0:T(8,128)S(1)}, u32[]{:S(2)}, u32[]{:S(2)}) %collective-permute-start.24) | collective-permute-done | bytes 1310752 | tf_op jit(solution)/shard_map/ppermute | solution.py:466
  416.7 2.8 collective-permute-done.25.refs_1_
  419.5 21.9 %collective-permute-done.26.refs_2_ = f32[512,640]{1,0:T(8,128)S(1)} collective-permute-done((f32[512,640]{1,0:T(8,128)}, f32[512,640]{1,0:T(8,128)S(1)}, u32[]{:S(2)}, u32[]{:S(2)}) %collective-permute-start.26) | collective-permute-done | bytes 1310752 | tf_op jit(solution)/shard_map/ppermute | solution.py:466
  441.4 3.2 collective-permute-start.22
  445.7 27.0 %collective-permute-done.30.refs_0_ = f32[512,640]{1,0:T(8,128)S(1)} collective-permute-done((f32[512,640]{1,0:T(8,128)S(1)}, f32[512,640]{1,0:T(8,128)S(1)}, u32[]{:S(2)}, u32[]{:S(2)}) %collective-permute-start.30) | collective-permute-done | bytes 1310752 | tf_op jit(solution)/shard_map/ppermute | solution.py:466
  473.8 4.7 place.23.refs_2_
  478.6 2.3 collective-permute-start.34
  480.9 21.0 %collective-permute-done.22.refs_0_ = f32[1024,640]{1,0:T(8,128)S(1)} collective-permute-done((f32[1024,640]{1,0:T(8,128)S(1)}, f32[1024,640]{1,0:T(8,128)S(1)}, u32[]{:S(2)}, u32[]{:S(2)}) %collective-permute-start.22) | collective-permute-done | bytes 2621472 | tf_op jit(solution)/shard_map/ppermute | solution.py:466
  501.9 31.8 %collective-permute-done.28.refs_0_ = f32[1024,640]{1,0:T(8,128)S(1)} collective-permute-done((f32[1024,640]{1,0:T(8,128)S(1)}, f32[1024,640]{1,0:T(8,128)S(1)}, u32[]{:S(2)}, u32[]{:S(2)}) %collective-permute-start.28) | collective-permute-done | bytes 2621472 | tf_op jit(solution)/shard_map/ppermute | solution.py:466
  536.9 4.2 place.24.refs_2_
  541.1 4.9 place.25.refs_2_
  546.1 4.3 place.26.refs_2_
  550.4 4.3 place.27.refs_4_
  556.0 4.2 place.28.refs_2_
  560.2 4.3 place.29.refs_2_
  566.3 20.8 %collective-permute-done.33.refs_1_ = f32[512,640]{1,0:T(8,128)} collective-permute-done((f32[512,640]{1,0:T(8,128)}, f32[512,640]{1,0:T(8,128)}, u32[]{:S(2)}, u32[]{:S(2)}) %collective-permute-start.33) | collective-permute-done | bytes 1310752 | tf_op jit(solution)/shard_map/ppermute | solution.py:466
  587.0 2.2 collective-permute-start.42
  589.7 17.6 %collective-permute-done.41.refs_1_ = f32[384,640]{1,0:T(8,128)S(1)} collective-permute-done((f32[384,640]{1,0:T(8,128)S(1)}, f32[384,640]{1,0:T(8,128)S(1)}, u32[]{:S(2)}, u32[]{:S(2)}) %collective-permute-start.41) | collective-permute-done | bytes 983072 | tf_op jit(solution)/shard_map/ppermute | solution.py:466
  607.3 2.9 collective-permute-start.38
  610.3 3.2 collective-permute-start.39
  618.5 10.9 %collective-permute-done.37.refs_1_ = f32[512,640]{1,0:T(8,128)S(1)} collective-permute-done((f32[512,640]{1,0:T(8,128)S(1)}, f32[512,640]{1,0:T(8,128)S(1)}, u32[]{:S(2)}, u32[]{:S(2)}) %collective-permute-start.37) | collective-permute-done | bytes 1310752 | tf_op jit(solution)/shard_map/ppermute | solution.py:466
  631.6 3.2 collective-permute-start.46
  635.8 3.2 collective-permute-start.47
  642.3 3.0 place.30.refs_2_
  645.3 2.6 place.31.refs_2_
  648.0 5.1 place.32.refs_4_
  653.5 4.2 place.33.refs_4_
  657.8 3.7 place.34.refs_4_
  (136 shorter events, 41.2 us)
Async XLA Ops:
  120.3 32.9 %collective-permute-start = (f32[512,640]{1,0:T(8,128)S(1)}, f32[512,640]{1,0:T(8,128)S(1)}, u32[]{:S(2)}, u32[]{:S(2)}) collective-permute-start(f32[512,640]{1,0:T(8,128)S(1)} %get-tuple-element.82.refs_0_), channel_id=1, source_target_pairs={{0,32},{8,40},{16,48},{24,56},{32,64},{40,72},{48,80},{56,88},{64,... | collective-permute-start | bytes 3932168 | tf_op jit(solution)/shard_map/ppermute | solution.py:466
  121.0 33.0 %collective-permute-start.1 = (f32[512,640]{1,0:T(8,128)S(1)}, f32[512,640]{1,0:T(8,128)S(1)}, u32[]{:S(2)}, u32[]{:S(2)}) collective-permute-start(f32[512,640]{1,0:T(8,128)S(1)} %get-tuple-element.83.refs_1_), channel_id=1, source_target_pairs={{0,8},{8,16},{16,24},{24,0},{32,40},{40,48},{48,56},{56,32},{64,72... | collective-permute-start | bytes 3932168 | tf_op jit(solution)/shard_map/ppermute | solution.py:466
  121.6 34.1 %collective-permute-start.2 = (f32[512,640]{1,0:T(8,128)S(1)}, f32[512,640]{1,0:T(8,128)S(1)}, u32[]{:S(2)}, u32[]{:S(2)}) collective-permute-start(f32[512,640]{1,0:T(8,128)S(1)} %get-tuple-element.82.refs_0_), channel_id=1, source_target_pairs={{0,96},{8,104},{16,112},{24,120},{32,0},{40,8},{48,16},{56,24},{64... | collective-permute-start | bytes 3932168 | tf_op jit(solution)/shard_map/ppermute | solution.py:466
  124.2 32.1 %collective-permute-start.3 = (f32[512,640]{1,0:T(8,128)S(1)}, f32[512,640]{1,0:T(8,128)S(1)}, u32[]{:S(2)}, u32[]{:S(2)}) collective-permute-start(f32[512,640]{1,0:T(8,128)S(1)} %get-tuple-element.83.refs_1_), channel_id=1, source_target_pairs={{0,24},{8,0},{16,8},{24,16},{32,56},{40,32},{48,40},{56,48},{64,88... | collective-permute-start | bytes 3932168 | tf_op jit(solution)/shard_map/ppermute | solution.py:466
  134.7 46.6 %collective-permute-start.4 = (f32[512,640]{1,0:T(8,128)S(1)}, f32[512,640]{1,0:T(8,128)S(1)}, u32[]{:S(2)}, u32[]{:S(2)}) collective-permute-start(f32[512,640]{1,0:T(8,128)S(1)} %get-tuple-element.153.refs_2_), channel_id=1, source_target_pairs={{0,32},{8,40},{16,48},{24,56},{32,64},{40,72},{48,80},{56,88},{64,... | collective-permute-start | bytes 3932168 | tf_op jit(solution)/shard_map/ppermute | solution.py:466
  153.2 32.9 %collective-permute-start.5 = (f32[512,640]{1,0:T(8,128)S(1)}, f32[512,640]{1,0:T(8,128)S(1)}, u32[]{:S(2)}, u32[]{:S(2)}) collective-permute-start(f32[512,640]{1,0:T(8,128)S(1)} %get-tuple-element.152.refs_3_), channel_id=1, source_target_pairs={{0,8},{8,16},{16,24},{24,0},{32,40},{40,48},{48,56},{56,32},{64,72... | collective-permute-start | bytes 3932168 | tf_op jit(solution)/shard_map/ppermute | solution.py:466
  154.0 32.6 %collective-permute-start.6 = (f32[512,640]{1,0:T(8,128)S(1)}, f32[512,640]{1,0:T(8,128)S(1)}, u32[]{:S(2)}, u32[]{:S(2)}) collective-permute-start(f32[512,640]{1,0:T(8,128)S(1)} %get-tuple-element.153.refs_2_), channel_id=1, source_target_pairs={{0,96},{8,104},{16,112},{24,120},{32,0},{40,8},{48,16},{56,24},{64... | collective-permute-start | bytes 3932168 | tf_op jit(solution)/shard_map/ppermute | solution.py:466
  155.7 115.1 %collective-permute-start.8 = (f32[1024,640]{1,0:T(8,128)S(1)}, f32[1024,640]{1,0:T(8,128)S(1)}, u32[]{:S(2)}, u32[]{:S(2)}) collective-permute-start(f32[1024,640]{1,0:T(8,128)S(1)} %pad_maximum_fusion), channel_id=1, source_target_pairs={{0,8},{8,16},{16,24},{24,0},{32,40},{40,48},{48,56},{56,32},{64,72... | collective-permute-start | bytes 7864328 | tf_op jit(solution)/shard_map/ppermute | solution.py:466
  156.3 115.1 %collective-permute-start.9 = (f32[1024,640]{1,0:T(8,128)S(1)}, f32[1024,640]{1,0:T(8,128)S(1)}, u32[]{:S(2)}, u32[]{:S(2)}) collective-permute-start(f32[1024,640]{1,0:T(8,128)S(1)} %pad_maximum_fusion.1), channel_id=1, source_target_pairs={{0,32},{8,40},{16,48},{24,56},{32,64},{40,72},{48,80},{56,88},{64,... | collective-permute-start | bytes 7864328 | tf_op jit(solution)/shard_map/ppermute | solution.py:466
  181.3 95.7 %collective-permute-start.10 = (f32[1024,640]{1,0:T(8,128)S(1)}, f32[1024,640]{1,0:T(8,128)S(1)}, u32[]{:S(2)}, u32[]{:S(2)}) collective-permute-start(f32[1024,640]{1,0:T(8,128)S(1)} %pad_maximum_fusion), channel_id=1, source_target_pairs={{0,24},{8,0},{16,8},{24,16},{32,56},{40,32},{48,40},{56,48},{64,88... | collective-permute-start | bytes 7864328 | tf_op jit(solution)/shard_map/ppermute | solution.py:466
  186.1 94.5 %collective-permute-start.11 = (f32[1024,640]{1,0:T(8,128)S(1)}, f32[1024,640]{1,0:T(8,128)S(1)}, u32[]{:S(2)}, u32[]{:S(2)}) collective-permute-start(f32[1024,640]{1,0:T(8,128)S(1)} %pad_maximum_fusion.1), channel_id=1, source_target_pairs={{0,96},{8,104},{16,112},{24,120},{32,0},{40,8},{48,16},{56,24},{64... | collective-permute-start | bytes 7864328 | tf_op jit(solution)/shard_map/ppermute | solution.py:466
  186.6 79.9 %collective-permute-start.7 = (f32[512,640]{1,0:T(8,128)S(1)}, f32[512,640]{1,0:T(8,128)S(1)}, u32[]{:S(2)}, u32[]{:S(2)}) collective-permute-start(f32[512,640]{1,0:T(8,128)S(1)} %get-tuple-element.152.refs_3_), channel_id=1, source_target_pairs={{0,24},{8,0},{16,8},{24,16},{32,56},{40,32},{48,40},{56,48},{64,88... | collective-permute-start | bytes 3932168 | tf_op jit(solution)/shard_map/ppermute | solution.py:466
  266.5 32.9 %collective-permute-start.12 = (f32[512,640]{1,0:T(8,128)S(1)}, f32[512,640]{1,0:T(8,128)S(1)}, u32[]{:S(2)}, u32[]{:S(2)}) collective-permute-start(f32[512,640]{1,0:T(8,128)S(1)} %collective-permute-done.refs_0_), channel_id=1, source_target_pairs={{0,32},{8,40},{16,48},{24,56},{32,64},{40,72},{48,80},{56,88},{64,... | collective-permute-start | bytes 3932168 | tf_op jit(solution)/shard_map/ppermute | solution.py:466
  270.7 33.0 %collective-permute-start.13 = (f32[512,640]{1,0:T(8,128)S(1)}, f32[512,640]{1,0:T(8,128)}, u32[]{:S(2)}, u32[]{:S(2)}) collective-permute-start(f32[512,640]{1,0:T(8,128)S(1)} %collective-permute-done.1.refs_1_), channel_id=1, source_target_pairs={{0,8},{8,16},{16,24},{24,0},{32,40},{40,48},{48,56},{56,32},{64,72... | collective-permute-start | bytes 3932168 | tf_op jit(solution)/shard_map/ppermute | solution.py:466
  271.4 34.0 %collective-permute-start.14 = (f32[512,640]{1,0:T(8,128)S(1)}, f32[512,640]{1,0:T(8,128)}, u32[]{:S(2)}, u32[]{:S(2)}) collective-permute-start(f32[512,640]{1,0:T(8,128)S(1)} %collective-permute-done.6.refs_2_), channel_id=1, source_target_pairs={{0,96},{8,104},{16,112},{24,120},{32,0},{40,8},{48,16},{56,24},{64... | collective-permute-start | bytes 3932168 | tf_op jit(solution)/shard_map/ppermute | solution.py:466
  277.0 110.6 %collective-permute-start.16 = (f32[1024,640]{1,0:T(8,128)}, f32[1024,640]{1,0:T(8,128)S(1)}, u32[]{:S(2)}, u32[]{:S(2)}) collective-permute-start(f32[1024,640]{1,0:T(8,128)} %constant_dynamic-update-slice_fusion), channel_id=1, source_target_pairs={{0,8},{8,16},{16,24},{24,0},{32,40},{40,48},{48,56},{56,32},{64,72... | collective-permute-start | bytes 7864328 | tf_op jit(solution)/shard_map/ppermute | solution.py:466
  280.6 107.0 %collective-permute-start.17 = (f32[1024,640]{1,0:T(8,128)}, f32[1024,640]{1,0:T(8,128)S(1)}, u32[]{:S(2)}, u32[]{:S(2)}) collective-permute-start(f32[1024,640]{1,0:T(8,128)} %constant_dynamic-update-slice_fusion.2), channel_id=1, source_target_pairs={{0,32},{8,40},{16,48},{24,56},{32,64},{40,72},{48,80},{56,88},{64,... | collective-permute-start | bytes 7864328 | tf_op jit(solution)/shard_map/ppermute | solution.py:466
  299.3 88.3 %collective-permute-start.18 = (f32[1024,640]{1,0:T(8,128)}, f32[1024,640]{1,0:T(8,128)}, u32[]{:S(2)}, u32[]{:S(2)}) collective-permute-start(f32[1024,640]{1,0:T(8,128)} %constant_dynamic-update-slice_fusion), channel_id=1, source_target_pairs={{0,24},{8,0},{16,8},{24,16},{32,56},{40,32},{48,40},{56,48},{64,88... | collective-permute-start | bytes 7864328 | tf_op jit(solution)/shard_map/ppermute | solution.py:466
  303.8 80.8 %collective-permute-start.15 = (f32[512,640]{1,0:T(8,128)S(1)}, f32[512,640]{1,0:T(8,128)}, u32[]{:S(2)}, u32[]{:S(2)}) collective-permute-start(f32[512,640]{1,0:T(8,128)S(1)} %collective-permute-done.7.refs_3_), channel_id=1, source_target_pairs={{0,24},{8,0},{16,8},{24,16},{32,56},{40,32},{48,40},{56,48},{64,88... | collective-permute-start | bytes 3932168 | tf_op jit(solution)/shard_map/ppermute | solution.py:466
  305.4 85.4 %collective-permute-start.19 = (f32[1024,640]{1,0:T(8,128)}, f32[1024,640]{1,0:T(8,128)}, u32[]{:S(2)}, u32[]{:S(2)}) collective-permute-start(f32[1024,640]{1,0:T(8,128)} %constant_dynamic-update-slice_fusion.2), channel_id=1, source_target_pairs={{0,96},{8,104},{16,112},{24,120},{32,0},{40,8},{48,16},{56,24},{64... | collective-permute-start | bytes 7864328 | tf_op jit(solution)/shard_map/ppermute | solution.py:466
  384.6 32.2 %collective-permute-start.24 = (f32[512,640]{1,0:T(8,128)S(1)}, f32[512,640]{1,0:T(8,128)S(1)}, u32[]{:S(2)}, u32[]{:S(2)}) collective-permute-start(f32[512,640]{1,0:T(8,128)S(1)} %collective-permute-done.12.refs_0_), channel_id=1, source_target_pairs={{0,24},{8,0},{16,8},{24,16},{32,56},{40,32},{48,40},{56,48},{64,88... | collective-permute-start | bytes 3932168 | tf_op jit(solution)/shard_map/ppermute | solution.py:466
  387.6 85.1 %collective-permute-start.20 = (f32[1024,640]{1,0:T(8,128)S(1)}, f32[1024,640]{1,0:T(8,128)S(1)}, u32[]{:S(2)}, u32[]{:S(2)}) collective-permute-start(f32[1024,640]{1,0:T(8,128)S(1)} %get-tuple-element.113), channel_id=1, source_target_pairs={{0,8},{8,16},{16,24},{24,0},{32,40},{40,48},{48,56},{56,32},{64,72... | collective-permute-start | bytes 7864328 | tf_op jit(solution)/shard_map/ppermute | solution.py:466
  387.6 31.9 %collective-permute-start.25 = (f32[512,640]{1,0:T(8,128)}, f32[512,640]{1,0:T(8,128)S(1)}, u32[]{:S(2)}, u32[]{:S(2)}) collective-permute-start(f32[512,640]{1,0:T(8,128)} %collective-permute-done.13.refs_1_), channel_id=1, source_target_pairs={{0,96},{8,104},{16,112},{24,120},{32,0},{40,8},{48,16},{56,24},{64... | collective-permute-start | bytes 3932168 | tf_op jit(solution)/shard_map/ppermute | solution.py:466
  387.7 53.7 %collective-permute-start.26 = (f32[512,640]{1,0:T(8,128)}, f32[512,640]{1,0:T(8,128)S(1)}, u32[]{:S(2)}, u32[]{:S(2)}) collective-permute-start(f32[512,640]{1,0:T(8,128)} %collective-permute-done.14.refs_2_), channel_id=1, source_target_pairs={{0,24},{8,0},{16,8},{24,16},{32,56},{40,32},{48,40},{56,48},{64,88... | collective-permute-start | bytes 3932168 | tf_op jit(solution)/shard_map/ppermute | solution.py:466
  390.9 53.7 %collective-permute-start.27 = (f32[512,640]{1,0:T(8,128)}, f32[512,640]{1,0:T(8,128)S(1)}, u32[]{:S(2)}, u32[]{:S(2)}) collective-permute-start(f32[512,640]{1,0:T(8,128)} %collective-permute-done.15.refs_3_), channel_id=1, source_target_pairs={{0,96},{8,104},{16,112},{24,120},{32,0},{40,8},{48,16},{56,24},{64... | collective-permute-start | bytes 3932168 | tf_op jit(solution)/shard_map/ppermute | solution.py:466
  416.7 56.0 %collective-permute-start.30 = (f32[512,640]{1,0:T(8,128)S(1)}, f32[512,640]{1,0:T(8,128)S(1)}, u32[]{:S(2)}, u32[]{:S(2)}) collective-permute-start(f32[512,640]{1,0:T(8,128)S(1)} %collective-permute-done.12.refs_0_), channel_id=1, source_target_pairs={{0,8},{8,16},{16,24},{24,0},{32,40},{40,48},{48,56},{56,32},{64,72... | collective-permute-start | bytes 3932168 | tf_op jit(solution)/shard_map/ppermute | solution.py:466
  419.5 59.1 %collective-permute-start.21 = (f32[1024,640]{1,0:T(8,128)S(1)}, f32[1024,640]{1,0:T(8,128)S(1)}, u32[]{:S(2)}, u32[]{:S(2)}) collective-permute-start(f32[1024,640]{1,0:T(8,128)S(1)} %get-tuple-element.114), channel_id=1, source_target_pairs={{0,32},{8,40},{16,48},{24,56},{32,64},{40,72},{48,80},{56,88},{64,... | collective-permute-start | bytes 7864328 | tf_op jit(solution)/shard_map/ppermute | solution.py:466
  441.4 60.5 %collective-permute-start.22 = (f32[1024,640]{1,0:T(8,128)S(1)}, f32[1024,640]{1,0:T(8,128)S(1)}, u32[]{:S(2)}, u32[]{:S(2)}) collective-permute-start(f32[1024,640]{1,0:T(8,128)S(1)} %get-tuple-element.113), channel_id=1, source_target_pairs={{0,24},{8,0},{16,8},{24,16},{32,56},{40,32},{48,40},{56,48},{64,88... | collective-permute-start | bytes 7864328 | tf_op jit(solution)/shard_map/ppermute | solution.py:466
  445.7 56.2 %collective-permute-start.23 = (f32[1024,640]{1,0:T(8,128)S(1)}, f32[1024,640]{1,0:T(8,128)S(1)}, u32[]{:S(2)}, u32[]{:S(2)}) collective-permute-start(f32[1024,640]{1,0:T(8,128)S(1)} %get-tuple-element.114), channel_id=1, source_target_pairs={{0,96},{8,104},{16,112},{24,120},{32,0},{40,8},{48,16},{56,24},{64... | collective-permute-start | bytes 7864328 | tf_op jit(solution)/shard_map/ppermute | solution.py:466
  472.7 60.9 %collective-permute-start.28 = (f32[1024,640]{1,0:T(8,128)S(1)}, f32[1024,640]{1,0:T(8,128)S(1)}, u32[]{:S(2)}, u32[]{:S(2)}) collective-permute-start(f32[1024,640]{1,0:T(8,128)S(1)} %collective-permute-done.8.refs_0_), channel_id=1, source_target_pairs={{0,8},{8,16},{16,24},{24,0},{32,40},{40,48},{48,56},{56,32},{64,72... | collective-permute-start | bytes 7864328 | tf_op jit(solution)/shard_map/ppermute | solution.py:466
  473.8 60.9 %collective-permute-start.29 = (f32[1024,640]{1,0:T(8,128)S(1)}, f32[1024,640]{1,0:T(8,128)S(1)}, u32[]{:S(2)}, u32[]{:S(2)}) collective-permute-start(f32[1024,640]{1,0:T(8,128)S(1)} %collective-permute-done.9.refs_1_), channel_id=1, source_target_pairs={{0,32},{8,40},{16,48},{24,56},{32,64},{40,72},{48,80},{56,88},{64,... | collective-permute-start | bytes 7864328 | tf_op jit(solution)/shard_map/ppermute | solution.py:466
  478.6 131.7 %collective-permute-start.34 = (f32[1024,640]{1,0:T(8,128)}, f32[1024,640]{1,0:T(8,128)}, u32[]{:S(2)}, u32[]{:S(2)}) collective-permute-start(f32[1024,640]{1,0:T(8,128)} %collective-permute-done.18.refs_0_), channel_id=1, source_target_pairs={{0,24},{8,0},{16,8},{24,16},{32,56},{40,32},{48,40},{56,48},{64,88... | collective-permute-start | bytes 7864328 | tf_op jit(solution)/shard_map/ppermute | solution.py:466
  501.8 62.7 %collective-permute-start.31 = (f32[512,640]{1,0:T(8,128)}, f32[512,640]{1,0:T(8,128)}, u32[]{:S(2)}, u32[]{:S(2)}) collective-permute-start(f32[512,640]{1,0:T(8,128)} %collective-permute-done.13.refs_1_), channel_id=1, source_target_pairs={{0,32},{8,40},{16,48},{24,56},{32,64},{40,72},{48,80},{56,88},{64,... | collective-permute-start | bytes 3932168 | tf_op jit(solution)/shard_map/ppermute | solution.py:466
  501.9 64.1 %collective-permute-start.32 = (f32[512,640]{1,0:T(8,128)}, f32[512,640]{1,0:T(8,128)}, u32[]{:S(2)}, u32[]{:S(2)}) collective-permute-start(f32[512,640]{1,0:T(8,128)} %collective-permute-done.14.refs_2_), channel_id=1, source_target_pairs={{0,8},{8,16},{16,24},{24,0},{32,40},{40,48},{48,56},{56,32},{64,72... | collective-permute-start | bytes 3932168 | tf_op jit(solution)/shard_map/ppermute | solution.py:466
  533.6 53.4 %collective-permute-start.33 = (f32[512,640]{1,0:T(8,128)}, f32[512,640]{1,0:T(8,128)}, u32[]{:S(2)}, u32[]{:S(2)}) collective-permute-start(f32[512,640]{1,0:T(8,128)} %collective-permute-done.15.refs_3_), channel_id=1, source_target_pairs={{0,32},{8,40},{16,48},{24,56},{32,64},{40,72},{48,80},{56,88},{64,... | collective-permute-start | bytes 3932168 | tf_op jit(solution)/shard_map/ppermute | solution.py:466
  534.8 79.6 %collective-permute-start.35 = (f32[1024,640]{1,0:T(8,128)}, f32[1024,640]{1,0:T(8,128)}, u32[]{:S(2)}, u32[]{:S(2)}) collective-permute-start(f32[1024,640]{1,0:T(8,128)} %collective-permute-done.19.refs_1_), channel_id=1, source_target_pairs={{0,96},{8,104},{16,112},{24,120},{32,0},{40,8},{48,16},{56,24},{64... | collective-permute-start | bytes 7864328 | tf_op jit(solution)/shard_map/ppermute | solution.py:466
  564.6 25.0 %collective-permute-start.40 = (f32[384,640]{1,0:T(8,128)S(1)}, f32[384,640]{1,0:T(8,128)S(1)}, u32[]{:S(2)}, u32[]{:S(2)}) collective-permute-start(f32[384,640]{1,0:T(8,128)S(1)} %slice.72), channel_id=1, source_target_pairs={{0,8},{8,16},{16,24},{24,0},{32,40},{40,48},{48,56},{56,32},{64,72... | collective-permute-start | bytes 2949128 | tf_op jit(solution)/shard_map/ppermute | solution.py:466
  566.0 41.3 %collective-permute-start.41 = (f32[384,640]{1,0:T(8,128)S(1)}, f32[384,640]{1,0:T(8,128)S(1)}, u32[]{:S(2)}, u32[]{:S(2)}) collective-permute-start(f32[384,640]{1,0:T(8,128)S(1)} %slice.73), channel_id=1, source_target_pairs={{0,32},{8,40},{16,48},{24,56},{32,64},{40,72},{48,80},{56,88},{64,... | collective-permute-start | bytes 2949128 | tf_op jit(solution)/shard_map/ppermute | solution.py:466
  587.0 20.3 %collective-permute-start.42 = (f32[384,640]{1,0:T(8,128)S(1)}, f32[384,640]{1,0:T(8,128)S(1)}, u32[]{:S(2)}, u32[]{:S(2)}) collective-permute-start(f32[384,640]{1,0:T(8,128)S(1)} %slice.74), channel_id=1, source_target_pairs={{0,24},{8,0},{16,8},{24,16},{32,56},{40,32},{48,40},{56,48},{64,88... | collective-permute-start | bytes 2949128 | tf_op jit(solution)/shard_map/ppermute | solution.py:466
  589.6 28.9 %collective-permute-start.36 = (f32[512,640]{1,0:T(8,128)S(1)}, f32[512,640]{1,0:T(8,128)S(1)}, u32[]{:S(2)}, u32[]{:S(2)}) collective-permute-start(f32[512,640]{1,0:T(8,128)S(1)} %slice.68), channel_id=1, source_target_pairs={{0,8},{8,16},{16,24},{24,0},{32,40},{40,48},{48,56},{56,32},{64,72... | collective-permute-start | bytes 3932168 | tf_op jit(solution)/shard_map/ppermute | solution.py:466
  607.3 22.0 %collective-permute-start.37 = (f32[512,640]{1,0:T(8,128)S(1)}, f32[512,640]{1,0:T(8,128)S(1)}, u32[]{:S(2)}, u32[]{:S(2)}) collective-permute-start(f32[512,640]{1,0:T(8,128)S(1)} %slice.69), channel_id=1, source_target_pairs={{0,32},{8,40},{16,48},{24,56},{32,64},{40,72},{48,80},{56,88},{64,... | collective-permute-start | bytes 3932168 | tf_op jit(solution)/shard_map/ppermute | solution.py:466
  607.3 23.1 %collective-permute-start.38 = (f32[512,640]{1,0:T(8,128)S(1)}, f32[512,640]{1,0:T(8,128)S(1)}, u32[]{:S(2)}, u32[]{:S(2)}) collective-permute-start(f32[512,640]{1,0:T(8,128)S(1)} %slice.70), channel_id=1, source_target_pairs={{0,24},{8,0},{16,8},{24,16},{32,56},{40,32},{48,40},{56,48},{64,88... | collective-permute-start | bytes 3932168 | tf_op jit(solution)/shard_map/ppermute | solution.py:466
  610.3 24.5 %collective-permute-start.39 = (f32[512,640]{1,0:T(8,128)S(1)}, f32[512,640]{1,0:T(8,128)S(1)}, u32[]{:S(2)}, u32[]{:S(2)}) collective-permute-start(f32[512,640]{1,0:T(8,128)S(1)} %slice.71), channel_id=1, source_target_pairs={{0,96},{8,104},{16,112},{24,120},{32,0},{40,8},{48,16},{56,24},{64... | collective-permute-start | bytes 3932168 | tf_op jit(solution)/shard_map/ppermute | solution.py:466
  614.4 43.3 %collective-permute-start.43 = (f32[384,640]{1,0:T(8,128)}, f32[384,640]{1,0:T(8,128)}, u32[]{:S(2)}, u32[]{:S(2)}) collective-permute-start(f32[384,640]{1,0:T(8,128)} %slice.75), channel_id=1, source_target_pairs={{0,96},{8,104},{16,112},{24,120},{32,0},{40,8},{48,16},{56,24},{64... | collective-permute-start | bytes 2949128 | tf_op jit(solution)/shard_map/ppermute | solution.py:466
  618.5 43.1 %collective-permute-start.44 = (f32[128,640]{1,0:T(8,128)}, f32[128,640]{1,0:T(8,128)}, u32[]{:S(2)}, u32[]{:S(2)}) collective-permute-start(f32[128,640]{1,0:T(8,128)} %slice.76), channel_id=1, source_target_pairs={{0,8},{8,16},{16,24},{24,0},{32,40},{40,48},{48,56},{56,32},{64,72... | collective-permute-start | bytes 983048 | tf_op jit(solution)/shard_map/ppermute | solution.py:466
  630.4 31.1 %collective-permute-start.45 = (f32[128,640]{1,0:T(8,128)}, f32[128,640]{1,0:T(8,128)}, u32[]{:S(2)}, u32[]{:S(2)}) collective-permute-start(f32[128,640]{1,0:T(8,128)} %slice.77), channel_id=1, source_target_pairs={{0,32},{8,40},{16,48},{24,56},{32,64},{40,72},{48,80},{56,88},{64,... | collective-permute-start | bytes 983048 | tf_op jit(solution)/shard_map/ppermute | solution.py:466
  631.6 30.0 %collective-permute-start.46 = (f32[128,640]{1,0:T(8,128)}, f32[128,640]{1,0:T(8,128)}, u32[]{:S(2)}, u32[]{:S(2)}) collective-permute-start(f32[128,640]{1,0:T(8,128)} %slice.78), channel_id=1, source_target_pairs={{0,24},{8,0},{16,8},{24,16},{32,56},{40,32},{48,40},{56,48},{64,88... | collective-permute-start | bytes 983048 | tf_op jit(solution)/shard_map/ppermute | solution.py:466
  635.8 25.7 %collective-permute-start.47 = (f32[128,640]{1,0:T(8,128)}, f32[128,640]{1,0:T(8,128)}, u32[]{:S(2)}, u32[]{:S(2)}) collective-permute-start(f32[128,640]{1,0:T(8,128)} %slice.79), channel_id=1, source_target_pairs={{0,96},{8,104},{16,112},{24,120},{32,0},{40,8},{48,16},{56,24},{64... | collective-permute-start | bytes 983048 | tf_op jit(solution)/shard_map/ppermute | solution.py:466
  (22 other events, 206.4 us)

commit v3 on v2

--- a/solution.py
+++ b/solution.py
@@ -232,6 +232,20 @@
             return 0
 
         lax.fori_loop(0, tokens // pack, keep, 0)
+
+        twin = col + 1 - 2 * lax.rem(col, 2)
+        arrive((*pay_came, *mask_came))
+        x_got[col] = pay_got[...]
+
+        def across(j, origin):
+            return remote(pay_got, x_got.at[origin], tp_sem.at[1, 0, mates[j]], tp_sem.at[1, 1, origin], me, mates[j])
+
+        def to_twin(j, origin):
+            return remote(x_got.at[origin], x_got.at[origin], tp_sem.at[1, 0, mates[j + 1]], tp_sem.at[1, 1, origin], me, twin)
+
+        evens = range(0, N_TP, 2)
+        xt_sends = [across(j, col) for j in evens[1:]]
+        start(xt_sends)
 
         def fold(v):
             total = v[:, :LANES]
@@ -273,14 +287,13 @@
         all_ref[me] = line
         dp_sends, dp_came = to_dp(own_row, all_ref, 2)
         start(dp_sends)
+        arrive([across(j, mates[j]) for j in evens[1:]])
+        twin_sends = [to_twin(j, mates[j]) for j in evens]
+        start(twin_sends)
         came(0)
         onward(1, True, None)
         onward(1, False, 0)
 
-        arrive((*pay_came, *mask_came))
-        x_got[col] = pay_got[...]
-        xt_sends, xt_came = to_tp(lambda c: pay_got, x_got, 1)
-        start(xt_sends)
         count = jnp.sum(added(mask_got, slice(1)), axis=1, keepdims=True)
         inv_s, inv_t, weight = 1.0 / total[:, 0:1], 1.0 / total[:, 1:2], mask_col / count
         dx[...] = jnp.zeros((tokens, dim), F32)
@@ -330,7 +343,7 @@
         onward(DOWN, True, 0)
         onward(2, True, 1)
         onward(1, False, 1)
-        arrive(xt_came)
+        arrive([to_twin(j, mates[j + 1]) for j in evens])
 
         def widen(d, _):
             rows = jnp.concatenate([x_got[j, d] for j in range(N_TP)], axis=0)
@@ -373,7 +386,7 @@
         for j, level, w in COPIES:
             if level:
                 hop(j, level, w).wait_send()
-        for cp in (*pay_sends, *mask_sends, *tp_sends, *dp_sends, *xt_sends, *rs_sends, *ag_sends, *gn_sends):
+        for cp in (*pay_sends, *mask_sends, *tp_sends, *dp_sends, *xt_sends, *twin_sends, *rs_sends, *ag_sends, *gn_sends):
             cp.wait_send()
 
     dma = pltpu.SemaphoreType.DMA
@@ -423,7 +436,7 @@
     dim = arrays[0].shape[1]
     rows = vocab // N_DP
     quarter = rows // SIDE
-    cut = 128
+    cut = 256
     chunks = [(i, r) for i in range(n) for r in range(0, arrays[i].shape[0], cut)]
 
     def kern(*refs):
@@ -431,8 +444,8 @@
         at = peers()[1]
         reads, writes = [], []
         for k, (i, r) in enumerate(chunks):
-            _, dz, dy, kind, half, start = pieces[i]
-            first = (2 * (half + r // quarter) + kind) * quarter + start + r % quarter
+            _, dz, dy, kind, half = pieces[i]
+            first = (2 * (half + r // quarter) + kind) * quarter + r % quarter
             there = aligned(at[dz, dy] * rows + first, cut, cut)
             reads.append(pltpu.make_async_copy(refs[i].at[pl.ds(r, cut)], buf.at[k], sem.at[0, k]))
             writes.append(pltpu.make_async_copy(buf.at[k], dst.at[there], sem.at[1, k]))
@@ -455,8 +468,6 @@
 def gather(first, rest, vocab):
     quarter = first[0].shape[0]
     sets, ways = range(2), (UP, DOWN)
-    most = quarter - LANES
-    cuts = slice(0, most), slice(most, quarter)
     table, event = None, 0
 
     def send(pair, axis, step):
@@ -466,8 +477,8 @@
             out.append(lax.ppermute(pair[k], 'dp', [(d, shift(d, dz, dy)) for d in range(N_DP)]))
         return out
 
-    def put(pair, a, b, c=0, start=0):
-        return [(pair[k], *((b, a) if k else (a, b)), k, c, start) for k in sets]
+    def put(pair, a, b, c=0):
+        return [(pair[k], *((b, a) if k else (a, b)), k, c) for k in sets]
 
     def settle(*pieces):
         nonlocal table
@@ -524,12 +535,12 @@
     settle(put(high_side[DOWN], UP, UP))
 
     far_side[0, DOWN], far_side[1, DOWN], side_far = wait(far_side[0, DOWN], far_side[1, DOWN], side_far)
-    last_down = [send([x[cut] for x in far_side[1, DOWN]], 1, DOWN) for cut in cuts]
+    last_down = send(far_side[1, DOWN], 1, DOWN)
     settle(put(far_side[0, DOWN], AWAY, UP, 0), put(far_side[1, DOWN], AWAY, UP, 1))
     settle(put(side_far, 0, AWAY))
 
     far_side[0, UP], = wait(far_side[0, UP])
-    last_up = [send([x[cut] for x in far_side[0, UP]], 1, UP) for cut in cuts]
+    last_up = send(far_side[0, UP], 1, UP)
     settle(put(far_side[0, UP], AWAY, DOWN, 0))
 
     far_side[1, UP], low_far = wait(far_side[1, UP], low_far)
@@ -538,9 +549,8 @@
 
     high_far = wait(*high_far)
     settle(put(high_far[0], UP, AWAY, 0), put(high_far[1], UP, AWAY, 1))
-    for up, down, cut in zip(last_up, last_down, cuts):
-        up, down = wait(up, down)
-        settle(put(up, AWAY, AWAY, 0, cut.start), put(down, AWAY, AWAY, 1, cut.start))
+    last_up, last_down = wait(last_up, last_down)
+    settle(put(last_up, AWAY, AWAY, 0), put(last_down, AWAY, AWAY, 1))
     return table
 
 

time: 672 us -> 650 us (0.967)
  the two profiles are of different devices: /device:TPU:6 before, /device:TPU:30 now
where the time goes in v3:
time: 650 us
  waiting for transfers between devices  381 us (59%)
  Pallas kernels  195 us (30%)
  starting transfers between devices  55.7 us (9%)
  local copies, waits for them, and re-layouts  10.5 us (2%)
    ppermute x44, waiting for transfers between devices, send(): lax.ppermute(pair[k], 'dp', [(d, shift(d, dz, dy)) for d in range(N_DP)])  381 us
    pallas_call x1, Pallas kernels, front(): pl.pallas_call(kern, out_shape=tuple((jax.ShapeDtypeStruct(shape, kind) f...  118 us
    pallas_call x17, Pallas kernels, place(): pl.pallas_call(kern, out_shape=jax.ShapeDtypeStruct((vocab, dim), F32), i...  69.6 us
    ppermute x44, starting transfers between devices, send(): lax.ppermute(pair[k], 'dp', [(d, shift(d, dz, dy)) for d in range(N_DP)])  55.7 us
  transfers between devices with their start and end apart: 44, of which 13 were waited for; matrix products, arithmetic and copies ran while one was open for 2% of the time, Pallas kernels for 11%

profile of v3, /device:TPU:30, one launch (start us, length us, event | category | flops | bytes accessed | tf_op | source)
XLA Modules:
  0.0 649.6 jit_solution(5304646908337034598)
XLA Ops:
  0.6 118.0 %front.1 = (f32[16,64,1024]{2,1,0:T(8,128)S(1)}, f32[2,512,640]{2,1,0:T(8,128)S(1)}, bf16[1024,640]{1,0:T(8,128)(2,1)S(1)}, bf16[2048,640]{1,0:T(8,128)(2,1)S(1)...) custom-call(bf16[64,640]{1,0:T(8,128)(2,1)} %hid_hbm.1, ...), custom_call_target="tpu_custom_call" | custom-call | flops 3000000000 | bytes 104857600 | tf_op jit(solution)/shard_map/front/pallas_call | solution.py:394
  120.0 2.2 collective-permute-start.2
  122.2 1.6 collective-permute-start.1
  124.2 7.2 %finish.1 = f32[2,512,640]{2,1,0:T(8,128)S(1)} custom-call(f32[16,64,1024]{2,1,0:T(8,128)S(1)} %get-tuple-element.79.tea_ref, bf16[1024,640]{1,0:T(8,128)(2,1)S(1)} %get-tuple-element.80.x_ref, bf16[2048,640]{1,0:T(8,128)(2,1)S(1)} %get-tuple-element.81.tab_ref, f32[128,128]{1,0:T(8,128)S(1)} %get-tuple-element.82.coef_ref), custom_call_target="tpu_custom_call" | custom-call | flops 1000000000 | bytes 8388608 | tf_op jit(solution)/shard_map/finish/pallas_call | solution.py:427
  131.8 19.9 %collective-permute-done.refs_0_ = f32[512,640]{1,0:T(8,128)S(1)} collective-permute-done((f32[512,640]{1,0:T(8,128)S(1)}, f32[512,640]{1,0:T(8,128)S(1)}, u32[]{:S(2)}, u32[]{:S(2)}) %collective-permute-start) | collective-permute-done | bytes 1310752 | tf_op jit(solution)/shard_map/ppermute | solution.py:477
  153.5 1.6 collective-permute-start.8
  155.1 3.2 collective-permute-start.6
  158.4 21.5 %collective-permute-done.4.refs_0_ = f32[512,640]{1,0:T(8,128)S(1)} collective-permute-done((f32[512,640]{1,0:T(8,128)S(1)}, f32[512,640]{1,0:T(8,128)S(1)}, u32[]{:S(2)}, u32[]{:S(2)}) %collective-permute-start.4) | collective-permute-done | bytes 1310752 | tf_op jit(solution)/shard_map/ppermute | solution.py:477
  180.6 2.8 collective-permute-done.5.refs_1_
  184.7 3.7 collective-permute-start.11
  188.4 4.1 place.17.refs_4_
  192.5 4.2 place.18.refs_4_
  196.6 69.6 %collective-permute-done.7.refs_3_ = f32[512,640]{1,0:T(8,128)S(1)} collective-permute-done((f32[512,640]{1,0:T(8,128)S(1)}, f32[512,640]{1,0:T(8,128)S(1)}, u32[]{:S(2)}, u32[]{:S(2)}) %collective-permute-start.7) | collective-permute-done | bytes 1310752 | tf_op jit(solution)/shard_map/ppermute | solution.py:477
  267.8 3.2 collective-permute-start.14
  275.2 23.9 %collective-permute-done.12.refs_0_ = f32[512,640]{1,0:T(8,128)S(1)} collective-permute-done((f32[512,640]{1,0:T(8,128)S(1)}, f32[512,640]{1,0:T(8,128)S(1)}, u32[]{:S(2)}, u32[]{:S(2)}) %collective-permute-start.12) | collective-permute-done | bytes 1310752 | tf_op jit(solution)/shard_map/ppermute | solution.py:477
  299.5 2.9 collective-permute-start.19
  302.4 4.1 place.19.refs_2_
  306.5 1.8 pad_maximum_fusion.2
  308.3 4.1 place.20.refs_2_
  312.4 4.1 place.21.refs_4_
  316.6 67.9 %collective-permute-done.15.refs_3_ = f32[512,640]{1,0:T(8,128)S(1)} collective-permute-done((f32[512,640]{1,0:T(8,128)S(1)}, f32[512,640]{1,0:T(8,128)S(1)}, u32[]{:S(2)}, u32[]{:S(2)}) %collective-permute-start.15) | collective-permute-done | bytes 1310752 | tf_op jit(solution)/shard_map/ppermute | solution.py:477
  385.1 2.9 collective-permute-start.30
  388.0 29.3 %collective-permute-done.24.refs_0_ = f32[512,640]{1,0:T(8,128)S(1)} collective-permute-done((f32[512,640]{1,0:T(8,128)S(1)}, f32[512,640]{1,0:T(8,128)S(1)}, u32[]{:S(2)}, u32[]{:S(2)}) %collective-permute-start.24) | collective-permute-done | bytes 1310752 | tf_op jit(solution)/shard_map/ppermute | solution.py:477
  417.3 2.0 collective-permute-start.20
  419.3 22.1 %collective-permute-done.26.refs_2_ = f32[512,640]{1,0:T(8,128)} collective-permute-done((f32[512,640]{1,0:T(8,128)S(1)}, f32[512,640]{1,0:T(8,128)}, u32[]{:S(2)}, u32[]{:S(2)}) %collective-permute-start.26) | collective-permute-done | bytes 1310752 | tf_op jit(solution)/shard_map/ppermute | solution.py:477
  441.5 3.3 collective-permute-start.23
  444.8 3.2 collective-permute-start.32
  448.0 52.8 %collective-permute-done.32.refs_0_ = f32[512,640]{1,0:T(8,128)S(1)} collective-permute-done((f32[512,640]{1,0:T(8,128)S(1)}, f32[512,640]{1,0:T(8,128)S(1)}, u32[]{:S(2)}, u32[]{:S(2)}) %collective-permute-start.32) | collective-permute-done | bytes 1310752 | tf_op jit(solution)/shard_map/ppermute | solution.py:477
  500.8 3.7 collective-permute-start.28
  504.5 4.1 place.22.refs_2_
  508.7 3.3 collective-permute-start.35
  512.0 4.1 place.23.refs_2_
  516.1 4.6 place.24.refs_2_
  523.1 66.2 %collective-permute-done.33.refs_1_ = f32[512,640]{1,0:T(8,128)S(1)} collective-permute-done((f32[512,640]{1,0:T(8,128)S(1)}, f32[512,640]{1,0:T(8,128)S(1)}, u32[]{:S(2)}, u32[]{:S(2)}) %collective-permute-start.33) | collective-permute-done | bytes 1310752 | tf_op jit(solution)/shard_map/ppermute | solution.py:477
  590.7 1.8 collective-permute-start.38
  593.8 4.1 place.25.refs_2_
  597.9 4.1 place.26.refs_4_
  602.0 4.7 place.27.refs_2_
  606.7 3.3 collective-permute-start.39
  610.0 4.1 place.28.refs_2_
  615.1 3.7 collective-permute-start.40
  618.8 3.6 collective-permute-done.37.refs_1_
  622.4 3.2 collective-permute-start.43
  628.8 2.8 place.29.refs_2_
  632.1 2.4 place.30.refs_2_
  634.5 4.6 place.31.refs_4_
  639.2 4.6 place.32.refs_4_
  643.9 4.6 place.33
  (85 shorter events, 21.0 us)
Async XLA Ops:
  118.9 32.9 %collective-permute-start = (f32[512,640]{1,0:T(8,128)S(1)}, f32[512,640]{1,0:T(8,128)S(1)}, u32[]{:S(2)}, u32[]{:S(2)}) collective-permute-start(f32[512,640]{1,0:T(8,128)S(1)} %get-tuple-element.77.refs_0_), channel_id=1, source_target_pairs={{0,32},{8,40},{16,48},{24,56},{32,64},{40,72},{48,80},{56,88},{64,... | collective-permute-start | bytes 3932168 | tf_op jit(solution)/shard_map/ppermute | solution.py:477
  120.0 35.2 %collective-permute-start.2 = (f32[512,640]{1,0:T(8,128)S(1)}, f32[512,640]{1,0:T(8,128)S(1)}, u32[]{:S(2)}, u32[]{:S(2)}) collective-permute-start(f32[512,640]{1,0:T(8,128)S(1)} %get-tuple-element.77.refs_0_), channel_id=1, source_target_pairs={{0,96},{8,104},{16,112},{24,120},{32,0},{40,8},{48,16},{56,24},{64... | collective-permute-start | bytes 3932168 | tf_op jit(solution)/shard_map/ppermute | solution.py:477
  122.2 31.4 %collective-permute-start.1 = (f32[512,640]{1,0:T(8,128)S(1)}, f32[512,640]{1,0:T(8,128)S(1)}, u32[]{:S(2)}, u32[]{:S(2)}) collective-permute-start(f32[512,640]{1,0:T(8,128)S(1)} %get-tuple-element.78.refs_1_), channel_id=1, source_target_pairs={{0,8},{8,16},{16,24},{24,0},{32,40},{40,48},{48,56},{56,32},{64,72... | collective-permute-start | bytes 3932168 | tf_op jit(solution)/shard_map/ppermute | solution.py:477
  123.7 31.4 %collective-permute-start.3 = (f32[512,640]{1,0:T(8,128)S(1)}, f32[512,640]{1,0:T(8,128)S(1)}, u32[]{:S(2)}, u32[]{:S(2)}) collective-permute-start(f32[512,640]{1,0:T(8,128)S(1)} %get-tuple-element.78.refs_1_), channel_id=1, source_target_pairs={{0,24},{8,0},{16,8},{24,16},{32,56},{40,32},{48,40},{56,48},{64,88... | collective-permute-start | bytes 3932168 | tf_op jit(solution)/shard_map/ppermute | solution.py:477
  131.6 48.3 %collective-permute-start.4 = (f32[512,640]{1,0:T(8,128)S(1)}, f32[512,640]{1,0:T(8,128)S(1)}, u32[]{:S(2)}, u32[]{:S(2)}) collective-permute-start(f32[512,640]{1,0:T(8,128)S(1)} %get-tuple-element.143.refs_2_), channel_id=1, source_target_pairs={{0,32},{8,40},{16,48},{24,56},{32,64},{40,72},{48,80},{56,88},{64,... | collective-permute-start | bytes 3932168 | tf_op jit(solution)/shard_map/ppermute | solution.py:477
  151.8 31.6 %collective-permute-start.5 = (f32[512,640]{1,0:T(8,128)S(1)}, f32[512,640]{1,0:T(8,128)S(1)}, u32[]{:S(2)}, u32[]{:S(2)}) collective-permute-start(f32[512,640]{1,0:T(8,128)S(1)} %get-tuple-element.142.refs_3_), channel_id=1, source_target_pairs={{0,8},{8,16},{16,24},{24,0},{32,40},{40,48},{48,56},{56,32},{64,72... | collective-permute-start | bytes 3932168 | tf_op jit(solution)/shard_map/ppermute | solution.py:477
  153.5 113.9 %collective-permute-start.8 = (f32[1024,640]{1,0:T(8,128)S(1)}, f32[1024,640]{1,0:T(8,128)S(1)}, u32[]{:S(2)}, u32[]{:S(2)}) collective-permute-start(f32[1024,640]{1,0:T(8,128)S(1)} %pad_maximum_fusion), channel_id=1, source_target_pairs={{0,8},{8,16},{16,24},{24,0},{32,40},{40,48},{48,56},{56,32},{64,72... | collective-permute-start | bytes 7864328 | tf_op jit(solution)/shard_map/ppermute | solution.py:477
  155.1 112.7 %collective-permute-start.9 = (f32[1024,640]{1,0:T(8,128)S(1)}, f32[1024,640]{1,0:T(8,128)S(1)}, u32[]{:S(2)}, u32[]{:S(2)}) collective-permute-start(f32[1024,640]{1,0:T(8,128)S(1)} %pad_maximum_fusion.1), channel_id=1, source_target_pairs={{0,32},{8,40},{16,48},{24,56},{32,64},{40,72},{48,80},{56,88},{64,... | collective-permute-start | bytes 7864328 | tf_op jit(solution)/shard_map/ppermute | solution.py:477
  155.1 29.5 %collective-permute-start.6 = (f32[512,640]{1,0:T(8,128)S(1)}, f32[512,640]{1,0:T(8,128)S(1)}, u32[]{:S(2)}, u32[]{:S(2)}) collective-permute-start(f32[512,640]{1,0:T(8,128)S(1)} %get-tuple-element.143.refs_2_), channel_id=1, source_target_pairs={{0,96},{8,104},{16,112},{24,120},{32,0},{40,8},{48,16},{56,24},{64... | collective-permute-start | bytes 3932168 | tf_op jit(solution)/shard_map/ppermute | solution.py:477
  179.9 92.4 %collective-permute-start.10 = (f32[1024,640]{1,0:T(8,128)S(1)}, f32[1024,640]{1,0:T(8,128)S(1)}, u32[]{:S(2)}, u32[]{:S(2)}) collective-permute-start(f32[1024,640]{1,0:T(8,128)S(1)} %pad_maximum_fusion), channel_id=1, source_target_pairs={{0,24},{8,0},{16,8},{24,16},{32,56},{40,32},{48,40},{56,48},{64,88... | collective-permute-start | bytes 7864328 | tf_op jit(solution)/shard_map/ppermute | solution.py:477
  183.4 82.8 %collective-permute-start.7 = (f32[512,640]{1,0:T(8,128)S(1)}, f32[512,640]{1,0:T(8,128)S(1)}, u32[]{:S(2)}, u32[]{:S(2)}) collective-permute-start(f32[512,640]{1,0:T(8,128)S(1)} %get-tuple-element.142.refs_3_), channel_id=1, source_target_pairs={{0,24},{8,0},{16,8},{24,16},{32,56},{40,32},{48,40},{56,48},{64,88... | collective-permute-start | bytes 3932168 | tf_op jit(solution)/shard_map/ppermute | solution.py:477
  184.7 90.6 %collective-permute-start.11 = (f32[1024,640]{1,0:T(8,128)S(1)}, f32[1024,640]{1,0:T(8,128)S(1)}, u32[]{:S(2)}, u32[]{:S(2)}) collective-permute-start(f32[1024,640]{1,0:T(8,128)S(1)} %pad_maximum_fusion.1), channel_id=1, source_target_pairs={{0,96},{8,104},{16,112},{24,120},{32,0},{40,8},{48,16},{56,24},{64... | collective-permute-start | bytes 7864328 | tf_op jit(solution)/shard_map/ppermute | solution.py:477
  266.3 32.9 %collective-permute-start.12 = (f32[512,640]{1,0:T(8,128)S(1)}, f32[512,640]{1,0:T(8,128)S(1)}, u32[]{:S(2)}, u32[]{:S(2)}) collective-permute-start(f32[512,640]{1,0:T(8,128)S(1)} %collective-permute-done.refs_0_), channel_id=1, source_target_pairs={{0,32},{8,40},{16,48},{24,56},{32,64},{40,72},{48,80},{56,88},{64,... | collective-permute-start | bytes 3932168 | tf_op jit(solution)/shard_map/ppermute | solution.py:477
  267.5 31.7 %collective-permute-start.13 = (f32[512,640]{1,0:T(8,128)S(1)}, f32[512,640]{1,0:T(8,128)S(1)}, u32[]{:S(2)}, u32[]{:S(2)}) collective-permute-start(f32[512,640]{1,0:T(8,128)S(1)} %collective-permute-done.1.refs_1_), channel_id=1, source_target_pairs={{0,8},{8,16},{16,24},{24,0},{32,40},{40,48},{48,56},{56,32},{64,72... | collective-permute-start | bytes 3932168 | tf_op jit(solution)/shard_map/ppermute | solution.py:477
  267.8 31.7 %collective-permute-start.14 = (f32[512,640]{1,0:T(8,128)S(1)}, f32[512,640]{1,0:T(8,128)S(1)}, u32[]{:S(2)}, u32[]{:S(2)}) collective-permute-start(f32[512,640]{1,0:T(8,128)S(1)} %collective-permute-done.6.refs_2_), channel_id=1, source_target_pairs={{0,96},{8,104},{16,112},{24,120},{32,0},{40,8},{48,16},{56,24},{64... | collective-permute-start | bytes 3932168 | tf_op jit(solution)/shard_map/ppermute | solution.py:477
  272.2 112.2 %collective-permute-start.16 = (f32[1024,640]{1,0:T(8,128)}, f32[1024,640]{1,0:T(8,128)S(1)}, u32[]{:S(2)}, u32[]{:S(2)}) collective-permute-start(f32[1024,640]{1,0:T(8,128)} %constant_dynamic-update-slice_fusion), channel_id=1, source_target_pairs={{0,8},{8,16},{16,24},{24,0},{32,40},{40,48},{48,56},{56,32},{64,72... | collective-permute-start | bytes 7864328 | tf_op jit(solution)/shard_map/ppermute | solution.py:477
  275.2 109.2 %collective-permute-start.17 = (f32[1024,640]{1,0:T(8,128)}, f32[1024,640]{1,0:T(8,128)S(1)}, u32[]{:S(2)}, u32[]{:S(2)}) collective-permute-start(f32[1024,640]{1,0:T(8,128)} %constant_dynamic-update-slice_fusion.2), channel_id=1, source_target_pairs={{0,32},{8,40},{16,48},{24,56},{32,64},{40,72},{48,80},{56,88},{64,... | collective-permute-start | bytes 7864328 | tf_op jit(solution)/shard_map/ppermute | solution.py:477
  299.1 85.9 %collective-permute-start.18 = (f32[1024,640]{1,0:T(8,128)}, f32[1024,640]{1,0:T(8,128)}, u32[]{:S(2)}, u32[]{:S(2)}) collective-permute-start(f32[1024,640]{1,0:T(8,128)} %constant_dynamic-update-slice_fusion), channel_id=1, source_target_pairs={{0,24},{8,0},{16,8},{24,16},{32,56},{40,32},{48,40},{56,48},{64,88... | collective-permute-start | bytes 7864328 | tf_op jit(solution)/shard_map/ppermute | solution.py:477
  299.1 85.3 %collective-permute-start.15 = (f32[512,640]{1,0:T(8,128)S(1)}, f32[512,640]{1,0:T(8,128)S(1)}, u32[]{:S(2)}, u32[]{:S(2)}) collective-permute-start(f32[512,640]{1,0:T(8,128)S(1)} %collective-permute-done.7.refs_3_), channel_id=1, source_target_pairs={{0,24},{8,0},{16,8},{24,16},{32,56},{40,32},{48,40},{56,48},{64,88... | collective-permute-start | bytes 3932168 | tf_op jit(solution)/shard_map/ppermute | solution.py:477
  299.5 85.6 %collective-permute-start.19 = (f32[1024,640]{1,0:T(8,128)}, f32[1024,640]{1,0:T(8,128)}, u32[]{:S(2)}, u32[]{:S(2)}) collective-permute-start(f32[1024,640]{1,0:T(8,128)} %constant_dynamic-update-slice_fusion.2), channel_id=1, source_target_pairs={{0,96},{8,104},{16,112},{24,120},{32,0},{40,8},{48,16},{56,24},{64... | collective-permute-start | bytes 7864328 | tf_op jit(solution)/shard_map/ppermute | solution.py:477
  312.4 104.9 %copy-start.4 = (f32[1024,640]{1,0:T(8,128)S(1)}, f32[1024,640]{1,0:T(8,128)}, u32[]{:S(2)}) copy-start(f32[1024,640]{1,0:T(8,128)} %get-tuple-element.108) | copy-start | bytes 7864324
  384.5 32.9 %collective-permute-start.24 = (f32[512,640]{1,0:T(8,128)S(1)}, f32[512,640]{1,0:T(8,128)S(1)}, u32[]{:S(2)}, u32[]{:S(2)}) collective-permute-start(f32[512,640]{1,0:T(8,128)S(1)} %collective-permute-done.12.refs_0_), channel_id=1, source_target_pairs={{0,24},{8,0},{16,8},{24,16},{32,56},{40,32},{48,40},{56,48},{64,88... | collective-permute-start | bytes 3932168 | tf_op jit(solution)/shard_map/ppermute | solution.py:477
  384.5 32.9 %collective-permute-start.25 = (f32[512,640]{1,0:T(8,128)S(1)}, f32[512,640]{1,0:T(8,128)S(1)}, u32[]{:S(2)}, u32[]{:S(2)}) collective-permute-start(f32[512,640]{1,0:T(8,128)S(1)} %collective-permute-done.13.refs_1_), channel_id=1, source_target_pairs={{0,96},{8,104},{16,112},{24,120},{32,0},{40,8},{48,16},{56,24},{64... | collective-permute-start | bytes 3932168 | tf_op jit(solution)/shard_map/ppermute | solution.py:477
  384.5 57.0 %collective-permute-start.26 = (f32[512,640]{1,0:T(8,128)S(1)}, f32[512,640]{1,0:T(8,128)}, u32[]{:S(2)}, u32[]{:S(2)}) collective-permute-start(f32[512,640]{1,0:T(8,128)S(1)} %collective-permute-done.14.refs_2_), channel_id=1, source_target_pairs={{0,24},{8,0},{16,8},{24,16},{32,56},{40,32},{48,40},{56,48},{64,88... | collective-permute-start | bytes 3932168 | tf_op jit(solution)/shard_map/ppermute | solution.py:477
  385.0 56.5 %collective-permute-start.27 = (f32[512,640]{1,0:T(8,128)S(1)}, f32[512,640]{1,0:T(8,128)}, u32[]{:S(2)}, u32[]{:S(2)}) collective-permute-start(f32[512,640]{1,0:T(8,128)S(1)} %collective-permute-done.15.refs_3_), channel_id=1, source_target_pairs={{0,96},{8,104},{16,112},{24,120},{32,0},{40,8},{48,16},{56,24},{64... | collective-permute-start | bytes 3932168 | tf_op jit(solution)/shard_map/ppermute | solution.py:477
  385.1 56.4 %collective-permute-start.30 = (f32[512,640]{1,0:T(8,128)S(1)}, f32[512,640]{1,0:T(8,128)}, u32[]{:S(2)}, u32[]{:S(2)}) collective-permute-start(f32[512,640]{1,0:T(8,128)S(1)} %collective-permute-done.12.refs_0_), channel_id=1, source_target_pairs={{0,8},{8,16},{16,24},{24,0},{32,40},{40,48},{48,56},{56,32},{64,72... | collective-permute-start | bytes 3932168 | tf_op jit(solution)/shard_map/ppermute | solution.py:477
  417.3 27.5 %collective-permute-start.31 = (f32[512,640]{1,0:T(8,128)S(1)}, f32[512,640]{1,0:T(8,128)}, u32[]{:S(2)}, u32[]{:S(2)}) collective-permute-start(f32[512,640]{1,0:T(8,128)S(1)} %collective-permute-done.13.refs_1_), channel_id=1, source_target_pairs={{0,32},{8,40},{16,48},{24,56},{32,64},{40,72},{48,80},{56,88},{64,... | collective-permute-start | bytes 3932168 | tf_op jit(solution)/shard_map/ppermute | solution.py:477
  417.3 87.1 %collective-permute-start.20 = (f32[1024,640]{1,0:T(8,128)S(1)}, f32[1024,640]{1,0:T(8,128)S(1)}, u32[]{:S(2)}, u32[]{:S(2)}) collective-permute-start(f32[1024,640]{1,0:T(8,128)S(1)} %copy-done.4), channel_id=1, source_target_pairs={{0,8},{8,16},{16,24},{24,0},{32,40},{40,48},{48,56},{56,32},{64,72... | collective-permute-start | bytes 7864328 | tf_op jit(solution)/shard_map/ppermute | solution.py:477
  441.5 67.1 %collective-permute-start.21 = (f32[1024,640]{1,0:T(8,128)S(1)}, f32[1024,640]{1,0:T(8,128)S(1)}, u32[]{:S(2)}, u32[]{:S(2)}) collective-permute-start(f32[1024,640]{1,0:T(8,128)S(1)} %get-tuple-element.109), channel_id=1, source_target_pairs={{0,32},{8,40},{16,48},{24,56},{32,64},{40,72},{48,80},{56,88},{64,... | collective-permute-start | bytes 7864328 | tf_op jit(solution)/shard_map/ppermute | solution.py:477
  441.5 67.2 %collective-permute-start.22 = (f32[1024,640]{1,0:T(8,128)S(1)}, f32[1024,640]{1,0:T(8,128)S(1)}, u32[]{:S(2)}, u32[]{:S(2)}) collective-permute-start(f32[1024,640]{1,0:T(8,128)S(1)} %copy-done.4), channel_id=1, source_target_pairs={{0,24},{8,0},{16,8},{24,16},{32,56},{40,32},{48,40},{56,48},{64,88... | collective-permute-start | bytes 7864328 | tf_op jit(solution)/shard_map/ppermute | solution.py:477
  441.5 70.5 %collective-permute-start.23 = (f32[1024,640]{1,0:T(8,128)S(1)}, f32[1024,640]{1,0:T(8,128)S(1)}, u32[]{:S(2)}, u32[]{:S(2)}) collective-permute-start(f32[1024,640]{1,0:T(8,128)S(1)} %get-tuple-element.109), channel_id=1, source_target_pairs={{0,96},{8,104},{16,112},{24,120},{32,0},{40,8},{48,16},{56,24},{64... | collective-permute-start | bytes 7864328 | tf_op jit(solution)/shard_map/ppermute | solution.py:477
  444.8 56.0 %collective-permute-start.32 = (f32[512,640]{1,0:T(8,128)S(1)}, f32[512,640]{1,0:T(8,128)S(1)}, u32[]{:S(2)}, u32[]{:S(2)}) collective-permute-start(f32[512,640]{1,0:T(8,128)S(1)} %collective-permute-done.14.refs_2_), channel_id=1, source_target_pairs={{0,8},{8,16},{16,24},{24,0},{32,40},{40,48},{48,56},{56,32},{64,72... | collective-permute-start | bytes 3932168 | tf_op jit(solution)/shard_map/ppermute | solution.py:477
  500.8 7.8 %copy-start = (f32[512,640]{1,0:T(8,128)}, f32[512,640]{1,0:T(8,128)S(1)}, u32[]{:S(2)}) copy-start(f32[512,640]{1,0:T(8,128)S(1)} %collective-permute-done.32.refs_0_) | copy-start | bytes 3932164
  500.8 88.6 %collective-permute-start.28 = (f32[1024,640]{1,0:T(8,128)S(1)}, f32[1024,640]{1,0:T(8,128)S(1)}, u32[]{:S(2)}, u32[]{:S(2)}) collective-permute-start(f32[1024,640]{1,0:T(8,128)S(1)} %collective-permute-done.8.refs_0_), channel_id=1, source_target_pairs={{0,8},{8,16},{16,24},{24,0},{32,40},{40,48},{48,56},{56,32},{64,72... | collective-permute-start | bytes 7864328 | tf_op jit(solution)/shard_map/ppermute | solution.py:477
  504.5 86.2 %collective-permute-start.29 = (f32[1024,640]{1,0:T(8,128)S(1)}, f32[1024,640]{1,0:T(8,128)S(1)}, u32[]{:S(2)}, u32[]{:S(2)}) collective-permute-start(f32[1024,640]{1,0:T(8,128)S(1)} %collective-permute-done.9.refs_1_), channel_id=1, source_target_pairs={{0,32},{8,40},{16,48},{24,56},{32,64},{40,72},{48,80},{56,88},{64,... | collective-permute-start | bytes 7864328 | tf_op jit(solution)/shard_map/ppermute | solution.py:477
  508.6 98.1 %collective-permute-start.34 = (f32[1024,640]{1,0:T(8,128)}, f32[1024,640]{1,0:T(8,128)}, u32[]{:S(2)}, u32[]{:S(2)}) collective-permute-start(f32[1024,640]{1,0:T(8,128)} %collective-permute-done.18.refs_0_), channel_id=1, source_target_pairs={{0,24},{8,0},{16,8},{24,16},{32,56},{40,32},{48,40},{56,48},{64,88... | collective-permute-start | bytes 7864328 | tf_op jit(solution)/shard_map/ppermute | solution.py:477
  508.7 105.5 %collective-permute-start.35 = (f32[1024,640]{1,0:T(8,128)}, f32[1024,640]{1,0:T(8,128)}, u32[]{:S(2)}, u32[]{:S(2)}) collective-permute-start(f32[1024,640]{1,0:T(8,128)} %collective-permute-done.19.refs_1_), channel_id=1, source_target_pairs={{0,96},{8,104},{16,112},{24,120},{32,0},{40,8},{48,16},{56,24},{64... | collective-permute-start | bytes 7864328 | tf_op jit(solution)/shard_map/ppermute | solution.py:477
  512.0 77.3 %collective-permute-start.33 = (f32[512,640]{1,0:T(8,128)S(1)}, f32[512,640]{1,0:T(8,128)S(1)}, u32[]{:S(2)}, u32[]{:S(2)}) collective-permute-start(f32[512,640]{1,0:T(8,128)S(1)} %collective-permute-done.15.refs_3_), channel_id=1, source_target_pairs={{0,32},{8,40},{16,48},{24,56},{32,64},{40,72},{48,80},{56,88},{64,... | collective-permute-start | bytes 3932168 | tf_op jit(solution)/shard_map/ppermute | solution.py:477
  589.3 8.6 %copy-start.2 = (f32[512,640]{1,0:T(8,128)}, f32[512,640]{1,0:T(8,128)S(1)}, u32[]{:S(2)}) copy-start(f32[512,640]{1,0:T(8,128)S(1)} %collective-permute-done.33.refs_1_) | copy-start | bytes 3932164
  589.3 25.8 %collective-permute-start.36 = (f32[512,640]{1,0:T(8,128)}, f32[512,640]{1,0:T(8,128)}, u32[]{:S(2)}, u32[]{:S(2)}) collective-permute-start(f32[512,640]{1,0:T(8,128)} %slice.44), channel_id=1, source_target_pairs={{0,8},{8,16},{16,24},{24,0},{32,40},{40,48},{48,56},{56,32},{64,72... | collective-permute-start | bytes 3932168 | tf_op jit(solution)/shard_map/ppermute | solution.py:477
  589.4 33.0 %collective-permute-start.37 = (f32[512,640]{1,0:T(8,128)}, f32[512,640]{1,0:T(8,128)}, u32[]{:S(2)}, u32[]{:S(2)}) collective-permute-start(f32[512,640]{1,0:T(8,128)} %slice.45), channel_id=1, source_target_pairs={{0,32},{8,40},{16,48},{24,56},{32,64},{40,72},{48,80},{56,88},{64,... | collective-permute-start | bytes 3932168 | tf_op jit(solution)/shard_map/ppermute | solution.py:477
  590.7 31.7 %collective-permute-start.38 = (f32[512,640]{1,0:T(8,128)}, f32[512,640]{1,0:T(8,128)}, u32[]{:S(2)}, u32[]{:S(2)}) collective-permute-start(f32[512,640]{1,0:T(8,128)} %slice.46), channel_id=1, source_target_pairs={{0,24},{8,0},{16,8},{24,16},{32,56},{40,32},{48,40},{56,48},{64,88... | collective-permute-start | bytes 3932168 | tf_op jit(solution)/shard_map/ppermute | solution.py:477
  606.7 32.4 %collective-permute-start.39 = (f32[512,640]{1,0:T(8,128)}, f32[512,640]{1,0:T(8,128)}, u32[]{:S(2)}, u32[]{:S(2)}) collective-permute-start(f32[512,640]{1,0:T(8,128)} %slice.47), channel_id=1, source_target_pairs={{0,96},{8,104},{16,112},{24,120},{32,0},{40,8},{48,16},{56,24},{64... | collective-permute-start | bytes 3932168 | tf_op jit(solution)/shard_map/ppermute | solution.py:477
  614.2 29.7 %collective-permute-start.42 = (f32[512,640]{1,0:T(8,128)}, f32[512,640]{1,0:T(8,128)}, u32[]{:S(2)}, u32[]{:S(2)}) collective-permute-start(f32[512,640]{1,0:T(8,128)} %collective-permute-done.26.refs_2_), channel_id=1, source_target_pairs={{0,24},{8,0},{16,8},{24,16},{32,56},{40,32},{48,40},{56,48},{64,88... | collective-permute-start | bytes 3932168 | tf_op jit(solution)/shard_map/ppermute | solution.py:477
  615.1 28.8 %collective-permute-start.40 = (f32[512,640]{1,0:T(8,128)}, f32[512,640]{1,0:T(8,128)}, u32[]{:S(2)}, u32[]{:S(2)}) collective-permute-start(f32[512,640]{1,0:T(8,128)} %collective-permute-done.30.refs_0_), channel_id=1, source_target_pairs={{0,8},{8,16},{16,24},{24,0},{32,40},{40,48},{48,56},{56,32},{64,72... | collective-permute-start | bytes 3932168 | tf_op jit(solution)/shard_map/ppermute | solution.py:477
  622.4 21.5 %collective-permute-start.41 = (f32[512,640]{1,0:T(8,128)}, f32[512,640]{1,0:T(8,128)}, u32[]{:S(2)}, u32[]{:S(2)}) collective-permute-start(f32[512,640]{1,0:T(8,128)} %collective-permute-done.31.refs_1_), channel_id=1, source_target_pairs={{0,32},{8,40},{16,48},{24,56},{32,64},{40,72},{48,80},{56,88},{64,... | collective-permute-start | bytes 3932168 | tf_op jit(solution)/shard_map/ppermute | solution.py:477
  622.4 21.5 %collective-permute-start.43 = (f32[512,640]{1,0:T(8,128)}, f32[512,640]{1,0:T(8,128)}, u32[]{:S(2)}, u32[]{:S(2)}) collective-permute-start(f32[512,640]{1,0:T(8,128)} %collective-permute-done.27.refs_3_), channel_id=1, source_target_pairs={{0,96},{8,104},{16,112},{24,120},{32,0},{40,8},{48,16},{56,24},{64... | collective-permute-start | bytes 3932168 | tf_op jit(solution)/shard_map/ppermute | solution.py:477
  628.8 3.3 copy-start.3
  (1 other events, 2.8 us)

commit v4 on v2

--- a/solution.py
+++ b/solution.py
@@ -84,10 +84,12 @@
     sub = 512
     per = part // sub
     tiles = vocab // sub
-    depth = 6
+    depth = 2 * per
+    ring = N_DP // 2
+    few_first = 3
 
     def kern(hid_hbm, gain_hbm, mask_hbm, tea_ref, tab_ref, got_late, blocks_ref, x_out, tab_out, coef_ref, all_ref, gh_ref, gg_ref,
-             hid_ref, gain_ref, mask_in, w_ref, raw, sends, stage, got_soon, tabs, n_buf, x_buf, inv_buf, square, pay, pay_got, mask_own, mask_got, x_got, tp_got, own_col,
+             hid_ref, gain_ref, mask_in, w_ref, raw, sends, stage, got_soon, g_buf, t_acc, c_acc, tabs, n_buf, x_buf, inv_buf, square, pay, pay_got, mask_own, mask_got, x_got, tp_got, own_col,
              own_row, rel, dx, rs_got, ag_own, ag_got, gn_own, gn_got, raw_sem, tab_sem, in_sem, hop_sem, dp_sem, tp_sem):
         me, at = peers()
         col = lax.axis_index('tp')
@@ -96,7 +98,7 @@
 
         def fetch(k):
             d = at[ORDER[k]]
-            return pltpu.make_async_copy(tea_ref.at[:, aligned(d * part, part)], raw.at[aligned(d * tokens, tokens, tokens)], raw_sem.at[k])
+            return pltpu.make_async_copy(tea_ref.at[:, aligned(d * part, part)], raw.at[pl.ds(k % ring * tokens, tokens)], raw_sem.at[k])
 
         def tab_copy(i):
             slot = lax.rem(i, depth)
@@ -107,9 +109,9 @@
         own_tab = pltpu.make_async_copy(tab_ref.at[aligned(me * part, part)], tab_out, in_sem.at[1])
         for cp in inputs:
             cp.start()
-        for k in range(N_DP):
+        for k in range(ring):
             fetch(k).start()
-        for i in range(depth - 1):
+        for i in range(per):
             tab_copy(i).start()
         own_tab.start()
         barrier = pltpu.get_barrier_semaphore()
@@ -118,6 +120,106 @@
         for j in range(1, N_TP):
             pl.semaphore_signal(barrier, inc=1, device_id=(me, mates[j]), device_id_type=MESH)
 
+        def fold(v):
+            total = v[:, :LANES]
+            for c in range(LANES, v.shape[1], LANES):
+                total = total + v[:, c:c + LANES]
+            return total
+
+        def weigh(k):
+            fetch(k).wait()
+            d = at[ORDER[k]]
+
+            def rows(r, _):
+                here = aligned(r * pack, pack, pack)
+                cap = jnp.tanh(raw[aligned(k % ring * tokens + r * pack, pack, pack)].astype(F32) * INV_CAP)
+                tea = jnp.exp(SOFT_CAP * cap - SOFT_CAP)
+                sends[aligned(d * tokens + r * pack, pack, pack)] = tea
+                t_acc[here] += fold(tea)
+                c_acc[here] += fold(tea * cap)
+                return 0
+
+            lax.fori_loop(0, tokens // pack, rows, 0)
+            if k + ring < N_DP:
+                fetch(k + ring).start()
+
+        t_acc[...] = jnp.zeros((tokens, LANES), F32)
+        c_acc[...] = jnp.zeros((tokens, LANES), F32)
+        weigh(0)
+        pl.semaphore_wait(barrier, N_DP + N_TP - 2)
+
+        def remote(src, dst, out, into, dp, tp):
+            return pltpu.make_async_remote_copy(src_ref=src, dst_ref=dst, send_sem=out, recv_sem=into, device_id=(dp, tp), device_id_type=MESH)
+
+        def to_dp(src, dst, x, rows=slice(None)):
+            def send(o):
+                d = at[o]
+                return remote(src.at[rows], dst.at[me, rows], dp_sem.at[x, 0, d], dp_sem.at[x, 1, me], d, col)
+
+            def into(o):
+                d = at[o]
+                return remote(src.at[rows], dst.at[d, rows], dp_sem.at[x, 0, d], dp_sem.at[x, 1, d], d, col)
+
+            return [send(o) for o in ORDER[:-1]], [into(o) for o in ORDER[:-1]]
+
+        def to_tp(srcs, dst, x):
+            def send(j):
+                c = mates[j]
+                return remote(srcs(c), dst.at[col], tp_sem.at[x, 0, c], tp_sem.at[x, 1, col], me, c)
+
+            def into(j):
+                c = mates[j]
+                return remote(srcs(c), dst.at[c], tp_sem.at[x, 0, c], tp_sem.at[x, 1, c], me, c)
+
+            return [send(j) for j in range(1, N_TP)], [into(j) for j in range(1, N_TP)]
+
+        def start(copies):
+            for cp in copies:
+                cp.start()
+
+        def arrive(copies):
+            for cp in copies:
+                cp.wait_recv()
+
+        def added(ref, here=slice(None)):
+            total = ref[0, here]
+            for d in range(1, ref.shape[0]):
+                total = total + ref[d, here]
+            return total
+
+        gots = (got_soon, got_late)
+        late = part // 2
+
+        def hop(j, level, w):
+            kind, (dz, dy) = JOBS[j]
+            tok = pl.ds(kind * half, half)
+            rows = slice(None) if w is None else pl.ds(w * late, late)
+            src = stage.at[MIDDLE.index((j, level - 1)), :, rows] if level else sends.at[aligned(at[dz, dy] * tokens + kind * half, half, half), rows]
+            dst = stage.at[MIDDLE.index((j, level)), :, rows] if (j, level) in MIDDLE else gots[w].at[dz * SIDE + dy, tok]
+            k = COPIES.index((j, level, w))
+            return remote(src, dst, hop_sem.at[0, k], hop_sem.at[1, k], at[PATHS[j][level]], col)
+
+        def came(level, w=None):
+            for j, at in MIDDLE:
+                if at == level:
+                    hop(j, level, w).wait_recv()
+
+        def onward(level, far, *ws):
+            for w in ws:
+                for j, at in MIDDLE:
+                    if at == level - 1 and far == (len(PATHS[j]) > 2):
+                        hop(j, level, w).start()
+
+        def issue(k):
+            for j, (_, to) in enumerate(JOBS):
+                if to == ORDER[k]:
+                    for w in waves(j, 0):
+                        hop(j, 0, w).start()
+
+        issue(0)
+        for k in range(1, few_first):
+            weigh(k)
+            issue(k)
         for cp in inputs:
             cp.wait()
         w_ref[...] = 1.0 + jnp.concatenate([gain_ref[i:i + 1] for i in range(dim // LANES)], axis=1)
@@ -131,99 +233,15 @@
         square[0:1, 0:tokens] = mask_in[...]
         mask_own[...] = square[0:few]
         mask_col = jnp.transpose(square[...])[0:tokens, 0:1]
-
-        def weigh(k):
-            fetch(k).wait()
-            d = at[ORDER[k]]
-
-            def rows(r, _):
-                here = aligned(d * tokens + r * pack, pack, pack)
-                cap = jnp.tanh(raw[here].astype(F32) * INV_CAP)
-                sends[here] = jnp.exp(SOFT_CAP * cap - SOFT_CAP)
-                return 0
-
-            lax.fori_loop(0, tokens // pack, rows, 0)
-
-        weigh(0)
-        weigh(1)
-        pl.semaphore_wait(barrier, N_DP + N_TP - 2)
-
-        def remote(src, dst, out, into, dp, tp):
-            return pltpu.make_async_remote_copy(src_ref=src, dst_ref=dst, send_sem=out, recv_sem=into, device_id=(dp, tp), device_id_type=MESH)
-
-        def to_dp(src, dst, x, rows=slice(None)):
-            def send(o):
-                d = at[o]
-                return remote(src.at[rows], dst.at[me, rows], dp_sem.at[x, 0, d], dp_sem.at[x, 1, me], d, col)
-
-            def into(o):
-                d = at[o]
-                return remote(src.at[rows], dst.at[d, rows], dp_sem.at[x, 0, d], dp_sem.at[x, 1, d], d, col)
-
-            return [send(o) for o in ORDER[:-1]], [into(o) for o in ORDER[:-1]]
-
-        def to_tp(srcs, dst, x):
-            def send(j):
-                c = mates[j]
-                return remote(srcs(c), dst.at[col], tp_sem.at[x, 0, c], tp_sem.at[x, 1, col], me, c)
-
-            def into(j):
-                c = mates[j]
-                return remote(srcs(c), dst.at[c], tp_sem.at[x, 0, c], tp_sem.at[x, 1, c], me, c)
-
-            return [send(j) for j in range(1, N_TP)], [into(j) for j in range(1, N_TP)]
-
-        def start(copies):
-            for cp in copies:
-                cp.start()
-
-        def arrive(copies):
-            for cp in copies:
-                cp.wait_recv()
-
-        def added(ref, here=slice(None)):
-            total = ref[0, here]
-            for d in range(1, ref.shape[0]):
-                total = total + ref[d, here]
-            return total
-
-        gots = (got_soon, got_late)
-        late = part // 2
-
-        def hop(j, level, w):
-            kind, (dz, dy) = JOBS[j]
-            tok = pl.ds(kind * half, half)
-            rows = slice(None) if w is None else pl.ds(w * late, late)
-            src = stage.at[MIDDLE.index((j, level - 1)), :, rows] if level else sends.at[aligned(at[dz, dy] * tokens + kind * half, half, half), rows]
-            dst = stage.at[MIDDLE.index((j, level)), :, rows] if (j, level) in MIDDLE else gots[w].at[dz * SIDE + dy, tok]
-            k = COPIES.index((j, level, w))
-            return remote(src, dst, hop_sem.at[0, k], hop_sem.at[1, k], at[PATHS[j][level]], col)
-
-        def came(level, w=None):
-            for j, at in MIDDLE:
-                if at == level:
-                    hop(j, level, w).wait_recv()
-
-        def onward(level, far, *ws):
-            for w in ws:
-                for j, at in MIDDLE:
-                    if at == level - 1 and far == (len(PATHS[j]) > 2):
-                        hop(j, level, w).start()
-
         pay_sends, pay_came = to_dp(pay, pay_got, 0)
         start(pay_sends)
         pay_got[me] = pay[...]
         mask_sends, mask_came = to_dp(mask_own, mask_got, 1, pl.ds(0, 1))
         start(mask_sends)
         mask_got[me] = mask_own[...]
-
-        for k, o in enumerate(ORDER):
-            if k > 1:
-                weigh(k)
-            for j, (_, to) in enumerate(JOBS):
-                if to == o:
-                    for w in waves(j, 0):
-                        hop(j, 0, w).start()
+        for k in range(few_first, N_DP):
+            weigh(k)
+            issue(k)
 
         def keep(r, _):
             here, there = aligned(me * tokens + r * pack, pack, pack), aligned(r * pack, pack, pack)
@@ -233,34 +251,37 @@
 
         lax.fori_loop(0, tokens // pack, keep, 0)
 
-        def fold(v):
-            total = v[:, :LANES]
-            for c in range(LANES, v.shape[1], LANES):
-                total = total + v[:, c:c + LANES]
-            return total
-
         def student(slot):
             z = lax.dot_general(x_buf[...], tabs[slot], ROWS_BY_ROWS, preferred_element_type=F32)
             ratio = jnp.tanh(z * INV_CAP)
             return ratio, jnp.exp(SOFT_CAP * ratio - SOFT_CAP)
 
+        def next_tiles(i):
+            for c in range(per):
+                tab_copy(i * per + c).wait()
+
+            @pl.when(i + 1 < 2 * N_DP)
+            def _():
+                for c in range(per):
+                    tab_copy((i + 1) * per + c).start()
+
+            return [lax.rem(i, 2) * per + c for c in range(per)]
+
         def forward(i, sums):
-            slot = lax.rem(i, depth)
-            tab_copy(i).wait()
-            tab_copy(i + depth - 1).start()
-            s_sum, t_sum, k_sum = sums
-            ratio, stu = student(slot)
-            toks, here = aligned(lax.div(i, per) * tokens, tokens, tokens), aligned(lax.rem(i, per) * sub, sub)
-            cap = jnp.tanh(raw[toks, here].astype(F32) * INV_CAP)
-            tea = sends[toks, here]
-            return s_sum + fold(stu), t_sum + fold(tea), k_sum + fold(tea * (cap - ratio))
+            s_sum, k_sum = sums
+            slots = next_tiles(i)
+            for c in range(per):
+                ratio, stu = student(slots[c])
+                tea = sends[aligned(i * tokens, tokens, tokens), pl.ds(c * sub, sub)]
+                s_sum, k_sum = s_sum + fold(stu), k_sum + fold(tea * ratio)
+            return s_sum, k_sum
 
         zero = jnp.zeros((tokens, LANES), F32)
-        s_sum, t_sum, k_sum = lax.fori_loop(0, tiles, forward, (zero, zero, zero))
+        s_sum, k_sum = lax.fori_loop(0, N_DP, forward, (zero, zero))
         lane = lax.broadcasted_iota(jnp.int32, (tokens, LANES), 1)
         sums = jnp.where(lane == 0, jnp.sum(s_sum, axis=1, keepdims=True), 0.0)
-        sums = jnp.where(lane == 1, jnp.sum(t_sum, axis=1, keepdims=True), sums)
-        sums = jnp.where(lane == AWAY, SOFT_CAP * jnp.sum(k_sum, axis=1, keepdims=True), sums)
+        sums = jnp.where(lane == 1, jnp.sum(t_acc[...], axis=1, keepdims=True), sums)
+        sums = jnp.where(lane == AWAY, SOFT_CAP * jnp.sum(c_acc[...] - k_sum, axis=1, keepdims=True), sums)
         own_col[...] = sums
         tp_got[col] = sums
         tp_sends, tp_came = to_tp(lambda c: own_col, tp_got, 0)
@@ -273,36 +294,46 @@
         all_ref[me] = line
         dp_sends, dp_came = to_dp(own_row, all_ref, 2)
         start(dp_sends)
+        twin = col + 1 - 2 * lax.rem(col, 2)
+        arrive((*pay_came, *mask_came))
+        x_got[col] = pay_got[...]
+
+        def across(j, origin):
+            return remote(pay_got, x_got.at[origin], tp_sem.at[1, 0, mates[j]], tp_sem.at[1, 1, origin], me, mates[j])
+
+        def to_twin(j, origin):
+            return remote(x_got.at[origin], x_got.at[origin], tp_sem.at[1, 0, mates[j + 1]], tp_sem.at[1, 1, origin], me, twin)
+
+        evens = range(0, N_TP, 2)
+        xt_sends = [across(j, col) for j in evens[1:]]
+        start(xt_sends)
         came(0)
         onward(1, True, None)
         onward(1, False, 0)
 
-        arrive((*pay_came, *mask_came))
-        x_got[col] = pay_got[...]
-        xt_sends, xt_came = to_tp(lambda c: pay_got, x_got, 1)
-        start(xt_sends)
         count = jnp.sum(added(mask_got, slice(1)), axis=1, keepdims=True)
         inv_s, inv_t, weight = 1.0 / total[:, 0:1], 1.0 / total[:, 1:2], mask_col / count
         dx[...] = jnp.zeros((tokens, dim), F32)
 
         def backward(i, _):
-            slot = lax.rem(i, depth)
-            tab_copy(i).wait()
-
-            @pl.when(i + depth - 1 < 2 * tiles)
-            def _():
-                tab_copy(i + depth - 1).start()
-
-            ratio, stu = student(slot)
-            tea = sends[aligned(lax.div(i - tiles, per) * tokens, tokens, tokens), aligned(lax.rem(i, per) * sub, sub)]
-            diff = (stu * inv_s - tea * inv_t) * weight
-            g = (diff * (1.0 - ratio * ratio)).astype(BF16)
-            dx[...] += jnp.dot(g, tabs[slot], preferred_element_type=F32)
+            slots = next_tiles(i)
+            total = dx[...]
+            for c in range(per):
+                ratio, stu = student(slots[c])
+                tea = sends[aligned((i - N_DP) * tokens, tokens, tokens), pl.ds(c * sub, sub)]
+                diff = (stu * inv_s - tea * inv_t) * weight
+                g = (diff * (1.0 - ratio * ratio)).astype(BF16)
+                total = total + jnp.dot(g, tabs[slots[c]], preferred_element_type=F32)
+            dx[...] = total
             return 0
 
-        lax.fori_loop(tiles, 2 * tiles, backward, 0)
+        lax.fori_loop(N_DP, 2 * N_DP, backward, 0)
         came(1)
         onward(2, True, 0)
+        onward(1, False, 1)
+        arrive([across(j, mates[j]) for j in evens[1:]])
+        twin_sends = [to_twin(j, mates[j]) for j in evens]
+        start(twin_sends)
 
         rs_got[col] = dx[my_few]
         rs_sends, rs_came = to_tp(lambda c: dx.at[aligned(c * few, few, few)], rs_got, 2)
@@ -329,8 +360,7 @@
         came(2, 0)
         onward(DOWN, True, 0)
         onward(2, True, 1)
-        onward(1, False, 1)
-        arrive(xt_came)
+        arrive([to_twin(j, mates[j + 1]) for j in evens])
 
         def widen(d, _):
             rows = jnp.concatenate([x_got[j, d] for j in range(N_TP)], axis=0)
@@ -362,7 +392,7 @@
                 came(2, 1)
                 onward(DOWN, True, 1)
 
-            grad_block(at, got_soon, x_out, tab_out[aligned(b * sub, sub)], coef_ref, sends, raw, blocks_ref, b)
+            grad_block(at, got_soon, x_out, tab_out[aligned(b * sub, sub)], coef_ref, sends, g_buf, blocks_ref, b)
             return 0
 
         lax.fori_loop(0, 2, block, 0)
@@ -373,7 +403,7 @@
         for j, level, w in COPIES:
             if level:
                 hop(j, level, w).wait_send()
-        for cp in (*pay_sends, *mask_sends, *tp_sends, *dp_sends, *xt_sends, *rs_sends, *ag_sends, *gn_sends):
+        for cp in (*pay_sends, *mask_sends, *tp_sends, *dp_sends, *xt_sends, *twin_sends, *rs_sends, *ag_sends, *gn_sends):
             cp.wait_send()
 
     dma = pltpu.SemaphoreType.DMA
@@ -385,8 +415,8 @@
             ((1, dim), F32))),
         in_specs=[HB] * 5, out_specs=(VM,) * 8,
         scratch_shapes=[pltpu.VMEM(shape, kind) for shape, kind in (
-            (wide, BF16), ((dim // LANES, LANES), F32), ((1, tokens), F32), ((1, dim), F32), ((N_DP * tokens, part), BF16), ((N_DP * tokens, part), F32),
-            ((len(MIDDLE), half, part), F32), ((N_DP, tokens, part // 2), F32),
+            (wide, BF16), ((dim // LANES, LANES), F32), ((1, tokens), F32), ((1, dim), F32), ((ring * tokens, part), BF16), ((N_DP * tokens, part), F32),
+            ((len(MIDDLE), half, part), F32), ((N_DP, tokens, part // 2), F32), ((N_DP * tokens, sub), BF16), ((tokens, LANES), F32), ((tokens, LANES), F32),
             ((depth, sub, dim), BF16), (wide, F32), (wide, BF16), ((tokens, LANES), F32), ((LANES, LANES), F32), ((few, dim), F32),
             ((N_DP, few, dim), F32), (flat, F32), ((N_DP, *flat), F32), ((N_TP, N_DP, few, dim), F32), ((N_TP, tokens, LANES), F32),
             ((tokens, LANES), F32), (flat, F32), ((LANES, LANES), F32), (wide, F32), ((N_TP, few, dim), F32), ((2 * few, dim), F32),
@@ -423,7 +453,7 @@
     dim = arrays[0].shape[1]
     rows = vocab // N_DP
     quarter = rows // SIDE
-    cut = 128
+    cut = 256
     chunks = [(i, r) for i in range(n) for r in range(0, arrays[i].shape[0], cut)]
 
     def kern(*refs):
@@ -431,8 +461,8 @@
         at = peers()[1]
         reads, writes = [], []
         for k, (i, r) in enumerate(chunks):
-            _, dz, dy, kind, half, start = pieces[i]
-            first = (2 * (half + r // quarter) + kind) * quarter + start + r % quarter
+            _, dz, dy, kind, half = pieces[i]
+            first = (2 * (half + r // quarter) + kind) * quarter + r % quarter
             there = aligned(at[dz, dy] * rows + first, cut, cut)
             reads.append(pltpu.make_async_copy(refs[i].at[pl.ds(r, cut)], buf.at[k], sem.at[0, k]))
             writes.append(pltpu.make_async_copy(buf.at[k], dst.at[there], sem.at[1, k]))
@@ -455,8 +485,6 @@
 def gather(first, rest, vocab):
     quarter = first[0].shape[0]
     sets, ways = range(2), (UP, DOWN)
-    most = quarter - LANES
-    cuts = slice(0, most), slice(most, quarter)
     table, event = None, 0
 
     def send(pair, axis, step):
@@ -466,8 +494,8 @@
             out.append(lax.ppermute(pair[k], 'dp', [(d, shift(d, dz, dy)) for d in range(N_DP)]))
         return out
 
-    def put(pair, a, b, c=0, start=0):
-        return [(pair[k], *((b, a) if k else (a, b)), k, c, start) for k in sets]
+    def put(pair, a, b, c=0):
+        return [(pair[k], *((b, a) if k else (a, b)), k, c) for k in sets]
 
     def settle(*pieces):
         nonlocal table
@@ -524,12 +552,12 @@
     settle(put(high_side[DOWN], UP, UP))
 
     far_side[0, DOWN], far_side[1, DOWN], side_far = wait(far_side[0, DOWN], far_side[1, DOWN], side_far)
-    last_down = [send([x[cut] for x in far_side[1, DOWN]], 1, DOWN) for cut in cuts]
+    last_down = send(far_side[1, DOWN], 1, DOWN)
     settle(put(far_side[0, DOWN], AWAY, UP, 0), put(far_side[1, DOWN], AWAY, UP, 1))
     settle(put(side_far, 0, AWAY))
 
     far_side[0, UP], = wait(far_side[0, UP])
-    last_up = [send([x[cut] for x in far_side[0, UP]], 1, UP) for cut in cuts]
+    last_up = send(far_side[0, UP], 1, UP)
     settle(put(far_side[0, UP], AWAY, DOWN, 0))
 
     far_side[1, UP], low_far = wait(far_side[1, UP], low_far)
@@ -538,9 +566,8 @@
 
     high_far = wait(*high_far)
     settle(put(high_far[0], UP, AWAY, 0), put(high_far[1], UP, AWAY, 1))
-    for up, down, cut in zip(last_up, last_down, cuts):
-        up, down = wait(up, down)
-        settle(put(up, AWAY, AWAY, 0, cut.start), put(down, AWAY, AWAY, 1, cut.start))
+    last_up, last_down = wait(last_up, last_down)
+    settle(put(last_up, AWAY, AWAY, 0), put(last_down, AWAY, AWAY, 1))
     return table
 
 

time: 672 us -> 636 us (0.946)
  the two profiles are of different devices: /device:TPU:6 before, /device:TPU:16 now
where the time goes in v4:
time: 636 us
  waiting for transfers between devices  373 us (59%)
  Pallas kernels  185 us (29%)
  starting transfers between devices  59.8 us (9%)
  local copies, waits for them, and re-layouts  10.4 us (2%)
    ppermute x44, waiting for transfers between devices, send(): lax.ppermute(pair[k], 'dp', [(d, shift(d, dz, dy)) for d in range(N_DP)])  373 us
    pallas_call x1, Pallas kernels, front(): pl.pallas_call(kern, out_shape=tuple((jax.ShapeDtypeStruct(shape, kind) f...  109 us
    pallas_call x17, Pallas kernels, place(): pl.pallas_call(kern, out_shape=jax.ShapeDtypeStruct((vocab, dim), F32), i...  69.6 us
    ppermute x44, starting transfers between devices, send(): lax.ppermute(pair[k], 'dp', [(d, shift(d, dz, dy)) for d in range(N_DP)])  59.8 us
  transfers between devices with their start and end apart: 44, of which 13 were waited for; matrix products, arithmetic and copies ran while one was open for 2% of the time, Pallas kernels for 11%

profile of v4, /device:TPU:16, one launch (start us, length us, event | category | flops | bytes accessed | tf_op | source)
XLA Modules:
  0.0 635.6 jit_solution(12333407143314737446)
XLA Ops:
  0.6 108.6 %front.1 = (f32[16,64,1024]{2,1,0:T(8,128)S(1)}, f32[2,512,640]{2,1,0:T(8,128)S(1)}, bf16[1024,640]{1,0:T(8,128)(2,1)S(1)}, bf16[2048,640]{1,0:T(8,128)(2,1)S(1)...) custom-call(bf16[64,640]{1,0:T(8,128)(2,1)} %hid_hbm.1, ...), custom_call_target="tpu_custom_call" | custom-call | flops 3000000000 | bytes 104857600 | tf_op jit(solution)/shard_map/front/pallas_call | solution.py:411
  109.5 3.2 collective-permute-start.2
  112.9 1.9 collective-permute-start.3
  114.7 7.2 %finish.1 = f32[2,512,640]{2,1,0:T(8,128)S(1)} custom-call(f32[16,64,1024]{2,1,0:T(8,128)S(1)} %get-tuple-element.79.tea_ref, bf16[1024,640]{1,0:T(8,128)(2,1)S(1)} %get-tuple-element.80.x_ref, bf16[2048,640]{1,0:T(8,128)(2,1)S(1)} %get-tuple-element.81.tab_ref, f32[128,128]{1,0:T(8,128)S(1)} %get-tuple-element.82.coef_ref), custom_call_target="tpu_custom_call" | custom-call | flops 1000000000 | bytes 8388608 | tf_op jit(solution)/shard_map/finish/pallas_call | solution.py:444
  122.4 19.9 %collective-permute-done.refs_0_ = f32[512,640]{1,0:T(8,128)S(1)} collective-permute-done((f32[512,640]{1,0:T(8,128)S(1)}, f32[512,640]{1,0:T(8,128)S(1)}, u32[]{:S(2)}, u32[]{:S(2)}) %collective-permute-start) | collective-permute-done | bytes 1310752 | tf_op jit(solution)/shard_map/ppermute | solution.py:494
  144.4 3.2 collective-permute-start.6
  147.6 22.8 %collective-permute-done.4.refs_0_ = f32[512,640]{1,0:T(8,128)S(1)} collective-permute-done((f32[512,640]{1,0:T(8,128)S(1)}, f32[512,640]{1,0:T(8,128)S(1)}, u32[]{:S(2)}, u32[]{:S(2)}) %collective-permute-start.4) | collective-permute-done | bytes 1310752 | tf_op jit(solution)/shard_map/ppermute | solution.py:494
  171.2 2.8 collective-permute-done.5.refs_1_
  176.6 4.1 place.17.refs_4_
  180.7 4.2 place.18.refs_4_
  184.9 67.4 %collective-permute-done.7.refs_3_ = f32[512,640]{1,0:T(8,128)S(1)} collective-permute-done((f32[512,640]{1,0:T(8,128)S(1)}, f32[512,640]{1,0:T(8,128)S(1)}, u32[]{:S(2)}, u32[]{:S(2)}) %collective-permute-start.7) | collective-permute-done | bytes 1310752 | tf_op jit(solution)/shard_map/ppermute | solution.py:494
  253.4 2.9 collective-permute-start.13
  256.3 3.2 collective-permute-start.14
  263.2 21.9 %collective-permute-done.12.refs_0_ = f32[512,640]{1,0:T(8,128)S(1)} collective-permute-done((f32[512,640]{1,0:T(8,128)S(1)}, f32[512,640]{1,0:T(8,128)S(1)}, u32[]{:S(2)}, u32[]{:S(2)}) %collective-permute-start.12) | collective-permute-done | bytes 1310752 | tf_op jit(solution)/shard_map/ppermute | solution.py:494
  286.9 2.2 collective-permute-start.19
  289.1 4.1 place.19.refs_2_
  295.0 4.1 place.20.refs_2_
  299.1 4.1 place.21.refs_4_
  303.3 67.0 %collective-permute-done.15.refs_3_ = f32[512,640]{1,0:T(8,128)S(1)} collective-permute-done((f32[512,640]{1,0:T(8,128)S(1)}, f32[512,640]{1,0:T(8,128)S(1)}, u32[]{:S(2)}, u32[]{:S(2)}) %collective-permute-start.15) | collective-permute-done | bytes 1310752 | tf_op jit(solution)/shard_map/ppermute | solution.py:494
  370.4 1.9 collective-permute-start.26
  373.6 29.3 %collective-permute-done.24.refs_0_ = f32[512,640]{1,0:T(8,128)S(1)} collective-permute-done((f32[512,640]{1,0:T(8,128)S(1)}, f32[512,640]{1,0:T(8,128)S(1)}, u32[]{:S(2)}, u32[]{:S(2)}) %collective-permute-start.24) | collective-permute-done | bytes 1310752 | tf_op jit(solution)/shard_map/ppermute | solution.py:494
  402.9 3.3 collective-permute-start.20
  406.2 21.1 %collective-permute-done.26.refs_2_ = f32[512,640]{1,0:T(8,128)} collective-permute-done((f32[512,640]{1,0:T(8,128)S(1)}, f32[512,640]{1,0:T(8,128)}, u32[]{:S(2)}, u32[]{:S(2)}) %collective-permute-start.26) | collective-permute-done | bytes 1310752 | tf_op jit(solution)/shard_map/ppermute | solution.py:494
  427.4 3.3 collective-permute-start.23
  430.7 2.2 collective-permute-done.31.refs_1_
  432.9 3.8 collective-permute-start.32
  436.7 49.3 %collective-permute-done.32.refs_0_ = f32[512,640]{1,0:T(8,128)S(1)} collective-permute-done((f32[512,640]{1,0:T(8,128)S(1)}, f32[512,640]{1,0:T(8,128)S(1)}, u32[]{:S(2)}, u32[]{:S(2)}) %collective-permute-start.32) | collective-permute-done | bytes 1310752 | tf_op jit(solution)/shard_map/ppermute | solution.py:494
  487.6 4.1 place.22.refs_2_
  491.8 2.0 collective-permute-start.34
  493.8 2.0 collective-permute-start.35
  497.1 4.1 place.23.refs_2_
  501.2 4.6 place.24.refs_2_
  508.2 61.3 %collective-permute-done.33.refs_1_ = f32[512,640]{1,0:T(8,128)S(1)} collective-permute-done((f32[512,640]{1,0:T(8,128)S(1)}, f32[512,640]{1,0:T(8,128)S(1)}, u32[]{:S(2)}, u32[]{:S(2)}) %collective-permute-start.33) | collective-permute-done | bytes 1310752 | tf_op jit(solution)/shard_map/ppermute | solution.py:494
  569.5 6.1 collective-permute-start.36
  578.0 4.1 place.25.refs_2_
  582.2 4.1 place.26.refs_4_
  586.3 4.7 place.27.refs_2_
  591.0 3.3 collective-permute-start.39
  594.3 4.1 place.28.refs_2_
  598.5 5.0 collective-permute-done.36.refs_0_
  603.6 2.5 collective-permute-start.40
  606.1 2.3 collective-permute-done.37.refs_1_
  608.4 3.2 collective-permute-start.43
  614.8 2.8 place.29.refs_2_
  618.1 2.4 place.30.refs_2_
  620.5 4.6 place.31.refs_4_
  625.2 4.6 place.32.refs_4_
  629.9 4.6 place.33
  (85 shorter events, 26.2 us)
Async XLA Ops:
  109.4 32.9 %collective-permute-start = (f32[512,640]{1,0:T(8,128)S(1)}, f32[512,640]{1,0:T(8,128)S(1)}, u32[]{:S(2)}, u32[]{:S(2)}) collective-permute-start(f32[512,640]{1,0:T(8,128)S(1)} %get-tuple-element.77.refs_0_), channel_id=1, source_target_pairs={{0,32},{8,40},{16,48},{24,56},{32,64},{40,72},{48,80},{56,88},{64,... | collective-permute-start | bytes 3932168 | tf_op jit(solution)/shard_map/ppermute | solution.py:494
  109.5 34.9 %collective-permute-start.2 = (f32[512,640]{1,0:T(8,128)S(1)}, f32[512,640]{1,0:T(8,128)S(1)}, u32[]{:S(2)}, u32[]{:S(2)}) collective-permute-start(f32[512,640]{1,0:T(8,128)S(1)} %get-tuple-element.77.refs_0_), channel_id=1, source_target_pairs={{0,96},{8,104},{16,112},{24,120},{32,0},{40,8},{48,16},{56,24},{64... | collective-permute-start | bytes 3932168 | tf_op jit(solution)/shard_map/ppermute | solution.py:494
  112.7 30.0 %collective-permute-start.1 = (f32[512,640]{1,0:T(8,128)S(1)}, f32[512,640]{1,0:T(8,128)S(1)}, u32[]{:S(2)}, u32[]{:S(2)}) collective-permute-start(f32[512,640]{1,0:T(8,128)S(1)} %get-tuple-element.78.refs_1_), channel_id=1, source_target_pairs={{0,8},{8,16},{16,24},{24,0},{32,40},{40,48},{48,56},{56,32},{64,72... | collective-permute-start | bytes 3932168 | tf_op jit(solution)/shard_map/ppermute | solution.py:494
  112.9 31.6 %collective-permute-start.3 = (f32[512,640]{1,0:T(8,128)S(1)}, f32[512,640]{1,0:T(8,128)S(1)}, u32[]{:S(2)}, u32[]{:S(2)}) collective-permute-start(f32[512,640]{1,0:T(8,128)S(1)} %get-tuple-element.78.refs_1_), channel_id=1, source_target_pairs={{0,24},{8,0},{16,8},{24,16},{32,56},{40,32},{48,40},{56,48},{64,88... | collective-permute-start | bytes 3932168 | tf_op jit(solution)/shard_map/ppermute | solution.py:494
  122.1 48.3 %collective-permute-start.4 = (f32[512,640]{1,0:T(8,128)S(1)}, f32[512,640]{1,0:T(8,128)S(1)}, u32[]{:S(2)}, u32[]{:S(2)}) collective-permute-start(f32[512,640]{1,0:T(8,128)S(1)} %get-tuple-element.143.refs_2_), channel_id=1, source_target_pairs={{0,32},{8,40},{16,48},{24,56},{32,64},{40,72},{48,80},{56,88},{64,... | collective-permute-start | bytes 3932168 | tf_op jit(solution)/shard_map/ppermute | solution.py:494
  142.3 31.6 %collective-permute-start.5 = (f32[512,640]{1,0:T(8,128)S(1)}, f32[512,640]{1,0:T(8,128)S(1)}, u32[]{:S(2)}, u32[]{:S(2)}) collective-permute-start(f32[512,640]{1,0:T(8,128)S(1)} %get-tuple-element.142.refs_3_), channel_id=1, source_target_pairs={{0,8},{8,16},{16,24},{24,0},{32,40},{40,48},{48,56},{56,32},{64,72... | collective-permute-start | bytes 3932168 | tf_op jit(solution)/shard_map/ppermute | solution.py:494
  142.7 110.8 %collective-permute-start.8 = (f32[1024,640]{1,0:T(8,128)S(1)}, f32[1024,640]{1,0:T(8,128)S(1)}, u32[]{:S(2)}, u32[]{:S(2)}) collective-permute-start(f32[1024,640]{1,0:T(8,128)S(1)} %pad_maximum_fusion), channel_id=1, source_target_pairs={{0,8},{8,16},{16,24},{24,0},{32,40},{40,48},{48,56},{56,32},{64,72... | collective-permute-start | bytes 7864328 | tf_op jit(solution)/shard_map/ppermute | solution.py:494
  144.4 111.9 %collective-permute-start.9 = (f32[1024,640]{1,0:T(8,128)S(1)}, f32[1024,640]{1,0:T(8,128)S(1)}, u32[]{:S(2)}, u32[]{:S(2)}) collective-permute-start(f32[1024,640]{1,0:T(8,128)S(1)} %pad_maximum_fusion.1), channel_id=1, source_target_pairs={{0,32},{8,40},{16,48},{24,56},{32,64},{40,72},{48,80},{56,88},{64,... | collective-permute-start | bytes 7864328 | tf_op jit(solution)/shard_map/ppermute | solution.py:494
  144.4 30.3 %collective-permute-start.6 = (f32[512,640]{1,0:T(8,128)S(1)}, f32[512,640]{1,0:T(8,128)S(1)}, u32[]{:S(2)}, u32[]{:S(2)}) collective-permute-start(f32[512,640]{1,0:T(8,128)S(1)} %get-tuple-element.143.refs_2_), channel_id=1, source_target_pairs={{0,96},{8,104},{16,112},{24,120},{32,0},{40,8},{48,16},{56,24},{64... | collective-permute-start | bytes 3932168 | tf_op jit(solution)/shard_map/ppermute | solution.py:494
  170.4 90.3 %collective-permute-start.10 = (f32[1024,640]{1,0:T(8,128)S(1)}, f32[1024,640]{1,0:T(8,128)S(1)}, u32[]{:S(2)}, u32[]{:S(2)}) collective-permute-start(f32[1024,640]{1,0:T(8,128)S(1)} %pad_maximum_fusion), channel_id=1, source_target_pairs={{0,24},{8,0},{16,8},{24,16},{32,56},{40,32},{48,40},{56,48},{64,88... | collective-permute-start | bytes 7864328 | tf_op jit(solution)/shard_map/ppermute | solution.py:494
  174.0 78.2 %collective-permute-start.7 = (f32[512,640]{1,0:T(8,128)S(1)}, f32[512,640]{1,0:T(8,128)S(1)}, u32[]{:S(2)}, u32[]{:S(2)}) collective-permute-start(f32[512,640]{1,0:T(8,128)S(1)} %get-tuple-element.142.refs_3_), channel_id=1, source_target_pairs={{0,24},{8,0},{16,8},{24,16},{32,56},{40,32},{48,40},{56,48},{64,88... | collective-permute-start | bytes 3932168 | tf_op jit(solution)/shard_map/ppermute | solution.py:494
  174.7 88.4 %collective-permute-start.11 = (f32[1024,640]{1,0:T(8,128)S(1)}, f32[1024,640]{1,0:T(8,128)S(1)}, u32[]{:S(2)}, u32[]{:S(2)}) collective-permute-start(f32[1024,640]{1,0:T(8,128)S(1)} %pad_maximum_fusion.1), channel_id=1, source_target_pairs={{0,96},{8,104},{16,112},{24,120},{32,0},{40,8},{48,16},{56,24},{64... | collective-permute-start | bytes 7864328 | tf_op jit(solution)/shard_map/ppermute | solution.py:494
  252.2 32.9 %collective-permute-start.12 = (f32[512,640]{1,0:T(8,128)S(1)}, f32[512,640]{1,0:T(8,128)S(1)}, u32[]{:S(2)}, u32[]{:S(2)}) collective-permute-start(f32[512,640]{1,0:T(8,128)S(1)} %collective-permute-done.refs_0_), channel_id=1, source_target_pairs={{0,32},{8,40},{16,48},{24,56},{32,64},{40,72},{48,80},{56,88},{64,... | collective-permute-start | bytes 3932168 | tf_op jit(solution)/shard_map/ppermute | solution.py:494
  253.4 32.4 %collective-permute-start.13 = (f32[512,640]{1,0:T(8,128)S(1)}, f32[512,640]{1,0:T(8,128)S(1)}, u32[]{:S(2)}, u32[]{:S(2)}) collective-permute-start(f32[512,640]{1,0:T(8,128)S(1)} %collective-permute-done.1.refs_1_), channel_id=1, source_target_pairs={{0,8},{8,16},{16,24},{24,0},{32,40},{40,48},{48,56},{56,32},{64,72... | collective-permute-start | bytes 3932168 | tf_op jit(solution)/shard_map/ppermute | solution.py:494
  256.3 30.6 %collective-permute-start.14 = (f32[512,640]{1,0:T(8,128)S(1)}, f32[512,640]{1,0:T(8,128)S(1)}, u32[]{:S(2)}, u32[]{:S(2)}) collective-permute-start(f32[512,640]{1,0:T(8,128)S(1)} %collective-permute-done.6.refs_2_), channel_id=1, source_target_pairs={{0,96},{8,104},{16,112},{24,120},{32,0},{40,8},{48,16},{56,24},{64... | collective-permute-start | bytes 3932168 | tf_op jit(solution)/shard_map/ppermute | solution.py:494
  260.7 109.6 %collective-permute-start.16 = (f32[1024,640]{1,0:T(8,128)}, f32[1024,640]{1,0:T(8,128)S(1)}, u32[]{:S(2)}, u32[]{:S(2)}) collective-permute-start(f32[1024,640]{1,0:T(8,128)} %constant_dynamic-update-slice_fusion), channel_id=1, source_target_pairs={{0,8},{8,16},{16,24},{24,0},{32,40},{40,48},{48,56},{56,32},{64,72... | collective-permute-start | bytes 7864328 | tf_op jit(solution)/shard_map/ppermute | solution.py:494
  263.2 107.2 %collective-permute-start.17 = (f32[1024,640]{1,0:T(8,128)}, f32[1024,640]{1,0:T(8,128)S(1)}, u32[]{:S(2)}, u32[]{:S(2)}) collective-permute-start(f32[1024,640]{1,0:T(8,128)} %constant_dynamic-update-slice_fusion.2), channel_id=1, source_target_pairs={{0,32},{8,40},{16,48},{24,56},{32,64},{40,72},{48,80},{56,88},{64,... | collective-permute-start | bytes 7864328 | tf_op jit(solution)/shard_map/ppermute | solution.py:494
  285.1 87.2 %collective-permute-start.18 = (f32[1024,640]{1,0:T(8,128)}, f32[1024,640]{1,0:T(8,128)}, u32[]{:S(2)}, u32[]{:S(2)}) collective-permute-start(f32[1024,640]{1,0:T(8,128)} %constant_dynamic-update-slice_fusion), channel_id=1, source_target_pairs={{0,24},{8,0},{16,8},{24,16},{32,56},{40,32},{48,40},{56,48},{64,88... | collective-permute-start | bytes 7864328 | tf_op jit(solution)/shard_map/ppermute | solution.py:494
  285.8 84.5 %collective-permute-start.15 = (f32[512,640]{1,0:T(8,128)S(1)}, f32[512,640]{1,0:T(8,128)S(1)}, u32[]{:S(2)}, u32[]{:S(2)}) collective-permute-start(f32[512,640]{1,0:T(8,128)S(1)} %collective-permute-done.7.refs_3_), channel_id=1, source_target_pairs={{0,24},{8,0},{16,8},{24,16},{32,56},{40,32},{48,40},{56,48},{64,88... | collective-permute-start | bytes 3932168 | tf_op jit(solution)/shard_map/ppermute | solution.py:494
  286.9 85.8 %collective-permute-start.19 = (f32[1024,640]{1,0:T(8,128)}, f32[1024,640]{1,0:T(8,128)}, u32[]{:S(2)}, u32[]{:S(2)}) collective-permute-start(f32[1024,640]{1,0:T(8,128)} %constant_dynamic-update-slice_fusion.2), channel_id=1, source_target_pairs={{0,96},{8,104},{16,112},{24,120},{32,0},{40,8},{48,16},{56,24},{64... | collective-permute-start | bytes 7864328 | tf_op jit(solution)/shard_map/ppermute | solution.py:494
  299.1 103.8 %copy-start.4 = (f32[1024,640]{1,0:T(8,128)S(1)}, f32[1024,640]{1,0:T(8,128)}, u32[]{:S(2)}) copy-start(f32[1024,640]{1,0:T(8,128)} %get-tuple-element.108) | copy-start | bytes 7864324
  370.3 32.6 %collective-permute-start.24 = (f32[512,640]{1,0:T(8,128)S(1)}, f32[512,640]{1,0:T(8,128)S(1)}, u32[]{:S(2)}, u32[]{:S(2)}) collective-permute-start(f32[512,640]{1,0:T(8,128)S(1)} %collective-permute-done.12.refs_0_), channel_id=1, source_target_pairs={{0,24},{8,0},{16,8},{24,16},{32,56},{40,32},{48,40},{56,48},{64,88... | collective-permute-start | bytes 3932168 | tf_op jit(solution)/shard_map/ppermute | solution.py:494
  370.3 32.6 %collective-permute-start.25 = (f32[512,640]{1,0:T(8,128)S(1)}, f32[512,640]{1,0:T(8,128)S(1)}, u32[]{:S(2)}, u32[]{:S(2)}) collective-permute-start(f32[512,640]{1,0:T(8,128)S(1)} %collective-permute-done.13.refs_1_), channel_id=1, source_target_pairs={{0,96},{8,104},{16,112},{24,120},{32,0},{40,8},{48,16},{56,24},{64... | collective-permute-start | bytes 3932168 | tf_op jit(solution)/shard_map/ppermute | solution.py:494
  370.4 57.0 %collective-permute-start.26 = (f32[512,640]{1,0:T(8,128)S(1)}, f32[512,640]{1,0:T(8,128)}, u32[]{:S(2)}, u32[]{:S(2)}) collective-permute-start(f32[512,640]{1,0:T(8,128)S(1)} %collective-permute-done.14.refs_2_), channel_id=1, source_target_pairs={{0,24},{8,0},{16,8},{24,16},{32,56},{40,32},{48,40},{56,48},{64,88... | collective-permute-start | bytes 3932168 | tf_op jit(solution)/shard_map/ppermute | solution.py:494
  372.3 55.1 %collective-permute-start.27 = (f32[512,640]{1,0:T(8,128)S(1)}, f32[512,640]{1,0:T(8,128)}, u32[]{:S(2)}, u32[]{:S(2)}) collective-permute-start(f32[512,640]{1,0:T(8,128)S(1)} %collective-permute-done.15.refs_3_), channel_id=1, source_target_pairs={{0,96},{8,104},{16,112},{24,120},{32,0},{40,8},{48,16},{56,24},{64... | collective-permute-start | bytes 3932168 | tf_op jit(solution)/shard_map/ppermute | solution.py:494
  372.7 54.7 %collective-permute-start.30 = (f32[512,640]{1,0:T(8,128)S(1)}, f32[512,640]{1,0:T(8,128)}, u32[]{:S(2)}, u32[]{:S(2)}) collective-permute-start(f32[512,640]{1,0:T(8,128)S(1)} %collective-permute-done.12.refs_0_), channel_id=1, source_target_pairs={{0,8},{8,16},{16,24},{24,0},{32,40},{40,48},{48,56},{56,32},{64,72... | collective-permute-start | bytes 3932168 | tf_op jit(solution)/shard_map/ppermute | solution.py:494
  402.9 30.0 %collective-permute-start.31 = (f32[512,640]{1,0:T(8,128)S(1)}, f32[512,640]{1,0:T(8,128)}, u32[]{:S(2)}, u32[]{:S(2)}) collective-permute-start(f32[512,640]{1,0:T(8,128)S(1)} %collective-permute-done.13.refs_1_), channel_id=1, source_target_pairs={{0,32},{8,40},{16,48},{24,56},{32,64},{40,72},{48,80},{56,88},{64,... | collective-permute-start | bytes 3932168 | tf_op jit(solution)/shard_map/ppermute | solution.py:494
  402.9 84.1 %collective-permute-start.20 = (f32[1024,640]{1,0:T(8,128)S(1)}, f32[1024,640]{1,0:T(8,128)S(1)}, u32[]{:S(2)}, u32[]{:S(2)}) collective-permute-start(f32[1024,640]{1,0:T(8,128)S(1)} %copy-done.4), channel_id=1, source_target_pairs={{0,8},{8,16},{16,24},{24,0},{32,40},{40,48},{48,56},{56,32},{64,72... | collective-permute-start | bytes 7864328 | tf_op jit(solution)/shard_map/ppermute | solution.py:494
  427.4 64.4 %collective-permute-start.21 = (f32[1024,640]{1,0:T(8,128)S(1)}, f32[1024,640]{1,0:T(8,128)S(1)}, u32[]{:S(2)}, u32[]{:S(2)}) collective-permute-start(f32[1024,640]{1,0:T(8,128)S(1)} %get-tuple-element.109), channel_id=1, source_target_pairs={{0,32},{8,40},{16,48},{24,56},{32,64},{40,72},{48,80},{56,88},{64,... | collective-permute-start | bytes 7864328 | tf_op jit(solution)/shard_map/ppermute | solution.py:494
  427.4 66.4 %collective-permute-start.22 = (f32[1024,640]{1,0:T(8,128)S(1)}, f32[1024,640]{1,0:T(8,128)S(1)}, u32[]{:S(2)}, u32[]{:S(2)}) collective-permute-start(f32[1024,640]{1,0:T(8,128)S(1)} %copy-done.4), channel_id=1, source_target_pairs={{0,24},{8,0},{16,8},{24,16},{32,56},{40,32},{48,40},{56,48},{64,88... | collective-permute-start | bytes 7864328 | tf_op jit(solution)/shard_map/ppermute | solution.py:494
  427.4 68.4 %collective-permute-start.23 = (f32[1024,640]{1,0:T(8,128)S(1)}, f32[1024,640]{1,0:T(8,128)S(1)}, u32[]{:S(2)}, u32[]{:S(2)}) collective-permute-start(f32[1024,640]{1,0:T(8,128)S(1)} %get-tuple-element.109), channel_id=1, source_target_pairs={{0,96},{8,104},{16,112},{24,120},{32,0},{40,8},{48,16},{56,24},{64... | collective-permute-start | bytes 7864328 | tf_op jit(solution)/shard_map/ppermute | solution.py:494
  432.9 53.1 %collective-permute-start.32 = (f32[512,640]{1,0:T(8,128)S(1)}, f32[512,640]{1,0:T(8,128)S(1)}, u32[]{:S(2)}, u32[]{:S(2)}) collective-permute-start(f32[512,640]{1,0:T(8,128)S(1)} %collective-permute-done.14.refs_2_), channel_id=1, source_target_pairs={{0,8},{8,16},{16,24},{24,0},{32,40},{40,48},{48,56},{56,32},{64,72... | collective-permute-start | bytes 3932168 | tf_op jit(solution)/shard_map/ppermute | solution.py:494
  486.0 5.8 copy-start
  486.0 89.6 %collective-permute-start.28 = (f32[1024,640]{1,0:T(8,128)S(1)}, f32[1024,640]{1,0:T(8,128)S(1)}, u32[]{:S(2)}, u32[]{:S(2)}) collective-permute-start(f32[1024,640]{1,0:T(8,128)S(1)} %collective-permute-done.8.refs_0_), channel_id=1, source_target_pairs={{0,8},{8,16},{16,24},{24,0},{32,40},{40,48},{48,56},{56,32},{64,72... | collective-permute-start | bytes 7864328 | tf_op jit(solution)/shard_map/ppermute | solution.py:494
  487.1 89.7 %collective-permute-start.29 = (f32[1024,640]{1,0:T(8,128)S(1)}, f32[1024,640]{1,0:T(8,128)S(1)}, u32[]{:S(2)}, u32[]{:S(2)}) collective-permute-start(f32[1024,640]{1,0:T(8,128)S(1)} %collective-permute-done.9.refs_1_), channel_id=1, source_target_pairs={{0,32},{8,40},{16,48},{24,56},{32,64},{40,72},{48,80},{56,88},{64,... | collective-permute-start | bytes 7864328 | tf_op jit(solution)/shard_map/ppermute | solution.py:494
  491.8 99.2 %collective-permute-start.34 = (f32[1024,640]{1,0:T(8,128)}, f32[1024,640]{1,0:T(8,128)}, u32[]{:S(2)}, u32[]{:S(2)}) collective-permute-start(f32[1024,640]{1,0:T(8,128)} %collective-permute-done.18.refs_0_), channel_id=1, source_target_pairs={{0,24},{8,0},{16,8},{24,16},{32,56},{40,32},{48,40},{56,48},{64,88... | collective-permute-start | bytes 7864328 | tf_op jit(solution)/shard_map/ppermute | solution.py:494
  493.8 104.6 %collective-permute-start.35 = (f32[1024,640]{1,0:T(8,128)}, f32[1024,640]{1,0:T(8,128)}, u32[]{:S(2)}, u32[]{:S(2)}) collective-permute-start(f32[1024,640]{1,0:T(8,128)} %collective-permute-done.19.refs_1_), channel_id=1, source_target_pairs={{0,96},{8,104},{16,112},{24,120},{32,0},{40,8},{48,16},{56,24},{64... | collective-permute-start | bytes 7864328 | tf_op jit(solution)/shard_map/ppermute | solution.py:494
  495.8 73.7 %collective-permute-start.33 = (f32[512,640]{1,0:T(8,128)S(1)}, f32[512,640]{1,0:T(8,128)S(1)}, u32[]{:S(2)}, u32[]{:S(2)}) collective-permute-start(f32[512,640]{1,0:T(8,128)S(1)} %collective-permute-done.15.refs_3_), channel_id=1, source_target_pairs={{0,32},{8,40},{16,48},{24,56},{32,64},{40,72},{48,80},{56,88},{64,... | collective-permute-start | bytes 3932168 | tf_op jit(solution)/shard_map/ppermute | solution.py:494
  569.5 12.7 %copy-start.2 = (f32[512,640]{1,0:T(8,128)}, f32[512,640]{1,0:T(8,128)S(1)}, u32[]{:S(2)}) copy-start(f32[512,640]{1,0:T(8,128)S(1)} %collective-permute-done.33.refs_1_) | copy-start | bytes 3932164
  569.5 34.1 %collective-permute-start.36 = (f32[512,640]{1,0:T(8,128)}, f32[512,640]{1,0:T(8,128)}, u32[]{:S(2)}, u32[]{:S(2)}) collective-permute-start(f32[512,640]{1,0:T(8,128)} %slice.44), channel_id=1, source_target_pairs={{0,8},{8,16},{16,24},{24,0},{32,40},{40,48},{48,56},{56,32},{64,72... | collective-permute-start | bytes 3932168 | tf_op jit(solution)/shard_map/ppermute | solution.py:494
  575.6 32.8 %collective-permute-start.37 = (f32[512,640]{1,0:T(8,128)}, f32[512,640]{1,0:T(8,128)}, u32[]{:S(2)}, u32[]{:S(2)}) collective-permute-start(f32[512,640]{1,0:T(8,128)} %slice.45), channel_id=1, source_target_pairs={{0,32},{8,40},{16,48},{24,56},{32,64},{40,72},{48,80},{56,88},{64,... | collective-permute-start | bytes 3932168 | tf_op jit(solution)/shard_map/ppermute | solution.py:494
  576.8 31.6 %collective-permute-start.38 = (f32[512,640]{1,0:T(8,128)}, f32[512,640]{1,0:T(8,128)}, u32[]{:S(2)}, u32[]{:S(2)}) collective-permute-start(f32[512,640]{1,0:T(8,128)} %slice.46), channel_id=1, source_target_pairs={{0,24},{8,0},{16,8},{24,16},{32,56},{40,32},{48,40},{56,48},{64,88... | collective-permute-start | bytes 3932168 | tf_op jit(solution)/shard_map/ppermute | solution.py:494
  591.0 34.2 %collective-permute-start.39 = (f32[512,640]{1,0:T(8,128)}, f32[512,640]{1,0:T(8,128)}, u32[]{:S(2)}, u32[]{:S(2)}) collective-permute-start(f32[512,640]{1,0:T(8,128)} %slice.47), channel_id=1, source_target_pairs={{0,96},{8,104},{16,112},{24,120},{32,0},{40,8},{48,16},{56,24},{64... | collective-permute-start | bytes 3932168 | tf_op jit(solution)/shard_map/ppermute | solution.py:494
  598.4 31.4 %collective-permute-start.42 = (f32[512,640]{1,0:T(8,128)}, f32[512,640]{1,0:T(8,128)}, u32[]{:S(2)}, u32[]{:S(2)}) collective-permute-start(f32[512,640]{1,0:T(8,128)} %collective-permute-done.26.refs_2_), channel_id=1, source_target_pairs={{0,24},{8,0},{16,8},{24,16},{32,56},{40,32},{48,40},{56,48},{64,88... | collective-permute-start | bytes 3932168 | tf_op jit(solution)/shard_map/ppermute | solution.py:494
  603.6 26.2 %collective-permute-start.40 = (f32[512,640]{1,0:T(8,128)}, f32[512,640]{1,0:T(8,128)}, u32[]{:S(2)}, u32[]{:S(2)}) collective-permute-start(f32[512,640]{1,0:T(8,128)} %collective-permute-done.30.refs_0_), channel_id=1, source_target_pairs={{0,8},{8,16},{16,24},{24,0},{32,40},{40,48},{48,56},{56,32},{64,72... | collective-permute-start | bytes 3932168 | tf_op jit(solution)/shard_map/ppermute | solution.py:494
  608.3 21.5 %collective-permute-start.41 = (f32[512,640]{1,0:T(8,128)}, f32[512,640]{1,0:T(8,128)}, u32[]{:S(2)}, u32[]{:S(2)}) collective-permute-start(f32[512,640]{1,0:T(8,128)} %collective-permute-done.31.refs_1_), channel_id=1, source_target_pairs={{0,32},{8,40},{16,48},{24,56},{32,64},{40,72},{48,80},{56,88},{64,... | collective-permute-start | bytes 3932168 | tf_op jit(solution)/shard_map/ppermute | solution.py:494
  608.4 21.5 %collective-permute-start.43 = (f32[512,640]{1,0:T(8,128)}, f32[512,640]{1,0:T(8,128)}, u32[]{:S(2)}, u32[]{:S(2)}) collective-permute-start(f32[512,640]{1,0:T(8,128)} %collective-permute-done.27.refs_3_), channel_id=1, source_target_pairs={{0,96},{8,104},{16,112},{24,120},{32,0},{40,8},{48,16},{56,24},{64... | collective-permute-start | bytes 3932168 | tf_op jit(solution)/shard_map/ppermute | solution.py:494
  614.8 3.3 copy-start.3
  (1 other events, 2.8 us)

commit v5 on v4

--- a/solution.py
+++ b/solution.py
@@ -53,9 +53,6 @@
 
 def waves(j, level):
     return (None,) if (j, level) in MIDDLE and level < 2 else (0, 1)
-
-
-COPIES = tuple((j, level, w) for j, path in enumerate(PATHS) for level in range(len(path)) for w in waves(j, level))
 
 
 def grad_block(at, tea_ref, x_ref, tab_rows, coef_ref, z_buf, g_buf, out_ref, block):
@@ -90,7 +87,7 @@
 
     def kern(hid_hbm, gain_hbm, mask_hbm, tea_ref, tab_ref, got_late, blocks_ref, x_out, tab_out, coef_ref, all_ref, gh_ref, gg_ref,
              hid_ref, gain_ref, mask_in, w_ref, raw, sends, stage, got_soon, g_buf, t_acc, c_acc, tabs, n_buf, x_buf, inv_buf, square, pay, pay_got, mask_own, mask_got, x_got, tp_got, own_col,
-             own_row, rel, dx, rs_got, ag_own, ag_got, gn_own, gn_got, raw_sem, tab_sem, in_sem, hop_sem, dp_sem, tp_sem):
+             own_row, rel, dx, rs_got, ag_own, ag_got, gn_own, gn_got, raw_sem, tab_sem, in_sem, hop_out, hop_in, dp_sem, tp_sem):
         me, at = peers()
         col = lax.axis_index('tp')
         mates = [lax.rem(col + j, N_TP) for j in range(N_TP)]
@@ -98,7 +95,7 @@
 
         def fetch(k):
             d = at[ORDER[k]]
-            return pltpu.make_async_copy(tea_ref.at[:, aligned(d * part, part)], raw.at[pl.ds(k % ring * tokens, tokens)], raw_sem.at[k])
+            return pltpu.make_async_copy(tea_ref.at[:, aligned(d * part, part)], raw.at[pl.ds(k % ring * tokens, tokens)], raw_sem.at[k % ring])
 
         def tab_copy(i):
             slot = lax.rem(i, depth)
@@ -151,35 +148,20 @@
         def remote(src, dst, out, into, dp, tp):
             return pltpu.make_async_remote_copy(src_ref=src, dst_ref=dst, send_sem=out, recv_sem=into, device_id=(dp, tp), device_id_type=MESH)
 
+        def whole(ref, sem):
+            pltpu.make_async_copy(ref, ref, sem).wait()
+
         def to_dp(src, dst, x, rows=slice(None)):
-            def send(o):
-                d = at[o]
-                return remote(src.at[rows], dst.at[me, rows], dp_sem.at[x, 0, d], dp_sem.at[x, 1, me], d, col)
-
-            def into(o):
-                d = at[o]
-                return remote(src.at[rows], dst.at[d, rows], dp_sem.at[x, 0, d], dp_sem.at[x, 1, d], d, col)
-
-            return [send(o) for o in ORDER[:-1]], [into(o) for o in ORDER[:-1]]
+            for o in ORDER[:-1]:
+                remote(src.at[rows], dst.at[me, rows], dp_sem.at[x, 0], dp_sem.at[x, 1], at[o], col).start()
+            others = dst.at[pl.ds(0, N_DP - 1), rows]
+            return [(others, dp_sem.at[x, 0])], lambda: whole(others, dp_sem.at[x, 1])
 
         def to_tp(srcs, dst, x):
-            def send(j):
-                c = mates[j]
-                return remote(srcs(c), dst.at[col], tp_sem.at[x, 0, c], tp_sem.at[x, 1, col], me, c)
-
-            def into(j):
-                c = mates[j]
-                return remote(srcs(c), dst.at[c], tp_sem.at[x, 0, c], tp_sem.at[x, 1, c], me, c)
-
-            return [send(j) for j in range(1, N_TP)], [into(j) for j in range(1, N_TP)]
-
-        def start(copies):
-            for cp in copies:
-                cp.start()
-
-        def arrive(copies):
-            for cp in copies:
-                cp.wait_recv()
+            for c in mates[1:]:
+                remote(srcs(c), dst.at[col], tp_sem.at[x, 0], tp_sem.at[x, 1], me, c).start()
+            others = dst.at[pl.ds(0, N_TP - 1)]
+            return [(others, tp_sem.at[x, 0])], lambda: whole(others, tp_sem.at[x, 1])
 
         def added(ref, here=slice(None)):
             total = ref[0, here]
@@ -196,13 +178,13 @@
             rows = slice(None) if w is None else pl.ds(w * late, late)
             src = stage.at[MIDDLE.index((j, level - 1)), :, rows] if level else sends.at[aligned(at[dz, dy] * tokens + kind * half, half, half), rows]
             dst = stage.at[MIDDLE.index((j, level)), :, rows] if (j, level) in MIDDLE else gots[w].at[dz * SIDE + dy, tok]
-            k = COPIES.index((j, level, w))
-            return remote(src, dst, hop_sem.at[0, k], hop_sem.at[1, k], at[PATHS[j][level]], col)
+            into = (level if w is None else level + w) if (j, level) in MIDDLE else SIDE + w
+            return remote(src, dst, hop_out.at[min(level, 1)], hop_in.at[into], at[PATHS[j][level]], col)
 
         def came(level, w=None):
-            for j, at in MIDDLE:
-                if at == level:
-                    hop(j, level, w).wait_recv()
+            n = sum(at == level for _, at in MIDDLE)
+            rows = slice(None) if w is None else pl.ds(0, late)
+            whole(stage.at[pl.ds(0, n), :, rows], hop_in.at[level + (w or 0)])
 
         def onward(level, far, *ws):
             for w in ws:
@@ -233,11 +215,9 @@
         square[0:1, 0:tokens] = mask_in[...]
         mask_own[...] = square[0:few]
         mask_col = jnp.transpose(square[...])[0:tokens, 0:1]
-        pay_sends, pay_came = to_dp(pay, pay_got, 0)
-        start(pay_sends)
+        pay_sent, pay_came = to_dp(pay, pay_got, 0)
         pay_got[me] = pay[...]
-        mask_sends, mask_came = to_dp(mask_own, mask_got, 1, pl.ds(0, 1))
-        start(mask_sends)
+        mask_sent, mask_came = to_dp(mask_own, mask_got, 1, pl.ds(0, 1))
         mask_got[me] = mask_own[...]
         for k in range(few_first, N_DP):
             weigh(k)
@@ -284,29 +264,22 @@
         sums = jnp.where(lane == AWAY, SOFT_CAP * jnp.sum(c_acc[...] - k_sum, axis=1, keepdims=True), sums)
         own_col[...] = sums
         tp_got[col] = sums
-        tp_sends, tp_came = to_tp(lambda c: own_col, tp_got, 0)
-        start(tp_sends)
-        arrive(tp_came)
+        tp_sent, tp_came = to_tp(lambda c: own_col, tp_got, 0)
+        tp_came()
         total = added(tp_got)
         square[0:tokens] = jnp.where(lane == DOWN, mask_col, total)
         line = jnp.transpose(square[...])[0:few]
         own_row[...] = line
         all_ref[me] = line
-        dp_sends, dp_came = to_dp(own_row, all_ref, 2)
-        start(dp_sends)
+        dp_sent, dp_came = to_dp(own_row, all_ref, 2)
         twin = col + 1 - 2 * lax.rem(col, 2)
-        arrive((*pay_came, *mask_came))
+        pay_came()
+        mask_came()
         x_got[col] = pay_got[...]
 
-        def across(j, origin):
-            return remote(pay_got, x_got.at[origin], tp_sem.at[1, 0, mates[j]], tp_sem.at[1, 1, origin], me, mates[j])
-
-        def to_twin(j, origin):
-            return remote(x_got.at[origin], x_got.at[origin], tp_sem.at[1, 0, mates[j + 1]], tp_sem.at[1, 1, origin], me, twin)
-
         evens = range(0, N_TP, 2)
-        xt_sends = [across(j, col) for j in evens[1:]]
-        start(xt_sends)
+        for j in evens[1:]:
+            remote(pay_got, x_got.at[col], tp_sem.at[1, 0], tp_sem.at[1, 1], me, mates[j]).start()
         came(0)
         onward(1, True, None)
         onward(1, False, 0)
@@ -331,14 +304,13 @@
         came(1)
         onward(2, True, 0)
         onward(1, False, 1)
-        arrive([across(j, mates[j]) for j in evens[1:]])
-        twin_sends = [to_twin(j, mates[j]) for j in evens]
-        start(twin_sends)
+        whole(x_got.at[pl.ds(0, SIDE - 1)], tp_sem.at[1, 1])
+        for j in evens:
+            remote(x_got.at[mates[j]], x_got.at[mates[j]], tp_sem.at[SIDE, 0], tp_sem.at[SIDE, 1], me, twin).start()
 
         rs_got[col] = dx[my_few]
-        rs_sends, rs_came = to_tp(lambda c: dx.at[aligned(c * few, few, few)], rs_got, 2)
-        start(rs_sends)
-        arrive(rs_came)
+        rs_sent, rs_came = to_tp(lambda c: dx.at[aligned(c * few, few, few)], rs_got, 2)
+        rs_came()
         my_x = added(rs_got)
         my_n = n_buf[my_few]
         grad_n = my_x * w_ref[...]
@@ -347,20 +319,18 @@
         ag_own[0:few] = my_h
         ag_own[few:few + 1] = jnp.sum(my_x * my_n, axis=0, keepdims=True)
         ag_got[col] = ag_own[...]
-        ag_sends, ag_came = to_tp(lambda c: ag_own, ag_got, DOWN)
-        start(ag_sends)
-        arrive(ag_came)
+        ag_sent, ag_came = to_tp(lambda c: ag_own, ag_got, DOWN)
+        ag_came()
         gh_ref[...] = jnp.concatenate([ag_got[j, 0:few] for j in range(N_TP)], axis=0)
         line = added(ag_got, slice(few, few + 1))
         gn_own[0:1] = line
         gn_got[me, 0:1] = line
-        gn_sends, gn_came = to_dp(gn_own, gn_got, DOWN, pl.ds(0, 1))
-        start(gn_sends)
+        gn_sent, gn_came = to_dp(gn_own, gn_got, DOWN, pl.ds(0, 1))
 
         came(2, 0)
         onward(DOWN, True, 0)
         onward(2, True, 1)
-        arrive([to_twin(j, mates[j + 1]) for j in evens])
+        whole(x_got.at[pl.ds(0, SIDE)], tp_sem.at[SIDE, 1])
 
         def widen(d, _):
             rows = jnp.concatenate([x_got[j, d] for j in range(N_TP)], axis=0)
@@ -368,7 +338,7 @@
             return 0
 
         lax.fori_loop(0, N_DP, widen, 0)
-        arrive(dp_came)
+        dp_came()
         row = lax.broadcasted_iota(jnp.int32, (few, LANES), 0)
         lanes = lax.broadcasted_iota(jnp.int32, (few, LANES), 1)
         for d in range(N_DP):
@@ -380,11 +350,8 @@
         coef_ref[...] = jnp.transpose(square[...])
 
         own_tab.wait()
-        for j, path in enumerate(PATHS):
-            hop(j, len(path) - 1, 0).wait_recv()
-        for j, level, w in COPIES:
-            if level == 0:
-                hop(j, level, w).wait_send()
+        whole(got_soon.at[pl.ds(0, N_DP - 1)], hop_in.at[SIDE])
+        whole(sends.at[pl.ds(0, len(JOBS) * half)], hop_out.at[0])
 
         def block(b, _):
             @pl.when(b == 1)
@@ -396,15 +363,14 @@
             return 0
 
         lax.fori_loop(0, 2, block, 0)
-        arrive(gn_came)
+        gn_came()
         gg_ref[...] = added(gn_got, slice(1))
-        for j, path in enumerate(PATHS):
-            hop(j, len(path) - 1, 1).wait_recv()
-        for j, level, w in COPIES:
-            if level:
-                hop(j, level, w).wait_send()
-        for cp in (*pay_sends, *mask_sends, *tp_sends, *dp_sends, *xt_sends, *twin_sends, *rs_sends, *ag_sends, *gn_sends):
-            cp.wait_send()
+        whole(got_late.at[pl.ds(0, N_DP - 1)], hop_in.at[SIDE + 1])
+        whole(stage, hop_out.at[1])
+        for ref, sem in (*pay_sent, *mask_sent, *tp_sent, *dp_sent, *rs_sent, *ag_sent, *gn_sent):
+            whole(ref, sem)
+        whole(x_got.at[pl.ds(0, SIDE - 1)], tp_sem.at[1, 0])
+        whole(x_got.at[pl.ds(0, SIDE)], tp_sem.at[SIDE, 0])
 
     dma = pltpu.SemaphoreType.DMA
     wide, flat = (tokens, dim), (few, LANES)
@@ -421,7 +387,7 @@
             ((N_DP, few, dim), F32), (flat, F32), ((N_DP, *flat), F32), ((N_TP, N_DP, few, dim), F32), ((N_TP, tokens, LANES), F32),
             ((tokens, LANES), F32), (flat, F32), ((LANES, LANES), F32), (wide, F32), ((N_TP, few, dim), F32), ((2 * few, dim), F32),
             ((N_TP, 2 * few, dim), F32), ((few, dim), F32), ((N_DP, few, dim), F32))] + [
-            dma((N_DP,)), dma((depth,)), dma((5,)), dma((2, len(COPIES))), dma((SIDE, 2, N_DP)), dma((SIDE, 2, N_TP))],
+            dma((ring,)), dma((depth,)), dma((5,)), dma((2,)), dma((SIDE + 2,)), dma((SIDE, 2)), dma((SIDE + 1, 2))],
         compiler_params=pltpu.CompilerParams(collective_id=0, has_side_effects=True, vmem_limit_bytes=L_FRONT * MIB),
         cost_estimate=pl.CostEstimate(flops=3 * 10 ** 9, bytes_accessed=100 * MIB, transcendentals=0), name='front')(
             *(pltpu.with_memory_space_constraint(a, pltpu.HBM) for a in (hidden, gain_row, mask_row, teacher, table)))

time: 636 us -> 633 us (level)
  no operation moved by 1% of the time
where the time goes in v5:
time: 633 us; the launch traced here: 632 us
  waiting for transfers between devices  373 us (59%)
  Pallas kernels  182 us (29%)
  starting transfers between devices  59.7 us (9%)
  local copies, waits for them, and re-layouts  10.4 us (2%)
    ppermute x44, waiting for transfers between devices, send(): lax.ppermute(pair[k], 'dp', [(d, shift(d, dz, dy)) for d in range(N_DP)])  373 us
    pallas_call x1, Pallas kernels, front(): pl.pallas_call(kern, out_shape=tuple((jax.ShapeDtypeStruct(shape, kind) f...  105 us
    pallas_call x17, Pallas kernels, place(): pl.pallas_call(kern, out_shape=jax.ShapeDtypeStruct((vocab, dim), F32), i...  69.6 us
    ppermute x44, starting transfers between devices, send(): lax.ppermute(pair[k], 'dp', [(d, shift(d, dz, dy)) for d in range(N_DP)])  59.7 us
  transfers between devices with their start and end apart: 44, of which 13 were waited for; matrix products, arithmetic and copies ran while one was open for 2% of the time, Pallas kernels for 11%

profile of v5, /device:TPU:16, one launch (start us, length us, event | category | flops | bytes accessed | tf_op | source)
XLA Modules:
  0.0 632.2 jit_solution(4476395104947149358)
XLA Ops:
  0.6 105.0 %front.1 = (f32[16,64,1024]{2,1,0:T(8,128)S(1)}, f32[2,512,640]{2,1,0:T(8,128)S(1)}, bf16[1024,640]{1,0:T(8,128)(2,1)S(1)}, bf16[2048,640]{1,0:T(8,128)(2,1)S(1)...) custom-call(bf16[64,640]{1,0:T(8,128)(2,1)} %hid_hbm.1, ...), custom_call_target="tpu_custom_call" | custom-call | flops 3000000000 | bytes 104857600 | tf_op jit(solution)/shard_map/front/pallas_call | solution.py:377
  105.9 3.2 collective-permute-start.2
  109.3 1.9 collective-permute-start.3
  111.2 7.2 %finish.1 = f32[2,512,640]{2,1,0:T(8,128)S(1)} custom-call(f32[16,64,1024]{2,1,0:T(8,128)S(1)} %get-tuple-element.79.tea_ref, bf16[1024,640]{1,0:T(8,128)(2,1)S(1)} %get-tuple-element.80.x_ref, bf16[2048,640]{1,0:T(8,128)(2,1)S(1)} %get-tuple-element.81.tab_ref, f32[128,128]{1,0:T(8,128)S(1)} %get-tuple-element.82.coef_ref), custom_call_target="tpu_custom_call" | custom-call | flops 1000000000 | bytes 8388608 | tf_op jit(solution)/shard_map/finish/pallas_call | solution.py:410
  119.0 19.7 %collective-permute-done.refs_0_ = f32[512,640]{1,0:T(8,128)S(1)} collective-permute-done((f32[512,640]{1,0:T(8,128)S(1)}, f32[512,640]{1,0:T(8,128)S(1)}, u32[]{:S(2)}, u32[]{:S(2)}) %collective-permute-start) | collective-permute-done | bytes 1310752 | tf_op jit(solution)/shard_map/ppermute | solution.py:460
  140.8 3.2 collective-permute-start.6
  144.1 22.8 %collective-permute-done.4.refs_0_ = f32[512,640]{1,0:T(8,128)S(1)} collective-permute-done((f32[512,640]{1,0:T(8,128)S(1)}, f32[512,640]{1,0:T(8,128)S(1)}, u32[]{:S(2)}, u32[]{:S(2)}) %collective-permute-start.4) | collective-permute-done | bytes 1310752 | tf_op jit(solution)/shard_map/ppermute | solution.py:460
  167.6 2.8 collective-permute-done.5.refs_1_
  171.2 1.8 collective-permute-start.11
  173.0 4.1 place.17.refs_4_
  177.1 4.2 place.18.refs_4_
  181.3 67.4 %collective-permute-done.7.refs_3_ = f32[512,640]{1,0:T(8,128)S(1)} collective-permute-done((f32[512,640]{1,0:T(8,128)S(1)}, f32[512,640]{1,0:T(8,128)S(1)}, u32[]{:S(2)}, u32[]{:S(2)}) %collective-permute-start.7) | collective-permute-done | bytes 1310752 | tf_op jit(solution)/shard_map/ppermute | solution.py:460
  249.9 2.9 collective-permute-start.13
  252.8 3.2 collective-permute-start.14
  259.7 21.9 %collective-permute-done.12.refs_0_ = f32[512,640]{1,0:T(8,128)S(1)} collective-permute-done((f32[512,640]{1,0:T(8,128)S(1)}, f32[512,640]{1,0:T(8,128)S(1)}, u32[]{:S(2)}, u32[]{:S(2)}) %collective-permute-start.12) | collective-permute-done | bytes 1310752 | tf_op jit(solution)/shard_map/ppermute | solution.py:460
  283.4 2.1 collective-permute-start.19
  285.5 4.1 place.19.refs_2_
  289.7 1.8 pad_maximum_fusion.2
  291.5 4.1 place.20.refs_2_
  295.6 4.1 place.21.refs_4_
  299.8 67.1 %collective-permute-done.15.refs_3_ = f32[512,640]{1,0:T(8,128)S(1)} collective-permute-done((f32[512,640]{1,0:T(8,128)S(1)}, f32[512,640]{1,0:T(8,128)S(1)}, u32[]{:S(2)}, u32[]{:S(2)}) %collective-permute-start.15) | collective-permute-done | bytes 1310752 | tf_op jit(solution)/shard_map/ppermute | solution.py:460
  366.9 1.9 collective-permute-start.26
  370.1 29.3 %collective-permute-done.24.refs_0_ = f32[512,640]{1,0:T(8,128)S(1)} collective-permute-done((f32[512,640]{1,0:T(8,128)S(1)}, f32[512,640]{1,0:T(8,128)S(1)}, u32[]{:S(2)}, u32[]{:S(2)}) %collective-permute-start.24) | collective-permute-done | bytes 1310752 | tf_op jit(solution)/shard_map/ppermute | solution.py:460
  399.4 3.3 collective-permute-start.20
  402.7 21.1 %collective-permute-done.26.refs_2_ = f32[512,640]{1,0:T(8,128)} collective-permute-done((f32[512,640]{1,0:T(8,128)S(1)}, f32[512,640]{1,0:T(8,128)}, u32[]{:S(2)}, u32[]{:S(2)}) %collective-permute-start.26) | collective-permute-done | bytes 1310752 | tf_op jit(solution)/shard_map/ppermute | solution.py:460
  423.9 3.5 collective-permute-start.23
  429.0 3.8 collective-permute-start.32
  432.8 49.7 %collective-permute-done.32.refs_0_ = f32[512,640]{1,0:T(8,128)S(1)} collective-permute-done((f32[512,640]{1,0:T(8,128)S(1)}, f32[512,640]{1,0:T(8,128)S(1)}, u32[]{:S(2)}, u32[]{:S(2)}) %collective-permute-start.32) | collective-permute-done | bytes 1310752 | tf_op jit(solution)/shard_map/ppermute | solution.py:460
  483.8 4.1 place.22.refs_2_
  487.9 2.6 collective-permute-start.34
  493.2 4.1 place.23.refs_2_
  497.3 4.6 place.24.refs_2_
  504.3 61.7 %collective-permute-done.33.refs_1_ = f32[512,640]{1,0:T(8,128)S(1)} collective-permute-done((f32[512,640]{1,0:T(8,128)S(1)}, f32[512,640]{1,0:T(8,128)S(1)}, u32[]{:S(2)}, u32[]{:S(2)}) %collective-permute-start.33) | collective-permute-done | bytes 1310752 | tf_op jit(solution)/shard_map/ppermute | solution.py:460
  566.0 6.1 collective-permute-start.36
  574.5 4.1 place.25.refs_2_
  578.7 4.1 place.26.refs_4_
  582.8 4.7 place.27.refs_2_
  587.5 3.3 collective-permute-start.39
  590.8 4.1 place.28.refs_2_
  595.0 5.0 collective-permute-done.36.refs_0_
  600.1 2.5 collective-permute-start.40
  602.6 2.3 collective-permute-done.37.refs_1_
  604.9 3.2 collective-permute-start.43
  611.4 2.8 place.29.refs_2_
  614.7 2.4 place.30.refs_2_
  617.0 4.6 place.31.refs_4_
  621.7 4.6 place.32.refs_4_
  626.4 4.6 place.33
  (85 shorter events, 25.3 us)
Async XLA Ops:
  105.8 32.9 %collective-permute-start = (f32[512,640]{1,0:T(8,128)S(1)}, f32[512,640]{1,0:T(8,128)S(1)}, u32[]{:S(2)}, u32[]{:S(2)}) collective-permute-start(f32[512,640]{1,0:T(8,128)S(1)} %get-tuple-element.77.refs_0_), channel_id=1, source_target_pairs={{0,32},{8,40},{16,48},{24,56},{32,64},{40,72},{48,80},{56,88},{64,... | collective-permute-start | bytes 3932168 | tf_op jit(solution)/shard_map/ppermute | solution.py:460
  105.9 34.9 %collective-permute-start.2 = (f32[512,640]{1,0:T(8,128)S(1)}, f32[512,640]{1,0:T(8,128)S(1)}, u32[]{:S(2)}, u32[]{:S(2)}) collective-permute-start(f32[512,640]{1,0:T(8,128)S(1)} %get-tuple-element.77.refs_0_), channel_id=1, source_target_pairs={{0,96},{8,104},{16,112},{24,120},{32,0},{40,8},{48,16},{56,24},{64... | collective-permute-start | bytes 3932168 | tf_op jit(solution)/shard_map/ppermute | solution.py:460
  109.2 29.9 %collective-permute-start.1 = (f32[512,640]{1,0:T(8,128)S(1)}, f32[512,640]{1,0:T(8,128)S(1)}, u32[]{:S(2)}, u32[]{:S(2)}) collective-permute-start(f32[512,640]{1,0:T(8,128)S(1)} %get-tuple-element.78.refs_1_), channel_id=1, source_target_pairs={{0,8},{8,16},{16,24},{24,0},{32,40},{40,48},{48,56},{56,32},{64,72... | collective-permute-start | bytes 3932168 | tf_op jit(solution)/shard_map/ppermute | solution.py:460
  109.3 31.6 %collective-permute-start.3 = (f32[512,640]{1,0:T(8,128)S(1)}, f32[512,640]{1,0:T(8,128)S(1)}, u32[]{:S(2)}, u32[]{:S(2)}) collective-permute-start(f32[512,640]{1,0:T(8,128)S(1)} %get-tuple-element.78.refs_1_), channel_id=1, source_target_pairs={{0,24},{8,0},{16,8},{24,16},{32,56},{40,32},{48,40},{56,48},{64,88... | collective-permute-start | bytes 3932168 | tf_op jit(solution)/shard_map/ppermute | solution.py:460
  118.6 48.3 %collective-permute-start.4 = (f32[512,640]{1,0:T(8,128)S(1)}, f32[512,640]{1,0:T(8,128)S(1)}, u32[]{:S(2)}, u32[]{:S(2)}) collective-permute-start(f32[512,640]{1,0:T(8,128)S(1)} %get-tuple-element.143.refs_2_), channel_id=1, source_target_pairs={{0,32},{8,40},{16,48},{24,56},{32,64},{40,72},{48,80},{56,88},{64,... | collective-permute-start | bytes 3932168 | tf_op jit(solution)/shard_map/ppermute | solution.py:460
  138.8 31.7 %collective-permute-start.5 = (f32[512,640]{1,0:T(8,128)S(1)}, f32[512,640]{1,0:T(8,128)S(1)}, u32[]{:S(2)}, u32[]{:S(2)}) collective-permute-start(f32[512,640]{1,0:T(8,128)S(1)} %get-tuple-element.142.refs_3_), channel_id=1, source_target_pairs={{0,8},{8,16},{16,24},{24,0},{32,40},{40,48},{48,56},{56,32},{64,72... | collective-permute-start | bytes 3932168 | tf_op jit(solution)/shard_map/ppermute | solution.py:460
  139.1 110.8 %collective-permute-start.8 = (f32[1024,640]{1,0:T(8,128)S(1)}, f32[1024,640]{1,0:T(8,128)S(1)}, u32[]{:S(2)}, u32[]{:S(2)}) collective-permute-start(f32[1024,640]{1,0:T(8,128)S(1)} %pad_maximum_fusion), channel_id=1, source_target_pairs={{0,8},{8,16},{16,24},{24,0},{32,40},{40,48},{48,56},{56,32},{64,72... | collective-permute-start | bytes 7864328 | tf_op jit(solution)/shard_map/ppermute | solution.py:460
  140.8 112.0 %collective-permute-start.9 = (f32[1024,640]{1,0:T(8,128)S(1)}, f32[1024,640]{1,0:T(8,128)S(1)}, u32[]{:S(2)}, u32[]{:S(2)}) collective-permute-start(f32[1024,640]{1,0:T(8,128)S(1)} %pad_maximum_fusion.1), channel_id=1, source_target_pairs={{0,32},{8,40},{16,48},{24,56},{32,64},{40,72},{48,80},{56,88},{64,... | collective-permute-start | bytes 7864328 | tf_op jit(solution)/shard_map/ppermute | solution.py:460
  140.8 30.3 %collective-permute-start.6 = (f32[512,640]{1,0:T(8,128)S(1)}, f32[512,640]{1,0:T(8,128)S(1)}, u32[]{:S(2)}, u32[]{:S(2)}) collective-permute-start(f32[512,640]{1,0:T(8,128)S(1)} %get-tuple-element.143.refs_2_), channel_id=1, source_target_pairs={{0,96},{8,104},{16,112},{24,120},{32,0},{40,8},{48,16},{56,24},{64... | collective-permute-start | bytes 3932168 | tf_op jit(solution)/shard_map/ppermute | solution.py:460
  166.9 90.4 %collective-permute-start.10 = (f32[1024,640]{1,0:T(8,128)S(1)}, f32[1024,640]{1,0:T(8,128)S(1)}, u32[]{:S(2)}, u32[]{:S(2)}) collective-permute-start(f32[1024,640]{1,0:T(8,128)S(1)} %pad_maximum_fusion), channel_id=1, source_target_pairs={{0,24},{8,0},{16,8},{24,16},{32,56},{40,32},{48,40},{56,48},{64,88... | collective-permute-start | bytes 7864328 | tf_op jit(solution)/shard_map/ppermute | solution.py:460
  170.4 78.3 %collective-permute-start.7 = (f32[512,640]{1,0:T(8,128)S(1)}, f32[512,640]{1,0:T(8,128)S(1)}, u32[]{:S(2)}, u32[]{:S(2)}) collective-permute-start(f32[512,640]{1,0:T(8,128)S(1)} %get-tuple-element.142.refs_3_), channel_id=1, source_target_pairs={{0,24},{8,0},{16,8},{24,16},{32,56},{40,32},{48,40},{56,48},{64,88... | collective-permute-start | bytes 3932168 | tf_op jit(solution)/shard_map/ppermute | solution.py:460
  171.2 88.5 %collective-permute-start.11 = (f32[1024,640]{1,0:T(8,128)S(1)}, f32[1024,640]{1,0:T(8,128)S(1)}, u32[]{:S(2)}, u32[]{:S(2)}) collective-permute-start(f32[1024,640]{1,0:T(8,128)S(1)} %pad_maximum_fusion.1), channel_id=1, source_target_pairs={{0,96},{8,104},{16,112},{24,120},{32,0},{40,8},{48,16},{56,24},{64... | collective-permute-start | bytes 7864328 | tf_op jit(solution)/shard_map/ppermute | solution.py:460
  248.7 32.9 %collective-permute-start.12 = (f32[512,640]{1,0:T(8,128)S(1)}, f32[512,640]{1,0:T(8,128)S(1)}, u32[]{:S(2)}, u32[]{:S(2)}) collective-permute-start(f32[512,640]{1,0:T(8,128)S(1)} %collective-permute-done.refs_0_), channel_id=1, source_target_pairs={{0,32},{8,40},{16,48},{24,56},{32,64},{40,72},{48,80},{56,88},{64,... | collective-permute-start | bytes 3932168 | tf_op jit(solution)/shard_map/ppermute | solution.py:460
  249.9 32.4 %collective-permute-start.13 = (f32[512,640]{1,0:T(8,128)S(1)}, f32[512,640]{1,0:T(8,128)S(1)}, u32[]{:S(2)}, u32[]{:S(2)}) collective-permute-start(f32[512,640]{1,0:T(8,128)S(1)} %collective-permute-done.1.refs_1_), channel_id=1, source_target_pairs={{0,8},{8,16},{16,24},{24,0},{32,40},{40,48},{48,56},{56,32},{64,72... | collective-permute-start | bytes 3932168 | tf_op jit(solution)/shard_map/ppermute | solution.py:460
  252.8 30.6 %collective-permute-start.14 = (f32[512,640]{1,0:T(8,128)S(1)}, f32[512,640]{1,0:T(8,128)S(1)}, u32[]{:S(2)}, u32[]{:S(2)}) collective-permute-start(f32[512,640]{1,0:T(8,128)S(1)} %collective-permute-done.6.refs_2_), channel_id=1, source_target_pairs={{0,96},{8,104},{16,112},{24,120},{32,0},{40,8},{48,16},{56,24},{64... | collective-permute-start | bytes 3932168 | tf_op jit(solution)/shard_map/ppermute | solution.py:460
  257.2 109.6 %collective-permute-start.16 = (f32[1024,640]{1,0:T(8,128)}, f32[1024,640]{1,0:T(8,128)S(1)}, u32[]{:S(2)}, u32[]{:S(2)}) collective-permute-start(f32[1024,640]{1,0:T(8,128)} %constant_dynamic-update-slice_fusion), channel_id=1, source_target_pairs={{0,8},{8,16},{16,24},{24,0},{32,40},{40,48},{48,56},{56,32},{64,72... | collective-permute-start | bytes 7864328 | tf_op jit(solution)/shard_map/ppermute | solution.py:460
  259.7 107.2 %collective-permute-start.17 = (f32[1024,640]{1,0:T(8,128)}, f32[1024,640]{1,0:T(8,128)S(1)}, u32[]{:S(2)}, u32[]{:S(2)}) collective-permute-start(f32[1024,640]{1,0:T(8,128)} %constant_dynamic-update-slice_fusion.2), channel_id=1, source_target_pairs={{0,32},{8,40},{16,48},{24,56},{32,64},{40,72},{48,80},{56,88},{64,... | collective-permute-start | bytes 7864328 | tf_op jit(solution)/shard_map/ppermute | solution.py:460
  281.6 87.2 %collective-permute-start.18 = (f32[1024,640]{1,0:T(8,128)}, f32[1024,640]{1,0:T(8,128)}, u32[]{:S(2)}, u32[]{:S(2)}) collective-permute-start(f32[1024,640]{1,0:T(8,128)} %constant_dynamic-update-slice_fusion), channel_id=1, source_target_pairs={{0,24},{8,0},{16,8},{24,16},{32,56},{40,32},{48,40},{56,48},{64,88... | collective-permute-start | bytes 7864328 | tf_op jit(solution)/shard_map/ppermute | solution.py:460
  282.3 84.5 %collective-permute-start.15 = (f32[512,640]{1,0:T(8,128)S(1)}, f32[512,640]{1,0:T(8,128)S(1)}, u32[]{:S(2)}, u32[]{:S(2)}) collective-permute-start(f32[512,640]{1,0:T(8,128)S(1)} %collective-permute-done.7.refs_3_), channel_id=1, source_target_pairs={{0,24},{8,0},{16,8},{24,16},{32,56},{40,32},{48,40},{56,48},{64,88... | collective-permute-start | bytes 3932168 | tf_op jit(solution)/shard_map/ppermute | solution.py:460
  283.4 85.7 %collective-permute-start.19 = (f32[1024,640]{1,0:T(8,128)}, f32[1024,640]{1,0:T(8,128)}, u32[]{:S(2)}, u32[]{:S(2)}) collective-permute-start(f32[1024,640]{1,0:T(8,128)} %constant_dynamic-update-slice_fusion.2), channel_id=1, source_target_pairs={{0,96},{8,104},{16,112},{24,120},{32,0},{40,8},{48,16},{56,24},{64... | collective-permute-start | bytes 7864328 | tf_op jit(solution)/shard_map/ppermute | solution.py:460
  295.6 103.8 %copy-start.4 = (f32[1024,640]{1,0:T(8,128)S(1)}, f32[1024,640]{1,0:T(8,128)}, u32[]{:S(2)}) copy-start(f32[1024,640]{1,0:T(8,128)} %get-tuple-element.108) | copy-start | bytes 7864324
  366.8 32.6 %collective-permute-start.24 = (f32[512,640]{1,0:T(8,128)S(1)}, f32[512,640]{1,0:T(8,128)S(1)}, u32[]{:S(2)}, u32[]{:S(2)}) collective-permute-start(f32[512,640]{1,0:T(8,128)S(1)} %collective-permute-done.12.refs_0_), channel_id=1, source_target_pairs={{0,24},{8,0},{16,8},{24,16},{32,56},{40,32},{48,40},{56,48},{64,88... | collective-permute-start | bytes 3932168 | tf_op jit(solution)/shard_map/ppermute | solution.py:460
  366.9 32.6 %collective-permute-start.25 = (f32[512,640]{1,0:T(8,128)S(1)}, f32[512,640]{1,0:T(8,128)S(1)}, u32[]{:S(2)}, u32[]{:S(2)}) collective-permute-start(f32[512,640]{1,0:T(8,128)S(1)} %collective-permute-done.13.refs_1_), channel_id=1, source_target_pairs={{0,96},{8,104},{16,112},{24,120},{32,0},{40,8},{48,16},{56,24},{64... | collective-permute-start | bytes 3932168 | tf_op jit(solution)/shard_map/ppermute | solution.py:460
  366.9 57.0 %collective-permute-start.26 = (f32[512,640]{1,0:T(8,128)S(1)}, f32[512,640]{1,0:T(8,128)}, u32[]{:S(2)}, u32[]{:S(2)}) collective-permute-start(f32[512,640]{1,0:T(8,128)S(1)} %collective-permute-done.14.refs_2_), channel_id=1, source_target_pairs={{0,24},{8,0},{16,8},{24,16},{32,56},{40,32},{48,40},{56,48},{64,88... | collective-permute-start | bytes 3932168 | tf_op jit(solution)/shard_map/ppermute | solution.py:460
  368.8 55.1 %collective-permute-start.27 = (f32[512,640]{1,0:T(8,128)S(1)}, f32[512,640]{1,0:T(8,128)}, u32[]{:S(2)}, u32[]{:S(2)}) collective-permute-start(f32[512,640]{1,0:T(8,128)S(1)} %collective-permute-done.15.refs_3_), channel_id=1, source_target_pairs={{0,96},{8,104},{16,112},{24,120},{32,0},{40,8},{48,16},{56,24},{64... | collective-permute-start | bytes 3932168 | tf_op jit(solution)/shard_map/ppermute | solution.py:460
  369.1 54.8 %collective-permute-start.30 = (f32[512,640]{1,0:T(8,128)S(1)}, f32[512,640]{1,0:T(8,128)}, u32[]{:S(2)}, u32[]{:S(2)}) collective-permute-start(f32[512,640]{1,0:T(8,128)S(1)} %collective-permute-done.12.refs_0_), channel_id=1, source_target_pairs={{0,8},{8,16},{16,24},{24,0},{32,40},{40,48},{48,56},{56,32},{64,72... | collective-permute-start | bytes 3932168 | tf_op jit(solution)/shard_map/ppermute | solution.py:460
  399.4 29.6 %collective-permute-start.31 = (f32[512,640]{1,0:T(8,128)S(1)}, f32[512,640]{1,0:T(8,128)}, u32[]{:S(2)}, u32[]{:S(2)}) collective-permute-start(f32[512,640]{1,0:T(8,128)S(1)} %collective-permute-done.13.refs_1_), channel_id=1, source_target_pairs={{0,32},{8,40},{16,48},{24,56},{32,64},{40,72},{48,80},{56,88},{64,... | collective-permute-start | bytes 3932168 | tf_op jit(solution)/shard_map/ppermute | solution.py:460
  399.4 84.1 %collective-permute-start.20 = (f32[1024,640]{1,0:T(8,128)S(1)}, f32[1024,640]{1,0:T(8,128)S(1)}, u32[]{:S(2)}, u32[]{:S(2)}) collective-permute-start(f32[1024,640]{1,0:T(8,128)S(1)} %copy-done.4), channel_id=1, source_target_pairs={{0,8},{8,16},{16,24},{24,0},{32,40},{40,48},{48,56},{56,32},{64,72... | collective-permute-start | bytes 7864328 | tf_op jit(solution)/shard_map/ppermute | solution.py:460
  423.9 64.0 %collective-permute-start.21 = (f32[1024,640]{1,0:T(8,128)S(1)}, f32[1024,640]{1,0:T(8,128)S(1)}, u32[]{:S(2)}, u32[]{:S(2)}) collective-permute-start(f32[1024,640]{1,0:T(8,128)S(1)} %get-tuple-element.109), channel_id=1, source_target_pairs={{0,32},{8,40},{16,48},{24,56},{32,64},{40,72},{48,80},{56,88},{64,... | collective-permute-start | bytes 7864328 | tf_op jit(solution)/shard_map/ppermute | solution.py:460
  423.9 66.7 %collective-permute-start.22 = (f32[1024,640]{1,0:T(8,128)S(1)}, f32[1024,640]{1,0:T(8,128)S(1)}, u32[]{:S(2)}, u32[]{:S(2)}) collective-permute-start(f32[1024,640]{1,0:T(8,128)S(1)} %copy-done.4), channel_id=1, source_target_pairs={{0,24},{8,0},{16,8},{24,16},{32,56},{40,32},{48,40},{56,48},{64,88... | collective-permute-start | bytes 7864328 | tf_op jit(solution)/shard_map/ppermute | solution.py:460
  423.9 68.4 %collective-permute-start.23 = (f32[1024,640]{1,0:T(8,128)S(1)}, f32[1024,640]{1,0:T(8,128)S(1)}, u32[]{:S(2)}, u32[]{:S(2)}) collective-permute-start(f32[1024,640]{1,0:T(8,128)S(1)} %get-tuple-element.109), channel_id=1, source_target_pairs={{0,96},{8,104},{16,112},{24,120},{32,0},{40,8},{48,16},{56,24},{64... | collective-permute-start | bytes 7864328 | tf_op jit(solution)/shard_map/ppermute | solution.py:460
  429.0 53.4 %collective-permute-start.32 = (f32[512,640]{1,0:T(8,128)S(1)}, f32[512,640]{1,0:T(8,128)S(1)}, u32[]{:S(2)}, u32[]{:S(2)}) collective-permute-start(f32[512,640]{1,0:T(8,128)S(1)} %collective-permute-done.14.refs_2_), channel_id=1, source_target_pairs={{0,8},{8,16},{16,24},{24,0},{32,40},{40,48},{48,56},{56,32},{64,72... | collective-permute-start | bytes 3932168 | tf_op jit(solution)/shard_map/ppermute | solution.py:460
  482.5 5.4 copy-start
  482.5 89.6 %collective-permute-start.28 = (f32[1024,640]{1,0:T(8,128)S(1)}, f32[1024,640]{1,0:T(8,128)S(1)}, u32[]{:S(2)}, u32[]{:S(2)}) collective-permute-start(f32[1024,640]{1,0:T(8,128)S(1)} %collective-permute-done.8.refs_0_), channel_id=1, source_target_pairs={{0,8},{8,16},{16,24},{24,0},{32,40},{40,48},{48,56},{56,32},{64,72... | collective-permute-start | bytes 7864328 | tf_op jit(solution)/shard_map/ppermute | solution.py:460
  483.6 89.7 %collective-permute-start.29 = (f32[1024,640]{1,0:T(8,128)S(1)}, f32[1024,640]{1,0:T(8,128)S(1)}, u32[]{:S(2)}, u32[]{:S(2)}) collective-permute-start(f32[1024,640]{1,0:T(8,128)S(1)} %collective-permute-done.9.refs_1_), channel_id=1, source_target_pairs={{0,32},{8,40},{16,48},{24,56},{32,64},{40,72},{48,80},{56,88},{64,... | collective-permute-start | bytes 7864328 | tf_op jit(solution)/shard_map/ppermute | solution.py:460
  487.9 99.6 %collective-permute-start.34 = (f32[1024,640]{1,0:T(8,128)}, f32[1024,640]{1,0:T(8,128)}, u32[]{:S(2)}, u32[]{:S(2)}) collective-permute-start(f32[1024,640]{1,0:T(8,128)} %collective-permute-done.18.refs_0_), channel_id=1, source_target_pairs={{0,24},{8,0},{16,8},{24,16},{32,56},{40,32},{48,40},{56,48},{64,88... | collective-permute-start | bytes 7864328 | tf_op jit(solution)/shard_map/ppermute | solution.py:460
  490.5 104.4 %collective-permute-start.35 = (f32[1024,640]{1,0:T(8,128)}, f32[1024,640]{1,0:T(8,128)}, u32[]{:S(2)}, u32[]{:S(2)}) collective-permute-start(f32[1024,640]{1,0:T(8,128)} %collective-permute-done.19.refs_1_), channel_id=1, source_target_pairs={{0,96},{8,104},{16,112},{24,120},{32,0},{40,8},{48,16},{56,24},{64... | collective-permute-start | bytes 7864328 | tf_op jit(solution)/shard_map/ppermute | solution.py:460
  492.3 73.7 %collective-permute-start.33 = (f32[512,640]{1,0:T(8,128)S(1)}, f32[512,640]{1,0:T(8,128)S(1)}, u32[]{:S(2)}, u32[]{:S(2)}) collective-permute-start(f32[512,640]{1,0:T(8,128)S(1)} %collective-permute-done.15.refs_3_), channel_id=1, source_target_pairs={{0,32},{8,40},{16,48},{24,56},{32,64},{40,72},{48,80},{56,88},{64,... | collective-permute-start | bytes 3932168 | tf_op jit(solution)/shard_map/ppermute | solution.py:460
  566.0 12.7 %copy-start.2 = (f32[512,640]{1,0:T(8,128)}, f32[512,640]{1,0:T(8,128)S(1)}, u32[]{:S(2)}) copy-start(f32[512,640]{1,0:T(8,128)S(1)} %collective-permute-done.33.refs_1_) | copy-start | bytes 3932164
  566.0 34.1 %collective-permute-start.36 = (f32[512,640]{1,0:T(8,128)}, f32[512,640]{1,0:T(8,128)}, u32[]{:S(2)}, u32[]{:S(2)}) collective-permute-start(f32[512,640]{1,0:T(8,128)} %slice.44), channel_id=1, source_target_pairs={{0,8},{8,16},{16,24},{24,0},{32,40},{40,48},{48,56},{56,32},{64,72... | collective-permute-start | bytes 3932168 | tf_op jit(solution)/shard_map/ppermute | solution.py:460
  572.1 32.8 %collective-permute-start.37 = (f32[512,640]{1,0:T(8,128)}, f32[512,640]{1,0:T(8,128)}, u32[]{:S(2)}, u32[]{:S(2)}) collective-permute-start(f32[512,640]{1,0:T(8,128)} %slice.45), channel_id=1, source_target_pairs={{0,32},{8,40},{16,48},{24,56},{32,64},{40,72},{48,80},{56,88},{64,... | collective-permute-start | bytes 3932168 | tf_op jit(solution)/shard_map/ppermute | solution.py:460
  573.3 31.6 %collective-permute-start.38 = (f32[512,640]{1,0:T(8,128)}, f32[512,640]{1,0:T(8,128)}, u32[]{:S(2)}, u32[]{:S(2)}) collective-permute-start(f32[512,640]{1,0:T(8,128)} %slice.46), channel_id=1, source_target_pairs={{0,24},{8,0},{16,8},{24,16},{32,56},{40,32},{48,40},{56,48},{64,88... | collective-permute-start | bytes 3932168 | tf_op jit(solution)/shard_map/ppermute | solution.py:460
  587.5 34.2 %collective-permute-start.39 = (f32[512,640]{1,0:T(8,128)}, f32[512,640]{1,0:T(8,128)}, u32[]{:S(2)}, u32[]{:S(2)}) collective-permute-start(f32[512,640]{1,0:T(8,128)} %slice.47), channel_id=1, source_target_pairs={{0,96},{8,104},{16,112},{24,120},{32,0},{40,8},{48,16},{56,24},{64... | collective-permute-start | bytes 3932168 | tf_op jit(solution)/shard_map/ppermute | solution.py:460
  595.0 31.4 %collective-permute-start.42 = (f32[512,640]{1,0:T(8,128)}, f32[512,640]{1,0:T(8,128)}, u32[]{:S(2)}, u32[]{:S(2)}) collective-permute-start(f32[512,640]{1,0:T(8,128)} %collective-permute-done.26.refs_2_), channel_id=1, source_target_pairs={{0,24},{8,0},{16,8},{24,16},{32,56},{40,32},{48,40},{56,48},{64,88... | collective-permute-start | bytes 3932168 | tf_op jit(solution)/shard_map/ppermute | solution.py:460
  600.1 26.2 %collective-permute-start.40 = (f32[512,640]{1,0:T(8,128)}, f32[512,640]{1,0:T(8,128)}, u32[]{:S(2)}, u32[]{:S(2)}) collective-permute-start(f32[512,640]{1,0:T(8,128)} %collective-permute-done.30.refs_0_), channel_id=1, source_target_pairs={{0,8},{8,16},{16,24},{24,0},{32,40},{40,48},{48,56},{56,32},{64,72... | collective-permute-start | bytes 3932168 | tf_op jit(solution)/shard_map/ppermute | solution.py:460
  604.9 21.5 %collective-permute-start.41 = (f32[512,640]{1,0:T(8,128)}, f32[512,640]{1,0:T(8,128)}, u32[]{:S(2)}, u32[]{:S(2)}) collective-permute-start(f32[512,640]{1,0:T(8,128)} %collective-permute-done.31.refs_1_), channel_id=1, source_target_pairs={{0,32},{8,40},{16,48},{24,56},{32,64},{40,72},{48,80},{56,88},{64,... | collective-permute-start | bytes 3932168 | tf_op jit(solution)/shard_map/ppermute | solution.py:460
  604.9 21.5 %collective-permute-start.43 = (f32[512,640]{1,0:T(8,128)}, f32[512,640]{1,0:T(8,128)}, u32[]{:S(2)}, u32[]{:S(2)}) collective-permute-start(f32[512,640]{1,0:T(8,128)} %collective-permute-done.27.refs_3_), channel_id=1, source_target_pairs={{0,96},{8,104},{16,112},{24,120},{32,0},{40,8},{48,16},{56,24},{64... | collective-permute-start | bytes 3932168 | tf_op jit(solution)/shard_map/ppermute | solution.py:460
  611.4 3.3 copy-start.3
  (1 other events, 2.8 us)

commit v6 on v5

--- a/solution.py
+++ b/solution.py
@@ -215,8 +215,10 @@
         square[0:1, 0:tokens] = mask_in[...]
         mask_own[...] = square[0:few]
         mask_col = jnp.transpose(square[...])[0:tokens, 0:1]
-        pay_sent, pay_came = to_dp(pay, pay_got, 0)
-        pay_got[me] = pay[...]
+        my_z, my_y = lax.div(me, SIDE), lax.rem(me, SIDE)
+        for d in range(1, SIDE):
+            remote(pay, pay_got.at[my_z, my_y], dp_sem.at[0, 0], dp_sem.at[0, 1], at[d, 0], col).start()
+        pay_got[my_z, my_y] = pay[...]
         mask_sent, mask_came = to_dp(mask_own, mask_got, 1, pl.ds(0, 1))
         mask_got[me] = mask_own[...]
         for k in range(few_first, N_DP):
@@ -272,14 +274,11 @@
         own_row[...] = line
         all_ref[me] = line
         dp_sent, dp_came = to_dp(own_row, all_ref, 2)
-        twin = col + 1 - 2 * lax.rem(col, 2)
-        pay_came()
+        whole(pay_got.at[0, pl.ds(0, SIDE - 1)], dp_sem.at[0, 1])
+        line = pay_got.at[:, my_y]
+        for d in range(1, SIDE):
+            remote(line, line, dp_sem.at[SIDE, 0], dp_sem.at[SIDE, 1], at[0, d], col).start()
         mask_came()
-        x_got[col] = pay_got[...]
-
-        evens = range(0, N_TP, 2)
-        for j in evens[1:]:
-            remote(pay_got, x_got.at[col], tp_sem.at[1, 0], tp_sem.at[1, 1], me, mates[j]).start()
         came(0)
         onward(1, True, None)
         onward(1, False, 0)
@@ -300,13 +299,17 @@
             dx[...] = total
             return 0
 
-        lax.fori_loop(N_DP, 2 * N_DP, backward, 0)
+        lax.fori_loop(N_DP, N_DP + SIDE, backward, 0)
+        lines = pay_got.at[pl.ds(0, SIDE - 1)]
+        whole(lines, dp_sem.at[SIDE, 1])
+        twin = col + 1 - 2 * lax.rem(col, 2)
+        x_got[col] = pay_got[...]
+        for j in range(2, N_TP, 2):
+            remote(pay_got, x_got.at[col], tp_sem.at[1, 0], tp_sem.at[1, 1], me, mates[j]).start()
+        lax.fori_loop(N_DP + SIDE, 2 * N_DP, backward, 0)
         came(1)
         onward(2, True, 0)
         onward(1, False, 1)
-        whole(x_got.at[pl.ds(0, SIDE - 1)], tp_sem.at[1, 1])
-        for j in evens:
-            remote(x_got.at[mates[j]], x_got.at[mates[j]], tp_sem.at[SIDE, 0], tp_sem.at[SIDE, 1], me, twin).start()
 
         rs_got[col] = dx[my_few]
         rs_sent, rs_came = to_tp(lambda c: dx.at[aligned(c * few, few, few)], rs_got, 2)
@@ -330,10 +333,13 @@
         came(2, 0)
         onward(DOWN, True, 0)
         onward(2, True, 1)
+        whole(x_got.at[pl.ds(0, SIDE - 1)], tp_sem.at[1, 1])
+        for j in range(0, N_TP, 2):
+            remote(x_got.at[mates[j]], x_got.at[mates[j]], tp_sem.at[SIDE, 0], tp_sem.at[SIDE, 1], me, twin).start()
         whole(x_got.at[pl.ds(0, SIDE)], tp_sem.at[SIDE, 1])
 
         def widen(d, _):
-            rows = jnp.concatenate([x_got[j, d] for j in range(N_TP)], axis=0)
+            rows = jnp.concatenate([x_got[j, lax.div(d, SIDE), lax.rem(d, SIDE)] for j in range(N_TP)], axis=0)
             x_out[aligned(d * tokens, tokens, tokens)] = (rows * w_ref[...]).astype(BF16)
             return 0
 
@@ -367,8 +373,10 @@
         gg_ref[...] = added(gn_got, slice(1))
         whole(got_late.at[pl.ds(0, N_DP - 1)], hop_in.at[SIDE + 1])
         whole(stage, hop_out.at[1])
-        for ref, sem in (*pay_sent, *mask_sent, *tp_sent, *dp_sent, *rs_sent, *ag_sent, *gn_sent):
+        for ref, sem in (*mask_sent, *tp_sent, *dp_sent, *rs_sent, *ag_sent, *gn_sent):
             whole(ref, sem)
+        whole(pay_got.at[0, pl.ds(0, SIDE - 1)], dp_sem.at[0, 0])
+        whole(lines, dp_sem.at[SIDE, 0])
         whole(x_got.at[pl.ds(0, SIDE - 1)], tp_sem.at[1, 0])
         whole(x_got.at[pl.ds(0, SIDE)], tp_sem.at[SIDE, 0])
 
@@ -384,10 +392,10 @@
             (wide, BF16), ((dim // LANES, LANES), F32), ((1, tokens), F32), ((1, dim), F32), ((ring * tokens, part), BF16), ((N_DP * tokens, part), F32),
             ((len(MIDDLE), half, part), F32), ((N_DP, tokens, part // 2), F32), ((N_DP * tokens, sub), BF16), ((tokens, LANES), F32), ((tokens, LANES), F32),
             ((depth, sub, dim), BF16), (wide, F32), (wide, BF16), ((tokens, LANES), F32), ((LANES, LANES), F32), ((few, dim), F32),
-            ((N_DP, few, dim), F32), (flat, F32), ((N_DP, *flat), F32), ((N_TP, N_DP, few, dim), F32), ((N_TP, tokens, LANES), F32),
+            ((SIDE, SIDE, few, dim), F32), (flat, F32), ((N_DP, *flat), F32), ((N_TP, SIDE, SIDE, few, dim), F32), ((N_TP, tokens, LANES), F32),
             ((tokens, LANES), F32), (flat, F32), ((LANES, LANES), F32), (wide, F32), ((N_TP, few, dim), F32), ((2 * few, dim), F32),
             ((N_TP, 2 * few, dim), F32), ((few, dim), F32), ((N_DP, few, dim), F32))] + [
-            dma((ring,)), dma((depth,)), dma((5,)), dma((2,)), dma((SIDE + 2,)), dma((SIDE, 2)), dma((SIDE + 1, 2))],
+            dma((ring,)), dma((depth,)), dma((5,)), dma((2,)), dma((SIDE + 2,)), dma((SIDE + 1, 2)), dma((SIDE + 1, 2))],
         compiler_params=pltpu.CompilerParams(collective_id=0, has_side_effects=True, vmem_limit_bytes=L_FRONT * MIB),
         cost_estimate=pl.CostEstimate(flops=3 * 10 ** 9, bytes_accessed=100 * MIB, transcendentals=0), name='front')(
             *(pltpu.with_memory_space_constraint(a, pltpu.HBM) for a in (hidden, gain_row, mask_row, teacher, table)))
@@ -420,18 +428,24 @@
     rows = vocab // N_DP
     quarter = rows // SIDE
     cut = 256
-    chunks = [(i, r) for i in range(n) for r in range(0, arrays[i].shape[0], cut)]
+    chunks = []
+    for i, (array, dz, dy, kind, start) in enumerate(pieces):
+        r = 0
+        while r < array.shape[0]:
+            half, row = divmod(start + r, quarter)
+            size = min(cut, array.shape[0] - r, quarter - row)
+            chunks.append((i, r, size, dz, dy, (2 * half + kind) * quarter + row))
+            r += size
 
     def kern(*refs):
         dst, buf, sem = refs[-DOWN:]
         at = peers()[1]
         reads, writes = [], []
-        for k, (i, r) in enumerate(chunks):
-            _, dz, dy, kind, half = pieces[i]
-            first = (2 * (half + r // quarter) + kind) * quarter + r % quarter
-            there = aligned(at[dz, dy] * rows + first, cut, cut)
-            reads.append(pltpu.make_async_copy(refs[i].at[pl.ds(r, cut)], buf.at[k], sem.at[0, k]))
-            writes.append(pltpu.make_async_copy(buf.at[k], dst.at[there], sem.at[1, k]))
+        for k, (i, r, size, dz, dy, first) in enumerate(chunks):
+            held = buf.at[k, pl.ds(0, size)]
+            there = aligned(at[dz, dy] * rows + first, size, 16)
+            reads.append(pltpu.make_async_copy(refs[i].at[pl.ds(r, size)], held, sem.at[0, k]))
+            writes.append(pltpu.make_async_copy(held, dst.at[there], sem.at[1, k]))
         for cp in reads:
             cp.start()
         for read, write in zip(reads, writes):
@@ -460,8 +474,8 @@
             out.append(lax.ppermute(pair[k], 'dp', [(d, shift(d, dz, dy)) for d in range(N_DP)]))
         return out
 
-    def put(pair, a, b, c=0):
-        return [(pair[k], *((b, a) if k else (a, b)), k, c) for k in sets]
+    def put(pair, a, b, start=0):
+        return [(pair[k], *((b, a) if k else (a, b)), k, start) for k in sets]
 
     def settle(*pieces):
         nonlocal table
@@ -485,7 +499,7 @@
     high.append(send(own[1], 0, DOWN))
     whole = join(*own)
     side = {way: send(whole, 1, way) for way in ways}
-    settle(put(own[0], 0, 0, 0), put(own[1], 0, 0, 1))
+    settle(put(own[0], 0, 0, 0), put(own[1], 0, 0, quarter))
 
     low[0], high[0] = wait(low[0], high[0])
     far_low = send(low[0], 0, UP)
@@ -495,7 +509,7 @@
     far_high = send(high[1], 0, DOWN)
     low_whole, high_whole = join(*low), join(*high)
     low_side = {way: send(low_whole, 1, way) for way in ways}
-    settle(put(low[1], DOWN, 0, 1), put(high[1], UP, 0, 1))
+    settle(put(low[1], DOWN, 0, quarter), put(high[1], UP, 0, quarter))
 
     side[UP], side[DOWN], high_whole = wait(side[UP], side[DOWN], high_whole)
     high_side = {way: send(high_whole, 1, way) for way in ways}
@@ -505,7 +519,7 @@
 
     far_low, far_high = wait(far_low, far_high)
     far_side = {(c, way): send(pair, 1, way) for way in ways for c, pair in enumerate((far_low, far_high))}
-    settle(put(far_low, AWAY, 0, 0), put(far_high, AWAY, 0, 1))
+    settle(put(far_low, AWAY, 0, 0), put(far_high, AWAY, 0, quarter))
 
     low_side[UP], low_side[DOWN] = wait(low_side[UP], low_side[DOWN])
     low_far = send(low_side[DOWN], 1, DOWN)
@@ -513,13 +527,14 @@
     settle(put(low_side[DOWN], DOWN, UP))
 
     high_side[UP], high_side[DOWN] = wait(high_side[UP], high_side[DOWN])
-    high_far = [send([x[:quarter] for x in high_side[UP]], 1, UP), send([x[quarter:] for x in high_side[DOWN]], 1, DOWN)]
+    cut = quarter + 16
+    high_far = [send([x[:cut] for x in high_side[UP]], 1, UP), send([x[cut:] for x in high_side[DOWN]], 1, DOWN)]
     settle(put(high_side[UP], UP, DOWN))
     settle(put(high_side[DOWN], UP, UP))
 
     far_side[0, DOWN], far_side[1, DOWN], side_far = wait(far_side[0, DOWN], far_side[1, DOWN], side_far)
     last_down = send(far_side[1, DOWN], 1, DOWN)
-    settle(put(far_side[0, DOWN], AWAY, UP, 0), put(far_side[1, DOWN], AWAY, UP, 1))
+    settle(put(far_side[0, DOWN], AWAY, UP, 0), put(far_side[1, DOWN], AWAY, UP, quarter))
     settle(put(side_far, 0, AWAY))
 
     far_side[0, UP], = wait(far_side[0, UP])
@@ -527,13 +542,14 @@
     settle(put(far_side[0, UP], AWAY, DOWN, 0))
 
     far_side[1, UP], low_far = wait(far_side[1, UP], low_far)
-    settle(put(far_side[1, UP], AWAY, DOWN, 1))
+    settle(put(far_side[1, UP], AWAY, DOWN, quarter))
     settle(put(low_far, DOWN, AWAY))
 
     high_far = wait(*high_far)
-    settle(put(high_far[0], UP, AWAY, 0), put(high_far[1], UP, AWAY, 1))
-    last_up, last_down = wait(last_up, last_down)
-    settle(put(last_up, AWAY, AWAY, 0), put(last_down, AWAY, AWAY, 1))
+    settle(put(high_far[0], UP, AWAY, 0), put(high_far[1], UP, AWAY, cut))
+    for k in reversed(sets):
+        table, up, down = lax.optimization_barrier((table, last_up[k], last_down[k]))
+        table = place(table, [put([up] * 2, AWAY, AWAY)[k], put([down] * 2, AWAY, AWAY, quarter)[k]], vocab)
     return table
 
 

time: 633 us -> 638 us (level)
  waiting for transfers between devices: 373 us -> 387 us
  starting transfers between devices: 59.7 us -> 49.5 us
    ppermute x44, waiting for transfers between devices: 373 us -> 387 us  [send(): lax.ppermute(pair[k], 'dp', [(d, shift(d, dz, dy)) for d in range(N_DP)])]
    ppermute x44, starting transfers between devices: 59.7 us -> 49.5 us  [send(): lax.ppermute(pair[k], 'dp', [(d, shift(d, dz, dy)) for d in range(N_DP)])]
    pallas_call x17 -> x18, Pallas kernels: 69.6 us -> 69.4 us  [place(): pl.pallas_call(kern, out_shape=jax.ShapeDtypeStruct((vocab, dim), F32), i...]
  transfers between devices with their start and end apart: 44 -> 44, of which waited for: 13 -> 14; matrix products, arithmetic and copies ran while one was open for 2% -> 2% of each run, Pallas kernels for 11% -> 12%
where the time goes in v6:
time: 638 us; the launch traced here: 637 us
  waiting for transfers between devices  387 us (61%)
  Pallas kernels  184 us (29%)
  starting transfers between devices  49.5 us (8%)
  local copies, waits for them, and re-layouts  9.16 us (1%)
    ppermute x44, waiting for transfers between devices, send(): lax.ppermute(pair[k], 'dp', [(d, shift(d, dz, dy)) for d in range(N_DP)])  387 us
    pallas_call x1, Pallas kernels, front(): pl.pallas_call(kern, out_shape=tuple((jax.ShapeDtypeStruct(shape, kind) f...  108 us
    pallas_call x18, Pallas kernels, place(): pl.pallas_call(kern, out_shape=jax.ShapeDtypeStruct((vocab, dim), F32), i...  69.4 us
    ppermute x44, starting transfers between devices, send(): lax.ppermute(pair[k], 'dp', [(d, shift(d, dz, dy)) for d in range(N_DP)])  49.5 us
  transfers between devices with their start and end apart: 44, of which 14 were waited for; matrix products, arithmetic and copies ran while one was open for 2% of the time, Pallas kernels for 12%

profile of v6, /device:TPU:16, one launch (start us, length us, event | category | flops | bytes accessed | tf_op | source)
XLA Modules:
  0.0 637.4 jit_solution(4626549371513598615)
XLA Ops:
  0.6 107.7 %front.1 = (f32[16,64,1024]{2,1,0:T(8,128)S(1)}, f32[2,512,640]{2,1,0:T(8,128)S(1)}, bf16[1024,640]{1,0:T(8,128)(2,1)S(1)}, bf16[2048,640]{1,0:T(8,128)(2,1)S(1)...) custom-call(bf16[64,640]{1,0:T(8,128)(2,1)} %hid_hbm.1, ...), custom_call_target="tpu_custom_call" | custom-call | flops 3000000000 | bytes 104857600 | tf_op jit(solution)/shard_map/front/pallas_call | solution.py:385
  109.2 2.7 collective-permute-start.2
  111.9 2.3 collective-permute-start.1
  114.2 7.2 %finish.1 = f32[2,512,640]{2,1,0:T(8,128)S(1)} custom-call(f32[16,64,1024]{2,1,0:T(8,128)S(1)} %get-tuple-element.80.tea_ref, bf16[1024,640]{1,0:T(8,128)(2,1)S(1)} %get-tuple-element.81.x_ref, bf16[2048,640]{1,0:T(8,128)(2,1)S(1)} %get-tuple-element.82.tab_ref, f32[128,128]{1,0:T(8,128)S(1)} %get-tuple-element.83.coef_ref), custom_call_target="tpu_custom_call" | custom-call | flops 1000000000 | bytes 8388608 | tf_op jit(solution)/shard_map/finish/pallas_call | solution.py:418
  121.8 19.7 %collective-permute-done.refs_0_ = f32[512,640]{1,0:T(8,128)S(1)} collective-permute-done((f32[512,640]{1,0:T(8,128)S(1)}, f32[512,640]{1,0:T(8,128)S(1)}, u32[]{:S(2)}, u32[]{:S(2)}) %collective-permute-start) | collective-permute-done | bytes 1310752 | tf_op jit(solution)/shard_map/ppermute | solution.py:474
  141.5 2.2 collective-permute-start.5
  145.8 2.0 collective-permute-start.6
  147.7 21.8 %collective-permute-done.4.refs_0_ = f32[512,640]{1,0:T(8,128)S(1)} collective-permute-done((f32[512,640]{1,0:T(8,128)S(1)}, f32[512,640]{1,0:T(8,128)S(1)}, u32[]{:S(2)}, u32[]{:S(2)}) %collective-permute-start.4) | collective-permute-done | bytes 1310752 | tf_op jit(solution)/shard_map/ppermute | solution.py:474
  171.0 2.1 collective-permute-done.5.refs_1_
  174.6 2.1 collective-permute-start.11
  176.7 4.1 place.18.refs_4_
  180.8 4.2 place.19.refs_4_
  185.0 68.7 %collective-permute-done.7.refs_3_ = f32[512,640]{1,0:T(8,128)S(1)} collective-permute-done((f32[512,640]{1,0:T(8,128)S(1)}, f32[512,640]{1,0:T(8,128)S(1)}, u32[]{:S(2)}, u32[]{:S(2)}) %collective-permute-start.7) | collective-permute-done | bytes 1310752 | tf_op jit(solution)/shard_map/ppermute | solution.py:474
  254.9 2.2 collective-permute-start.13
  257.1 3.2 collective-permute-start.14
  263.9 22.6 %collective-permute-done.12.refs_0_ = f32[512,640]{1,0:T(8,128)S(1)} collective-permute-done((f32[512,640]{1,0:T(8,128)S(1)}, f32[512,640]{1,0:T(8,128)S(1)}, u32[]{:S(2)}, u32[]{:S(2)}) %collective-permute-start.12) | collective-permute-done | bytes 1310752 | tf_op jit(solution)/shard_map/ppermute | solution.py:474
  287.2 2.6 collective-permute-start.19
  290.4 4.1 place.20.refs_2_
  294.6 1.8 pad_maximum_fusion.2
  296.4 4.1 place.21.refs_2_
  300.5 4.1 place.22.refs_4_
  304.7 67.3 %collective-permute-done.15.refs_3_ = f32[512,640]{1,0:T(8,128)S(1)} collective-permute-done((f32[512,640]{1,0:T(8,128)S(1)}, f32[512,640]{1,0:T(8,128)S(1)}, u32[]{:S(2)}, u32[]{:S(2)}) %collective-permute-start.15) | collective-permute-done | bytes 1310752 | tf_op jit(solution)/shard_map/ppermute | solution.py:474
  372.8 1.7 collective-permute-start.30
  374.5 29.2 %collective-permute-done.24.refs_0_ = f32[512,640]{1,0:T(8,128)S(1)} collective-permute-done((f32[512,640]{1,0:T(8,128)S(1)}, f32[512,640]{1,0:T(8,128)S(1)}, u32[]{:S(2)}, u32[]{:S(2)}) %collective-permute-start.24) | collective-permute-done | bytes 1310752 | tf_op jit(solution)/shard_map/ppermute | solution.py:474
  403.7 3.0 collective-permute-start.20
  406.7 22.2 %collective-permute-done.26.refs_2_ = f32[512,640]{1,0:T(8,128)} collective-permute-done((f32[512,640]{1,0:T(8,128)S(1)}, f32[512,640]{1,0:T(8,128)}, u32[]{:S(2)}, u32[]{:S(2)}) %collective-permute-start.26) | collective-permute-done | bytes 1310752 | tf_op jit(solution)/shard_map/ppermute | solution.py:474
  429.0 1.7 collective-permute-start.32
  432.1 2.2 collective-permute-start.23
  434.2 52.6 %collective-permute-done.32.refs_0_ = f32[512,640]{1,0:T(8,128)S(1)} collective-permute-done((f32[512,640]{1,0:T(8,128)S(1)}, f32[512,640]{1,0:T(8,128)S(1)}, u32[]{:S(2)}, u32[]{:S(2)}) %collective-permute-start.32) | collective-permute-done | bytes 1310752 | tf_op jit(solution)/shard_map/ppermute | solution.py:474
  490.9 4.1 place.23.refs_2_
  495.0 2.6 collective-permute-start.34
  497.7 4.1 place.24.refs_2_
  501.8 4.6 place.25.refs_2_
  507.6 55.3 %collective-permute-done.33.refs_1_ = f32[512,640]{1,0:T(8,128)S(1)} collective-permute-done((f32[512,640]{1,0:T(8,128)S(1)}, f32[512,640]{1,0:T(8,128)S(1)}, u32[]{:S(2)}, u32[]{:S(2)}) %collective-permute-start.33) | collective-permute-done | bytes 1310752 | tf_op jit(solution)/shard_map/ppermute | solution.py:474
  562.9 3.0 collective-permute-start.36
  568.4 14.8 %collective-permute-done.38.refs_2_ = f32[496,640]{1,0:T(8,128)S(1)} collective-permute-done((f32[496,640]{1,0:T(8,128)S(1)}, f32[496,640]{1,0:T(8,128)S(1)}, u32[]{:S(2)}, u32[]{:S(2)}) %collective-permute-start.38) | collective-permute-done | bytes 1269792 | tf_op jit(solution)/shard_map/ppermute | solution.py:474
  583.3 4.1 place.26.refs_2_
  587.4 4.1 place.27.refs_4_
  591.5 4.7 place.28.refs_2_
  596.2 4.1 place.29.refs_2_
  600.5 3.3 collective-permute-start.41
  609.1 2.8 place.30.refs_2_
  612.4 2.4 place.31.refs_2_
  614.8 4.7 place.32.refs_4_
  619.5 3.6 place.33.refs_2_
  623.1 7.8 %collective-permute-done.40.refs_0_ = f32[512,640]{1,0:T(8,128)} collective-permute-done((f32[512,640]{1,0:T(8,128)}, f32[512,640]{1,0:T(8,128)}, u32[]{:S(2)}, u32[]{:S(2)}) %collective-permute-start.40) | collective-permute-done | bytes 1310752 | tf_op jit(solution)/shard_map/ppermute | solution.py:474
  630.9 2.6 place.34.refs_2_
  633.6 2.6 place.35
  (90 shorter events, 26.7 us)
Async XLA Ops:
  108.6 32.9 %collective-permute-start = (f32[512,640]{1,0:T(8,128)S(1)}, f32[512,640]{1,0:T(8,128)S(1)}, u32[]{:S(2)}, u32[]{:S(2)}) collective-permute-start(f32[512,640]{1,0:T(8,128)S(1)} %get-tuple-element.78.refs_0_), channel_id=1, source_target_pairs={{0,32},{8,40},{16,48},{24,56},{32,64},{40,72},{48,80},{56,88},{64,... | collective-permute-start | bytes 3932168 | tf_op jit(solution)/shard_map/ppermute | solution.py:474
  109.2 35.3 %collective-permute-start.2 = (f32[512,640]{1,0:T(8,128)S(1)}, f32[512,640]{1,0:T(8,128)S(1)}, u32[]{:S(2)}, u32[]{:S(2)}) collective-permute-start(f32[512,640]{1,0:T(8,128)S(1)} %get-tuple-element.78.refs_0_), channel_id=1, source_target_pairs={{0,96},{8,104},{16,112},{24,120},{32,0},{40,8},{48,16},{56,24},{64... | collective-permute-start | bytes 3932168 | tf_op jit(solution)/shard_map/ppermute | solution.py:474
  111.9 32.0 %collective-permute-start.1 = (f32[512,640]{1,0:T(8,128)S(1)}, f32[512,640]{1,0:T(8,128)S(1)}, u32[]{:S(2)}, u32[]{:S(2)}) collective-permute-start(f32[512,640]{1,0:T(8,128)S(1)} %get-tuple-element.79.refs_1_), channel_id=1, source_target_pairs={{0,8},{8,16},{16,24},{24,0},{32,40},{40,48},{48,56},{56,32},{64,72... | collective-permute-start | bytes 3932168 | tf_op jit(solution)/shard_map/ppermute | solution.py:474
  114.1 31.6 %collective-permute-start.3 = (f32[512,640]{1,0:T(8,128)S(1)}, f32[512,640]{1,0:T(8,128)S(1)}, u32[]{:S(2)}, u32[]{:S(2)}) collective-permute-start(f32[512,640]{1,0:T(8,128)S(1)} %get-tuple-element.79.refs_1_), channel_id=1, source_target_pairs={{0,24},{8,0},{16,8},{24,16},{32,56},{40,32},{48,40},{56,48},{64,88... | collective-permute-start | bytes 3932168 | tf_op jit(solution)/shard_map/ppermute | solution.py:474
  121.6 48.0 %collective-permute-start.4 = (f32[512,640]{1,0:T(8,128)S(1)}, f32[512,640]{1,0:T(8,128)S(1)}, u32[]{:S(2)}, u32[]{:S(2)}) collective-permute-start(f32[512,640]{1,0:T(8,128)S(1)} %get-tuple-element.145.refs_2_), channel_id=1, source_target_pairs={{0,32},{8,40},{16,48},{24,56},{32,64},{40,72},{48,80},{56,88},{64,... | collective-permute-start | bytes 3932168 | tf_op jit(solution)/shard_map/ppermute | solution.py:474
  141.5 31.7 %collective-permute-start.5 = (f32[512,640]{1,0:T(8,128)S(1)}, f32[512,640]{1,0:T(8,128)S(1)}, u32[]{:S(2)}, u32[]{:S(2)}) collective-permute-start(f32[512,640]{1,0:T(8,128)S(1)} %get-tuple-element.144.refs_3_), channel_id=1, source_target_pairs={{0,8},{8,16},{16,24},{24,0},{32,40},{40,48},{48,56},{56,32},{64,72... | collective-permute-start | bytes 3932168 | tf_op jit(solution)/shard_map/ppermute | solution.py:474
  143.9 111.0 %collective-permute-start.8 = (f32[1024,640]{1,0:T(8,128)S(1)}, f32[1024,640]{1,0:T(8,128)S(1)}, u32[]{:S(2)}, u32[]{:S(2)}) collective-permute-start(f32[1024,640]{1,0:T(8,128)S(1)} %pad_maximum_fusion), channel_id=1, source_target_pairs={{0,8},{8,16},{16,24},{24,0},{32,40},{40,48},{48,56},{56,32},{64,72... | collective-permute-start | bytes 7864328 | tf_op jit(solution)/shard_map/ppermute | solution.py:474
  144.5 112.6 %collective-permute-start.9 = (f32[1024,640]{1,0:T(8,128)S(1)}, f32[1024,640]{1,0:T(8,128)S(1)}, u32[]{:S(2)}, u32[]{:S(2)}) collective-permute-start(f32[1024,640]{1,0:T(8,128)S(1)} %pad_maximum_fusion.1), channel_id=1, source_target_pairs={{0,32},{8,40},{16,48},{24,56},{32,64},{40,72},{48,80},{56,88},{64,... | collective-permute-start | bytes 7864328 | tf_op jit(solution)/shard_map/ppermute | solution.py:474
  145.8 28.8 %collective-permute-start.6 = (f32[512,640]{1,0:T(8,128)S(1)}, f32[512,640]{1,0:T(8,128)S(1)}, u32[]{:S(2)}, u32[]{:S(2)}) collective-permute-start(f32[512,640]{1,0:T(8,128)S(1)} %get-tuple-element.145.refs_2_), channel_id=1, source_target_pairs={{0,96},{8,104},{16,112},{24,120},{32,0},{40,8},{48,16},{56,24},{64... | collective-permute-start | bytes 3932168 | tf_op jit(solution)/shard_map/ppermute | solution.py:474
  169.6 91.9 %collective-permute-start.10 = (f32[1024,640]{1,0:T(8,128)S(1)}, f32[1024,640]{1,0:T(8,128)S(1)}, u32[]{:S(2)}, u32[]{:S(2)}) collective-permute-start(f32[1024,640]{1,0:T(8,128)S(1)} %pad_maximum_fusion), channel_id=1, source_target_pairs={{0,24},{8,0},{16,8},{24,16},{32,56},{40,32},{48,40},{56,48},{64,88... | collective-permute-start | bytes 7864328 | tf_op jit(solution)/shard_map/ppermute | solution.py:474
  173.1 80.6 %collective-permute-start.7 = (f32[512,640]{1,0:T(8,128)S(1)}, f32[512,640]{1,0:T(8,128)S(1)}, u32[]{:S(2)}, u32[]{:S(2)}) collective-permute-start(f32[512,640]{1,0:T(8,128)S(1)} %get-tuple-element.144.refs_3_), channel_id=1, source_target_pairs={{0,24},{8,0},{16,8},{24,16},{32,56},{40,32},{48,40},{56,48},{64,88... | collective-permute-start | bytes 3932168 | tf_op jit(solution)/shard_map/ppermute | solution.py:474
  174.6 89.3 %collective-permute-start.11 = (f32[1024,640]{1,0:T(8,128)S(1)}, f32[1024,640]{1,0:T(8,128)S(1)}, u32[]{:S(2)}, u32[]{:S(2)}) collective-permute-start(f32[1024,640]{1,0:T(8,128)S(1)} %pad_maximum_fusion.1), channel_id=1, source_target_pairs={{0,96},{8,104},{16,112},{24,120},{32,0},{40,8},{48,16},{56,24},{64... | collective-permute-start | bytes 7864328 | tf_op jit(solution)/shard_map/ppermute | solution.py:474
  253.7 32.9 %collective-permute-start.12 = (f32[512,640]{1,0:T(8,128)S(1)}, f32[512,640]{1,0:T(8,128)S(1)}, u32[]{:S(2)}, u32[]{:S(2)}) collective-permute-start(f32[512,640]{1,0:T(8,128)S(1)} %collective-permute-done.refs_0_), channel_id=1, source_target_pairs={{0,32},{8,40},{16,48},{24,56},{32,64},{40,72},{48,80},{56,88},{64,... | collective-permute-start | bytes 3932168 | tf_op jit(solution)/shard_map/ppermute | solution.py:474
  254.9 32.3 %collective-permute-start.13 = (f32[512,640]{1,0:T(8,128)S(1)}, f32[512,640]{1,0:T(8,128)S(1)}, u32[]{:S(2)}, u32[]{:S(2)}) collective-permute-start(f32[512,640]{1,0:T(8,128)S(1)} %collective-permute-done.1.refs_1_), channel_id=1, source_target_pairs={{0,8},{8,16},{16,24},{24,0},{32,40},{40,48},{48,56},{56,32},{64,72... | collective-permute-start | bytes 3932168 | tf_op jit(solution)/shard_map/ppermute | solution.py:474
  257.1 32.7 %collective-permute-start.14 = (f32[512,640]{1,0:T(8,128)S(1)}, f32[512,640]{1,0:T(8,128)S(1)}, u32[]{:S(2)}, u32[]{:S(2)}) collective-permute-start(f32[512,640]{1,0:T(8,128)S(1)} %collective-permute-done.6.refs_2_), channel_id=1, source_target_pairs={{0,96},{8,104},{16,112},{24,120},{32,0},{40,8},{48,16},{56,24},{64... | collective-permute-start | bytes 3932168 | tf_op jit(solution)/shard_map/ppermute | solution.py:474
  261.5 110.9 %collective-permute-start.16 = (f32[1024,640]{1,0:T(8,128)}, f32[1024,640]{1,0:T(8,128)S(1)}, u32[]{:S(2)}, u32[]{:S(2)}) collective-permute-start(f32[1024,640]{1,0:T(8,128)} %constant_dynamic-update-slice_fusion), channel_id=1, source_target_pairs={{0,8},{8,16},{16,24},{24,0},{32,40},{40,48},{48,56},{56,32},{64,72... | collective-permute-start | bytes 7864328 | tf_op jit(solution)/shard_map/ppermute | solution.py:474
  263.9 108.4 %collective-permute-start.17 = (f32[1024,640]{1,0:T(8,128)}, f32[1024,640]{1,0:T(8,128)S(1)}, u32[]{:S(2)}, u32[]{:S(2)}) collective-permute-start(f32[1024,640]{1,0:T(8,128)} %constant_dynamic-update-slice_fusion.2), channel_id=1, source_target_pairs={{0,32},{8,40},{16,48},{24,56},{32,64},{40,72},{48,80},{56,88},{64,... | collective-permute-start | bytes 7864328 | tf_op jit(solution)/shard_map/ppermute | solution.py:474
  286.5 86.3 %collective-permute-start.18 = (f32[1024,640]{1,0:T(8,128)}, f32[1024,640]{1,0:T(8,128)}, u32[]{:S(2)}, u32[]{:S(2)}) collective-permute-start(f32[1024,640]{1,0:T(8,128)} %constant_dynamic-update-slice_fusion), channel_id=1, source_target_pairs={{0,24},{8,0},{16,8},{24,16},{32,56},{40,32},{48,40},{56,48},{64,88... | collective-permute-start | bytes 7864328 | tf_op jit(solution)/shard_map/ppermute | solution.py:474
  287.2 85.6 %collective-permute-start.19 = (f32[1024,640]{1,0:T(8,128)}, f32[1024,640]{1,0:T(8,128)}, u32[]{:S(2)}, u32[]{:S(2)}) collective-permute-start(f32[1024,640]{1,0:T(8,128)} %constant_dynamic-update-slice_fusion.2), channel_id=1, source_target_pairs={{0,96},{8,104},{16,112},{24,120},{32,0},{40,8},{48,16},{56,24},{64... | collective-permute-start | bytes 7864328 | tf_op jit(solution)/shard_map/ppermute | solution.py:474
  289.8 82.2 %collective-permute-start.15 = (f32[512,640]{1,0:T(8,128)S(1)}, f32[512,640]{1,0:T(8,128)S(1)}, u32[]{:S(2)}, u32[]{:S(2)}) collective-permute-start(f32[512,640]{1,0:T(8,128)S(1)} %collective-permute-done.7.refs_3_), channel_id=1, source_target_pairs={{0,24},{8,0},{16,8},{24,16},{32,56},{40,32},{48,40},{56,48},{64,88... | collective-permute-start | bytes 3932168 | tf_op jit(solution)/shard_map/ppermute | solution.py:474
  300.5 103.2 %copy-start.6 = (f32[1024,640]{1,0:T(8,128)S(1)}, f32[1024,640]{1,0:T(8,128)}, u32[]{:S(2)}) copy-start(f32[1024,640]{1,0:T(8,128)} %get-tuple-element.109) | copy-start | bytes 7864324
  372.0 31.6 %collective-permute-start.24 = (f32[512,640]{1,0:T(8,128)S(1)}, f32[512,640]{1,0:T(8,128)S(1)}, u32[]{:S(2)}, u32[]{:S(2)}) collective-permute-start(f32[512,640]{1,0:T(8,128)S(1)} %collective-permute-done.12.refs_0_), channel_id=1, source_target_pairs={{0,24},{8,0},{16,8},{24,16},{32,56},{40,32},{48,40},{56,48},{64,88... | collective-permute-start | bytes 3932168 | tf_op jit(solution)/shard_map/ppermute | solution.py:474
  372.3 31.4 %collective-permute-start.25 = (f32[512,640]{1,0:T(8,128)S(1)}, f32[512,640]{1,0:T(8,128)S(1)}, u32[]{:S(2)}, u32[]{:S(2)}) collective-permute-start(f32[512,640]{1,0:T(8,128)S(1)} %collective-permute-done.13.refs_1_), channel_id=1, source_target_pairs={{0,96},{8,104},{16,112},{24,120},{32,0},{40,8},{48,16},{56,24},{64... | collective-permute-start | bytes 3932168 | tf_op jit(solution)/shard_map/ppermute | solution.py:474
  372.3 56.6 %collective-permute-start.26 = (f32[512,640]{1,0:T(8,128)S(1)}, f32[512,640]{1,0:T(8,128)}, u32[]{:S(2)}, u32[]{:S(2)}) collective-permute-start(f32[512,640]{1,0:T(8,128)S(1)} %collective-permute-done.14.refs_2_), channel_id=1, source_target_pairs={{0,24},{8,0},{16,8},{24,16},{32,56},{40,32},{48,40},{56,48},{64,88... | collective-permute-start | bytes 3932168 | tf_op jit(solution)/shard_map/ppermute | solution.py:474
  372.8 56.1 %collective-permute-start.27 = (f32[512,640]{1,0:T(8,128)S(1)}, f32[512,640]{1,0:T(8,128)}, u32[]{:S(2)}, u32[]{:S(2)}) collective-permute-start(f32[512,640]{1,0:T(8,128)S(1)} %collective-permute-done.15.refs_3_), channel_id=1, source_target_pairs={{0,96},{8,104},{16,112},{24,120},{32,0},{40,8},{48,16},{56,24},{64... | collective-permute-start | bytes 3932168 | tf_op jit(solution)/shard_map/ppermute | solution.py:474
  372.8 57.9 %collective-permute-start.30 = (f32[512,640]{1,0:T(8,128)S(1)}, f32[512,640]{1,0:T(8,128)}, u32[]{:S(2)}, u32[]{:S(2)}) collective-permute-start(f32[512,640]{1,0:T(8,128)S(1)} %collective-permute-done.12.refs_0_), channel_id=1, source_target_pairs={{0,8},{8,16},{16,24},{24,0},{32,40},{40,48},{48,56},{56,32},{64,72... | collective-permute-start | bytes 3932168 | tf_op jit(solution)/shard_map/ppermute | solution.py:474
  403.7 28.4 %collective-permute-start.31 = (f32[512,640]{1,0:T(8,128)S(1)}, f32[512,640]{1,0:T(8,128)}, u32[]{:S(2)}, u32[]{:S(2)}) collective-permute-start(f32[512,640]{1,0:T(8,128)S(1)} %collective-permute-done.13.refs_1_), channel_id=1, source_target_pairs={{0,32},{8,40},{16,48},{24,56},{32,64},{40,72},{48,80},{56,88},{64,... | collective-permute-start | bytes 3932168 | tf_op jit(solution)/shard_map/ppermute | solution.py:474
  403.7 84.8 %collective-permute-start.20 = (f32[1024,640]{1,0:T(8,128)S(1)}, f32[1024,640]{1,0:T(8,128)S(1)}, u32[]{:S(2)}, u32[]{:S(2)}) collective-permute-start(f32[1024,640]{1,0:T(8,128)S(1)} %copy-done.6), channel_id=1, source_target_pairs={{0,8},{8,16},{16,24},{24,0},{32,40},{40,48},{48,56},{56,32},{64,72... | collective-permute-start | bytes 7864328 | tf_op jit(solution)/shard_map/ppermute | solution.py:474
  429.0 61.0 %collective-permute-start.21 = (f32[1024,640]{1,0:T(8,128)S(1)}, f32[1024,640]{1,0:T(8,128)S(1)}, u32[]{:S(2)}, u32[]{:S(2)}) collective-permute-start(f32[1024,640]{1,0:T(8,128)S(1)} %get-tuple-element.110), channel_id=1, source_target_pairs={{0,32},{8,40},{16,48},{24,56},{32,64},{40,72},{48,80},{56,88},{64,... | collective-permute-start | bytes 7864328 | tf_op jit(solution)/shard_map/ppermute | solution.py:474
  429.0 57.9 %collective-permute-start.32 = (f32[512,640]{1,0:T(8,128)S(1)}, f32[512,640]{1,0:T(8,128)S(1)}, u32[]{:S(2)}, u32[]{:S(2)}) collective-permute-start(f32[512,640]{1,0:T(8,128)S(1)} %collective-permute-done.14.refs_2_), channel_id=1, source_target_pairs={{0,8},{8,16},{16,24},{24,0},{32,40},{40,48},{48,56},{56,32},{64,72... | collective-permute-start | bytes 3932168 | tf_op jit(solution)/shard_map/ppermute | solution.py:474
  430.7 64.3 %collective-permute-start.22 = (f32[1024,640]{1,0:T(8,128)S(1)}, f32[1024,640]{1,0:T(8,128)S(1)}, u32[]{:S(2)}, u32[]{:S(2)}) collective-permute-start(f32[1024,640]{1,0:T(8,128)S(1)} %copy-done.6), channel_id=1, source_target_pairs={{0,24},{8,0},{16,8},{24,16},{32,56},{40,32},{48,40},{56,48},{64,88... | collective-permute-start | bytes 7864328 | tf_op jit(solution)/shard_map/ppermute | solution.py:474
  432.1 65.6 %collective-permute-start.23 = (f32[1024,640]{1,0:T(8,128)S(1)}, f32[1024,640]{1,0:T(8,128)S(1)}, u32[]{:S(2)}, u32[]{:S(2)}) collective-permute-start(f32[1024,640]{1,0:T(8,128)S(1)} %get-tuple-element.110), channel_id=1, source_target_pairs={{0,96},{8,104},{16,112},{24,120},{32,0},{40,8},{48,16},{56,24},{64... | collective-permute-start | bytes 7864328 | tf_op jit(solution)/shard_map/ppermute | solution.py:474
  486.9 8.1 %copy-start = (f32[512,640]{1,0:T(8,128)}, f32[512,640]{1,0:T(8,128)S(1)}, u32[]{:S(2)}) copy-start(f32[512,640]{1,0:T(8,128)S(1)} %collective-permute-done.32.refs_0_) | copy-start | bytes 3932164
  486.9 79.1 %collective-permute-start.28 = (f32[1024,640]{1,0:T(8,128)S(1)}, f32[1024,640]{1,0:T(8,128)S(1)}, u32[]{:S(2)}, u32[]{:S(2)}) collective-permute-start(f32[1024,640]{1,0:T(8,128)S(1)} %collective-permute-done.8.refs_0_), channel_id=1, source_target_pairs={{0,8},{8,16},{16,24},{24,0},{32,40},{40,48},{48,56},{56,32},{64,72... | collective-permute-start | bytes 7864328 | tf_op jit(solution)/shard_map/ppermute | solution.py:474
  488.4 78.8 %collective-permute-start.29 = (f32[1024,640]{1,0:T(8,128)S(1)}, f32[1024,640]{1,0:T(8,128)S(1)}, u32[]{:S(2)}, u32[]{:S(2)}) collective-permute-start(f32[1024,640]{1,0:T(8,128)S(1)} %collective-permute-done.9.refs_1_), channel_id=1, source_target_pairs={{0,32},{8,40},{16,48},{24,56},{32,64},{40,72},{48,80},{56,88},{64,... | collective-permute-start | bytes 7864328 | tf_op jit(solution)/shard_map/ppermute | solution.py:474
  489.9 73.0 %collective-permute-start.33 = (f32[512,640]{1,0:T(8,128)S(1)}, f32[512,640]{1,0:T(8,128)S(1)}, u32[]{:S(2)}, u32[]{:S(2)}) collective-permute-start(f32[512,640]{1,0:T(8,128)S(1)} %collective-permute-done.15.refs_3_), channel_id=1, source_target_pairs={{0,32},{8,40},{16,48},{24,56},{32,64},{40,72},{48,80},{56,88},{64,... | collective-permute-start | bytes 3932168 | tf_op jit(solution)/shard_map/ppermute | solution.py:474
  495.0 105.5 %collective-permute-start.34 = (f32[1024,640]{1,0:T(8,128)}, f32[1024,640]{1,0:T(8,128)}, u32[]{:S(2)}, u32[]{:S(2)}) collective-permute-start(f32[1024,640]{1,0:T(8,128)} %collective-permute-done.18.refs_0_), channel_id=1, source_target_pairs={{0,24},{8,0},{16,8},{24,16},{32,56},{40,32},{48,40},{56,48},{64,88... | collective-permute-start | bytes 7864328 | tf_op jit(solution)/shard_map/ppermute | solution.py:474
  497.7 106.1 %collective-permute-start.35 = (f32[1024,640]{1,0:T(8,128)}, f32[1024,640]{1,0:T(8,128)}, u32[]{:S(2)}, u32[]{:S(2)}) collective-permute-start(f32[1024,640]{1,0:T(8,128)} %collective-permute-done.19.refs_1_), channel_id=1, source_target_pairs={{0,96},{8,104},{16,112},{24,120},{32,0},{40,8},{48,16},{56,24},{64... | collective-permute-start | bytes 7864328 | tf_op jit(solution)/shard_map/ppermute | solution.py:474
  562.9 5.5 copy-start.2
  562.9 42.1 %collective-permute-start.36 = (f32[528,640]{1,0:T(8,128)}, f32[528,640]{1,0:T(8,128)}, u32[]{:S(2)}, u32[]{:S(2)}) collective-permute-start(f32[528,640]{1,0:T(8,128)} %slice.44), channel_id=1, source_target_pairs={{0,8},{8,16},{16,24},{24,0},{32,40},{40,48},{48,56},{56,32},{64,72... | collective-permute-start | bytes 4055048 | tf_op jit(solution)/shard_map/ppermute | solution.py:474
  566.0 17.2 %collective-permute-start.38 = (f32[496,640]{1,0:T(8,128)S(1)}, f32[496,640]{1,0:T(8,128)S(1)}, u32[]{:S(2)}, u32[]{:S(2)}) collective-permute-start(f32[496,640]{1,0:T(8,128)S(1)} %slice.46), channel_id=1, source_target_pairs={{0,24},{8,0},{16,8},{24,16},{32,56},{40,32},{48,40},{56,48},{64,88... | collective-permute-start | bytes 3809288 | tf_op jit(solution)/shard_map/ppermute | solution.py:474
  567.2 33.2 %collective-permute-start.39 = (f32[496,640]{1,0:T(8,128)}, f32[496,640]{1,0:T(8,128)}, u32[]{:S(2)}, u32[]{:S(2)}) collective-permute-start(f32[496,640]{1,0:T(8,128)} %slice.47), channel_id=1, source_target_pairs={{0,96},{8,104},{16,112},{24,120},{32,0},{40,8},{48,16},{56,24},{64... | collective-permute-start | bytes 3809288 | tf_op jit(solution)/shard_map/ppermute | solution.py:474
  583.3 36.2 %collective-permute-start.37 = (f32[528,640]{1,0:T(8,128)}, f32[528,640]{1,0:T(8,128)}, u32[]{:S(2)}, u32[]{:S(2)}) collective-permute-start(f32[528,640]{1,0:T(8,128)} %slice.45), channel_id=1, source_target_pairs={{0,32},{8,40},{16,48},{24,56},{32,64},{40,72},{48,80},{56,88},{64,... | collective-permute-start | bytes 4055048 | tf_op jit(solution)/shard_map/ppermute | solution.py:474
  600.4 30.5 %collective-permute-start.40 = (f32[512,640]{1,0:T(8,128)}, f32[512,640]{1,0:T(8,128)}, u32[]{:S(2)}, u32[]{:S(2)}) collective-permute-start(f32[512,640]{1,0:T(8,128)} %collective-permute-done.31.refs_1_), channel_id=1, source_target_pairs={{0,32},{8,40},{16,48},{24,56},{32,64},{40,72},{48,80},{56,88},{64,... | collective-permute-start | bytes 3932168 | tf_op jit(solution)/shard_map/ppermute | solution.py:474
  600.5 30.4 %collective-permute-start.41 = (f32[512,640]{1,0:T(8,128)}, f32[512,640]{1,0:T(8,128)}, u32[]{:S(2)}, u32[]{:S(2)}) collective-permute-start(f32[512,640]{1,0:T(8,128)} %collective-permute-done.27.refs_3_), channel_id=1, source_target_pairs={{0,96},{8,104},{16,112},{24,120},{32,0},{40,8},{48,16},{56,24},{64... | collective-permute-start | bytes 3932168 | tf_op jit(solution)/shard_map/ppermute | solution.py:474
  603.8 29.8 %collective-permute-start.42 = (f32[512,640]{1,0:T(8,128)}, f32[512,640]{1,0:T(8,128)}, u32[]{:S(2)}, u32[]{:S(2)}) collective-permute-start(f32[512,640]{1,0:T(8,128)} %collective-permute-done.30.refs_0_), channel_id=1, source_target_pairs={{0,8},{8,16},{16,24},{24,0},{32,40},{40,48},{48,56},{56,32},{64,72... | collective-permute-start | bytes 3932168 | tf_op jit(solution)/shard_map/ppermute | solution.py:474
  605.0 28.6 %collective-permute-start.43 = (f32[512,640]{1,0:T(8,128)}, f32[512,640]{1,0:T(8,128)}, u32[]{:S(2)}, u32[]{:S(2)}) collective-permute-start(f32[512,640]{1,0:T(8,128)} %collective-permute-done.26.refs_2_), channel_id=1, source_target_pairs={{0,24},{8,0},{16,8},{24,16},{32,56},{40,32},{48,40},{56,48},{64,88... | collective-permute-start | bytes 3932168 | tf_op jit(solution)/shard_map/ppermute | solution.py:474
  614.7 4.8 copy-start.5
  (3 other events, 10.2 us)

commit v7 on v5

--- a/solution.py
+++ b/solution.py
@@ -11,6 +11,7 @@
 NORM_EPS = 1e-6
 SIDE, N_DP, N_TP, LANES = 4, 16, 8, 128
 UP, DOWN, AWAY = 1, 3, 2
+TILT = 8
 MIB = 2 ** 20
 L_FRONT = 41
 MESH = pl.DeviceIdType.MESH
@@ -420,18 +421,24 @@
     rows = vocab // N_DP
     quarter = rows // SIDE
     cut = 256
-    chunks = [(i, r) for i in range(n) for r in range(0, arrays[i].shape[0], cut)]
+    chunks = []
+    for i, (array, dz, dy, kind, start) in enumerate(pieces):
+        r = 0
+        while r < array.shape[0]:
+            row = start + r
+            size = min(cut, array.shape[0] - r, quarter - row if row < quarter else cut)
+            chunks.append((i, r, size, dz, dy, row + kind * quarter if row < quarter else row + quarter + kind * (quarter - TILT)))
+            r += size
 
     def kern(*refs):
         dst, buf, sem = refs[-DOWN:]
         at = peers()[1]
         reads, writes = [], []
-        for k, (i, r) in enumerate(chunks):
-            _, dz, dy, kind, half = pieces[i]
-            first = (2 * (half + r // quarter) + kind) * quarter + r % quarter
-            there = aligned(at[dz, dy] * rows + first, cut, cut)
-            reads.append(pltpu.make_async_copy(refs[i].at[pl.ds(r, cut)], buf.at[k], sem.at[0, k]))
-            writes.append(pltpu.make_async_copy(buf.at[k], dst.at[there], sem.at[1, k]))
+        for k, (i, r, size, dz, dy, first) in enumerate(chunks):
+            held = buf.at[k, pl.ds(0, size)]
+            there = aligned(at[dz, dy] * rows + first, size, 8)
+            reads.append(pltpu.make_async_copy(refs[i].at[pl.ds(r, size)], held, sem.at[0, k]))
+            writes.append(pltpu.make_async_copy(held, dst.at[there], sem.at[1, k]))
         for cp in reads:
             cp.start()
         for read, write in zip(reads, writes):
@@ -460,8 +467,9 @@
             out.append(lax.ppermute(pair[k], 'dp', [(d, shift(d, dz, dy)) for d in range(N_DP)]))
         return out
 
-    def put(pair, a, b, c=0):
-        return [(pair[k], *((b, a) if k else (a, b)), k, c) for k in sets]
+    def put(pair, a, b, start=0):
+        starts = start if isinstance(start, tuple) else (start, start)
+        return [(pair[k], *((b, a) if k else (a, b)), k, starts[k]) for k in sets]
 
     def settle(*pieces):
         nonlocal table
@@ -480,12 +488,12 @@
     low, high = ([send(own[0], 0, way)] for way in ways)
     later = rest()
     event = 1
-    own.append([later[k] for k in sets])
+    own.append([later[:quarter - TILT], later[quarter - TILT:]])
     low.append(send(own[1], 0, UP))
     high.append(send(own[1], 0, DOWN))
     whole = join(*own)
     side = {way: send(whole, 1, way) for way in ways}
-    settle(put(own[0], 0, 0, 0), put(own[1], 0, 0, 1))
+    settle(put(own[0], 0, 0, 0), put(own[1], 0, 0, quarter))
 
     low[0], high[0] = wait(low[0], high[0])
     far_low = send(low[0], 0, UP)
@@ -495,7 +503,7 @@
     far_high = send(high[1], 0, DOWN)
     low_whole, high_whole = join(*low), join(*high)
     low_side = {way: send(low_whole, 1, way) for way in ways}
-    settle(put(low[1], DOWN, 0, 1), put(high[1], UP, 0, 1))
+    settle(put(low[1], DOWN, 0, quarter), put(high[1], UP, 0, quarter))
 
     side[UP], side[DOWN], high_whole = wait(side[UP], side[DOWN], high_whole)
     high_side = {way: send(high_whole, 1, way) for way in ways}
@@ -505,7 +513,7 @@
 
     far_low, far_high = wait(far_low, far_high)
     far_side = {(c, way): send(pair, 1, way) for way in ways for c, pair in enumerate((far_low, far_high))}
-    settle(put(far_low, AWAY, 0, 0), put(far_high, AWAY, 0, 1))
+    settle(put(far_low, AWAY, 0, 0), put(far_high, AWAY, 0, quarter))
 
     low_side[UP], low_side[DOWN] = wait(low_side[UP], low_side[DOWN])
     low_far = send(low_side[DOWN], 1, DOWN)
@@ -513,13 +521,14 @@
     settle(put(low_side[DOWN], DOWN, UP))
 
     high_side[UP], high_side[DOWN] = wait(high_side[UP], high_side[DOWN])
-    high_far = [send([x[:quarter] for x in high_side[UP]], 1, UP), send([x[quarter:] for x in high_side[DOWN]], 1, DOWN)]
+    cuts = quarter + TILT, quarter + 2 * TILT
+    high_far = [send([x[:cut] for x, cut in zip(high_side[UP], cuts)], 1, UP), send([x[cut:] for x, cut in zip(high_side[DOWN], cuts)], 1, DOWN)]
     settle(put(high_side[UP], UP, DOWN))
     settle(put(high_side[DOWN], UP, UP))
 
     far_side[0, DOWN], far_side[1, DOWN], side_far = wait(far_side[0, DOWN], far_side[1, DOWN], side_far)
     last_down = send(far_side[1, DOWN], 1, DOWN)
-    settle(put(far_side[0, DOWN], AWAY, UP, 0), put(far_side[1, DOWN], AWAY, UP, 1))
+    settle(put(far_side[0, DOWN], AWAY, UP, 0), put(far_side[1, DOWN], AWAY, UP, quarter))
     settle(put(side_far, 0, AWAY))
 
     far_side[0, UP], = wait(far_side[0, UP])
@@ -527,13 +536,13 @@
     settle(put(far_side[0, UP], AWAY, DOWN, 0))
 
     far_side[1, UP], low_far = wait(far_side[1, UP], low_far)
-    settle(put(far_side[1, UP], AWAY, DOWN, 1))
+    settle(put(far_side[1, UP], AWAY, DOWN, quarter))
     settle(put(low_far, DOWN, AWAY))
 
     high_far = wait(*high_far)
-    settle(put(high_far[0], UP, AWAY, 0), put(high_far[1], UP, AWAY, 1))
+    settle(put(high_far[0], UP, AWAY, 0), put(high_far[1], UP, AWAY, cuts))
     last_up, last_down = wait(last_up, last_down)
-    settle(put(last_up, AWAY, AWAY, 0), put(last_down, AWAY, AWAY, 1))
+    settle(put(last_up, AWAY, AWAY, 0), put(last_down, AWAY, AWAY, quarter))
     return table
 
 
@@ -542,7 +551,7 @@
         tokens = hid_rows.shape[0]
         late, soon, x_all, tab_part, coef, stats, grad_h, gain_line = front(hid_rows, w_final.reshape(-1, LANES), mask_rows[None], tea_rows, tab_rows)
         coef, *first = lax.optimization_barrier((coef, soon[0], soon[1]))
-        table = gather(first, lambda: finish(late, x_all, tab_part, coef), tab_rows.shape[0])
+        table = gather(first, lambda: finish(late, x_all, tab_part, coef).reshape(-1, x_all.shape[1]), tab_rows.shape[0])
         s_sum, t_sum, k_sum, masks = (stats[:, i, :tokens] for i in range(SIDE))
         all_kl = k_sum / t_sum + jnp.log(s_sum) - jnp.log(t_sum)
         loss_val = jnp.sum(masks * all_kl) / jnp.sum(masks)

time: 633 us -> 679 us (1.073)
  the two profiles are of different devices: /device:TPU:16 before, /device:TPU:1 now
where the time goes in v7:
time: 679 us; the launch traced here: 670 us
  waiting for transfers between devices  415 us (61%)
  Pallas kernels  181 us (27%)
  starting transfers between devices  61.7 us (9%)
  local copies, waits for them, and re-layouts  7.17 us (1%)
    ppermute x44, waiting for transfers between devices, send(): lax.ppermute(pair[k], 'dp', [(d, shift(d, dz, dy)) for d in range(N_DP)])  415 us
    pallas_call x1, Pallas kernels, front(): pl.pallas_call(kern, out_shape=tuple((jax.ShapeDtypeStruct(shape, kind) f...  105 us
    pallas_call x17, Pallas kernels, place(): pl.pallas_call(kern, out_shape=jax.ShapeDtypeStruct((vocab, dim), F32), i...  68.8 us
    ppermute x44, starting transfers between devices, send(): lax.ppermute(pair[k], 'dp', [(d, shift(d, dz, dy)) for d in range(N_DP)])  61.7 us
  transfers between devices with their start and end apart: 44, of which 22 were waited for; matrix products, arithmetic and copies ran while one was open for 1% of the time, Pallas kernels for 10%

profile of v7, /device:TPU:1, one launch (start us, length us, event | category | flops | bytes accessed | tf_op | source)
XLA Modules:
  0.0 670.4 jit_solution(9077060977508365737)
XLA Ops:
  0.6 104.7 %front.1 = (f32[16,64,1024]{2,1,0:T(8,128)S(1)}, f32[2,512,640]{2,1,0:T(8,128)S(1)}, bf16[1024,640]{1,0:T(8,128)(2,1)S(1)}, bf16[2048,640]{1,0:T(8,128)(2,1)S(1)...) custom-call(bf16[64,640]{1,0:T(8,128)(2,1)} %hid_hbm.1, ...), custom_call_target="tpu_custom_call" | custom-call | flops 3000000000 | bytes 104857600 | tf_op jit(solution)/shard_map/front/pallas_call | solution.py:378
  105.5 7.2 %finish.1 = f32[2,512,640]{2,1,0:T(8,128)S(1)} custom-call(f32[16,64,1024]{2,1,0:T(8,128)S(1)} %get-tuple-element.79.tea_ref, bf16[1024,640]{1,0:T(8,128)(2,1)S(1)} %get-tuple-element.80.x_ref, bf16[2048,640]{1,0:T(8,128)(2,1)S(1)} %get-tuple-element.81.tab_ref, f32[128,128]{1,0:T(8,128)S(1)} %get-tuple-element.82.coef_ref), custom_call_target="tpu_custom_call" | custom-call | flops 1000000000 | bytes 8388608 | tf_op jit(solution)/shard_map/finish/pallas_call | solution.py:411
  119.8 22.1 %collective-permute-done.4.refs_0_ = f32[504,640]{1,0:T(8,128)S(1)} collective-permute-done((f32[504,640]{1,0:T(8,128)S(1)}, f32[504,640]{1,0:T(8,128)S(1)}, u32[]{:S(2)}, u32[]{:S(2)}) %collective-permute-start.4) | collective-permute-done | bytes 1290272 | tf_op jit(solution)/shard_map/ppermute | solution.py:467
  144.8 25.2 %collective-permute-done.refs_0_ = f32[512,640]{1,0:T(8,128)S(1)} collective-permute-done((f32[512,640]{1,0:T(8,128)S(1)}, f32[512,640]{1,0:T(8,128)S(1)}, u32[]{:S(2)}, u32[]{:S(2)}) %collective-permute-start) | collective-permute-done | bytes 1310752 | tf_op jit(solution)/shard_map/ppermute | solution.py:467
  170.0 2.9 collective-permute-start.3
  175.9 47.6 %collective-permute-done.3.refs_3_ = f32[512,640]{1,0:T(8,128)S(1)} collective-permute-done((f32[512,640]{1,0:T(8,128)S(1)}, f32[512,640]{1,0:T(8,128)S(1)}, u32[]{:S(2)}, u32[]{:S(2)}) %collective-permute-start.3) | collective-permute-done | bytes 1310752 | tf_op jit(solution)/shard_map/ppermute | solution.py:467
  223.5 4.1 collective-permute-done.5.refs_1_
  227.6 4.1 collective-permute-start.11
  231.7 4.1 place.17.refs_4_
  235.9 16.2 %collective-permute-done.7.refs_3_ = f32[520,640]{1,0:T(8,128)S(1)} collective-permute-done((f32[520,640]{1,0:T(8,128)S(1)}, f32[520,640]{1,0:T(8,128)S(1)}, u32[]{:S(2)}, u32[]{:S(2)}) %collective-permute-start.7) | collective-permute-done | bytes 1331232 | tf_op jit(solution)/shard_map/ppermute | solution.py:467
  252.0 4.1 place.18.refs_4_
  260.1 39.3 %collective-permute-done.12.refs_0_ = f32[512,640]{1,0:T(8,128)S(1)} collective-permute-done((f32[512,640]{1,0:T(8,128)S(1)}, f32[512,640]{1,0:T(8,128)S(1)}, u32[]{:S(2)}, u32[]{:S(2)}) %collective-permute-start.12) | collective-permute-done | bytes 1310752 | tf_op jit(solution)/shard_map/ppermute | solution.py:467
  300.1 8.4 %collective-permute-done.14.refs_2_ = f32[504,640]{1,0:T(8,128)S(1)} collective-permute-done((f32[504,640]{1,0:T(8,128)S(1)}, f32[504,640]{1,0:T(8,128)S(1)}, u32[]{:S(2)}, u32[]{:S(2)}) %collective-permute-start.14) | collective-permute-done | bytes 1290272 | tf_op jit(solution)/shard_map/ppermute | solution.py:467
  309.2 3.4 collective-permute-start.19
  312.6 4.1 place.19.refs_2_
  317.1 4.2 place.20.refs_2_
  321.3 4.2 place.21.refs_4_
  326.3 13.5 %collective-permute-done.16.refs_0_ = f32[1016,640]{1,0:T(8,128)S(1)} collective-permute-done((f32[1016,640]{1,0:T(8,128)S(1)}, f32[1016,640]{1,0:T(8,128)S(1)}, u32[]{:S(2)}, u32[]{:S(2)}) %collective-permute-start.16) | collective-permute-done | bytes 2600992 | tf_op jit(solution)/shard_map/ppermute | solution.py:467
  339.8 5.0 collective-permute-start.32
  344.8 37.0 %collective-permute-done.18.refs_0_ = f32[1016,640]{1,0:T(8,128)} collective-permute-done((f32[1016,640]{1,0:T(8,128)S(1)}, f32[1016,640]{1,0:T(8,128)}, u32[]{:S(2)}, u32[]{:S(2)}) %collective-permute-start.18) | collective-permute-done | bytes 2600992 | tf_op jit(solution)/shard_map/ppermute | solution.py:467
  381.8 27.6 %collective-permute-done.26.refs_2_ = f32[504,640]{1,0:T(8,128)} collective-permute-done((f32[504,640]{1,0:T(8,128)S(1)}, f32[504,640]{1,0:T(8,128)}, u32[]{:S(2)}, u32[]{:S(2)}) %collective-permute-start.26) | collective-permute-done | bytes 1290272 | tf_op jit(solution)/shard_map/ppermute | solution.py:467
  409.4 4.0 collective-permute-start.25
  414.6 22.8 %collective-permute-done.24.refs_0_ = f32[512,640]{1,0:T(8,128)S(1)} collective-permute-done((f32[512,640]{1,0:T(8,128)S(1)}, f32[512,640]{1,0:T(8,128)S(1)}, u32[]{:S(2)}, u32[]{:S(2)}) %collective-permute-start.24) | collective-permute-done | bytes 1310752 | tf_op jit(solution)/shard_map/ppermute | solution.py:467
  438.8 3.6 collective-permute-start.27
  443.9 25.5 %collective-permute-done.27.refs_3_ = f32[520,640]{1,0:T(8,128)} collective-permute-done((f32[520,640]{1,0:T(8,128)S(1)}, f32[520,640]{1,0:T(8,128)}, u32[]{:S(2)}, u32[]{:S(2)}) %collective-permute-start.27) | collective-permute-done | bytes 1331232 | tf_op jit(solution)/shard_map/ppermute | solution.py:467
  469.7 5.1 collective-permute-done.20.refs_0_
  474.8 5.6 collective-permute-done.22.refs_0_
  480.4 4.1 place.22.refs_2_
  484.5 13.5 %collective-permute-done.21.refs_1_ = f32[1032,640]{1,0:T(8,128)S(1)} collective-permute-done((f32[1032,640]{1,0:T(8,128)S(1)}, f32[1032,640]{1,0:T(8,128)S(1)}, u32[]{:S(2)}, u32[]{:S(2)}) %collective-permute-start.21) | collective-permute-done | bytes 2641952 | tf_op jit(solution)/shard_map/ppermute | solution.py:467
  498.0 3.8 collective-permute-start.35
  501.9 21.5 %collective-permute-done.23.refs_1_ = f32[1032,640]{1,0:T(8,128)S(1)} collective-permute-done((f32[1032,640]{1,0:T(8,128)S(1)}, f32[1032,640]{1,0:T(8,128)S(1)}, u32[]{:S(2)}, u32[]{:S(2)}) %collective-permute-start.23) | collective-permute-done | bytes 2641952 | tf_op jit(solution)/shard_map/ppermute | solution.py:467
  523.3 4.1 place.23.refs_2_
  527.5 4.6 place.24.refs_2_
  532.2 51.0 %collective-permute-done.33.refs_1_ = f32[520,640]{1,0:T(8,128)S(1)} collective-permute-done((f32[520,640]{1,0:T(8,128)S(1)}, f32[520,640]{1,0:T(8,128)S(1)}, u32[]{:S(2)}, u32[]{:S(2)}) %collective-permute-start.33) | collective-permute-done | bytes 1331232 | tf_op jit(solution)/shard_map/ppermute | solution.py:467
  587.0 3.9 collective-permute-start.39
  592.0 15.8 %collective-permute-done.38.refs_2_ = f32[496,640]{1,0:T(8,128)S(1)} collective-permute-done((f32[496,640]{1,0:T(8,128)S(1)}, f32[496,640]{1,0:T(8,128)S(1)}, u32[]{:S(2)}, u32[]{:S(2)}) %collective-permute-start.38) | collective-permute-done | bytes 1269792 | tf_op jit(solution)/shard_map/ppermute | solution.py:467
  607.9 4.1 place.25.refs_2_
  612.0 4.2 place.26.refs_4_
  616.2 6.1 collective-permute-start.43
  622.3 4.7 place.27.refs_2_
  627.0 4.2 place.28.refs_2_
  631.4 3.6 collective-permute-start.42
  638.2 2.8 place.29.refs_2_
  643.9 4.7 place.31.refs_4_
  648.6 3.6 place.32.refs_4_
  652.3 2.8 collective-permute-done.42.refs_2_
  656.3 8.3 %collective-permute-done.41.refs_1_ = f32[512,640]{1,0:T(8,128)} collective-permute-done((f32[512,640]{1,0:T(8,128)}, f32[512,640]{1,0:T(8,128)}, u32[]{:S(2)}, u32[]{:S(2)}) %collective-permute-start.41) | collective-permute-done | bytes 1310752 | tf_op jit(solution)/shard_map/ppermute | solution.py:467
  664.6 4.6 place.33
  (93 shorter events, 35.3 us)
Async XLA Ops:
  112.8 29.1 %collective-permute-start.4 = (f32[504,640]{1,0:T(8,128)S(1)}, f32[504,640]{1,0:T(8,128)S(1)}, u32[]{:S(2)}, u32[]{:S(2)}) collective-permute-start(f32[504,640]{1,0:T(8,128)S(1)} %slice.48.refs_2_), channel_id=1, source_target_pairs={{0,32},{8,40},{16,48},{24,56},{32,64},{40,72},{48,80},{56,88},{64,... | collective-permute-start | bytes 3870728 | tf_op jit(solution)/shard_map/ppermute | solution.py:467
  113.9 29.4 %collective-permute-start.6 = (f32[504,640]{1,0:T(8,128)S(1)}, f32[504,640]{1,0:T(8,128)S(1)}, u32[]{:S(2)}, u32[]{:S(2)}) collective-permute-start(f32[504,640]{1,0:T(8,128)S(1)} %slice.48.refs_2_), channel_id=1, source_target_pairs={{0,96},{8,104},{16,112},{24,120},{32,0},{40,8},{48,16},{56,24},{64... | collective-permute-start | bytes 3870728 | tf_op jit(solution)/shard_map/ppermute | solution.py:467
  115.6 54.4 %collective-permute-start = (f32[512,640]{1,0:T(8,128)S(1)}, f32[512,640]{1,0:T(8,128)S(1)}, u32[]{:S(2)}, u32[]{:S(2)}) collective-permute-start(f32[512,640]{1,0:T(8,128)S(1)} %get-tuple-element.77.refs_0_), channel_id=1, source_target_pairs={{0,32},{8,40},{16,48},{24,56},{32,64},{40,72},{48,80},{56,88},{64,... | collective-permute-start | bytes 3932168 | tf_op jit(solution)/shard_map/ppermute | solution.py:467
  115.6 57.4 %collective-permute-start.1 = (f32[512,640]{1,0:T(8,128)S(1)}, f32[512,640]{1,0:T(8,128)S(1)}, u32[]{:S(2)}, u32[]{:S(2)}) collective-permute-start(f32[512,640]{1,0:T(8,128)S(1)} %get-tuple-element.78.refs_1_), channel_id=1, source_target_pairs={{0,8},{8,16},{16,24},{24,0},{32,40},{40,48},{48,56},{56,32},{64,72... | collective-permute-start | bytes 3932168 | tf_op jit(solution)/shard_map/ppermute | solution.py:467
  116.9 56.1 %collective-permute-start.2 = (f32[512,640]{1,0:T(8,128)S(1)}, f32[512,640]{1,0:T(8,128)S(1)}, u32[]{:S(2)}, u32[]{:S(2)}) collective-permute-start(f32[512,640]{1,0:T(8,128)S(1)} %get-tuple-element.77.refs_0_), channel_id=1, source_target_pairs={{0,96},{8,104},{16,112},{24,120},{32,0},{40,8},{48,16},{56,24},{64... | collective-permute-start | bytes 3932168 | tf_op jit(solution)/shard_map/ppermute | solution.py:467
  141.9 114.4 %collective-permute-start.8 = (f32[1016,640]{1,0:T(8,128)S(1)}, f32[1016,640]{1,0:T(8,128)S(1)}, u32[]{:S(2)}, u32[]{:S(2)}) collective-permute-start(f32[1016,640]{1,0:T(8,128)S(1)} %pad_maximum_fusion.2), channel_id=1, source_target_pairs={{0,8},{8,16},{16,24},{24,0},{32,40},{40,48},{48,56},{56,32},{64,72... | collective-permute-start | bytes 7802888 | tf_op jit(solution)/shard_map/ppermute | solution.py:467
  143.2 114.1 %collective-permute-start.10 = (f32[1016,640]{1,0:T(8,128)S(1)}, f32[1016,640]{1,0:T(8,128)S(1)}, u32[]{:S(2)}, u32[]{:S(2)}) collective-permute-start(f32[1016,640]{1,0:T(8,128)S(1)} %pad_maximum_fusion.2), channel_id=1, source_target_pairs={{0,24},{8,0},{16,8},{24,16},{32,56},{40,32},{48,40},{56,48},{64,88... | collective-permute-start | bytes 7802888 | tf_op jit(solution)/shard_map/ppermute | solution.py:467
  170.0 53.5 %collective-permute-start.3 = (f32[512,640]{1,0:T(8,128)S(1)}, f32[512,640]{1,0:T(8,128)S(1)}, u32[]{:S(2)}, u32[]{:S(2)}) collective-permute-start(f32[512,640]{1,0:T(8,128)S(1)} %get-tuple-element.78.refs_1_), channel_id=1, source_target_pairs={{0,24},{8,0},{16,8},{24,16},{32,56},{40,32},{48,40},{56,48},{64,88... | collective-permute-start | bytes 3932168 | tf_op jit(solution)/shard_map/ppermute | solution.py:467
  173.0 54.7 %collective-permute-start.5 = (f32[520,640]{1,0:T(8,128)S(1)}, f32[520,640]{1,0:T(8,128)S(1)}, u32[]{:S(2)}, u32[]{:S(2)}) collective-permute-start(f32[520,640]{1,0:T(8,128)S(1)} %slice.49.refs_3_), channel_id=1, source_target_pairs={{0,8},{8,16},{16,24},{24,0},{32,40},{40,48},{48,56},{56,32},{64,72... | collective-permute-start | bytes 3993608 | tf_op jit(solution)/shard_map/ppermute | solution.py:467
  173.1 79.0 %collective-permute-start.7 = (f32[520,640]{1,0:T(8,128)S(1)}, f32[520,640]{1,0:T(8,128)S(1)}, u32[]{:S(2)}, u32[]{:S(2)}) collective-permute-start(f32[520,640]{1,0:T(8,128)S(1)} %slice.49.refs_3_), channel_id=1, source_target_pairs={{0,24},{8,0},{16,8},{24,16},{32,56},{40,32},{48,40},{56,48},{64,88... | collective-permute-start | bytes 3993608 | tf_op jit(solution)/shard_map/ppermute | solution.py:467
  223.5 84.9 %collective-permute-start.9 = (f32[1032,640]{1,0:T(8,128)S(1)}, f32[1032,640]{1,0:T(8,128)S(1)}, u32[]{:S(2)}, u32[]{:S(2)}) collective-permute-start(f32[1032,640]{1,0:T(8,128)S(1)} %pad_maximum_fusion), channel_id=1, source_target_pairs={{0,32},{8,40},{16,48},{24,56},{32,64},{40,72},{48,80},{56,88},{64,... | collective-permute-start | bytes 7925768 | tf_op jit(solution)/shard_map/ppermute | solution.py:467
  227.6 81.5 %collective-permute-start.11 = (f32[1032,640]{1,0:T(8,128)S(1)}, f32[1032,640]{1,0:T(8,128)S(1)}, u32[]{:S(2)}, u32[]{:S(2)}) collective-permute-start(f32[1032,640]{1,0:T(8,128)S(1)} %pad_maximum_fusion), channel_id=1, source_target_pairs={{0,96},{8,104},{16,112},{24,120},{32,0},{40,8},{48,16},{56,24},{64... | collective-permute-start | bytes 7925768 | tf_op jit(solution)/shard_map/ppermute | solution.py:467
  252.0 47.4 %collective-permute-start.12 = (f32[512,640]{1,0:T(8,128)S(1)}, f32[512,640]{1,0:T(8,128)S(1)}, u32[]{:S(2)}, u32[]{:S(2)}) collective-permute-start(f32[512,640]{1,0:T(8,128)S(1)} %collective-permute-done.refs_0_), channel_id=1, source_target_pairs={{0,32},{8,40},{16,48},{24,56},{32,64},{40,72},{48,80},{56,88},{64,... | collective-permute-start | bytes 3932168 | tf_op jit(solution)/shard_map/ppermute | solution.py:467
  256.3 43.7 %collective-permute-start.13 = (f32[512,640]{1,0:T(8,128)S(1)}, f32[512,640]{1,0:T(8,128)S(1)}, u32[]{:S(2)}, u32[]{:S(2)}) collective-permute-start(f32[512,640]{1,0:T(8,128)S(1)} %collective-permute-done.1.refs_1_), channel_id=1, source_target_pairs={{0,8},{8,16},{16,24},{24,0},{32,40},{40,48},{48,56},{56,32},{64,72... | collective-permute-start | bytes 3932168 | tf_op jit(solution)/shard_map/ppermute | solution.py:467
  257.4 51.1 %collective-permute-start.14 = (f32[504,640]{1,0:T(8,128)S(1)}, f32[504,640]{1,0:T(8,128)S(1)}, u32[]{:S(2)}, u32[]{:S(2)}) collective-permute-start(f32[504,640]{1,0:T(8,128)S(1)} %collective-permute-done.6.refs_2_), channel_id=1, source_target_pairs={{0,96},{8,104},{16,112},{24,120},{32,0},{40,8},{48,16},{56,24},{64... | collective-permute-start | bytes 3870728 | tf_op jit(solution)/shard_map/ppermute | solution.py:467
  299.4 40.4 %collective-permute-start.16 = (f32[1016,640]{1,0:T(8,128)S(1)}, f32[1016,640]{1,0:T(8,128)S(1)}, u32[]{:S(2)}, u32[]{:S(2)}) collective-permute-start(f32[1016,640]{1,0:T(8,128)S(1)} %constant_dynamic-update-slice_fusion), channel_id=1, source_target_pairs={{0,8},{8,16},{16,24},{24,0},{32,40},{40,48},{48,56},{56,32},{64,72... | collective-permute-start | bytes 7802888 | tf_op jit(solution)/shard_map/ppermute | solution.py:467
  300.0 114.6 %collective-permute-start.17 = (f32[1032,640]{1,0:T(8,128)S(1)}, f32[1032,640]{1,0:T(8,128)S(1)}, u32[]{:S(2)}, u32[]{:S(2)}) collective-permute-start(f32[1032,640]{1,0:T(8,128)S(1)} %constant_dynamic-update-slice_fusion.2), channel_id=1, source_target_pairs={{0,32},{8,40},{16,48},{24,56},{32,64},{40,72},{48,80},{56,88},{64,... | collective-permute-start | bytes 7925768 | tf_op jit(solution)/shard_map/ppermute | solution.py:467
  308.4 17.5 %collective-permute-start.15 = (f32[520,640]{1,0:T(8,128)S(1)}, f32[520,640]{1,0:T(8,128)S(1)}, u32[]{:S(2)}, u32[]{:S(2)}) collective-permute-start(f32[520,640]{1,0:T(8,128)S(1)} %collective-permute-done.7.refs_3_), channel_id=1, source_target_pairs={{0,24},{8,0},{16,8},{24,16},{32,56},{40,32},{48,40},{56,48},{64,88... | collective-permute-start | bytes 3993608 | tf_op jit(solution)/shard_map/ppermute | solution.py:467
  308.4 73.3 %collective-permute-start.18 = (f32[1016,640]{1,0:T(8,128)S(1)}, f32[1016,640]{1,0:T(8,128)}, u32[]{:S(2)}, u32[]{:S(2)}) collective-permute-start(f32[1016,640]{1,0:T(8,128)S(1)} %constant_dynamic-update-slice_fusion), channel_id=1, source_target_pairs={{0,24},{8,0},{16,8},{24,16},{32,56},{40,32},{48,40},{56,48},{64,88... | collective-permute-start | bytes 7802888 | tf_op jit(solution)/shard_map/ppermute | solution.py:467
  309.2 105.4 %collective-permute-start.19 = (f32[1032,640]{1,0:T(8,128)S(1)}, f32[1032,640]{1,0:T(8,128)}, u32[]{:S(2)}, u32[]{:S(2)}) collective-permute-start(f32[1032,640]{1,0:T(8,128)S(1)} %constant_dynamic-update-slice_fusion.2), channel_id=1, source_target_pairs={{0,96},{8,104},{16,112},{24,120},{32,0},{40,8},{48,16},{56,24},{64... | collective-permute-start | bytes 7925768 | tf_op jit(solution)/shard_map/ppermute | solution.py:467
  325.9 83.5 %collective-permute-start.26 = (f32[504,640]{1,0:T(8,128)S(1)}, f32[504,640]{1,0:T(8,128)}, u32[]{:S(2)}, u32[]{:S(2)}) collective-permute-start(f32[504,640]{1,0:T(8,128)S(1)} %collective-permute-done.14.refs_2_), channel_id=1, source_target_pairs={{0,24},{8,0},{16,8},{24,16},{32,56},{40,32},{48,40},{56,48},{64,88... | collective-permute-start | bytes 3870728 | tf_op jit(solution)/shard_map/ppermute | solution.py:467
  339.8 73.6 %collective-permute-start.32 = (f32[504,640]{1,0:T(8,128)S(1)}, f32[504,640]{1,0:T(8,128)S(1)}, u32[]{:S(2)}, u32[]{:S(2)}) collective-permute-start(f32[504,640]{1,0:T(8,128)S(1)} %collective-permute-done.14.refs_2_), channel_id=1, source_target_pairs={{0,8},{8,16},{16,24},{24,0},{32,40},{40,48},{48,56},{56,32},{64,72... | collective-permute-start | bytes 3870728 | tf_op jit(solution)/shard_map/ppermute | solution.py:467
  381.8 55.6 %collective-permute-start.24 = (f32[512,640]{1,0:T(8,128)S(1)}, f32[512,640]{1,0:T(8,128)S(1)}, u32[]{:S(2)}, u32[]{:S(2)}) collective-permute-start(f32[512,640]{1,0:T(8,128)S(1)} %collective-permute-done.12.refs_0_), channel_id=1, source_target_pairs={{0,24},{8,0},{16,8},{24,16},{32,56},{40,32},{48,40},{56,48},{64,88... | collective-permute-start | bytes 3932168 | tf_op jit(solution)/shard_map/ppermute | solution.py:467
  409.4 29.4 %collective-permute-start.25 = (f32[512,640]{1,0:T(8,128)S(1)}, f32[512,640]{1,0:T(8,128)S(1)}, u32[]{:S(2)}, u32[]{:S(2)}) collective-permute-start(f32[512,640]{1,0:T(8,128)S(1)} %collective-permute-done.13.refs_1_), channel_id=1, source_target_pairs={{0,96},{8,104},{16,112},{24,120},{32,0},{40,8},{48,16},{56,24},{64... | collective-permute-start | bytes 3932168 | tf_op jit(solution)/shard_map/ppermute | solution.py:467
  414.5 27.9 %collective-permute-start.30 = (f32[512,640]{1,0:T(8,128)S(1)}, f32[512,640]{1,0:T(8,128)}, u32[]{:S(2)}, u32[]{:S(2)}) collective-permute-start(f32[512,640]{1,0:T(8,128)S(1)} %collective-permute-done.12.refs_0_), channel_id=1, source_target_pairs={{0,8},{8,16},{16,24},{24,0},{32,40},{40,48},{48,56},{56,32},{64,72... | collective-permute-start | bytes 3932168 | tf_op jit(solution)/shard_map/ppermute | solution.py:467
  414.5 29.4 %collective-permute-start.31 = (f32[512,640]{1,0:T(8,128)S(1)}, f32[512,640]{1,0:T(8,128)}, u32[]{:S(2)}, u32[]{:S(2)}) collective-permute-start(f32[512,640]{1,0:T(8,128)S(1)} %collective-permute-done.13.refs_1_), channel_id=1, source_target_pairs={{0,32},{8,40},{16,48},{24,56},{32,64},{40,72},{48,80},{56,88},{64,... | collective-permute-start | bytes 3932168 | tf_op jit(solution)/shard_map/ppermute | solution.py:467
  414.6 60.2 %collective-permute-start.20 = (f32[1016,640]{1,0:T(8,128)S(1)}, f32[1016,640]{1,0:T(8,128)S(1)}, u32[]{:S(2)}, u32[]{:S(2)}) collective-permute-start(f32[1016,640]{1,0:T(8,128)S(1)} %pad_maximum_fusion.3), channel_id=1, source_target_pairs={{0,8},{8,16},{16,24},{24,0},{32,40},{40,48},{48,56},{56,32},{64,72... | collective-permute-start | bytes 7802888 | tf_op jit(solution)/shard_map/ppermute | solution.py:467
  438.5 59.5 %collective-permute-start.21 = (f32[1032,640]{1,0:T(8,128)S(1)}, f32[1032,640]{1,0:T(8,128)S(1)}, u32[]{:S(2)}, u32[]{:S(2)}) collective-permute-start(f32[1032,640]{1,0:T(8,128)S(1)} %pad_maximum_fusion.1), channel_id=1, source_target_pairs={{0,32},{8,40},{16,48},{24,56},{32,64},{40,72},{48,80},{56,88},{64,... | collective-permute-start | bytes 7925768 | tf_op jit(solution)/shard_map/ppermute | solution.py:467
  438.8 30.6 %collective-permute-start.27 = (f32[520,640]{1,0:T(8,128)S(1)}, f32[520,640]{1,0:T(8,128)}, u32[]{:S(2)}, u32[]{:S(2)}) collective-permute-start(f32[520,640]{1,0:T(8,128)S(1)} %collective-permute-done.15.refs_3_), channel_id=1, source_target_pairs={{0,96},{8,104},{16,112},{24,120},{32,0},{40,8},{48,16},{56,24},{64... | collective-permute-start | bytes 3993608 | tf_op jit(solution)/shard_map/ppermute | solution.py:467
  442.5 80.9 %collective-permute-start.23 = (f32[1032,640]{1,0:T(8,128)S(1)}, f32[1032,640]{1,0:T(8,128)S(1)}, u32[]{:S(2)}, u32[]{:S(2)}) collective-permute-start(f32[1032,640]{1,0:T(8,128)S(1)} %pad_maximum_fusion.1), channel_id=1, source_target_pairs={{0,96},{8,104},{16,112},{24,120},{32,0},{40,8},{48,16},{56,24},{64... | collective-permute-start | bytes 7925768 | tf_op jit(solution)/shard_map/ppermute | solution.py:467
  443.9 36.5 %collective-permute-start.22 = (f32[1016,640]{1,0:T(8,128)S(1)}, f32[1016,640]{1,0:T(8,128)S(1)}, u32[]{:S(2)}, u32[]{:S(2)}) collective-permute-start(f32[1016,640]{1,0:T(8,128)S(1)} %pad_maximum_fusion.3), channel_id=1, source_target_pairs={{0,24},{8,0},{16,8},{24,16},{32,56},{40,32},{48,40},{56,48},{64,88... | collective-permute-start | bytes 7802888 | tf_op jit(solution)/shard_map/ppermute | solution.py:467
  469.4 117.5 %collective-permute-start.29 = (f32[1032,640]{1,0:T(8,128)S(1)}, f32[1032,640]{1,0:T(8,128)S(1)}, u32[]{:S(2)}, u32[]{:S(2)}) collective-permute-start(f32[1032,640]{1,0:T(8,128)S(1)} %collective-permute-done.9.refs_1_), channel_id=1, source_target_pairs={{0,32},{8,40},{16,48},{24,56},{32,64},{40,72},{48,80},{56,88},{64,... | collective-permute-start | bytes 7925768 | tf_op jit(solution)/shard_map/ppermute | solution.py:467
  474.8 109.7 %collective-permute-start.28 = (f32[1016,640]{1,0:T(8,128)S(1)}, f32[1016,640]{1,0:T(8,128)S(1)}, u32[]{:S(2)}, u32[]{:S(2)}) collective-permute-start(f32[1016,640]{1,0:T(8,128)S(1)} %collective-permute-done.8.refs_0_), channel_id=1, source_target_pairs={{0,8},{8,16},{16,24},{24,0},{32,40},{40,48},{48,56},{56,32},{64,72... | collective-permute-start | bytes 7802888 | tf_op jit(solution)/shard_map/ppermute | solution.py:467
  480.4 102.8 %collective-permute-start.33 = (f32[520,640]{1,0:T(8,128)S(1)}, f32[520,640]{1,0:T(8,128)S(1)}, u32[]{:S(2)}, u32[]{:S(2)}) collective-permute-start(f32[520,640]{1,0:T(8,128)S(1)} %collective-permute-done.15.refs_3_), channel_id=1, source_target_pairs={{0,32},{8,40},{16,48},{24,56},{32,64},{40,72},{48,80},{56,88},{64,... | collective-permute-start | bytes 3993608 | tf_op jit(solution)/shard_map/ppermute | solution.py:467
  498.0 133.2 %collective-permute-start.35 = (f32[1032,640]{1,0:T(8,128)}, f32[1032,640]{1,0:T(8,128)}, u32[]{:S(2)}, u32[]{:S(2)}) collective-permute-start(f32[1032,640]{1,0:T(8,128)} %collective-permute-done.19.refs_1_), channel_id=1, source_target_pairs={{0,96},{8,104},{16,112},{24,120},{32,0},{40,8},{48,16},{56,24},{64... | collective-permute-start | bytes 7925768 | tf_op jit(solution)/shard_map/ppermute | solution.py:467
  523.3 92.9 %collective-permute-start.34 = (f32[1016,640]{1,0:T(8,128)}, f32[1016,640]{1,0:T(8,128)}, u32[]{:S(2)}, u32[]{:S(2)}) collective-permute-start(f32[1016,640]{1,0:T(8,128)} %collective-permute-done.18.refs_0_), channel_id=1, source_target_pairs={{0,24},{8,0},{16,8},{24,16},{32,56},{40,32},{48,40},{56,48},{64,88... | collective-permute-start | bytes 7802888 | tf_op jit(solution)/shard_map/ppermute | solution.py:467
  583.2 3.8 copy-start
  583.2 24.7 %collective-permute-start.38 = (f32[496,640]{1,0:T(8,128)S(1)}, f32[496,640]{1,0:T(8,128)S(1)}, u32[]{:S(2)}, u32[]{:S(2)}) collective-permute-start(f32[496,640]{1,0:T(8,128)S(1)} %slice.46), channel_id=1, source_target_pairs={{0,24},{8,0},{16,8},{24,16},{32,56},{40,32},{48,40},{56,48},{64,88... | collective-permute-start | bytes 3809288 | tf_op jit(solution)/shard_map/ppermute | solution.py:467
  584.5 46.9 %collective-permute-start.36 = (f32[520,640]{1,0:T(8,128)}, f32[520,640]{1,0:T(8,128)}, u32[]{:S(2)}, u32[]{:S(2)}) collective-permute-start(f32[520,640]{1,0:T(8,128)} %slice.44), channel_id=1, source_target_pairs={{0,8},{8,16},{16,24},{24,0},{32,40},{40,48},{48,56},{56,32},{64,72... | collective-permute-start | bytes 3993608 | tf_op jit(solution)/shard_map/ppermute | solution.py:467
  587.0 44.2 %collective-permute-start.39 = (f32[504,640]{1,0:T(8,128)}, f32[504,640]{1,0:T(8,128)}, u32[]{:S(2)}, u32[]{:S(2)}) collective-permute-start(f32[504,640]{1,0:T(8,128)} %slice.47), channel_id=1, source_target_pairs={{0,96},{8,104},{16,112},{24,120},{32,0},{40,8},{48,16},{56,24},{64... | collective-permute-start | bytes 3870728 | tf_op jit(solution)/shard_map/ppermute | solution.py:467
  607.9 4.1 copy-start.6
  607.9 40.7 %collective-permute-start.37 = (f32[528,640]{1,0:T(8,128)}, f32[528,640]{1,0:T(8,128)}, u32[]{:S(2)}, u32[]{:S(2)}) collective-permute-start(f32[528,640]{1,0:T(8,128)} %slice.45), channel_id=1, source_target_pairs={{0,32},{8,40},{16,48},{24,56},{32,64},{40,72},{48,80},{56,88},{64,... | collective-permute-start | bytes 4055048 | tf_op jit(solution)/shard_map/ppermute | solution.py:467
  612.0 10.3 %copy-start.3 = (f32[512,640]{1,0:T(8,128)S(1)}, f32[512,640]{1,0:T(8,128)}, u32[]{:S(2)}) copy-start(f32[512,640]{1,0:T(8,128)} %copy-done.2) | copy-start | bytes 3932164
  616.2 48.4 %collective-permute-start.43 = (f32[520,640]{1,0:T(8,128)}, f32[520,640]{1,0:T(8,128)}, u32[]{:S(2)}, u32[]{:S(2)}) collective-permute-start(f32[520,640]{1,0:T(8,128)} %collective-permute-done.27.refs_3_), channel_id=1, source_target_pairs={{0,96},{8,104},{16,112},{24,120},{32,0},{40,8},{48,16},{56,24},{64... | collective-permute-start | bytes 3993608 | tf_op jit(solution)/shard_map/ppermute | solution.py:467
  631.2 25.1 %collective-permute-start.40 = (f32[512,640]{1,0:T(8,128)}, f32[512,640]{1,0:T(8,128)}, u32[]{:S(2)}, u32[]{:S(2)}) collective-permute-start(f32[512,640]{1,0:T(8,128)} %collective-permute-done.30.refs_0_), channel_id=1, source_target_pairs={{0,8},{8,16},{16,24},{24,0},{32,40},{40,48},{48,56},{56,32},{64,72... | collective-permute-start | bytes 3932168 | tf_op jit(solution)/shard_map/ppermute | solution.py:467
  631.3 33.3 %collective-permute-start.41 = (f32[512,640]{1,0:T(8,128)}, f32[512,640]{1,0:T(8,128)}, u32[]{:S(2)}, u32[]{:S(2)}) collective-permute-start(f32[512,640]{1,0:T(8,128)} %collective-permute-done.31.refs_1_), channel_id=1, source_target_pairs={{0,32},{8,40},{16,48},{24,56},{32,64},{40,72},{48,80},{56,88},{64,... | collective-permute-start | bytes 3932168 | tf_op jit(solution)/shard_map/ppermute | solution.py:467
  631.4 23.7 %collective-permute-start.42 = (f32[504,640]{1,0:T(8,128)}, f32[504,640]{1,0:T(8,128)}, u32[]{:S(2)}, u32[]{:S(2)}) collective-permute-start(f32[504,640]{1,0:T(8,128)} %collective-permute-done.26.refs_2_), channel_id=1, source_target_pairs={{0,24},{8,0},{16,8},{24,16},{32,56},{40,32},{48,40},{56,48},{64,88... | collective-permute-start | bytes 3870728 | tf_op jit(solution)/shard_map/ppermute | solution.py:467
  643.9 4.8 copy-start.7
  (4 other events, 8.4 us)
